TPU v7x, 32 devices: a whole 2x2x4 slice. The times are simulated.
32 devices in a mesh: dp: 8 (over z, y), mp: 4 (over x, core).
Axes of the slice: x: 2, y: 2, z: 4, core: 2. Of those that a mesh axis runs over, the one named last changes fastest.
Arguments:
- tokens: bfloat16 [32768, 768], P(('dp', 'mp')), may hold values from -6 to 6
- cotangent: bfloat16 [32768, 768], P(('dp', 'mp')), may hold values from -6 to 6
- prompts: float32 [50, 768], replicated, may hold values from -6 to 6
- segments: int32 [32768], P(('dp', 'mp')), may hold values from 0 to 6, as said below
- prompt_slot_index: int32 [32768], P(('dp', 'mp')), may hold values from 0 to 50, as said below
- norm_gain: float32 [2, 768], replicated, may hold values from 0.5 to 1.5
- norm_shift: float32 [2, 768], replicated, may hold values from -2 to 2
- attn_qkv: bfloat16 [3, 768, 768], P(None, ('dp', 'mp')), may hold values from -0.21875 to 0.21875
- attn_bias: float32 [3, 768], replicated, may hold values from -2 to 2
- attn_out: bfloat16 [768, 768], P(('dp', 'mp')), may hold values from -0.625 to 0.625
- mlp_weight: bfloat16 [2, 768, 3072], P(None, 'dp', 'mp'), may hold values from -0.21875 to 0.21875
- mlp_bias_up: float32 [3072], replicated, may hold values from -2 to 2
- mlp_bias_down: float32 [768], replicated, may hold values from -2 to 2
Outputs:
- block_output: bfloat16 [32768, 768], P(('dp', 'mp'))
- input_grad: float32 [32768, 768], P(('dp', 'mp'))
- prompt_grad: float32 [50, 768], replicated
- gain_grad: float32 [2, 768], replicated
- shift_grad: float32 [2, 768], replicated
- qkv_grad: float32 [3, 768, 768], P(None, ('dp', 'mp'))
- attn_bias_grad: float32 [3, 768], replicated
- attn_out_grad: float32 [768, 768], P(('dp', 'mp'))
- mlp_grad: float32 [2, 768, 3072], P(None, 'dp', 'mp')
- up_bias_grad: float32 [3072], replicated
- down_bias_grad: float32 [768], replicated
Inputs may be any that keep to these rules, and one draw needn't show every extreme that they name: Every packed row holds images of one size: from the row's start, as many whole segments of 151, of 247 or of 627 tokens as fit, numbered from 0, then one segment of the remaining tokens. Row 0 holds the smallest images. `prompt_slot_index`: in each image segment, tokens 1 to 50 carry slots 0 to 49; all other tokens carry 50.
All inputs are finite; a program needn't handle non-finite values.
Results may differ from a plain program's by a relative error of at most 0.014.
Values may be sent and summed in bfloat16 or wider, within the bound.
No kernel may reach another device: no remote copies, remote signals or barrier semaphores. Data moves between devices by JAX's collectives and lax.ppermute only.
A program may use at most 256 MiB of HBM per device.

v0:
```python
from functools import partial

import jax
import jax.numpy as jnp
from jax import lax
from jax.sharding import PartitionSpec as P

HEAD_SIZE = 64
NPROMPT = 50
PACKED_ROW_LENGTH = 1024


EPS = 1e-06
HIGHEST = lax.Precision.HIGHEST
MASKED = -1e30


def layer_norm(value_list, gain_row, shift_row):
    centre = jnp.mean(value_list, axis=-1, keepdims=True)
    centred = value_list - centre
    spread = jnp.mean(centred * centred, axis=-1, keepdims=True)
    return centred * lax.rsqrt(spread + EPS) * gain_row + shift_row


def gelu_exact(value_list):
    return jax.nn.gelu(value_list, approximate=False)


def masked_scores(query_tile, key_heads, seg_tile, seg_row, factor):
    scores = (
        jnp.einsum("qhd,khd->hqk", query_tile, key_heads, preferred_element_type=jnp.float32)
        * factor
    )
    allowed = seg_tile[:, None] == seg_row[None, :]
    return jnp.where(allowed[None], scores, MASKED)


def attend_forward(packed, tile_row_list):
    query_heads, key_heads, value_heads, seg_row = packed
    factor = query_heads.shape[2] ** (-0.5)

    def one_tile(tile_number):
        first_row = tile_number * tile_row_list
        query_tile = lax.dynamic_slice_in_dim(query_heads, first_row, tile_row_list, 0)
        seg_tile = lax.dynamic_slice_in_dim(seg_row, first_row, tile_row_list, 0)
        scores = masked_scores(query_tile, key_heads, seg_tile, seg_row, factor)
        row_peak = jnp.max(scores, axis=-1, keepdims=True)
        raised = jnp.exp(scores - row_peak)
        totals_row = jnp.sum(raised, axis=-1, keepdims=True)
        weights = (raised / totals_row).astype(jnp.bfloat16)
        mixed = jnp.einsum("hqk,khd->qhd", weights, value_heads, preferred_element_type=jnp.float32)
        return (mixed.astype(jnp.bfloat16), (row_peak + jnp.log(totals_row))[:, :, 0])

    return lax.map(one_tile, jnp.arange(query_heads.shape[0] // tile_row_list))


def attend_backward(packed, tile_row_list):
    query_heads, key_heads, value_heads, seg_row, log_sums, grad_heads = packed
    length, head_count, head_width = key_heads.shape
    factor = head_width ** (-0.5)

    def one_tile(running, tile_number):
        grad_keys, grad_values = running
        first_row = tile_number * tile_row_list
        query_tile = lax.dynamic_slice_in_dim(query_heads, first_row, tile_row_list, 0)
        seg_tile = lax.dynamic_slice_in_dim(seg_row, first_row, tile_row_list, 0)
        grad_tile = lax.dynamic_slice_in_dim(grad_heads, first_row, tile_row_list, 0)
        scores = masked_scores(query_tile, key_heads, seg_tile, seg_row, factor)
        weights = jnp.exp(scores - log_sums[tile_number][:, :, None])
        grad_weights = jnp.einsum(
            "qhd,khd->hqk", grad_tile, value_heads, preferred_element_type=jnp.float32
        )
        weighted = jnp.sum(weights * grad_weights, axis=-1, keepdims=True)
        grad_scores = (weights * (grad_weights - weighted)).astype(jnp.bfloat16)
        grad_query = (
            jnp.einsum("hqk,khd->qhd", grad_scores, key_heads, preferred_element_type=jnp.float32)
            * factor
        )
        grad_keys = (
            grad_keys
            + jnp.einsum(
                "hqk,qhd->khd", grad_scores, query_tile, preferred_element_type=jnp.float32
            )
            * factor
        )
        grad_values = grad_values + jnp.einsum(
            "hqk,qhd->khd",
            weights.astype(jnp.bfloat16),
            grad_tile,
            preferred_element_type=jnp.float32,
        )
        return ((grad_keys, grad_values), grad_query)

    zeros_heads = jnp.zeros((length, head_count, head_width), jnp.float32)
    (grad_keys, grad_values), grad_queries = lax.scan(
        one_tile, (zeros_heads, zeros_heads), jnp.arange(length // tile_row_list)
    )
    return (grad_queries.reshape(length, head_count, head_width), grad_keys, grad_values)


def split_heads(value_list, row_count_total):
    return value_list.reshape(row_count_total, PACKED_ROW_LENGTH, -1, HEAD_SIZE)


def local(
    tokens,
    cotangent,
    prompts,
    segments,
    prompt_slot_index,
    norm_gain,
    norm_shift,
    attn_qkv,
    attn_bias,
    attn_out,
    mlp_weight,
    mlp_bias_up,
    mlp_bias_down,
):
    token_tally = tokens.shape[0]
    feature_count = tokens.shape[1]
    row_count_total = token_tally // PACKED_ROW_LENGTH
    tile_row_list = min(512, PACKED_ROW_LENGTH)
    qkv_all, out_all = (
        lax.all_gather(attn_qkv, ("dp", "mp"), axis=1, tiled=True),
        lax.all_gather(attn_out, ("dp", "mp"), axis=0, tiled=True),
    )
    mlp_part = lax.all_gather(mlp_weight, "dp", axis=1, tiled=True)
    input_list = tokens.astype(jnp.float32)
    prompt_table = jnp.concatenate([prompts, jnp.zeros((1, feature_count), jnp.float32)], 0)
    onehot = (
        prompt_slot_index[:, None] == jnp.arange(NPROMPT + 1, dtype=jnp.int32)[None, :]
    ).astype(jnp.float32)
    is_prompt = (prompt_slot_index < NPROMPT)[:, None]
    start = jnp.where(is_prompt, jnp.dot(onehot, prompt_table, precision=HIGHEST), input_list)
    normed_one = layer_norm(start, norm_gain[0], norm_shift[0]).astype(jnp.bfloat16)
    projected = jnp.einsum("td,cde->cte", normed_one, qkv_all, preferred_element_type=jnp.float32)
    queries = (projected[0] + attn_bias[0]).astype(jnp.bfloat16)
    key_rows = projected[1].astype(jnp.bfloat16)
    value_rows = (projected[2] + attn_bias[1]).astype(jnp.bfloat16)
    segment_row_list = segments.reshape(row_count_total, PACKED_ROW_LENGTH)
    query_split = split_heads(queries, row_count_total)
    key_split = split_heads(key_rows, row_count_total)
    value_split = split_heads(value_rows, row_count_total)
    mixed, log_sums = lax.map(
        partial(attend_forward, tile_row_list=tile_row_list),
        (query_split, key_split, value_split, segment_row_list),
    )
    mixed = mixed.reshape(token_tally, feature_count)
    middle = start + jnp.dot(mixed, out_all, preferred_element_type=jnp.float32) + attn_bias[2]
    normed_two = layer_norm(middle, norm_gain[1], norm_shift[1]).astype(jnp.bfloat16)
    grad_output = cotangent.astype(jnp.float32)
    grad_down = jnp.sum(grad_output, axis=0)
    gathered = lax.all_gather(normed_two, "mp", axis=0, tiled=True)
    unit_count = mlp_part.shape[2]
    offset = lax.axis_index("mp") * unit_count
    bias_part = lax.dynamic_slice_in_dim(mlp_bias_up, offset, unit_count, 0)
    before = jnp.dot(gathered, mlp_part[0], preferred_element_type=jnp.float32) + bias_part
    hidden = gelu_exact(before).astype(jnp.bfloat16)
    piece = hidden
    branch = lax.psum_scatter(
        jnp.einsum("tf,df->td", piece, mlp_part[1], preferred_element_type=jnp.float32).astype(
            jnp.bfloat16
        ),
        "mp",
        scatter_dimension=0,
        tiled=True,
    ).astype(jnp.float32)
    output = middle + branch + mlp_bias_down
    grad_gathered = lax.all_gather(cotangent, "mp", axis=0, tiled=True)
    grad_hidden = jnp.dot(grad_gathered, mlp_part[1], preferred_element_type=jnp.float32)
    before_out, gelu_pull = jax.vjp(gelu_exact, before)
    grad_before = gelu_pull(grad_hidden)[0].astype(jnp.bfloat16)
    grad_mlp = jnp.stack(
        [
            jnp.einsum("td,tf->df", gathered, grad_before, preferred_element_type=jnp.float32),
            jnp.einsum("td,tf->df", grad_gathered, hidden, preferred_element_type=jnp.float32),
        ]
    )
    grad_up = lax.dynamic_update_slice_in_dim(
        jnp.zeros_like(mlp_bias_up), jnp.sum(grad_before.astype(jnp.float32), axis=0), offset, 0
    )
    piece = grad_before
    grad_normed_two = lax.psum_scatter(
        jnp.einsum("tf,df->td", piece, mlp_part[0], preferred_element_type=jnp.float32).astype(
            jnp.bfloat16
        ),
        "mp",
        scatter_dimension=0,
        tiled=True,
    ).astype(jnp.float32)
    mlp_grad = lax.psum_scatter(grad_mlp, "dp", scatter_dimension=1, tiled=True)
    norm_out_two, pull_two = jax.vjp(layer_norm, middle, norm_gain[1], norm_shift[1])
    grad_from_two, grad_gain_two, grad_shift_two = pull_two(grad_normed_two)
    grad_middle = grad_output + grad_from_two
    grad_branch = grad_middle.astype(jnp.bfloat16)
    grad_bias_out = jnp.sum(grad_branch.astype(jnp.float32), axis=0)
    grad_out_weight = jnp.einsum(
        "td,te->de", mixed, grad_branch, preferred_element_type=jnp.float32
    )
    grad_mixed = jnp.einsum(
        "te,de->td", grad_branch, out_all, preferred_element_type=jnp.float32
    ).astype(jnp.bfloat16)
    grad_queries, grad_keys, grad_values = lax.map(
        partial(attend_backward, tile_row_list=tile_row_list),
        (
            query_split,
            key_split,
            value_split,
            segment_row_list,
            log_sums,
            split_heads(grad_mixed, row_count_total),
        ),
    )
    grad_projected = jnp.stack(
        [
            grad_queries.reshape(token_tally, feature_count),
            grad_keys.reshape(token_tally, feature_count),
            grad_values.reshape(token_tally, feature_count),
        ]
    ).astype(jnp.bfloat16)
    grad_qkv = jnp.einsum(
        "td,cte->cde", normed_one, grad_projected, preferred_element_type=jnp.float32
    )
    grad_attn_bias = jnp.stack(
        [
            jnp.sum(grad_projected[0].astype(jnp.float32), axis=0),
            jnp.sum(grad_projected[2].astype(jnp.float32), axis=0),
            grad_bias_out,
        ]
    )
    grad_normed_one = jnp.einsum(
        "cte,cde->td", grad_projected, qkv_all, preferred_element_type=jnp.float32
    )
    norm_out_one, pull_one = jax.vjp(layer_norm, start, norm_gain[0], norm_shift[0])
    grad_from_one, grad_gain_one, grad_shift_one = pull_one(grad_normed_one)
    grad_start = grad_middle + grad_from_one
    input_grad = jnp.where(is_prompt, 0.0, grad_start)
    grad_prompts = jnp.dot(onehot.T, grad_start, precision=HIGHEST)[:NPROMPT]
    qkv_grad, out_grad = (
        lax.psum_scatter(grad_qkv, ("dp", "mp"), scatter_dimension=1, tiled=True),
        lax.psum_scatter(grad_out_weight, ("dp", "mp"), scatter_dimension=0, tiled=True),
    )
    summed = lax.psum(
        (
            grad_prompts,
            jnp.stack([grad_gain_one, grad_gain_two]),
            jnp.stack([grad_shift_one, grad_shift_two]),
            grad_attn_bias,
            grad_up,
            grad_down,
        ),
        ("dp", "mp"),
    )
    return (
        output.astype(jnp.bfloat16),
        input_grad,
        summed[0],
        summed[1],
        summed[2],
        qkv_grad,
        summed[3],
        out_grad,
        mlp_grad,
        summed[4],
        summed[5],
    )


def solution(mesh):
    return jax.shard_map(
        local,
        mesh=mesh,
        in_specs=(
            P(("dp", "mp"), None),
            P(("dp", "mp"), None),
            P(),
            P(("dp", "mp")),
            P(("dp", "mp")),
            P(),
            P(),
            P(None, ("dp", "mp"), None),
            P(),
            P(("dp", "mp"), None),
            P(None, "dp", "mp"),
            P(),
            P(),
        ),
        out_specs=(
            P(("dp", "mp"), None),
            P(("dp", "mp"), None),
            P(),
            P(),
            P(),
            P(None, ("dp", "mp"), None),
            P(),
            P(("dp", "mp"), None),
            P(None, "dp", "mp"),
            P(),
            P(),
        ),
        check_vma=False,
    )
```

profile of v0, /device:TPU:16, one launch (start us, length us, event | category | flops | bytes accessed | tf_op | source)
XLA Modules:
  0.0 1015.9 jit_solution(4451620781767088363)
XLA Ops:
  14.5 2.6 copy.58
  17.1 3.2 fusion.59
  21.6 49.0 %all-gather.6.cloned.1.call-done = bf16[3,768,768]{2,1,0:T(8,128)(2,1)} async-done(((bf16[3,24,768]{2,1,0:T(8,128)(2,1)}), bf16[3,768,768]{2,1,0:T(8,128)(2,1)}) %all-gather.6.cloned.1.call-update) | async-done | bytes 3538960 | tf_op jit(solution)/shard_map/all_gather | solution.py:125
  70.6 6.2 convolution_bitcast_fusion
  79.8 73.1 %while.47 = (s32[]{:T(128)}, bf16[2,512,12,64]{1,3,2,0:T(8,128)(2,1)}, f32[2,12,512]{2,1,0:T(8,128)S(1)}, s32[2]{0:T(128)S(1)}, s32[1024]{0:T(1024)S(1)}, /*inde...) while((s32[]{:T(128)}, ...), condition=%wide.region_5.6_spmd, body=%wide.region_2.5_spmd.sunk | while | flops 1687021568 | bytes 189499632 | solution.py:54
  81.6 10.6 %fusion.103 = (f32[12,512]{1,0:T(8,128)S(1)}, f32[12,512,1024]{2,1,0:T(8,128)}) fusion(pred[512,1024]{1,0:T(8,128)(4,1)S(1)} %broadcast_compare_fusion.5, bf16[1024,12,64]{0,2,1:T(8,128)(2,1)S(1)} %get-tuple-element.478, bf16[1024,12,64]{0,2,1:T(8,128)(2,1)S(1)} %get-tuple-element.477, s32[]{:T(128)S(6)} %select_n.77), kind=kOutput, calls=%fused_computation.3.clone.1 | convolution fusion | flops 824174592 | bytes 28073988 | tf_op jit(solution)/shard_map/while/body/eval_jaxpr/while/body/eval_jaxpr/qhd,khd->hqk/dot_general | solution.py:31
  92.3 12.3 %fusion.104 = f32[12,512]{1,0:T(8,128)S(1)} fusion(f32[12,512,1024]{2,1,0:T(8,128)} %get-tuple-element.433, f32[12,512]{1,0:T(8,128)S(1)} %get-tuple-element.434, pred[512,1024]{1,0:T(8,128)(4,1)S(1)} %broadcast_compare_fusion.5), kind=kLoop, calls=%fused_computation.4.clone.1 | loop fusion | flops 25159680 | bytes 25739264 | tf_op jit(solution)/shard_map/while/body/eval_jaxpr/while/body/eval_jaxpr/reduce_sum | solution.py:49
  104.6 3.1 copy-done
  107.7 8.5 fusion.105
  117.9 10.7 %fusion.103 = (f32[12,512]{1,0:T(8,128)S(1)}, f32[12,512,1024]{2,1,0:T(8,128)}) fusion(pred[512,1024]{1,0:T(8,128)(4,1)S(1)} %broadcast_compare_fusion.5, bf16[1024,12,64]{0,2,1:T(8,128)(2,1)S(1)} %get-tuple-element.478, bf16[1024,12,64]{0,2,1:T(8,128)(2,1)S(1)} %get-tuple-element.477, s32[]{:T(128)S(6)} %select_n.77), kind=kOutput, calls=%fused_computation.3.clone.1 | convolution fusion | flops 824174592 | bytes 28073988 | tf_op jit(solution)/shard_map/while/body/eval_jaxpr/while/body/eval_jaxpr/qhd,khd->hqk/dot_general | solution.py:31
  128.6 12.5 %fusion.104 = f32[12,512]{1,0:T(8,128)S(1)} fusion(f32[12,512,1024]{2,1,0:T(8,128)} %get-tuple-element.433, f32[12,512]{1,0:T(8,128)S(1)} %get-tuple-element.434, pred[512,1024]{1,0:T(8,128)(4,1)S(1)} %broadcast_compare_fusion.5), kind=kLoop, calls=%fused_computation.4.clone.1 | loop fusion | flops 25159680 | bytes 25739264 | tf_op jit(solution)/shard_map/while/body/eval_jaxpr/while/body/eval_jaxpr/reduce_sum | solution.py:49
  141.2 3.2 copy-done
  144.4 8.5 fusion.105
  152.9 4.2 copy.60
  158.8 4.3 fusion.60
  167.9 12.3 %all-gather.12.cloned.1.call-done = bf16[2,768,768]{2,1,0:T(8,128)(2,1)} async-done(((bf16[2,96,768]{2,1,0:T(8,128)(2,1)}), bf16[2,768,768]{2,1,0:T(8,128)(2,1)}) %all-gather.12.cloned.1.call-update) | async-done | bytes 2359312 | tf_op jit(solution)/shard_map/all_gather | solution.py:128
  180.1 47.5 %all-gather.10.cloned.1.call-done = bf16[4096,768]{0,1:T(8,128)(2,1)} async-done(((bf16[1024,768]{0,1:T(8,128)(2,1)}), bf16[4096,768]{0,1:T(8,128)(2,1)}) %all-gather.10.cloned.1.call-update) | async-done | bytes 6291472 | tf_op jit(solution)/shard_map/all_gather | solution.py:154
  227.6 35.6 %multiply_convert_fusion.1 = (bf16[4096,768]{1,0:T(8,128)(2,1)}, f32[4096,768]{1,0:T(8,128)}, f32[4096,768]{1,0:T(8,128)}) fusion(f32[768]{0:T(1024)S(1)} %dynamic_slice.51, bf16[4096,768]{0,1:T(8,128)(2,1)} %all-gather.10.cloned.1.call-done, bf16[2,768,768]{2,1,0:T(8,128)(2,1)} %all-gather.12.cloned.1.call-done), kind=kOutput, calls=%fused_computation.43 | convolution fusion | flops 5039456256 | bytes 38931456 | tf_op jit(solution)/shard_map/dot_general | solution.py:158
  263.2 12.1 %all-gather.14.cloned.1.call-done = bf16[4096,768]{1,0:T(8,128)(2,1)} async-done(((bf16[1024,768]{1,0:T(8,128)(2,1)}), bf16[4096,768]{1,0:T(8,128)(2,1)}) %all-gather.14.cloned.1.call-update) | async-done | bytes 6291472 | tf_op jit(solution)/shard_map/all_gather | solution.py:170
  275.4 15.2 %convert_reduce_fusion = (f32[768]{0:T(1024)}, bf16[4096,768]{1,0:T(8,128)(2,1)S(1)}) fusion(f32[4096,768]{1,0:T(8,128)} %get-tuple-element.303, bf16[4096,768]{1,0:T(8,128)(2,1)} %all-gather.14.cloned.1.call-done, bf16[2,768,768]{2,1,0:T(8,128)(2,1)S(1)} %copy-done.65, f32[4096,768]{1,0:T(8,128)} %get-tuple-element.317, f32[768]{0:T(1024)S(1)} %dynamic_slice.51), kind=kOutput, calls=%fused_computation.41 | convolution fusion | flops 4885314560 | bytes 38935552 | tf_op jit(solution)/shard_map/dot_general | solution.py:171
  290.6 2.6 copy-done.67
  293.2 6.9 convolution_convert_fusion
  304.1 9.5 convolution_convert_fusion.1
  313.7 44.5 %reduce-scatter.7.cloned.1.call-done = bf16[1024,768]{0,1:T(8,128)(2,1)} async-done(((bf16[4096,768]{0,1:T(8,128)(2,1)}), bf16[1024,768]{0,1:T(8,128)(2,1)}) %reduce-scatter.7.cloned.1.call-update) | async-done | bytes 1572880 | tf_op jit(solution)/shard_map/reduce_scatter | solution.py:184
  358.2 3.1 convert_reduce_fusion.1
  361.4 2.2 fusion.38
  363.6 2.0 convert_reduce_fusion.3
  365.7 2.6 convolution_convert_fusion.2
  368.3 175.1 %while.48 = (s32[]{:T(128)}, f32[1024,12,64]{0,2,1:T(8,128)}, f32[1024,12,64]{0,2,1:T(8,128)}, bf16[2,512,12,64]{1,3,2,0:T(8,128)(2,1)}, s32[2]{0:T(128)S(1)}, /...) while((s32[]{:T(128)}, f32[1024,12,64]{0,2,1:T(8,128)}, ...), condition=%wide.region_14.15_spmd.clone, body=%wide.region_12.14_spmd.clone.sunk | while | flops 4125747200 | bytes 225634640 | solution.py:95
  372.2 12.1 %fusion.115 = f32[12,512,1024]{2,1,0:T(8,128)} fusion(bf16[1024,12,64]{0,2,1:T(8,128)(2,1)S(1)} %get-tuple-element.523, bf16[1024,12,64]{0,2,1:T(8,128)(2,1)} %get-tuple-element.521, s32[]{:T(128)S(6)} %select_n.81), kind=kOutput, calls=%fused_computation.30.clone.1 | convolution fusion | flops 805306368 | bytes 27525124 | tf_op jit(solution)/shard_map/while/body/eval_jaxpr/while/body/eval_jaxpr/qhd,khd->hqk/dot_general | solution.py:31
  384.3 13.3 %bitcast_add_fusion.5 = f32[1024,12,64]{0,2,1:T(8,128)} fusion(f32[1024,12,64]{0,2,1:T(8,128)} %get-tuple-element.502, f32[12,512,1024]{2,1,0:T(8,128)} %fusion.115, f32[12,512]{1,0:T(8,128)S(1)} %dynamic-slice_bitcast_fusion.2, pred[512,1024]{1,0:T(8,128)(4,1)S(1)} %broadcast_compare_fusion.6, pred[]{:T(512)S(6)} %compare.4, ...), kind=kOutput, calls=%fused_computation.22.clone.1 | convolution fusion | flops 832045056 | bytes 32800772 | tf_op jit(solution)/shard_map/while/body/eval_jaxpr/while/body/eval_jaxpr/hqk,qhd->khd/dot_general | solution.py:86
  397.6 18.3 %multiply_reduce_fusion.6 = (f32[12,512]{1,0:T(8,128)S(1)}, f32[12,512,1024]{2,1,0:T(8,128)}) fusion(f32[12,512,1024]{2,1,0:T(8,128)} %fusion.115, f32[12,512]{1,0:T(8,128)S(1)} %dynamic-slice_bitcast_fusion.2, pred[512,1024]{1,0:T(8,128)(4,1)S(1)} %broadcast_compare_fusion.6, bf16[1024,12,64]{0,2,1:T(8,128)(2,1)} %get-tuple-element.526, ...), kind=kOutput, calls=%fused_computation.17.clone.1 | convolution fusion | flops 836757504 | bytes 53264388 | tf_op jit(solution)/shard_map/while/body/eval_jaxpr/while/body/eval_jaxpr/qhd,khd->hqk/dot_general | solution.py:70
  415.9 21.4 %multiply_convert_fusion.3 = bf16[12,512,1024]{2,1,0:T(8,128)(2,1)} fusion(f32[12,512,1024]{2,1,0:T(8,128)} %get-tuple-element.446, f32[12,512,1024]{2,1,0:T(8,128)} %fusion.115, f32[12,512]{1,0:T(8,128)S(1)} %get-tuple-element.447, f32[12,512]{1,0:T(8,128)S(1)} %dynamic-slice_bitcast_fusion.2, pred[512,1024]{1,0:T(8,128)(4,1)S(1)} %broadcast_compare_fusion.6), kind=kLoop, calls=%fused_computation.16.clone.1 | loop fusion | flops 37748736 | bytes 63488000 | tf_op jit(solution)/shard_map/while/body/eval_jaxpr/while/body/eval_jaxpr/convert_element_type | solution.py:74
  437.3 9.5 bitcast_dynamic-update-slice_fusion.5
  446.8 8.6 bitcast_add_fusion.4
  459.0 11.5 %fusion.115 = f32[12,512,1024]{2,1,0:T(8,128)} fusion(bf16[1024,12,64]{0,2,1:T(8,128)(2,1)S(1)} %get-tuple-element.523, bf16[1024,12,64]{0,2,1:T(8,128)(2,1)} %get-tuple-element.521, s32[]{:T(128)S(6)} %select_n.81), kind=kOutput, calls=%fused_computation.30.clone.1 | convolution fusion | flops 805306368 | bytes 27525124 | tf_op jit(solution)/shard_map/while/body/eval_jaxpr/while/body/eval_jaxpr/qhd,khd->hqk/dot_general | solution.py:31
  470.4 14.2 %bitcast_add_fusion.5 = f32[1024,12,64]{0,2,1:T(8,128)} fusion(f32[1024,12,64]{0,2,1:T(8,128)} %get-tuple-element.502, f32[12,512,1024]{2,1,0:T(8,128)} %fusion.115, f32[12,512]{1,0:T(8,128)S(1)} %dynamic-slice_bitcast_fusion.2, pred[512,1024]{1,0:T(8,128)(4,1)S(1)} %broadcast_compare_fusion.6, pred[]{:T(512)S(6)} %compare.4, ...), kind=kOutput, calls=%fused_computation.22.clone.1 | convolution fusion | flops 832045056 | bytes 32800772 | tf_op jit(solution)/shard_map/while/body/eval_jaxpr/while/body/eval_jaxpr/hqk,qhd->khd/dot_general | solution.py:86
  484.7 18.1 %multiply_reduce_fusion.6 = (f32[12,512]{1,0:T(8,128)S(1)}, f32[12,512,1024]{2,1,0:T(8,128)}) fusion(f32[12,512,1024]{2,1,0:T(8,128)} %fusion.115, f32[12,512]{1,0:T(8,128)S(1)} %dynamic-slice_bitcast_fusion.2, pred[512,1024]{1,0:T(8,128)(4,1)S(1)} %broadcast_compare_fusion.6, bf16[1024,12,64]{0,2,1:T(8,128)(2,1)} %get-tuple-element.526, ...), kind=kOutput, calls=%fused_computation.17.clone.1 | convolution fusion | flops 836757504 | bytes 53264388 | tf_op jit(solution)/shard_map/while/body/eval_jaxpr/while/body/eval_jaxpr/qhd,khd->hqk/dot_general | solution.py:70
  502.8 21.2 %multiply_convert_fusion.3 = bf16[12,512,1024]{2,1,0:T(8,128)(2,1)} fusion(f32[12,512,1024]{2,1,0:T(8,128)} %get-tuple-element.446, f32[12,512,1024]{2,1,0:T(8,128)} %fusion.115, f32[12,512]{1,0:T(8,128)S(1)} %get-tuple-element.447, f32[12,512]{1,0:T(8,128)S(1)} %dynamic-slice_bitcast_fusion.2, pred[512,1024]{1,0:T(8,128)(4,1)S(1)} %broadcast_compare_fusion.6), kind=kLoop, calls=%fused_computation.16.clone.1 | loop fusion | flops 37748736 | bytes 63488000 | tf_op jit(solution)/shard_map/while/body/eval_jaxpr/while/body/eval_jaxpr/convert_element_type | solution.py:74
  524.0 9.5 bitcast_dynamic-update-slice_fusion.5
  533.5 9.5 bitcast_add_fusion.4
  543.4 4.2 copy.64
  547.6 4.0 stack_reshape.12
  551.6 2.6 copy.65
  555.6 2.6 copy.66
  558.2 3.4 convert_reduce_fusion.4
  561.5 2.6 copy.67
  564.2 9.4 convolution_bitcast_fusion.1
  573.6 11.0 %copy.72 = f32[3,768,768]{2,0,1:T(4,128)} copy(f32[3,768,768]{1,2,0:T(8,128)} %convolution_bitcast_fusion.1) | data formatting | bytes 14155776 | tf_op jit(solution)/shard_map/td,cte->cde/transpose | solution.py:222
  584.6 9.0 fusion.61
  593.5 3.9 copy.68
  597.4 3.0 multiply_reduce_fusion.1
  605.2 3.8 fusion.45
  609.1 9.1 convolution_bitcast_fusion.2
  618.1 9.1 convolution_bitcast_fusion.3
  627.3 2.5 pad_maximum_fusion.1
  629.9 4.8 fusion.62
  635.3 1.7 convert_reduce_fusion.5
  637.0 5.9 broadcast_select_fusion
  643.0 3.7 copy.75
  648.2 41.4 %all-reduce.2 = (f32[2,768]{1,0:T(2,128)}, f32[2,768]{1,0:T(2,128)}, f32[3,768]{1,0:T(4,128)}, f32[3072]{0:T(1024)}, f32[768]{0:T(1024)}) all-reduce(f32[2,768]{1,0:T(2,128)S(1)} %pad_maximum_fusion.7, f32[2,768]{1,0:T(2,128)S(1)} %pad_maximum_fusion.8, ...), channel_id=1, replica_groups=mesh['dp'=8,'mp'=4] {'dp','mp'}, use_global_device_ids=true, to_apply=%region_20.21 | all-reduce | flops 9216 | bytes 73728 | tf_op jit(solution)/shard_map/psum | solution.py:244
  689.6 113.7 %all-reduce.6.cloned.1.call-done = (f32[50,768]{1,0:T(8,128)}, f32[3,768,768]{2,0,1:T(4,128)}) async-done(((f32[50,768]{1,0:T(8,128)}, f32[3,768,768]{2,0,1:T(4,128)}), (f32[50,768]{1,0:T(8,128)}, f32[3,768,768]{2,0,1:T(4,128)})) %all-reduce.6.cloned.1.call-update) | async-done | bytes 7231504 | tf_op jit(solution)/shard_map/psum | solution.py:244
  805.1 97.9 %reduce-scatter.11.cloned.1.call-done = f32[2,96,768]{2,1,0:T(8,128)} async-done(((f32[2,768,768]{2,1,0:T(8,128)}), f32[2,96,768]{2,1,0:T(8,128)}) %reduce-scatter.11.cloned.1.call-update) | async-done | bytes 589840 | tf_op jit(solution)/shard_map/reduce_scatter | solution.py:192
  903.0 104.3 %reduce-scatter.9.cloned.1.call-done = f32[24,768]{1,0:T(8,128)} async-done(((f32[768,768]{1,0:T(8,128)}), f32[24,768]{1,0:T(8,128)}) %reduce-scatter.9.cloned.1.call-update) | async-done | bytes 73744 | tf_op jit(solution)/shard_map/reduce_scatter | solution.py:242
  (228 shorter events, 37.7 us)
Async XLA Ops:
  7.2 9.9 copy-start.50
  7.2 9.9 copy-start.30
  7.2 63.4 %all-gather.6.cloned.1.call-start = ((), (), s32[]{:S(2)}) async-start(), calls=%async_computation.4 | async-start | bytes 3649536 | tf_op jit(solution)/shard_map/all_gather | solution.py:125
  7.9 150.8 %all-gather.8.cloned.1.call-start = ((), (), s32[]{:S(2)}) async-start(), calls=%async_computation.5 | async-start | bytes 1216512 | tf_op jit(solution)/shard_map/all_gather | solution.py:126
  8.7 171.5 %all-gather.12.cloned.1.call-start = ((), (), s32[]{:S(2)}) async-start(), calls=%async_computation.7 | async-start | bytes 2654208 | tf_op jit(solution)/shard_map/all_gather | solution.py:128
  9.4 218.2 %all-gather.10.cloned.1.call-start = ((), (), s32[]{:S(2)}) async-start(), calls=%async_computation.6 | async-start | bytes 7864320 | tf_op jit(solution)/shard_map/all_gather | solution.py:154
  10.2 10.1 copy-start.58
  11.6 59.1 %copy-start.46 = (f32[768]{0:T(1024)}, f32[768]{0:T(1024)S(1)}, u32[]{:S(2)}) copy-start(f32[768]{0:T(1024)S(1)} %get-tuple-element.248) | copy-start | bytes 9220
  12.9 57.7 %copy-start.60 = (f32[768]{0:T(1024)}, f32[768]{0:T(1024)S(1)}, u32[]{:S(2)}) copy-start(f32[768]{0:T(1024)S(1)} %get-tuple-element.250) | copy-start | bytes 9220
  20.3 50.3 %copy-start.10 = (f32[1024,768]{0,1:T(8,128)}, f32[1024,768]{0,1:T(8,128)S(1)}, u32[]{:S(2)}) copy-start(f32[1024,768]{0,1:T(8,128)S(1)} %get-tuple-element.314) | copy-start | bytes 9437188
  20.3 56.5 %copy-start.38 = (f32[1024]{0:T(1024)}, f32[1024]{0:T(1024)S(1)}, u32[]{:S(2)}) copy-start(f32[1024]{0:T(1024)S(1)} %broadcast_multiply_fusion.1) | copy-start | bytes 12292
  21.6 55.2 %copy-start.48 = (f32[1024]{0:T(1024)}, f32[1024]{0:T(1024)S(1)}, u32[]{:S(2)}) copy-start(f32[1024]{0:T(1024)S(1)} %fusion.47) | copy-start | bytes 12292
  81.6 22.9 %copy-start.9 = (bf16[1024,12,64]{0,2,1:T(8,128)(2,1)S(1)}, bf16[1024,12,64]{0,2,1:T(8,128)(2,1)}, u32[]{:S(2)}) copy-start(bf16[1024,12,64]{0,2,1:T(8,128)(2,1)} %get-tuple-element.479) | copy-start | bytes 4718596 | tf_op jit(solution)/shard_map/while/body/eval_jaxpr/while
  92.3 15.4 %copy-start = (f32[12,512,1024]{2,1,0:T(8,128)S(1)}, f32[12,512,1024]{2,1,0:T(8,128)}, u32[]{:S(2)}) copy-start(f32[12,512,1024]{2,1,0:T(8,128)} %get-tuple-element.433) | copy-start | bytes 75497472 | tf_op jit(solution)/shard_map/while/body/eval_jaxpr/while
  117.9 23.3 %copy-start.9 = (bf16[1024,12,64]{0,2,1:T(8,128)(2,1)S(1)}, bf16[1024,12,64]{0,2,1:T(8,128)(2,1)}, u32[]{:S(2)}) copy-start(bf16[1024,12,64]{0,2,1:T(8,128)(2,1)} %get-tuple-element.479) | copy-start | bytes 4718596 | tf_op jit(solution)/shard_map/while/body/eval_jaxpr/while
  128.6 15.7 %copy-start = (f32[12,512,1024]{2,1,0:T(8,128)S(1)}, f32[12,512,1024]{2,1,0:T(8,128)}, u32[]{:S(2)}) copy-start(f32[12,512,1024]{2,1,0:T(8,128)} %get-tuple-element.433) | copy-start | bytes 75497472 | tf_op jit(solution)/shard_map/while/body/eval_jaxpr/while
  152.9 5.8 copy-start.1
  152.9 5.8 copy-start.4
  152.9 5.8 copy-start.25
  152.9 5.8 copy-start.63
  166.4 109.0 %all-gather.14.cloned.1.call-start = ((), (), s32[]{:S(2)}) async-start(), calls=%async_computation.9 | async-start | bytes 7864320 | tf_op jit(solution)/shard_map/all_gather | solution.py:170
  167.0 191.2 %reduce-scatter.7.cloned.1.call-start = ((), (), s32[]{:S(2)}) async-start(), calls=%async_computation.10 | async-start | bytes 7864320 | tf_op jit(solution)/shard_map/reduce_scatter | solution.py:184
  180.1 95.3 %copy-start.65 = (bf16[2,768,768]{2,1,0:T(8,128)(2,1)S(1)}, bf16[2,768,768]{2,1,0:T(8,128)(2,1)}, u32[]{:S(2)}) copy-start(bf16[2,768,768]{2,1,0:T(8,128)(2,1)} %all-gather.12.cloned.1.call-done) | copy-start | bytes 7077892
  290.6 2.6 copy-start.67
  300.2 3.0 copy-start.51
  300.2 336.8 %reduce-scatter.5.cloned.1.call-start = ((), (), s32[]{:S(2)}) async-start(), calls=%async_computation.8 | async-start | bytes 7864320 | tf_op jit(solution)/shard_map/reduce_scatter | solution.py:161
  313.6 44.7 %copy-start.7 = (f32[1024,768]{0,1:T(8,128)S(1)}, f32[1024,768]{0,1:T(8,128)}, u32[]{:S(2)}) copy-start(f32[1024,768]{0,1:T(8,128)} %copy-done.6) | copy-start | bytes 9437188
  313.6 44.7 %copy-start.28 = (f32[1024]{0:T(1024)S(1)}, f32[1024]{0:T(1024)}, u32[]{:S(2)}) copy-start(f32[1024]{0:T(1024)} %copy-done.27) | copy-start | bytes 12292
  313.6 44.7 %copy-start.32 = (f32[768]{0:T(1024)S(1)}, f32[768]{0:T(1024)}, u32[]{:S(2)}) copy-start(f32[768]{0:T(1024)} %get-tuple-element.247) | copy-start | bytes 9220
  313.6 47.7 %copy-start.45 = (f32[1024]{0:T(1024)S(1)}, f32[1024]{0:T(1024)}, u32[]{:S(2)}) copy-start(f32[1024]{0:T(1024)} %copy-done.44) | copy-start | bytes 12292
  313.6 47.7 %copy-start.36 = (f32[1024]{0:T(1024)S(1)}, f32[1024]{0:T(1024)}, u32[]{:S(2)}) copy-start(f32[1024]{0:T(1024)} %copy-done.35) | copy-start | bytes 12292
  313.6 489.7 %all-reduce.6.cloned.1.call-start = ((), (), s32[]{:S(2)}) async-start(), calls=%async_computation.13 | async-start | bytes 19218432 | tf_op jit(solution)/shard_map/psum | solution.py:244
  358.2 3.1 copy-start.14
  361.3 4.3 copy-start.40
  365.6 2.6 copy-start.22
  365.6 2.6 copy-start.2
  372.2 12.1 %copy-start.19 = (bf16[1024,12,64]{0,2,1:T(8,128)(2,1)S(1)}, bf16[1024,12,64]{0,2,1:T(8,128)(2,1)}, u32[]{:S(2)}) copy-start(bf16[1024,12,64]{0,2,1:T(8,128)(2,1)} %get-tuple-element.525) | copy-start | bytes 4718596 | tf_op jit(solution)/shard_map/while/body/eval_jaxpr/while
  437.3 9.5 copy-start.5
  459.0 11.5 %copy-start.19 = (bf16[1024,12,64]{0,2,1:T(8,128)(2,1)S(1)}, bf16[1024,12,64]{0,2,1:T(8,128)(2,1)}, u32[]{:S(2)}) copy-start(bf16[1024,12,64]{0,2,1:T(8,128)(2,1)} %get-tuple-element.525) | copy-start | bytes 4718596 | tf_op jit(solution)/shard_map/while/body/eval_jaxpr/while
  524.0 9.5 copy-start.5
  547.6 6.6 copy-start.3
  558.2 6.0 copy-start.11
  558.2 6.0 copy-start.39
  558.2 6.0 copy-start.47
  558.2 6.0 copy-start.49
  558.2 6.0 copy-start.61
  597.4 3.0 copy-start.43
  597.4 3.0 copy-start.12
  597.4 3.8 copy-start.13
  601.2 3.5 copy-start.15
  601.2 4.0 copy-start.17
  601.2 4.0 copy-start.29
  601.2 4.0 copy-start.33
  601.2 4.0 copy-start.34
  601.2 3.9 copy-start.37
  601.3 3.9 copy-start.41
  601.3 3.9 copy-start.53
  609.0 294.0 %reduce-scatter.11.cloned.1.call-start = ((), (), s32[]{:S(2)}) async-start(), calls=%async_computation.12 | async-start | bytes 5308416 | tf_op jit(solution)/shard_map/reduce_scatter | solution.py:192
  629.8 4.9 copy-start.62
  629.8 5.4 copy-start.55
  629.8 5.4 copy-start.56
  629.8 5.4 copy-start.57
  629.8 377.4 %reduce-scatter.9.cloned.1.call-start = ((), (), s32[]{:S(2)}) async-start(), calls=%async_computation.11 | async-start | bytes 2433024 | tf_op jit(solution)/shard_map/reduce_scatter | solution.py:242
  643.0 3.7 copy-start.21
  (18 other events, 32.0 us)
Sparse Core Ops, SparseCore 0:
  10.9 59.6 all-gather.5
  73.5 53.0 all-gather.7
  128.8 51.3 all-gather.11
  182.1 45.4 all-gather.9
  229.0 46.3 all-gather.13
  300.3 57.8 reduce-scatter.6
  360.8 57.8 reduce-scatter.4
  609.1 194.1 all-reduce.5
  807.6 95.3 reduce-scatter.10
  908.7 98.5 reduce-scatter.8
where the time goes:
time: 1030 us; the launch traced here: 1020 us
  waiting for transfers between devices  484 us (47%)
  matrix products  292 us (28%)
  other arithmetic  100 us (10%)
  local copies, waits for them, and re-layouts  75.6 us (7%)
  blocking collectives  41.4 us (4%)
  between operations  15.1 us (1%)
    psum x1, waiting for transfers between devices, local(): lax.psum((grad_prompts, jnp.stack([grad_gain_one, grad_gain_two]), jnp.st...  114 us
    reduce_scatter x1, waiting for transfers between devices, local(): lax.psum_scatter(grad_out_weight, ('dp', 'mp'), scatter_dimension=0, tile...  104 us
    reduce_scatter x1, waiting for transfers between devices, local(): mlp_grad = lax.psum_scatter(grad_mlp, 'dp', scatter_dimension=1, tiled=True)  97.9 us
    all_gather x1, waiting for transfers between devices, local(): lax.all_gather(attn_qkv, ('dp', 'mp'), axis=1, tiled=True)  49 us
    all_gather x1, waiting for transfers between devices, local(): gathered = lax.all_gather(normed_two, 'mp', axis=0, tiled=True)  47.5 us
    dot_general x4, matrix products, masked_scores(): jnp.einsum('qhd,khd->hqk', query_tile, key_heads, preferred_element_type=...  44.9 us
    reduce_scatter x1, waiting for transfers between devices, local(): lax.psum_scatter(jnp.einsum('tf,df->td', piece, mlp_part[0], preferred_el...  44.5 us
    convert_element_type x2, other arithmetic, one_tile(): grad_scores = (weights * (grad_weights - weighted)).astype(jnp.bfloat16)  42.6 us
  transfers between devices with their start and end apart: 10, of which 8 were waited for; matrix products, arithmetic and copies ran while one was open for 42% of the time, Pallas kernels for 0%

commit v1 on v0

v1 whole, which is shorter than its diff:
```python
from functools import partial

import jax
import jax.numpy as jnp
from jax import lax
from jax.experimental import pallas as pl
from jax.experimental.pallas import tpu as pltpu
from jax.sharding import PartitionSpec as P

NPROMPT = 50
ROW = 1024
SPANS = (151, 247, 627)
EPS = 1e-06
HIGHEST = lax.Precision.HIGHEST
BIG = 1e30
B16 = jnp.bfloat16
F32 = jnp.float32
AXES = ("dp", "mp")
TILE = 256
NT = (((1,), (1,)), ((), ()))
TN = (((0,), (0,)), ((), ()))
VMEM_LIMIT = 60 * 1024 * 1024


def layer_norm(value_list, gain_row, shift_row):
    centre = jnp.mean(value_list, axis=-1, keepdims=True)
    centred = value_list - centre
    spread = jnp.mean(centred * centred, axis=-1, keepdims=True)
    return centred * lax.rsqrt(spread + EPS) * gain_row + shift_row


def key_window(first, count):
    low, high = ROW, 0
    for span in SPANS:
        whole = ROW // span
        for row in (first, first + count - 1):
            seg = min(row // span, whole)
            low = min(low, seg * span)
            high = max(high, ROW if seg == whole else (seg + 1) * span)
    return low // 128 * 128, -(-high // 128) * 128


def dotf(a, b, dims=None):
    if dims is None:
        return jnp.dot(a, b, preferred_element_type=F32)
    return lax.dot_general(a, b, dims, preferred_element_type=F32)


def px(x, k):
    return lax.ppermute(x, AXES, [(i, i ^ k) for i in range(32)])


def gather_pieces(piece):
    zs = jnp.stack([piece] + [px(piece, 8 * k) for k in range(1, 4)])
    qs = [zs] + [px(zs, 2 * k) for k in range(1, 4)]
    return qs + [px(q, 1) for q in qs]


def reduce_pieces(own, other):
    got = px(other, 1)
    parts = [own[k].astype(F32) + got[k].astype(F32) for k in range(4)]
    moved = [px(parts[k].astype(B16), 2 * k).astype(F32) for k in range(1, 4)]
    col = (parts[0] + moved[0]) + (moved[1] + moved[2])
    last = [px(col[z].astype(B16), 8 * z).astype(F32) for z in range(1, 4)]
    return (col[0] + last[0]) + (last[1] + last[2])


def all_reduce(x):
    x = x + px(x, 1)
    x = (x + px(x, 2)) + (px(x, 4) + px(x, 6))
    return (x + px(x, 8)) + (px(x, 16) + px(x, 24))


def pair_halves(weight, core):
    half = weight.shape[2] // 2
    mine = lax.dynamic_slice_in_dim(weight, core * half, half, 2)
    theirs = lax.dynamic_slice_in_dim(weight, (1 - core) * half, half, 2)
    got = px(theirs, 1)
    return jnp.where(
        core == 0, jnp.concatenate([mine, got], 1), jnp.concatenate([got, mine], 1)
    )


def assemble_kernel(meta, *refs):
    pieces, out, sems = refs[:8], refs[8], refs[9]
    chip, core = meta[0] // 2, meta[0] % 2
    copies = []
    for b in range(2):
        for xy in range(4):
            for z in range(4):
                rows = pl.multiple_of(48 * jnp.bitwise_xor(chip, xy + 4 * z), 16)
                cols = pl.multiple_of(384 * jnp.bitwise_xor(core, b), 128)
                copies.append(
                    pltpu.make_async_copy(
                        pieces[4 * b + xy].at[z],
                        out.at[:, pl.ds(rows, 48), pl.ds(cols, 384)],
                        sems.at[16 * b + 4 * xy + z],
                    )
                )
    for copy in copies:
        copy.start()
    for copy in copies:
        copy.wait()


def assemble(meta, pieces, name):
    count = pieces[0].shape[1]
    return pl.pallas_call(
        assemble_kernel,
        name=name,
        out_shape=jax.ShapeDtypeStruct((count, 768, 768), B16),
        in_specs=[pl.BlockSpec(memory_space=pltpu.SMEM)]
        + [pl.BlockSpec(memory_space=pl.ANY)] * 8,
        out_specs=pl.BlockSpec(memory_space=pltpu.VMEM),
        scratch_shapes=[pltpu.SemaphoreType.DMA((32,))],
    )(meta, *pieces)


def reorder_kernel(meta, g_ref, own_ref, other_ref):
    core = meta[0] % 2
    own_ref[0, 0] = g_ref[:, 0, pl.ds(pl.multiple_of(24 * core, 8), 24), :].astype(B16)
    other_ref[0, 0] = g_ref[:, 0, pl.ds(pl.multiple_of(24 * (1 - core), 8), 24), :].astype(B16)


def reorder(meta, grads, name):
    count = grads.shape[0]
    shape = jax.ShapeDtypeStruct((4, 4, count, 24, 768), B16)
    out_spec = pl.BlockSpec((1, 1, count, 24, 768), lambda i, j, meta: (i, j, 0, 0, 0))
    return pl.pallas_call(
        reorder_kernel,
        name=name,
        out_shape=(shape, shape),
        grid_spec=pltpu.PrefetchScalarGridSpec(
            num_scalar_prefetch=1,
            grid=(4, 4),
            in_specs=[
                pl.BlockSpec(
                    (count, 1, 48, 768),
                    lambda i, j, meta: (0, jnp.bitwise_xor(meta[0] // 2, i + 4 * j), 0, 0),
                )
            ],
            out_specs=[out_spec, out_spec],
        ),
    )(meta, grads.reshape(count, 16, 48, 768))


def three_parts(x):
    high = x.astype(B16).astype(F32)
    mid = (x - high).astype(B16).astype(F32)
    return high, mid, (x - high) - mid


def attention_forward_kernel(qf_ref, kf_ref, q_ref, k_ref, v_ref, mixed_ref, lse_ref):
    half = lax.broadcasted_iota(jnp.int32, (1, 128), 1) < 64
    q = q_ref[...] * jnp.asarray(0.125, B16)
    k, v = k_ref[...], v_ref[...]
    qf, kf = qf_ref[...], kf_ref[...]
    one = jnp.ones((), B16)
    sides = []
    for e in range(2):
        own = half if e == 0 else ~half
        sides.append((jnp.where(own, q, qf), jnp.where(own, k, kf), jnp.where(own, v, one)))
    for first in range(0, ROW, TILE):
        low, high = key_window(first, TILE)
        outs, peaks = [], []
        for qe, ke, ve in sides:
            s = dotf(qe[first : first + TILE], ke[low:high], NT)
            peak = jnp.max(s, axis=-1, keepdims=True)
            p = jnp.exp(s - peak).astype(B16)
            outs.append(dotf(p, ve[low:high]))
            peaks.append(peak)
        data = jnp.where(half, outs[0], outs[1])
        total = pltpu.roll(jnp.where(half, outs[1], outs[0]), 64, 1)
        mixed_ref[first : first + TILE, :] = (data / total).astype(B16)
        lse_ref[first : first + TILE, :] = jnp.where(half, peaks[0], peaks[1]) + jnp.log(total)


def attention_forward(qf, kf, qkv, pairs):
    rows = qkv.shape[0]
    full = pl.BlockSpec((ROW, 128), lambda r, p: (r, 0))

    def block(c):
        return pl.BlockSpec((ROW, 128), lambda r, p: (r, c * pairs + p))

    out = pl.BlockSpec((ROW, 128), lambda r, p: (r, p))
    return pl.pallas_call(
        attention_forward_kernel,
        name="attention_forward",
        grid=(rows // ROW, pairs),
        in_specs=[full, full, block(0), block(1), block(2)],
        out_specs=[out, out],
        out_shape=(
            jax.ShapeDtypeStruct((rows, 128 * pairs), B16),
            jax.ShapeDtypeStruct((rows, 128 * pairs), F32),
        ),
        compiler_params=pltpu.CompilerParams(vmem_limit_bytes=VMEM_LIMIT),
    )(qf, kf, qkv, qkv, qkv)


def attention_backward_kernel(
    qf_ref, kf_ref, q_ref, k_ref, v_ref, g_ref, mixed_ref, lse_ref, dq_ref, dk_ref, dv_ref, dk_acc, dv_acc
):
    lane = lax.broadcasted_iota(jnp.int32, (1, 128), 1)
    half = lane < 64
    spot = lane % 64
    q = q_ref[...] * jnp.asarray(0.125, B16)
    k, v, g = k_ref[...], v_ref[...], g_ref[...]
    qf, kf = qf_ref[...].astype(F32), kf_ref[...]
    prod = g.astype(F32) * mixed_ref[...].astype(F32)
    d0 = jnp.sum(jnp.where(half, prod, 0.0), axis=-1, keepdims=True)
    d1 = jnp.sum(jnp.where(half, 0.0, prod), axis=-1, keepdims=True)
    delta = jnp.where(half, d1, d0)
    lse = pltpu.roll(lse_ref[...], 64, 1)

    def spread(base, x):
        a, b, c = three_parts(-x)
        return jnp.where(spot == 7, a, jnp.where(spot == 8, b, jnp.where(spot == 9, c, base))).astype(B16)

    q_extra = spread(qf, lse)
    g_extra = spread(jnp.zeros_like(qf), delta)
    v_extra = jnp.where((spot >= 7) & (spot <= 9), 1.0, 0.0).astype(B16)
    dk_acc[...] = jnp.zeros_like(dk_acc)
    dv_acc[...] = jnp.zeros_like(dv_acc)
    sides = []
    for e in range(2):
        own = half if e == 0 else ~half
        sides.append(
            (
                jnp.where(own, q, q_extra),
                jnp.where(own, k, kf),
                jnp.where(own, g, g_extra),
                jnp.where(own, v, v_extra),
            )
        )
    for first in range(0, ROW, TILE):
        low, high = key_window(first, TILE)
        dqs, dks, dvs = [], [], []
        for qe, ke, ge, ve in sides:
            s = dotf(qe[first : first + TILE], ke[low:high], NT)
            p = jnp.exp(s)
            d = dotf(ge[first : first + TILE], ve[low:high], NT)
            ds = (p * d).astype(B16)
            dqs.append(dotf(ds, k[low:high]))
            dks.append(dotf(ds, q[first : first + TILE], TN))
            dvs.append(dotf(p.astype(B16), g[first : first + TILE], TN))
        dq_ref[first : first + TILE, :] = (jnp.where(half, dqs[0], dqs[1]) * 0.125).astype(B16)
        dk_acc[low:high, :] += jnp.where(half, dks[0], dks[1])
        dv_acc[low:high, :] += jnp.where(half, dvs[0], dvs[1])
    dk_ref[...] = dk_acc[...].astype(B16)
    dv_ref[...] = dv_acc[...].astype(B16)


def attention_backward(qf, kf, qkv, grad, mixed, lse, pairs):
    rows = qkv.shape[0]
    full = pl.BlockSpec((ROW, 128), lambda r, p: (r, 0))

    def block(c):
        return pl.BlockSpec((ROW, 128), lambda r, p: (r, c * pairs + p))

    out = pl.BlockSpec((ROW, 128), lambda r, p: (r, p))
    shape = jax.ShapeDtypeStruct((rows, 128 * pairs), B16)
    return pl.pallas_call(
        attention_backward_kernel,
        name="attention_backward",
        grid=(rows // ROW, pairs),
        in_specs=[full, full, block(0), block(1), block(2), out, out, out],
        out_specs=[out, out, out],
        out_shape=(shape, shape, shape),
        scratch_shapes=[pltpu.VMEM((ROW, 128), F32), pltpu.VMEM((ROW, 128), F32)],
        compiler_params=pltpu.CompilerParams(vmem_limit_bytes=VMEM_LIMIT),
    )(qf, kf, qkv, qkv, qkv, grad, mixed, lse)


SUB = 256
PER = 768 // SUB


def mlp_kernel(fast, *refs):
    meta, n_ref, c_ref, b_ref = refs[:4]
    count = 8 if fast else 1
    pieces, refs = refs[4 : 4 + count], refs[4 + count :]
    branch_ref, gn_ref, db_ref, own_ref, other_ref = refs[:5]
    w, nt, ct, dw, wsem, dsem = refs[5:]
    t = pl.program_id(0)
    jr, sub = t // PER, t % PER
    me_mp, me_dp = meta[0] % 4, meta[0] // 4

    def loads(j):
        if not fast:
            return [pltpu.make_async_copy(pieces[0].at[:, :, pl.ds(768 * j, 768)], w.at[j], wsem.at[j, 0])]
        out = []
        for dr in range(8):
            rows = pl.multiple_of(96 * jnp.bitwise_xor(me_dp, dr), 32)
            source = pieces[4 * (j & 1) + (j >> 1) + 2 * (dr & 1)].at[dr >> 1]
            out.append(pltpu.make_async_copy(source, w.at[j, :, pl.ds(rows, 96), :], wsem.at[j, dr]))
        return out

    def stores(j):
        if not fast:
            return [pltpu.make_async_copy(dw.at[j], own_ref.at[j], dsem.at[j, 0])]
        out = []
        for dr in range(8):
            target = (other_ref if j & 1 else own_ref).at[(j >> 1) + 2 * (dr & 1), dr >> 1]
            out.append(pltpu.make_async_copy(dw.at[j, dr], target, dsem.at[j, dr]))
        return out

    @pl.when(t == 0)
    def _():
        for j in range(4):
            for copy in loads(j):
                copy.start()
        nt[...] = n_ref[...].T
        ct[...] = c_ref[...].T
        branch_ref[...] = jnp.zeros_like(branch_ref)
        gn_ref[...] = jnp.zeros_like(gn_ref)

    for j in range(4):

        @pl.when(t == PER * j)
        def _():
            for copy in loads(j):
                copy.wait()

    spot = jnp.bitwise_xor(me_mp, jr) if fast else jr
    cols = pl.ds(pl.multiple_of(sub * SUB, SUB), SUB)
    w1 = w[jr, 0, :, cols]
    w2 = w[jr, 1, :, cols]
    u = dotf(n_ref[...], w1) + b_ref[spot, :, cols]
    cdf = 0.5 * (1.0 + lax.erf(u * 0.7071067811865476))
    hidden = (u * cdf).astype(B16)
    slope = cdf + u * (0.3989422804014327 * jnp.exp(-0.5 * u * u))
    gb32 = dotf(c_ref[...], w2) * slope
    gb = gb32.astype(B16)
    db_ref[spot, :, cols] = jnp.sum(gb.astype(F32), axis=0, keepdims=True)
    branch_ref[...] += dotf(hidden, w2, NT)
    gn_ref[...] += dotf(gb, w1, NT)
    dw1 = dotf(nt[...], gb).astype(B16)
    dw2 = dotf(ct[...], hidden).astype(B16)
    for a in range(8):
        dr = jnp.bitwise_xor(me_dp, a) if fast else a
        dw[jr, dr, 0, :, cols] = dw1[96 * a : 96 * a + 96]
        dw[jr, dr, 1, :, cols] = dw2[96 * a : 96 * a + 96]

    for j in range(4):

        @pl.when(t == PER * j + PER - 1)
        def _():
            for copy in stores(j):
                copy.start()

    @pl.when(t == 4 * PER - 1)
    def _():
        for j in range(4):
            for copy in stores(j):
                copy.wait()


def mlp(meta, normed, cot, bias, pieces):
    fast = len(pieces) == 8
    tokens = normed.shape[0]
    vmem = pl.BlockSpec(memory_space=pltpu.VMEM)
    anys = pl.BlockSpec(memory_space=pl.ANY)
    if fast:
        shape = jax.ShapeDtypeStruct((4, 4, 2, 96, 768), B16)
    else:
        shape = jax.ShapeDtypeStruct((4, 8, 2, 96, 768), B16)
    return pl.pallas_call(
        partial(mlp_kernel, fast),
        name="mlp",
        grid=(4 * PER,),
        in_specs=[pl.BlockSpec(memory_space=pltpu.SMEM), vmem, vmem, vmem] + [anys] * len(pieces),
        out_specs=[vmem, vmem, vmem, anys, anys],
        out_shape=(
            jax.ShapeDtypeStruct((tokens, 768), F32),
            jax.ShapeDtypeStruct((tokens, 768), F32),
            jax.ShapeDtypeStruct((4, 1, 768), F32),
            shape,
            shape,
        ),
        scratch_shapes=[
            pltpu.VMEM((4, 2, 768, 768), B16),
            pltpu.VMEM((768, tokens), B16),
            pltpu.VMEM((768, tokens), B16),
            pltpu.VMEM((4, 8, 2, 96, 768), B16),
            pltpu.SemaphoreType.DMA((4, 8)),
            pltpu.SemaphoreType.DMA((4, 8)),
        ],
        compiler_params=pltpu.CompilerParams(vmem_limit_bytes=VMEM_LIMIT),
    )(meta, normed, cot, bias.reshape(4, 1, 768), *pieces)


def local(
    fast,
    tokens,
    cotangent,
    prompts,
    segments,
    prompt_slot_index,
    norm_gain,
    norm_shift,
    attn_qkv,
    attn_bias,
    attn_out,
    mlp_weight,
    mlp_bias_up,
    mlp_bias_down,
):
    width = tokens.shape[1]
    pairs = width // 128
    device = lax.axis_index("dp") * lax.axis_size("mp") + lax.axis_index("mp")
    meta = jnp.reshape(device, (1,)).astype(jnp.int32)
    if fast:
        core = device % 2
        qkv_pieces = gather_pieces(pair_halves(attn_qkv, core))
        qkv_all = assemble(meta, qkv_pieces, "assemble_qkv")
        attn_out_tied, mlp_tied, _ = lax.optimization_barrier((attn_out, mlp_weight, qkv_pieces[3]))
        out_pieces = gather_pieces(pair_halves(attn_out_tied[None], core))
        out_all = assemble(meta, out_pieces, "assemble_out")[0]
        mlp_tied, _ = lax.optimization_barrier((mlp_tied, out_pieces[3]))
        mlp_pieces = gather_pieces(mlp_tied)
    else:
        qkv_all = lax.all_gather(attn_qkv, AXES, axis=1, tiled=True)
        out_all = lax.all_gather(attn_out, AXES, axis=0, tiled=True)
        mlp_all = lax.all_gather(mlp_weight, "dp", axis=1, tiled=True)
        mlp_pieces = [lax.all_gather(mlp_all, "mp", axis=2, tiled=True)]

    table = jnp.concatenate([prompts, jnp.zeros((1, width), F32)], 0)
    onehot = (prompt_slot_index[:, None] == jnp.arange(NPROMPT + 1, dtype=jnp.int32)[None, :]).astype(F32)
    is_prompt = (prompt_slot_index < NPROMPT)[:, None]
    start = jnp.where(is_prompt, jnp.dot(onehot, table, precision=HIGHEST), tokens.astype(F32))
    normed_one = layer_norm(start, norm_gain[0], norm_shift[0]).astype(B16)
    lane = jnp.arange(128, dtype=jnp.int32)[None, :] % 64
    same = (segments[:, None] == lane) & (lane < 7)
    qf = same.astype(B16)
    kf = jnp.where(lane < 7, jnp.where(same, 0.0, -BIG), jnp.where(lane < 10, 1.0, 0.0)).astype(B16)

    bias_row = jnp.concatenate([attn_bias[0], jnp.zeros_like(attn_bias[0]), attn_bias[1]])
    qkv = jnp.concatenate([dotf(normed_one, qkv_all[c]) for c in range(3)], 1) + bias_row
    qkv = qkv.astype(B16)
    mixed, lse = attention_forward(qf, kf, qkv, pairs)
    middle = start + dotf(mixed, out_all) + attn_bias[2]
    normed_two = layer_norm(middle, norm_gain[1], norm_shift[1]).astype(B16)
    grad_output = cotangent.astype(F32)
    grad_down = jnp.sum(grad_output, axis=0)
    branch, grad_normed_two, grad_up, own_mlp, other_mlp = mlp(
        meta, normed_two, cotangent, mlp_bias_up, mlp_pieces
    )
    output = middle + branch + mlp_bias_down
    norm_out_two, pull_two = jax.vjp(layer_norm, middle, norm_gain[1], norm_shift[1])
    grad_from_two, grad_gain_two, grad_shift_two = pull_two(grad_normed_two)
    grad_middle = grad_output + grad_from_two
    grad_branch = grad_middle.astype(B16)
    grad_bias_out = jnp.sum(grad_branch.astype(F32), axis=0)
    grad_out_weight = dotf(mixed, grad_branch, TN)
    grad_mixed = dotf(grad_branch, out_all, NT).astype(B16)
    dq, dk, dv = attention_backward(qf, kf, qkv, grad_mixed, mixed, lse, pairs)
    grad_qkv = jnp.stack([dotf(normed_one, x, TN) for x in (dq, dk, dv)])
    grad_attn_bias = jnp.stack([jnp.sum(dq.astype(F32), axis=0), jnp.sum(dv.astype(F32), axis=0), grad_bias_out])
    grad_normed_one = sum(dotf(x, qkv_all[c], NT) for c, x in enumerate((dq, dk, dv)))
    norm_out_one, pull_one = jax.vjp(layer_norm, start, norm_gain[0], norm_shift[0])
    grad_from_one, grad_gain_one, grad_shift_one = pull_one(grad_normed_one)
    grad_start = grad_middle + grad_from_one
    input_grad = jnp.where(is_prompt, 0.0, grad_start)
    grad_prompts = jnp.dot(onehot.T, grad_start, precision=HIGHEST)[:NPROMPT]
    small = jnp.concatenate(
        [
            grad_prompts,
            grad_gain_one[None],
            grad_gain_two[None],
            grad_shift_one[None],
            grad_shift_two[None],
            grad_attn_bias,
            grad_down[None],
            grad_up.reshape(4, width),
        ]
    )
    if fast:
        mlp_grad = reduce_pieces(own_mlp, other_mlp)
        out_grad = reduce_pieces(*reorder(meta, grad_out_weight[None], "reorder_out"))[0]
        qkv_grad = reduce_pieces(*reorder(meta, grad_qkv, "reorder_qkv"))
        small = all_reduce(small)
    else:
        mlp_grad = own_mlp.transpose(2, 1, 3, 0, 4).reshape(2, 768, 3072)
        mlp_grad = lax.psum_scatter(mlp_grad, "dp", scatter_dimension=1, tiled=True)
        mlp_grad = lax.psum_scatter(mlp_grad, "mp", scatter_dimension=2, tiled=True).astype(F32)
        qkv_grad = lax.psum_scatter(grad_qkv, AXES, scatter_dimension=1, tiled=True)
        out_grad = lax.psum_scatter(grad_out_weight, AXES, scatter_dimension=0, tiled=True)
        small = lax.psum(small, AXES)
    at = NPROMPT
    return (
        output.astype(B16),
        input_grad,
        small[:at],
        small[at : at + 2],
        small[at + 2 : at + 4],
        qkv_grad,
        small[at + 4 : at + 7],
        out_grad,
        mlp_grad,
        small[at + 8 :].reshape(-1),
        small[at + 7],
    )


def solution(mesh):
    fast = dict(mesh.shape) == {"dp": 8, "mp": 4}
    return jax.shard_map(
        partial(local, fast),
        mesh=mesh,
        in_specs=(
            P(AXES, None),
            P(AXES, None),
            P(),
            P(AXES),
            P(AXES),
            P(),
            P(),
            P(None, AXES, None),
            P(),
            P(AXES, None),
            P(None, "dp", "mp"),
            P(),
            P(),
        ),
        out_specs=(
            P(AXES, None),
            P(AXES, None),
            P(),
            P(),
            P(),
            P(None, AXES, None),
            P(),
            P(AXES, None),
            P(None, "dp", "mp"),
            P(),
            P(),
        ),
        check_vma=False,
    )
```

time: 1030 us -> 448 us (0.43)
  waiting for transfers between devices: 484 us -> 164 us
  matrix products: 292 us -> 32.3 us
  Pallas kernels: 0 us -> 127 us
  local copies, waits for them, and re-layouts: 75.6 us -> 15.9 us
  other arithmetic: 100 us -> 46.1 us
  starting transfers between devices: 0.4 us -> 53.5 us
  blocking collectives: 41.4 us -> 0 us
  between operations: 15.1 us -> 1.72 us
    dot_general x27 -> x13, matrix products: 288 us -> 31 us  [the longest x8 18.3 us: dotf(): return lax.dot_general(a, b, dims, preferred_element_type=F32)]
    reduce_scatter x4 -> x0, waiting for transfers between devices: 247 us -> none  [the longest x1 104 us: local(): lax.psum_scatter(grad_out_weight, ('dp', 'mp'), scatter_dimension=0, tile...]
    ppermute x0 -> x60, waiting for transfers between devices: none -> 164 us  [px(): return lax.ppermute(x, AXES, [(i, i ^ k) for i in range(32)])]
    pallas_call x0 -> x7, Pallas kernels: none -> 127 us  [the longest x1 45.3 us: mlp(): pl.pallas_call(partial(mlp_kernel, fast), name='mlp', grid=(4 * PER,), in...]
    all_gather x5 -> x0, waiting for transfers between devices: 121 us -> none  [the longest x1 49 us: local(): lax.all_gather(attn_qkv, ('dp', 'mp'), axis=1, tiled=True)]
    psum x1 -> x0, waiting for transfers between devices: 114 us -> none  [local(): lax.psum((grad_prompts, jnp.stack([grad_gain_one, grad_gain_two]), jnp.st...]
    ppermute x0 -> x60, starting transfers between devices: none -> 53.5 us  [px(): return lax.ppermute(x, AXES, [(i, i ^ k) for i in range(32)])]
    psum x1 -> x0, blocking collectives: 41.4 us -> none  [local(): lax.psum((grad_prompts, jnp.stack([grad_gain_one, grad_gain_two]), jnp.st...]
  transfers between devices with their start and end apart: 10 -> 60, of which waited for: 8 -> 22; matrix products, arithmetic and copies ran while one was open for 42% -> 18% of each run, Pallas kernels for 0% -> 19%
where the time goes in v1:
time: 448 us; the launch traced here: 440 us
  waiting for transfers between devices  164 us (37%)
  Pallas kernels  127 us (28%)
  starting transfers between devices  53.5 us (12%)
  other arithmetic  46.1 us (10%)
  matrix products  32.3 us (7%)
  local copies, waits for them, and re-layouts  15.9 us (4%)
    ppermute x60, waiting for transfers between devices, px(): return lax.ppermute(x, AXES, [(i, i ^ k) for i in range(32)])  164 us
    ppermute x60, starting transfers between devices, px(): return lax.ppermute(x, AXES, [(i, i ^ k) for i in range(32)])  53.5 us
    pallas_call x1, Pallas kernels, mlp(): pl.pallas_call(partial(mlp_kernel, fast), name='mlp', grid=(4 * PER,), in...  45.3 us
    pallas_call x1, Pallas kernels, attention_backward(): pl.pallas_call(attention_backward_kernel, name='attention_backward', grid...  31.5 us
    pallas_call x1, Pallas kernels, attention_forward(): pl.pallas_call(attention_forward_kernel, name='attention_forward', grid=(...  22.9 us
    pallas_call x2, Pallas kernels, reorder(): pl.pallas_call(reorder_kernel, name=name, out_shape=(shape, shape), grid_...  20.3 us
    dot_general x8, matrix products, dotf(): return lax.dot_general(a, b, dims, preferred_element_type=F32)  18.3 us
    dot_general x4, matrix products, dotf(): return jnp.dot(a, b, preferred_element_type=F32)  9.32 us
  transfers between devices with their start and end apart: 60, of which 22 were waited for; matrix products, arithmetic and copies ran while one was open for 18% of the time, Pallas kernels for 19%

profile of v1, /device:TPU:16, one launch (start us, length us, event | category | flops | bytes accessed | tf_op | source)
XLA Modules:
  0.0 439.8 jit_solution(4066492907217359930)
XLA Ops:
  2.3 3.4 fusion.46
  6.4 1.6 collective-permute-start.1
  8.3 1.6 collective-permute-start.3
  9.9 2.4 collective-permute-done.1
  12.3 4.2 collective-permute-done.2
  16.5 3.7 collective-permute-done.3
  21.1 2.5 collective-permute-start.6
  23.5 1.7 add_convert_fusion.2
  25.2 8.5 %collective-permute-done.6.refs_3_ = bf16[4,3,48,384]{3,2,1,0:T(8,128)(2,1)} collective-permute-done((bf16[4,3,48,384]{3,2,1,0:T(8,128)(2,1)}, bf16[4,3,48,384]{3,2,1,0:T(8,128)(2,1)}, u32[]{:S(2)}, u32[]{:S(2)}) %collective-permute-start.6) | collective-permute-done | bytes 442400 | tf_op jit(solution)/shard_map/ppermute | solution.py:50
  33.8 1.6 collective-permute-start.4
  35.4 1.5 collective-permute-start.5
  37.0 1.9 collective-permute-start.13
  38.9 1.6 collective-permute-start.14
  40.9 1.5 collective-permute-done.13
  46.7 1.5 collective-permute-start.16
  48.2 2.3 collective-permute-done.15.refs_1_
  51.9 2.1 collective-permute-done.17.refs_3_
  59.8 2.5 assemble_out.1
  62.4 1.5 collective-permute-start.23
  65.3 4.2 assemble_qkv.1
  69.5 3.3 fusion.9
  74.2 10.0 %collective-permute-done.23 = bf16[2,96,768]{2,1,0:T(8,128)(2,1)S(1)} collective-permute-done((bf16[2,96,768]{2,1,0:T(8,128)(2,1)}, bf16[2,96,768]{2,1,0:T(8,128)(2,1)S(1)}, u32[]{:S(2)}, u32[]{:S(2)}) %collective-permute-start.23) | collective-permute-done | bytes 294944 | tf_op jit(solution)/shard_map/ppermute | solution.py:50
  84.2 7.1 %collective-permute-done.24 = bf16[2,96,768]{2,1,0:T(8,128)(2,1)} collective-permute-done((bf16[2,96,768]{2,1,0:T(8,128)(2,1)}, bf16[2,96,768]{2,1,0:T(8,128)(2,1)}, u32[]{:S(2)}, u32[]{:S(2)}) %collective-permute-start.24) | collective-permute-done | bytes 294944 | tf_op jit(solution)/shard_map/ppermute | solution.py:50
  91.4 2.3 pad_maximum_fusion.1.refs_4_
  95.7 1.5 collective-permute-start.27
  98.6 2.6 fusion.q_ref.k_ref.v_ref
  101.2 22.9 %attention_forward.1 = (bf16[1024,768]{1,0:T(8,128)(2,1)}, f32[1024,768]{1,0:T(8,128)}) custom-call(bf16[1024,128]{1,0:T(8,128)(2,1)} %fusion.19.qf_ref, bf16[1024,128]{1,0:T(8,128)(2,1)} %select_convert_fusion.kf_ref, bf16[1024,2304]{1,0:T(8,128)(2,1)} %fusion.q_ref.k_ref.v_ref, bf16[1024,2304]{1,0:T(8,128)(2,1)} %fusion.q_ref.k_ref.v_ref, ...), custom_call_target="tpu_custom_call" | custom-call | tf_op jit(solution)/shard_map/attention_forward/pallas_call | solution.py:186
  124.6 22.5 %collective-permute-done.26.refs_6_ = bf16[4,2,96,768]{3,2,1,0:T(8,128)(2,1)} collective-permute-done((bf16[4,2,96,768]{3,2,1,0:T(8,128)(2,1)}, bf16[4,2,96,768]{3,2,1,0:T(8,128)(2,1)}, u32[]{:S(2)}, u32[]{:S(2)}) %collective-permute-start.26) | collective-permute-done | bytes 1179680 | tf_op jit(solution)/shard_map/ppermute | solution.py:50
  147.6 3.3 fusion.47
  151.4 1.7 add_convert_fusion.1.refs_1_
  157.3 45.3 %mlp.1 = (f32[1024,768]{1,0:T(8,128)}, f32[1024,768]{1,0:T(8,128)}, f32[4,1,768]{2,1,0:T(1,128)}, bf16[4,4,2,96,768]{4,3,2,1,0:T(8,128)(2,1)}, bf16[4,4,2,96,768]{4,3,2,1,0:T(8,128)(2,1)}) custom-call(s32[1]{0:T(128)} %bitcast.meta.refs_0_, bf16[1024,768]{1,0:T(8,128)(2,1)} %add_convert_fusion.1.refs_1_, bf16[1024,768]{1,0:T(8,128)(2,1)} %refs_2_.1, ...), custom_call_target="tpu_custom_call" | custom-call | tf_op jit(solution)/shard_map/mlp/pallas_call | solution.py:367
  202.7 3.7 multiply_reduce_fusion
  207.4 4.1 fusion.44
  213.7 2.6 convolution_convert_fusion.g_ref
  216.3 31.5 %attention_backward.1 = (bf16[1024,768]{1,0:T(8,128)(2,1)}, bf16[1024,768]{1,0:T(8,128)(2,1)}, bf16[1024,768]{1,0:T(8,128)(2,1)}) custom-call(bf16[1024,128]{1,0:T(8,128)(2,1)} %fusion.19.qf_ref, bf16[1024,128]{1,0:T(8,128)(2,1)} %select_convert_fusion.kf_ref, bf16[1024,2304]{1,0:T(8,128)(2,1)} %fusion.q_ref.k_ref.v_ref, ...), custom_call_target="tpu_custom_call" | custom-call | tf_op jit(solution)/shard_map/attention_backward/pallas_call | solution.py:262
  247.8 3.3 fusion.10
  252.6 2.4 multiply_reduce_fusion.1
  258.3 2.7 broadcast_select_fusion
  265.8 1.5 fusion.49
  270.2 2.2 collective-permute-start.35
  272.4 3.4 pad_maximum_fusion.g_ref
  275.7 10.7 %reorder_qkv.1 = (bf16[4,4,3,24,768]{4,3,2,1,0:T(8,128)(2,1)}, bf16[4,4,3,24,768]{4,3,2,1,0:T(8,128)(2,1)}) custom-call(s32[1]{0:T(128)} %bitcast.meta.refs_0_, f32[3,16,48,768]{3,2,1,0:T(8,128)} %pad_maximum_fusion.g_ref), custom_call_target="tpu_custom_call" | custom-call | tf_op jit(solution)/shard_map/reorder_qkv/pallas_call | solution.py:129
  286.5 1.8 add_add_fusion.6
  288.3 1.5 collective-permute-start.37
  289.9 2.0 collective-permute-start.38
  291.8 4.2 fusion.51
  296.1 9.6 %reorder_out.1 = (bf16[4,4,1,24,768]{4,3,2,1,0:T(8,128)(2,1)}, bf16[4,4,1,24,768]{4,3,2,1,0:T(8,128)(2,1)}) custom-call(s32[1]{0:T(128)} %bitcast.meta.refs_0_, f32[1,16,48,768]{3,2,1,0:T(8,128)} %bitcast.157), custom_call_target="tpu_custom_call" | custom-call | tf_op jit(solution)/shard_map/reorder_out/pallas_call | solution.py:129
  305.8 4.0 collective-permute-done.38
  319.4 2.2 collective-permute-start.49
  322.9 4.2 fusion.3
  329.2 1.5 collective-permute-start.56
  332.3 4.4 collective-permute-done.40
  336.7 1.5 collective-permute-start.42
  338.1 60.3 %collective-permute-done.41 = bf16[4,3,24,768]{3,2,1,0:T(8,128)(2,1)S(1)} collective-permute-done((bf16[4,3,24,768]{3,2,1,0:T(8,128)(2,1)S(1)}, bf16[4,3,24,768]{3,2,1,0:T(8,128)(2,1)S(1)}, u32[]{:S(2)}, u32[]{:S(2)}) %collective-permute-start.41) | collective-permute-done | bytes 442400 | tf_op jit(solution)/shard_map/ppermute | solution.py:50
  398.4 1.5 collective-permute-start.51
  400.3 2.0 collective-permute-start.52
  403.9 2.4 fusion.38
  406.3 2.0 collective-permute-start.45
  408.3 1.8 collective-permute-start.57
  410.2 1.6 collective-permute-start.59
  412.5 4.8 %collective-permute-done.45 = bf16[3,24,768]{2,1,0:T(8,128)(2,1)S(1)} collective-permute-done((bf16[3,24,768]{2,1,0:T(8,128)(2,1)S(1)}, bf16[3,24,768]{2,1,0:T(8,128)(2,1)S(1)}, u32[]{:S(2)}, u32[]{:S(2)}) %collective-permute-start.45) | collective-permute-done | bytes 110624 | tf_op jit(solution)/shard_map/ppermute | solution.py:50
  418.0 2.4 collective-permute-done.57
  420.4 11.8 %collective-permute-done.58 = bf16[2,96,768]{2,1,0:T(8,128)(2,1)S(1)} collective-permute-done((bf16[2,96,768]{2,1,0:T(8,128)(2,1)S(1)}, bf16[2,96,768]{2,1,0:T(8,128)(2,1)S(1)}, u32[]{:S(2)}, u32[]{:S(2)}) %collective-permute-start.58) | collective-permute-done | bytes 294944 | tf_op jit(solution)/shard_map/ppermute | solution.py:50
  432.1 6.5 %collective-permute-done.59 = bf16[2,96,768]{2,1,0:T(8,128)(2,1)S(1)} collective-permute-done((bf16[2,96,768]{2,1,0:T(8,128)(2,1)S(1)}, bf16[2,96,768]{2,1,0:T(8,128)(2,1)S(1)}, u32[]{:S(2)}, u32[]{:S(2)}) %collective-permute-start.59) | collective-permute-done | bytes 294944 | tf_op jit(solution)/shard_map/ppermute | solution.py:50
  (235 shorter events, 61.9 us)
Async XLA Ops:
  1.5 4.8 %collective-permute-start = (bf16[3,24,384]{2,1,0:T(8,128)(2,1)S(1)}, bf16[3,24,384]{2,1,0:T(8,128)(2,1)S(1)}, u32[]{:S(2)}, u32[]{:S(2)}) collective-permute-start(bf16[3,24,384]{2,1,0:T(8,128)(2,1)S(1)} %get-tuple-element.93), channel_id=1, source_target_pairs={{0,1},{1,0},{2,3},{3,2},{4,5},{5,4},{6,7},{7,6},{8,9},{9,8},{10,11... | collective-permute-start | bytes 165896 | tf_op jit(solution)/shard_map/ppermute | solution.py:50
  6.2 27.5 %copy-start.33 = (bf16[24,768]{1,0:T(8,128)(2,1)S(1)}, bf16[24,768]{1,0:T(8,128)(2,1)}, u32[]{:S(2)}) copy-start(bf16[24,768]{1,0:T(8,128)(2,1)} %param.22) | copy-start | bytes 110596
  6.4 6.0 %collective-permute-start.1 = (bf16[3,48,384]{2,1,0:T(8,128)(2,1)S(1)}, bf16[3,48,384]{2,1,0:T(8,128)(2,1)S(1)}, u32[]{:S(2)}, u32[]{:S(2)}) collective-permute-start(bf16[3,48,384]{2,1,0:T(8,128)(2,1)S(1)} %maximum_select_fusion.1), channel_id=1, source_target_pairs={{0,8},{1,9},{2,10},{3,11},{4,12},{5,13},{6,14},{7,15},{8,0},{9,1},... | collective-permute-start | bytes 331784 | tf_op jit(solution)/shard_map/ppermute | solution.py:50
  8.0 8.5 %collective-permute-start.2 = (bf16[3,48,384]{2,1,0:T(8,128)(2,1)S(1)}, bf16[3,48,384]{2,1,0:T(8,128)(2,1)S(1)}, u32[]{:S(2)}, u32[]{:S(2)}) collective-permute-start(bf16[3,48,384]{2,1,0:T(8,128)(2,1)S(1)} %maximum_select_fusion.1), channel_id=1, source_target_pairs={{0,16},{1,17},{2,18},{3,19},{4,20},{5,21},{6,22},{7,23},{8,24},{9,... | collective-permute-start | bytes 331784 | tf_op jit(solution)/shard_map/ppermute | solution.py:50
  8.3 11.9 %collective-permute-start.3 = (bf16[3,48,384]{2,1,0:T(8,128)(2,1)S(1)}, bf16[3,48,384]{2,1,0:T(8,128)(2,1)S(1)}, u32[]{:S(2)}, u32[]{:S(2)}) collective-permute-start(bf16[3,48,384]{2,1,0:T(8,128)(2,1)S(1)} %maximum_select_fusion.1), channel_id=1, source_target_pairs={{0,24},{1,25},{2,26},{3,27},{4,28},{5,29},{6,30},{7,31},{8,16},{9,... | collective-permute-start | bytes 331784 | tf_op jit(solution)/shard_map/ppermute | solution.py:50
  9.9 34.4 %copy-start.35 = (s32[1024]{0:T(1024)S(1)}, s32[1024]{0:T(1024)}, u32[]{:S(2)}) copy-start(s32[1024]{0:T(1024)} %param.16) | copy-start | bytes 12292
  20.2 35.3 %copy-start.34 = (s32[1024]{0:T(1024)S(1)}, s32[1024]{0:T(1024)}, u32[]{:S(2)}) copy-start(s32[1024]{0:T(1024)} %param.17) | copy-start | bytes 12292
  21.1 36.9 %copy-start.37 = (f32[3,768]{1,0:T(4,128)S(1)}, f32[3,768]{1,0:T(4,128)}, u32[]{:S(2)}) copy-start(f32[3,768]{1,0:T(4,128)} %param.21) | copy-start | bytes 27652
  21.1 12.6 %collective-permute-start.6 = (bf16[4,3,48,384]{3,2,1,0:T(8,128)(2,1)}, bf16[4,3,48,384]{3,2,1,0:T(8,128)(2,1)}, u32[]{:S(2)}, u32[]{:S(2)}) collective-permute-start(bf16[4,3,48,384]{3,2,1,0:T(8,128)(2,1)} %pad_maximum_fusion.2.refs_0_), channel_id=1, source_target_pairs={{0,6},{1,7},{2,4},{3,5},{4,2},{5,3},{6,0},{7,1},{8,14},{9,15},{10,... | collective-permute-start | bytes 1327112 | tf_op jit(solution)/shard_map/ppermute | solution.py:50
  33.7 3.2 collective-permute-start.11
  33.8 14.4 %collective-permute-start.4 = (bf16[4,3,48,384]{3,2,1,0:T(8,128)(2,1)}, bf16[4,3,48,384]{3,2,1,0:T(8,128)(2,1)}, u32[]{:S(2)}, u32[]{:S(2)}) collective-permute-start(bf16[4,3,48,384]{3,2,1,0:T(8,128)(2,1)} %pad_maximum_fusion.2.refs_0_), channel_id=1, source_target_pairs={{0,2},{1,3},{2,0},{3,1},{4,6},{5,7},{6,4},{7,5},{8,10},{9,11},{10,... | collective-permute-start | bytes 1327112 | tf_op jit(solution)/shard_map/ppermute | solution.py:50
  35.4 16.0 %collective-permute-start.5 = (bf16[4,3,48,384]{3,2,1,0:T(8,128)(2,1)}, bf16[4,3,48,384]{3,2,1,0:T(8,128)(2,1)}, u32[]{:S(2)}, u32[]{:S(2)}) collective-permute-start(bf16[4,3,48,384]{3,2,1,0:T(8,128)(2,1)} %pad_maximum_fusion.2.refs_0_), channel_id=1, source_target_pairs={{0,4},{1,5},{2,6},{3,7},{4,0},{5,1},{6,2},{7,3},{8,12},{9,13},{10,... | collective-permute-start | bytes 1327112 | tf_op jit(solution)/shard_map/ppermute | solution.py:50
  36.9 4.0 collective-permute-start.12
  37.0 5.4 %collective-permute-start.13 = (bf16[1,48,384]{2,1,0:T(8,128)(2,1)S(1)}, bf16[1,48,384]{2,1,0:T(8,128)(2,1)S(1)}, u32[]{:S(2)}, u32[]{:S(2)}) collective-permute-start(bf16[1,48,384]{2,1,0:T(8,128)(2,1)S(1)} %maximum_select_fusion.3), channel_id=1, source_target_pairs={{0,16},{1,17},{2,18},{3,19},{4,20},{5,21},{6,22},{7,23},{8,24},{9,... | collective-permute-start | bytes 110600 | tf_op jit(solution)/shard_map/ppermute | solution.py:50
  38.9 4.8 %collective-permute-start.14 = (bf16[1,48,384]{2,1,0:T(8,128)(2,1)S(1)}, bf16[1,48,384]{2,1,0:T(8,128)(2,1)S(1)}, u32[]{:S(2)}, u32[]{:S(2)}) collective-permute-start(bf16[1,48,384]{2,1,0:T(8,128)(2,1)S(1)} %maximum_select_fusion.3), channel_id=1, source_target_pairs={{0,24},{1,25},{2,26},{3,27},{4,28},{5,29},{6,30},{7,31},{8,16},{9,... | collective-permute-start | bytes 110600 | tf_op jit(solution)/shard_map/ppermute | solution.py:50
  43.7 6.8 %collective-permute-start.15 = (bf16[4,1,48,384]{3,2,1,0:T(8,128)(2,1)S(1)}, bf16[4,1,48,384]{3,2,1,0:T(8,128)(2,1)S(1)}, u32[]{:S(2)}, u32[]{:S(2)}) collective-permute-start(bf16[4,1,48,384]{3,2,1,0:T(8,128)(2,1)S(1)} %pad_maximum_fusion.3.refs_0_), channel_id=1, source_target_pairs={{0,2},{1,3},{2,0},{3,1},{4,6},{5,7},{6,4},{7,5},{8,10},{9,11},{10,... | collective-permute-start | bytes 442376 | tf_op jit(solution)/shard_map/ppermute | solution.py:50
  45.2 8.7 %collective-permute-start.17 = (bf16[4,1,48,384]{3,2,1,0:T(8,128)(2,1)S(1)}, bf16[4,1,48,384]{3,2,1,0:T(8,128)(2,1)S(1)}, u32[]{:S(2)}, u32[]{:S(2)}) collective-permute-start(bf16[4,1,48,384]{3,2,1,0:T(8,128)(2,1)S(1)} %pad_maximum_fusion.3.refs_0_), channel_id=1, source_target_pairs={{0,6},{1,7},{2,4},{3,5},{4,2},{5,3},{6,0},{7,1},{8,14},{9,15},{10,... | collective-permute-start | bytes 442376 | tf_op jit(solution)/shard_map/ppermute | solution.py:50
  46.7 8.3 %collective-permute-start.16 = (bf16[4,1,48,384]{3,2,1,0:T(8,128)(2,1)S(1)}, bf16[4,1,48,384]{3,2,1,0:T(8,128)(2,1)S(1)}, u32[]{:S(2)}, u32[]{:S(2)}) collective-permute-start(bf16[4,1,48,384]{3,2,1,0:T(8,128)(2,1)S(1)} %pad_maximum_fusion.3.refs_0_), channel_id=1, source_target_pairs={{0,4},{1,5},{2,6},{3,7},{4,0},{5,1},{6,2},{7,3},{8,12},{9,13},{10,... | collective-permute-start | bytes 442376 | tf_op jit(solution)/shard_map/ppermute | solution.py:50
  48.2 6.8 %collective-permute-start.18 = (bf16[4,1,48,384]{3,2,1,0:T(8,128)(2,1)S(1)}, bf16[4,1,48,384]{3,2,1,0:T(8,128)(2,1)S(1)}, u32[]{:S(2)}, u32[]{:S(2)}) collective-permute-start(bf16[4,1,48,384]{3,2,1,0:T(8,128)(2,1)S(1)} %pad_maximum_fusion.3.refs_0_), channel_id=1, source_target_pairs={{0,1},{1,0},{2,3},{3,2},{4,5},{5,4},{6,7},{7,6},{8,9},{9,8},{10,11... | collective-permute-start | bytes 442376 | tf_op jit(solution)/shard_map/ppermute | solution.py:50
  50.5 5.0 %collective-permute-start.19 = (bf16[4,1,48,384]{3,2,1,0:T(8,128)(2,1)S(1)}, bf16[4,1,48,384]{3,2,1,0:T(8,128)(2,1)S(1)}, u32[]{:S(2)}, u32[]{:S(2)}) collective-permute-start(bf16[4,1,48,384]{3,2,1,0:T(8,128)(2,1)S(1)} %collective-permute-done.15.refs_1_), channel_id=1, source_target_pairs={{0,1},{1,0},{2,3},{3,2},{4,5},{5,4},{6,7},{7,6},{8,9},{9,8},{10,11... | collective-permute-start | bytes 442376 | tf_op jit(solution)/shard_map/ppermute | solution.py:50
  51.4 11.0 %collective-permute-start.7 = (bf16[4,3,48,384]{3,2,1,0:T(8,128)(2,1)}, bf16[4,3,48,384]{3,2,1,0:T(8,128)(2,1)}, u32[]{:S(2)}, u32[]{:S(2)}) collective-permute-start(bf16[4,3,48,384]{3,2,1,0:T(8,128)(2,1)} %pad_maximum_fusion.2.refs_0_), channel_id=1, source_target_pairs={{0,1},{1,0},{2,3},{3,2},{4,5},{5,4},{6,7},{7,6},{8,9},{9,8},{10,11... | collective-permute-start | bytes 1327112 | tf_op jit(solution)/shard_map/ppermute | solution.py:50
  54.0 9.9 %collective-permute-start.10 = (bf16[4,3,48,384]{3,2,1,0:T(8,128)(2,1)}, bf16[4,3,48,384]{3,2,1,0:T(8,128)(2,1)}, u32[]{:S(2)}, u32[]{:S(2)}) collective-permute-start(bf16[4,3,48,384]{3,2,1,0:T(8,128)(2,1)} %collective-permute-done.6.refs_3_), channel_id=1, source_target_pairs={{0,1},{1,0},{2,3},{3,2},{4,5},{5,4},{6,7},{7,6},{8,9},{9,8},{10,11... | collective-permute-start | bytes 1327112 | tf_op jit(solution)/shard_map/ppermute | solution.py:50
  54.9 10.4 %collective-permute-start.8 = (bf16[4,3,48,384]{3,2,1,0:T(8,128)(2,1)}, bf16[4,3,48,384]{3,2,1,0:T(8,128)(2,1)}, u32[]{:S(2)}, u32[]{:S(2)}) collective-permute-start(bf16[4,3,48,384]{3,2,1,0:T(8,128)(2,1)} %collective-permute-done.4.refs_1_), channel_id=1, source_target_pairs={{0,1},{1,0},{2,3},{3,2},{4,5},{5,4},{6,7},{7,6},{8,9},{9,8},{10,11... | collective-permute-start | bytes 1327112 | tf_op jit(solution)/shard_map/ppermute | solution.py:50
  54.9 10.4 %collective-permute-start.9 = (bf16[4,3,48,384]{3,2,1,0:T(8,128)(2,1)}, bf16[4,3,48,384]{3,2,1,0:T(8,128)(2,1)}, u32[]{:S(2)}, u32[]{:S(2)}) collective-permute-start(bf16[4,3,48,384]{3,2,1,0:T(8,128)(2,1)} %collective-permute-done.5.refs_2_), channel_id=1, source_target_pairs={{0,1},{1,0},{2,3},{3,2},{4,5},{5,4},{6,7},{7,6},{8,9},{9,8},{10,11... | collective-permute-start | bytes 1327112 | tf_op jit(solution)/shard_map/ppermute | solution.py:50
  55.4 2.3 collective-permute-start.20
  57.8 1.4 collective-permute-start.21
  59.2 15.1 %collective-permute-start.22 = (bf16[2,96,768]{2,1,0:T(8,128)(2,1)}, bf16[2,96,768]{2,1,0:T(8,128)(2,1)}, u32[]{:S(2)}, u32[]{:S(2)}) collective-permute-start(bf16[2,96,768]{2,1,0:T(8,128)(2,1)} %param.23), channel_id=1, source_target_pairs={{0,8},{1,9},{2,10},{3,11},{4,12},{5,13},{6,14},{7,15},{8,0},{9,1},... | collective-permute-start | bytes 884744 | tf_op jit(solution)/shard_map/ppermute | solution.py:50
  62.4 21.9 %collective-permute-start.23 = (bf16[2,96,768]{2,1,0:T(8,128)(2,1)}, bf16[2,96,768]{2,1,0:T(8,128)(2,1)S(1)}, u32[]{:S(2)}, u32[]{:S(2)}) collective-permute-start(bf16[2,96,768]{2,1,0:T(8,128)(2,1)} %param.23), channel_id=1, source_target_pairs={{0,16},{1,17},{2,18},{3,19},{4,20},{5,21},{6,22},{7,23},{8,24},{9,... | collective-permute-start | bytes 884744 | tf_op jit(solution)/shard_map/ppermute | solution.py:50
  63.9 27.5 %collective-permute-start.24 = (bf16[2,96,768]{2,1,0:T(8,128)(2,1)}, bf16[2,96,768]{2,1,0:T(8,128)(2,1)}, u32[]{:S(2)}, u32[]{:S(2)}) collective-permute-start(bf16[2,96,768]{2,1,0:T(8,128)(2,1)} %param.23), channel_id=1, source_target_pairs={{0,24},{1,25},{2,26},{3,27},{4,28},{5,29},{6,30},{7,31},{8,16},{9,... | collective-permute-start | bytes 884744 | tf_op jit(solution)/shard_map/ppermute | solution.py:50
  93.7 30.4 %collective-permute-start.25 = (bf16[4,2,96,768]{3,2,1,0:T(8,128)(2,1)}, bf16[4,2,96,768]{3,2,1,0:T(8,128)(2,1)}, u32[]{:S(2)}, u32[]{:S(2)}) collective-permute-start(bf16[4,2,96,768]{3,2,1,0:T(8,128)(2,1)} %pad_maximum_fusion.1.refs_4_), channel_id=1, source_target_pairs={{0,2},{1,3},{2,0},{3,1},{4,6},{5,7},{6,4},{7,5},{8,10},{9,11},{10,... | collective-permute-start | bytes 3538952 | tf_op jit(solution)/shard_map/ppermute | solution.py:50
  94.9 52.2 %collective-permute-start.26 = (bf16[4,2,96,768]{3,2,1,0:T(8,128)(2,1)}, bf16[4,2,96,768]{3,2,1,0:T(8,128)(2,1)}, u32[]{:S(2)}, u32[]{:S(2)}) collective-permute-start(bf16[4,2,96,768]{3,2,1,0:T(8,128)(2,1)} %pad_maximum_fusion.1.refs_4_), channel_id=1, source_target_pairs={{0,4},{1,5},{2,6},{3,7},{4,0},{5,1},{6,2},{7,3},{8,12},{9,13},{10,... | collective-permute-start | bytes 3538952 | tf_op jit(solution)/shard_map/ppermute | solution.py:50
  95.7 51.4 %collective-permute-start.27 = (bf16[4,2,96,768]{3,2,1,0:T(8,128)(2,1)}, bf16[4,2,96,768]{3,2,1,0:T(8,128)(2,1)}, u32[]{:S(2)}, u32[]{:S(2)}) collective-permute-start(bf16[4,2,96,768]{3,2,1,0:T(8,128)(2,1)} %pad_maximum_fusion.1.refs_4_), channel_id=1, source_target_pairs={{0,6},{1,7},{2,4},{3,5},{4,2},{5,3},{6,0},{7,1},{8,14},{9,15},{10,... | collective-permute-start | bytes 3538952 | tf_op jit(solution)/shard_map/ppermute | solution.py:50
  124.1 29.0 %collective-permute-start.28 = (bf16[4,2,96,768]{3,2,1,0:T(8,128)(2,1)}, bf16[4,2,96,768]{3,2,1,0:T(8,128)(2,1)S(1)}, u32[]{:S(2)}, u32[]{:S(2)}) collective-permute-start(bf16[4,2,96,768]{3,2,1,0:T(8,128)(2,1)} %pad_maximum_fusion.1.refs_4_), channel_id=1, source_target_pairs={{0,1},{1,0},{2,3},{3,2},{4,5},{5,4},{6,7},{7,6},{8,9},{9,8},{10,11... | collective-permute-start | bytes 3538952 | tf_op jit(solution)/shard_map/ppermute | solution.py:50
  124.1 30.1 %collective-permute-start.29 = (bf16[4,2,96,768]{3,2,1,0:T(8,128)(2,1)}, bf16[4,2,96,768]{3,2,1,0:T(8,128)(2,1)S(1)}, u32[]{:S(2)}, u32[]{:S(2)}) collective-permute-start(bf16[4,2,96,768]{3,2,1,0:T(8,128)(2,1)} %collective-permute-done.25.refs_5_), channel_id=1, source_target_pairs={{0,1},{1,0},{2,3},{3,2},{4,5},{5,4},{6,7},{7,6},{8,9},{9,8},{10,11... | collective-permute-start | bytes 3538952 | tf_op jit(solution)/shard_map/ppermute | solution.py:50
  147.1 8.1 %collective-permute-start.30 = (bf16[4,2,96,768]{3,2,1,0:T(8,128)(2,1)}, bf16[4,2,96,768]{3,2,1,0:T(8,128)(2,1)S(1)}, u32[]{:S(2)}, u32[]{:S(2)}) collective-permute-start(bf16[4,2,96,768]{3,2,1,0:T(8,128)(2,1)} %collective-permute-done.26.refs_6_), channel_id=1, source_target_pairs={{0,1},{1,0},{2,3},{3,2},{4,5},{5,4},{6,7},{7,6},{8,9},{9,8},{10,11... | collective-permute-start | bytes 3538952 | tf_op jit(solution)/shard_map/ppermute | solution.py:50
  147.1 9.1 %collective-permute-start.31 = (bf16[4,2,96,768]{3,2,1,0:T(8,128)(2,1)}, bf16[4,2,96,768]{3,2,1,0:T(8,128)(2,1)S(1)}, u32[]{:S(2)}, u32[]{:S(2)}) collective-permute-start(bf16[4,2,96,768]{3,2,1,0:T(8,128)(2,1)} %collective-permute-done.27.refs_7_), channel_id=1, source_target_pairs={{0,1},{1,0},{2,3},{3,2},{4,5},{5,4},{6,7},{7,6},{8,9},{9,8},{10,11... | collective-permute-start | bytes 3538952 | tf_op jit(solution)/shard_map/ppermute | solution.py:50
  202.6 120.3 %collective-permute-start.53 = (bf16[4,4,2,96,768]{4,3,2,1,0:T(8,128)(2,1)}, bf16[4,4,2,96,768]{4,3,2,1,0:T(8,128)(2,1)}, u32[]{:S(2)}, u32[]{:S(2)}) collective-permute-start(bf16[4,4,2,96,768]{4,3,2,1,0:T(8,128)(2,1)} %get-tuple-element.44), channel_id=1, source_target_pairs={{0,1},{1,0},{2,3},{3,2},{4,5},{5,4},{6,7},{7,6},{8,9},{9,8},{10,11... | collective-permute-start | bytes 14155784 | tf_op jit(solution)/shard_map/ppermute | solution.py:50
  263.8 5.0 %collective-permute-start.32 = (f32[62,768]{1,0:T(8,128)S(1)}, f32[62,768]{1,0:T(8,128)S(1)}, u32[]{:S(2)}, u32[]{:S(2)}) collective-permute-start(f32[62,768]{1,0:T(8,128)S(1)} %concatenate.103), channel_id=1, source_target_pairs={{0,1},{1,0},{2,3},{3,2},{4,5},{5,4},{6,7},{7,6},{8,9},{9,8},{10,11... | collective-permute-start | bytes 571400 | tf_op jit(solution)/shard_map/ppermute | solution.py:50
  268.8 17.7 %collective-permute-start.33 = (f32[62,768]{1,0:T(8,128)S(1)}, f32[62,768]{1,0:T(8,128)}, u32[]{:S(2)}, u32[]{:S(2)}) collective-permute-start(f32[62,768]{1,0:T(8,128)S(1)} %add.313), channel_id=1, source_target_pairs={{0,2},{1,3},{2,0},{3,1},{4,6},{5,7},{6,4},{7,5},{8,10},{9,11},{10,... | collective-permute-start | bytes 571400 | tf_op jit(solution)/shard_map/ppermute | solution.py:50
  269.7 16.7 %collective-permute-start.34 = (f32[62,768]{1,0:T(8,128)S(1)}, f32[62,768]{1,0:T(8,128)}, u32[]{:S(2)}, u32[]{:S(2)}) collective-permute-start(f32[62,768]{1,0:T(8,128)S(1)} %add.313), channel_id=1, source_target_pairs={{0,4},{1,5},{2,6},{3,7},{4,0},{5,1},{6,2},{7,3},{8,12},{9,13},{10,... | collective-permute-start | bytes 571400 | tf_op jit(solution)/shard_map/ppermute | solution.py:50
  270.2 16.3 %collective-permute-start.35 = (f32[62,768]{1,0:T(8,128)S(1)}, f32[62,768]{1,0:T(8,128)}, u32[]{:S(2)}, u32[]{:S(2)}) collective-permute-start(f32[62,768]{1,0:T(8,128)S(1)} %add.313), channel_id=1, source_target_pairs={{0,6},{1,7},{2,4},{3,5},{4,2},{5,3},{6,0},{7,1},{8,14},{9,15},{10,... | collective-permute-start | bytes 571400 | tf_op jit(solution)/shard_map/ppermute | solution.py:50
  286.5 35.2 %collective-permute-start.39 = (bf16[4,4,3,24,768]{4,3,2,1,0:T(8,128)(2,1)}, bf16[4,4,3,24,768]{4,3,2,1,0:T(8,128)(2,1)S(1)}, u32[]{:S(2)}, u32[]{:S(2)}) collective-permute-start(bf16[4,4,3,24,768]{4,3,2,1,0:T(8,128)(2,1)} %get-tuple-element.40), channel_id=1, source_target_pairs={{0,1},{1,0},{2,3},{3,2},{4,5},{5,4},{6,7},{7,6},{8,9},{9,8},{10,11... | collective-permute-start | bytes 5308424 | tf_op jit(solution)/shard_map/ppermute | solution.py:50
  288.3 17.4 %collective-permute-start.36 = (f32[62,768]{1,0:T(8,128)}, f32[62,768]{1,0:T(8,128)}, u32[]{:S(2)}, u32[]{:S(2)}) collective-permute-start(f32[62,768]{1,0:T(8,128)} %add_add_fusion.6), channel_id=1, source_target_pairs={{0,8},{1,9},{2,10},{3,11},{4,12},{5,13},{6,14},{7,15},{8,0},{9,1},... | collective-permute-start | bytes 571400 | tf_op jit(solution)/shard_map/ppermute | solution.py:50
  288.3 17.4 %collective-permute-start.37 = (f32[62,768]{1,0:T(8,128)}, f32[62,768]{1,0:T(8,128)}, u32[]{:S(2)}, u32[]{:S(2)}) collective-permute-start(f32[62,768]{1,0:T(8,128)} %add_add_fusion.6), channel_id=1, source_target_pairs={{0,16},{1,17},{2,18},{3,19},{4,20},{5,21},{6,22},{7,23},{8,24},{9,... | collective-permute-start | bytes 571400 | tf_op jit(solution)/shard_map/ppermute | solution.py:50
  289.9 19.9 %collective-permute-start.38 = (f32[62,768]{1,0:T(8,128)}, f32[62,768]{1,0:T(8,128)}, u32[]{:S(2)}, u32[]{:S(2)}) collective-permute-start(f32[62,768]{1,0:T(8,128)} %add_add_fusion.6), channel_id=1, source_target_pairs={{0,24},{1,25},{2,26},{3,27},{4,28},{5,29},{6,30},{7,31},{8,16},{9,... | collective-permute-start | bytes 571400 | tf_op jit(solution)/shard_map/ppermute | solution.py:50
  305.7 10.1 %collective-permute-start.46 = (bf16[4,4,1,24,768]{4,3,2,1,0:T(8,128)(2,1)}, bf16[4,4,1,24,768]{4,3,2,1,0:T(8,128)(2,1)}, u32[]{:S(2)}, u32[]{:S(2)}) collective-permute-start(bf16[4,4,1,24,768]{4,3,2,1,0:T(8,128)(2,1)} %get-tuple-element.42), channel_id=1, source_target_pairs={{0,1},{1,0},{2,3},{3,2},{4,5},{5,4},{6,7},{7,6},{8,9},{9,8},{10,11... | collective-permute-start | bytes 1769480 | tf_op jit(solution)/shard_map/ppermute | solution.py:50
  317.0 11.4 %collective-permute-start.47 = (bf16[4,1,24,768]{3,2,0,1:T(8,128)(2,1)S(1)}, bf16[4,1,24,768]{3,2,0,1:T(8,128)(2,1)S(1)}, u32[]{:S(2)}, u32[]{:S(2)}) collective-permute-start(bf16[4,1,24,768]{3,2,0,1:T(8,128)(2,1)S(1)} %get-tuple-element.83), channel_id=1, source_target_pairs={{0,2},{1,3},{2,0},{3,1},{4,6},{5,7},{6,4},{7,5},{8,10},{9,11},{10,... | collective-permute-start | bytes 442376 | tf_op jit(solution)/shard_map/ppermute | solution.py:50
  317.9 11.3 %collective-permute-start.48 = (bf16[4,1,24,768]{3,2,0,1:T(8,128)(2,1)S(1)}, bf16[4,1,24,768]{3,2,0,1:T(8,128)(2,1)S(1)}, u32[]{:S(2)}, u32[]{:S(2)}) collective-permute-start(bf16[4,1,24,768]{3,2,0,1:T(8,128)(2,1)S(1)} %get-tuple-element.84), channel_id=1, source_target_pairs={{0,4},{1,5},{2,6},{3,7},{4,0},{5,1},{6,2},{7,3},{8,12},{9,13},{10,... | collective-permute-start | bytes 442376 | tf_op jit(solution)/shard_map/ppermute | solution.py:50
  319.4 11.3 %collective-permute-start.49 = (bf16[4,1,24,768]{3,2,0,1:T(8,128)(2,1)S(1)}, bf16[4,1,24,768]{3,2,0,1:T(8,128)(2,1)S(1)}, u32[]{:S(2)}, u32[]{:S(2)}) collective-permute-start(bf16[4,1,24,768]{3,2,0,1:T(8,128)(2,1)S(1)} %fusion.29), channel_id=1, source_target_pairs={{0,6},{1,7},{2,4},{3,5},{4,2},{5,3},{6,0},{7,1},{8,14},{9,15},{10,... | collective-permute-start | bytes 442376 | tf_op jit(solution)/shard_map/ppermute | solution.py:50
  321.9 14.7 %collective-permute-start.40 = (bf16[4,3,24,768]{3,2,1,0:T(8,128)(2,1)S(1)}, bf16[4,3,24,768]{3,2,1,0:T(8,128)(2,1)S(1)}, u32[]{:S(2)}, u32[]{:S(2)}) collective-permute-start(bf16[4,3,24,768]{3,2,1,0:T(8,128)(2,1)S(1)} %get-tuple-element.73), channel_id=1, source_target_pairs={{0,2},{1,3},{2,0},{3,1},{4,6},{5,7},{6,4},{7,5},{8,10},{9,11},{10,... | collective-permute-start | bytes 1327112 | tf_op jit(solution)/shard_map/ppermute | solution.py:50
  327.1 73.2 %collective-permute-start.54 = (bf16[4,2,96,768]{3,2,1,0:T(8,128)(2,1)S(1)}, bf16[4,2,96,768]{3,2,1,0:T(8,128)(2,1)S(1)}, u32[]{:S(2)}, u32[]{:S(2)}) collective-permute-start(bf16[4,2,96,768]{3,2,1,0:T(8,128)(2,1)S(1)} %get-tuple-element.70), channel_id=1, source_target_pairs={{0,2},{1,3},{2,0},{3,1},{4,6},{5,7},{6,4},{7,5},{8,10},{9,11},{10,... | collective-permute-start | bytes 3538952 | tf_op jit(solution)/shard_map/ppermute | solution.py:50
  328.3 74.0 %collective-permute-start.55 = (bf16[4,2,96,768]{3,2,1,0:T(8,128)(2,1)S(1)}, bf16[4,2,96,768]{3,2,1,0:T(8,128)(2,1)S(1)}, u32[]{:S(2)}, u32[]{:S(2)}) collective-permute-start(bf16[4,2,96,768]{3,2,1,0:T(8,128)(2,1)S(1)} %get-tuple-element.72), channel_id=1, source_target_pairs={{0,4},{1,5},{2,6},{3,7},{4,0},{5,1},{6,2},{7,3},{8,12},{9,13},{10,... | collective-permute-start | bytes 3538952 | tf_op jit(solution)/shard_map/ppermute | solution.py:50
  329.2 74.0 %collective-permute-start.56 = (bf16[4,2,96,768]{3,2,1,0:T(8,128)(2,1)S(1)}, bf16[4,2,96,768]{3,2,1,0:T(8,128)(2,1)S(1)}, u32[]{:S(2)}, u32[]{:S(2)}) collective-permute-start(bf16[4,2,96,768]{3,2,1,0:T(8,128)(2,1)S(1)} %get-tuple-element.71), channel_id=1, source_target_pairs={{0,6},{1,7},{2,4},{3,5},{4,2},{5,3},{6,0},{7,1},{8,14},{9,15},{10,... | collective-permute-start | bytes 3538952 | tf_op jit(solution)/shard_map/ppermute | solution.py:50
  331.8 66.6 %collective-permute-start.41 = (bf16[4,3,24,768]{3,2,1,0:T(8,128)(2,1)S(1)}, bf16[4,3,24,768]{3,2,1,0:T(8,128)(2,1)S(1)}, u32[]{:S(2)}, u32[]{:S(2)}) collective-permute-start(bf16[4,3,24,768]{3,2,1,0:T(8,128)(2,1)S(1)} %get-tuple-element.75), channel_id=1, source_target_pairs={{0,4},{1,5},{2,6},{3,7},{4,0},{5,1},{6,2},{7,3},{8,12},{9,13},{10,... | collective-permute-start | bytes 1327112 | tf_op jit(solution)/shard_map/ppermute | solution.py:50
  336.7 61.7 %collective-permute-start.42 = (bf16[4,3,24,768]{3,2,1,0:T(8,128)(2,1)S(1)}, bf16[4,3,24,768]{3,2,1,0:T(8,128)(2,1)S(1)}, u32[]{:S(2)}, u32[]{:S(2)}) collective-permute-start(bf16[4,3,24,768]{3,2,1,0:T(8,128)(2,1)S(1)} %get-tuple-element.74), channel_id=1, source_target_pairs={{0,6},{1,7},{2,4},{3,5},{4,2},{5,3},{6,0},{7,1},{8,14},{9,15},{10,... | collective-permute-start | bytes 1327112 | tf_op jit(solution)/shard_map/ppermute | solution.py:50
  398.4 7.9 %collective-permute-start.50 = (bf16[1,24,768]{2,1,0:T(8,128)(2,1)S(1)}, bf16[1,24,768]{2,1,0:T(8,128)(2,1)S(1)}, u32[]{:S(2)}, u32[]{:S(2)}) collective-permute-start(bf16[1,24,768]{2,1,0:T(8,128)(2,1)S(1)} %get-tuple-element.90), channel_id=1, source_target_pairs={{0,8},{1,9},{2,10},{3,11},{4,12},{5,13},{6,14},{7,15},{8,0},{9,1},... | collective-permute-start | bytes 110600 | tf_op jit(solution)/shard_map/ppermute | solution.py:50
  398.4 9.9 %collective-permute-start.51 = (bf16[1,24,768]{2,1,0:T(8,128)(2,1)S(1)}, bf16[1,24,768]{2,1,0:T(8,128)(2,1)S(1)}, u32[]{:S(2)}, u32[]{:S(2)}) collective-permute-start(bf16[1,24,768]{2,1,0:T(8,128)(2,1)S(1)} %get-tuple-element.91), channel_id=1, source_target_pairs={{0,16},{1,17},{2,18},{3,19},{4,20},{5,21},{6,22},{7,23},{8,24},{9,... | collective-permute-start | bytes 110600 | tf_op jit(solution)/shard_map/ppermute | solution.py:50
  400.3 9.9 %collective-permute-start.52 = (bf16[1,24,768]{2,1,0:T(8,128)(2,1)S(1)}, bf16[1,24,768]{2,1,0:T(8,128)(2,1)S(1)}, u32[]{:S(2)}, u32[]{:S(2)}) collective-permute-start(bf16[1,24,768]{2,1,0:T(8,128)(2,1)S(1)} %slice_bitcast_fusion.20), channel_id=1, source_target_pairs={{0,24},{1,25},{2,26},{3,27},{4,28},{5,29},{6,30},{7,31},{8,16},{9,... | collective-permute-start | bytes 110600 | tf_op jit(solution)/shard_map/ppermute | solution.py:50
  402.3 7.9 %collective-permute-start.43 = (bf16[3,24,768]{2,1,0:T(8,128)(2,1)S(1)}, bf16[3,24,768]{2,1,0:T(8,128)(2,1)S(1)}, u32[]{:S(2)}, u32[]{:S(2)}) collective-permute-start(bf16[3,24,768]{2,1,0:T(8,128)(2,1)S(1)} %get-tuple-element.85), channel_id=1, source_target_pairs={{0,8},{1,9},{2,10},{3,11},{4,12},{5,13},{6,14},{7,15},{8,0},{9,1},... | collective-permute-start | bytes 331784 | tf_op jit(solution)/shard_map/ppermute | solution.py:50
  403.2 9.3 %collective-permute-start.44 = (bf16[3,24,768]{2,1,0:T(8,128)(2,1)S(1)}, bf16[3,24,768]{2,1,0:T(8,128)(2,1)S(1)}, u32[]{:S(2)}, u32[]{:S(2)}) collective-permute-start(bf16[3,24,768]{2,1,0:T(8,128)(2,1)S(1)} %get-tuple-element.87), channel_id=1, source_target_pairs={{0,16},{1,17},{2,18},{3,19},{4,20},{5,21},{6,22},{7,23},{8,24},{9,... | collective-permute-start | bytes 331784 | tf_op jit(solution)/shard_map/ppermute | solution.py:50
  406.3 10.9 %collective-permute-start.45 = (bf16[3,24,768]{2,1,0:T(8,128)(2,1)S(1)}, bf16[3,24,768]{2,1,0:T(8,128)(2,1)S(1)}, u32[]{:S(2)}, u32[]{:S(2)}) collective-permute-start(bf16[3,24,768]{2,1,0:T(8,128)(2,1)S(1)} %get-tuple-element.86), channel_id=1, source_target_pairs={{0,24},{1,25},{2,26},{3,27},{4,28},{5,29},{6,30},{7,31},{8,16},{9,... | collective-permute-start | bytes 331784 | tf_op jit(solution)/shard_map/ppermute | solution.py:50
  408.3 12.0 %collective-permute-start.57 = (bf16[2,96,768]{2,1,0:T(8,128)(2,1)S(1)}, bf16[2,96,768]{2,1,0:T(8,128)(2,1)S(1)}, u32[]{:S(2)}, u32[]{:S(2)}) collective-permute-start(bf16[2,96,768]{2,1,0:T(8,128)(2,1)S(1)} %get-tuple-element.80), channel_id=1, source_target_pairs={{0,8},{1,9},{2,10},{3,11},{4,12},{5,13},{6,14},{7,15},{8,0},{9,1},... | collective-permute-start | bytes 884744 | tf_op jit(solution)/shard_map/ppermute | solution.py:50
  410.1 22.0 %collective-permute-start.58 = (bf16[2,96,768]{2,1,0:T(8,128)(2,1)S(1)}, bf16[2,96,768]{2,1,0:T(8,128)(2,1)S(1)}, u32[]{:S(2)}, u32[]{:S(2)}) collective-permute-start(bf16[2,96,768]{2,1,0:T(8,128)(2,1)S(1)} %get-tuple-element.82), channel_id=1, source_target_pairs={{0,16},{1,17},{2,18},{3,19},{4,20},{5,21},{6,22},{7,23},{8,24},{9,... | collective-permute-start | bytes 884744 | tf_op jit(solution)/shard_map/ppermute | solution.py:50
  410.2 28.5 %collective-permute-start.59 = (bf16[2,96,768]{2,1,0:T(8,128)(2,1)S(1)}, bf16[2,96,768]{2,1,0:T(8,128)(2,1)S(1)}, u32[]{:S(2)}, u32[]{:S(2)}) collective-permute-start(bf16[2,96,768]{2,1,0:T(8,128)(2,1)S(1)} %get-tuple-element.81), channel_id=1, source_target_pairs={{0,24},{1,25},{2,26},{3,27},{4,28},{5,29},{6,30},{7,31},{8,16},{9,... | collective-permute-start | bytes 884744 | tf_op jit(solution)/shard_map/ppermute | solution.py:50
  (38 other events, 159.9 us)

commit v2 on v1

v2 whole, which is shorter than its diff:
```python
from functools import partial

import jax
import jax.numpy as jnp
from jax import lax
from jax.experimental import pallas as pl
from jax.experimental.pallas import tpu as pltpu
from jax.sharding import PartitionSpec as P

NPROMPT = 50
ROW = 1024
SPANS = (151, 247, 627)
EPS = 1e-06
HIGHEST = lax.Precision.HIGHEST
BIG = 1e30
B16 = jnp.bfloat16
F32 = jnp.float32
AXES = ("dp", "mp")
TILE = 256
NT = (((1,), (1,)), ((), ()))
TN = (((0,), (0,)), ((), ()))
VMEM_LIMIT = 60 * 1024 * 1024


def layer_norm(value_list, gain_row, shift_row):
    centre = jnp.mean(value_list, axis=-1, keepdims=True)
    centred = value_list - centre
    spread = jnp.mean(centred * centred, axis=-1, keepdims=True)
    return centred * lax.rsqrt(spread + EPS) * gain_row + shift_row


def key_window(first, count):
    low, high = ROW, 0
    for span in SPANS:
        whole = ROW // span
        for row in (first, first + count - 1):
            seg = min(row // span, whole)
            low = min(low, seg * span)
            high = max(high, ROW if seg == whole else (seg + 1) * span)
    return low // 128 * 128, -(-high // 128) * 128


def dotf(a, b, dims=None):
    if dims is None:
        return jnp.dot(a, b, preferred_element_type=F32)
    return lax.dot_general(a, b, dims, preferred_element_type=F32)


def px(x, k):
    return lax.ppermute(x, AXES, [(i, i ^ k) for i in range(32)])


def tie(*trees):
    return lax.optimization_barrier(trees)


def stack_kernel(*refs):
    for i, ref in enumerate(refs[:-1]):
        refs[-1][i] = ref[...]


def stack(parts, name):
    vmem = pl.BlockSpec(memory_space=pltpu.VMEM)
    return pl.pallas_call(
        stack_kernel,
        name=name,
        out_shape=jax.ShapeDtypeStruct((len(parts),) + parts[0].shape, parts[0].dtype),
        in_specs=[vmem] * len(parts),
        out_specs=vmem,
    )(*parts)


def z_stage(piece):
    return stack([piece] + [px(piece, 8 * k) for k in range(1, 4)], "stack_z")


def xy_stage(parts):
    return [parts] + [px(parts, 2 * k) for k in range(1, 4)]


def split_kernel(meta, qkv_ref, out_ref, mine_ref, theirs_ref):
    core = meta[0] % 2
    for ref, half in ((mine_ref, core), (theirs_ref, 1 - core)):
        cols = pl.ds(pl.multiple_of(384 * half, 128), 384)
        ref[0:3] = qkv_ref[:, :, cols]
        ref[3] = out_ref[:, cols]


def join_kernel(meta, mine_ref, got_ref, out_ref):
    for core in range(2):

        @pl.when(meta[0] % 2 == core)
        def _():
            out_ref[...] = jnp.concatenate([mine_ref[...], got_ref[...]][:: 1 - 2 * core], 1)


def pair_rows(meta, qkv, out):
    vmem = pl.BlockSpec(memory_space=pltpu.VMEM)
    smem = pl.BlockSpec(memory_space=pltpu.SMEM)
    half = jax.ShapeDtypeStruct((4, 24, 384), B16)
    mine, theirs = pl.pallas_call(
        split_kernel, name="split", out_shape=(half, half), in_specs=[smem, vmem, vmem], out_specs=(vmem, vmem)
    )(meta, qkv, out)
    return pl.pallas_call(
        join_kernel,
        name="join",
        out_shape=jax.ShapeDtypeStruct((4, 48, 384), B16),
        in_specs=[smem, vmem, vmem],
        out_specs=vmem,
    )(meta, mine, px(theirs, 1))


def assemble_kernel(meta, *refs):
    pieces, out, sems = refs[:4], refs[4], refs[5]
    copies = []
    for xy in range(4):
        for z in range(4):
            rows = pl.multiple_of(48 * jnp.bitwise_xor(meta[0] // 2, xy + 4 * z), 16)
            copies.append(
                pltpu.make_async_copy(pieces[xy].at[z], out.at[:, pl.ds(rows, 48), :], sems.at[4 * xy + z])
            )
    for copy in copies:
        copy.start()
    for copy in copies:
        copy.wait()


def assemble(meta, pieces, name):
    return pl.pallas_call(
        assemble_kernel,
        name=name,
        out_shape=jax.ShapeDtypeStruct((4, 768, 384), B16),
        in_specs=[pl.BlockSpec(memory_space=pltpu.SMEM)] + [pl.BlockSpec(memory_space=pl.ANY)] * 4,
        out_specs=pl.BlockSpec(memory_space=pltpu.VMEM),
        scratch_shapes=[pltpu.SemaphoreType.DMA((16,))],
    )(meta, *pieces)


def project_kernel(side, meta, x_ref, w_ref, b_ref, *refs):
    half = jnp.bitwise_xor(meta[0] % 2, side)
    cols = pl.ds(pl.multiple_of(384 * half, 128), 384)
    for c in range(3):
        y = dotf(x_ref[...], w_ref[c]) + b_ref[c, :, cols]
        refs[-1][:, 384 * c : 384 * c + 384] = y.astype(B16)


def project(meta, x, weight, bias, side, held):
    rows = x.shape[0]
    vmem = pl.BlockSpec(memory_space=pltpu.VMEM)
    return pl.pallas_call(
        partial(project_kernel, side),
        name="project",
        grid=(rows // TILE,),
        out_shape=jax.ShapeDtypeStruct((rows, 2304), B16),
        in_specs=[
            pl.BlockSpec(memory_space=pltpu.SMEM),
            pl.BlockSpec((TILE, 768), lambda i: (i, 0)),
            pl.BlockSpec((3, 768, 384), lambda i: (0, 0, 0), pipeline_mode=pl.Buffered(1)),
            vmem,
        ]
        + [pl.BlockSpec(memory_space=pl.ANY)] * len(held),
        out_specs=pl.BlockSpec((TILE, 1152), lambda i: (i, side)),
        input_output_aliases={4 + i: i for i in range(len(held))},
        compiler_params=pltpu.CompilerParams(vmem_limit_bytes=VMEM_LIMIT),
    )(meta, x, weight, bias, *held)


def embed_kernel(tokens_ref, slots_ref, segs_ref, table_ref, p_ref, start_ref, normed_ref, hot_ref, qf_ref, kf_ref):
    lane = lax.broadcasted_iota(jnp.int32, (TILE, 128), 1)
    slots, segs = slots_ref[...], segs_ref[...]
    is_prompt = slots < NPROMPT
    hot = jnp.where((lane == slots) & is_prompt, 1.0, 0.0).astype(B16)
    hot_ref[...] = hot
    rows = None
    for part in three_parts(table_ref[...]):
        term = dotf(hot, part.astype(B16))
        rows = term if rows is None else rows + term
    start = jnp.where(is_prompt, rows, tokens_ref[...].astype(F32))
    start_ref[...] = start
    normed_ref[...] = (centred(start)[0] * p_ref[0:1] + p_ref[1:2]).astype(B16)
    spot = lane % 64
    same = (spot == segs) & (spot < 7)
    qf_ref[...] = jnp.where(same, 1.0, 0.0).astype(B16)
    kf = jnp.where(spot < 7, jnp.where(same, 0.0, -BIG), jnp.where(spot < 10, 1.0, 0.0))
    kf_ref[...] = kf.astype(B16)


def embed(tokens, slots, segs, table, params):
    rows = tokens.shape[0]

    def block(width):
        return pl.BlockSpec((TILE, width), lambda i: (i, 0))

    vmem = pl.BlockSpec(memory_space=pltpu.VMEM)
    lanes = jax.ShapeDtypeStruct((rows, 128), B16)
    return pl.pallas_call(
        embed_kernel,
        name="embed",
        grid=(rows // TILE,),
        in_specs=[block(768), block(1), block(1), vmem, vmem],
        out_specs=[block(768), block(768), block(128), block(128), block(128)],
        out_shape=(
            jax.ShapeDtypeStruct((rows, 768), F32),
            jax.ShapeDtypeStruct((rows, 768), B16),
            lanes,
            lanes,
            lanes,
        ),
    )(tokens, slots[:, None], segs[:, None], table, params)


def gather_sums_kernel(own_ref, got_ref, own_out_ref, got_out_ref, keep_ref, *sends):
    for k in range(4):
        for z in range(4):
            for m in range(4):
                if m < 3:
                    x = add_parts(own_ref[k, z, m], got_ref[k, z, m])
                else:
                    x = add_parts(own_out_ref[k, z, 0], got_out_ref[k, z, 0])
                if k:
                    sends[k - 1][z, m] = x.astype(B16)
                else:
                    keep_ref[z, m] = x


def gather_sums(own, got, own_out, got_out):
    vmem = pl.BlockSpec(memory_space=pltpu.VMEM)
    send = jax.ShapeDtypeStruct((4, 4, 24, 768), B16)
    return pl.pallas_call(
        gather_sums_kernel,
        name="gather_sums",
        in_specs=[vmem] * 4,
        out_specs=[vmem] * 4,
        out_shape=(jax.ShapeDtypeStruct((4, 4, 24, 768), F32), send, send, send),
        compiler_params=pltpu.CompilerParams(vmem_limit_bytes=VMEM_LIMIT),
    )(own, got, own_out, got_out)


def four(values):
    return (values[0] + values[1]) + (values[2] + values[3])


def plane_sums_kernel(keep_ref, *refs):
    moved, (col_ref, *sends) = refs[:3], refs[3:]
    for z in range(4):
        for m in range(4):
            x = four([keep_ref[z, m]] + [ref[z, m].astype(F32) for ref in moved])
            if z:
                sends[z - 1][m] = x.astype(B16)
            else:
                col_ref[m] = x


def plane_sums(keep, moved):
    vmem = pl.BlockSpec(memory_space=pltpu.VMEM)
    send = jax.ShapeDtypeStruct((4, 24, 768), B16)
    return pl.pallas_call(
        plane_sums_kernel,
        name="plane_sums",
        in_specs=[vmem] * 4,
        out_specs=[vmem] * 4,
        out_shape=(jax.ShapeDtypeStruct((4, 24, 768), F32), send, send, send),
        compiler_params=pltpu.CompilerParams(vmem_limit_bytes=VMEM_LIMIT),
    )(keep, *moved)


def line_sums_kernel(col_ref, *refs):
    last, (qkv_ref, out_ref) = refs[:3], refs[3:]
    for m in range(4):
        x = four([col_ref[m]] + [ref[m].astype(F32) for ref in last])
        if m < 3:
            qkv_ref[m] = x
        else:
            out_ref[...] = x


def line_sums(col, last):
    vmem = pl.BlockSpec(memory_space=pltpu.VMEM)
    return pl.pallas_call(
        line_sums_kernel,
        name="line_sums",
        in_specs=[vmem] * 4,
        out_specs=[vmem] * 2,
        out_shape=(jax.ShapeDtypeStruct((3, 24, 768), F32), jax.ShapeDtypeStruct((24, 768), F32)),
    )(col, *last)


def centred(x):
    mean = jnp.mean(x, axis=-1, keepdims=True)
    x = x - mean
    rate = lax.rsqrt(jnp.mean(x * x, axis=-1, keepdims=True) + EPS)
    return x * rate, rate


def out_kernel(meta, x_ref, start_ref, own_ref, other_ref, p_ref, middle_ref, normed_ref, w_ref):
    core = meta[0] % 2

    @pl.when(pl.program_id(0) == 0)
    def _():
        for ref, half in ((own_ref, core), (other_ref, 1 - core)):
            w_ref[:, pl.ds(pl.multiple_of(384 * half, 128), 384)] = ref[3]

    middle = start_ref[...] + dotf(x_ref[...], w_ref[...]) + p_ref[0:1]
    middle_ref[...] = middle
    normed_ref[...] = (centred(middle)[0] * p_ref[1:2] + p_ref[2:3]).astype(B16)


def out_projection(meta, mixed, start, own, other, params):
    rows = mixed.shape[0]
    block = pl.BlockSpec((TILE, 768), lambda i: (i, 0))
    vmem = pl.BlockSpec(memory_space=pltpu.VMEM)
    return pl.pallas_call(
        out_kernel,
        name="out_projection",
        grid=(rows // TILE,),
        in_specs=[pl.BlockSpec(memory_space=pltpu.SMEM), block, block, vmem, vmem, vmem],
        out_specs=[block, block, vmem],
        out_shape=(
            jax.ShapeDtypeStruct((rows, 768), F32),
            jax.ShapeDtypeStruct((rows, 768), B16),
            jax.ShapeDtypeStruct((768, 768), B16),
        ),
        compiler_params=pltpu.CompilerParams(vmem_limit_bytes=VMEM_LIMIT),
    )(meta, mixed, start, own, other, params)


def norm_backward(normal, rate, grad, gain):
    u = grad * gain
    return rate * (u - jnp.mean(u, axis=-1, keepdims=True) - normal * jnp.mean(u * normal, axis=-1, keepdims=True))


def row_sum(x):
    return jnp.sum(x, axis=0, keepdims=True)


def put_parts(meta, acc, own_ref, other_ref, m):
    chip, core = meta[0] // 2, meta[0] % 2
    for z in range(4):
        for xy in range(4):
            row = 48 * jnp.bitwise_xor(chip, xy + 4 * z)
            own_ref[xy, z, m] = acc[pl.ds(pl.multiple_of(row + 24 * core, 8), 24), :].astype(B16)
            other_ref[xy, z, m] = acc[pl.ds(pl.multiple_of(row + 24 * (1 - core), 8), 24), :].astype(B16)


def turn_kernel(
    meta, middle_ref, branch_ref, grad_ref, cot_ref, mixed_ref, w_ref, p_ref,
    output_ref, gmiddle_ref, gmixed_ref, own_ref, other_ref, sums_ref, acc,
):
    i = pl.program_id(0)

    @pl.when(i == 0)
    def _():
        sums_ref[...] = jnp.zeros_like(sums_ref)
        acc[...] = jnp.zeros_like(acc)

    middle, grad = middle_ref[...], grad_ref[...]
    cot = cot_ref[...].astype(F32)
    output_ref[...] = (middle + branch_ref[...] + p_ref[1:2]).astype(B16)
    normal, rate = centred(middle)
    gmiddle = cot + norm_backward(normal, rate, grad, p_ref[0:1])
    gmiddle_ref[...] = gmiddle
    low = gmiddle.astype(B16)
    for row, x in enumerate((normal * grad, grad, low.astype(F32), cot)):
        sums_ref[row : row + 1, :] += row_sum(x)
    gmixed_ref[...] = dotf(low, w_ref[...], NT).astype(B16)
    acc[...] += dotf(mixed_ref[...], low, TN)

    @pl.when(i == pl.num_programs(0) - 1)
    def _():
        put_parts(meta, acc, own_ref, other_ref, 0)


def turn(meta, middle, branch, grad, cot, mixed, weight, params):
    rows = middle.shape[0]
    block = pl.BlockSpec((TILE, 768), lambda i: (i, 0))
    vmem = pl.BlockSpec(memory_space=pltpu.VMEM)
    parts = jax.ShapeDtypeStruct((4, 4, 1, 24, 768), B16)
    return pl.pallas_call(
        turn_kernel,
        name="turn",
        grid=(rows // TILE,),
        in_specs=[pl.BlockSpec(memory_space=pltpu.SMEM)] + [block] * 5 + [vmem, vmem],
        out_specs=[block, block, block, vmem, vmem, vmem],
        out_shape=(
            jax.ShapeDtypeStruct((rows, 768), B16),
            jax.ShapeDtypeStruct((rows, 768), F32),
            jax.ShapeDtypeStruct((rows, 768), B16),
            parts,
            parts,
            jax.ShapeDtypeStruct((8, 768), F32),
        ),
        scratch_shapes=[pltpu.VMEM((768, 768), F32)],
        compiler_params=pltpu.CompilerParams(vmem_limit_bytes=VMEM_LIMIT),
    )(meta, middle, branch, grad, cot, mixed, weight, params)


def tail_kernel(meta, start_ref, gmiddle_ref, slots_ref, p_ref, *refs):
    weights, grads = refs[:2], refs[2:5]
    input_ref, prompt_ref, sums_ref = refs[5:]
    core = meta[0] % 2

    @pl.when(pl.program_id(0) == 0)
    def _():
        prompt_ref[...] = jnp.zeros_like(prompt_ref)
        sums_ref[...] = jnp.zeros_like(sums_ref)

    total = None
    for c in range(3):
        for side in range(2):
            half = jnp.bitwise_xor(core, side)
            left = grads[c][:, pl.ds(pl.multiple_of(384 * half, 128), 384)]
            term = dotf(left, weights[side][c], NT)
            total = term if total is None else total + term
    normal, rate = centred(start_ref[...])
    for row, x in enumerate((normal * total, total, grads[0][...].astype(F32), grads[2][...].astype(F32))):
        sums_ref[row : row + 1, :] += row_sum(x)
    gstart = gmiddle_ref[...] + norm_backward(normal, rate, total, p_ref[0:1])
    slots = slots_ref[...]
    is_prompt = jnp.sum(slots.astype(F32), axis=-1, keepdims=True) > 0.5
    input_ref[...] = jnp.where(is_prompt, 0.0, gstart)
    for part in three_parts(gstart):
        prompt_ref[...] += dotf(slots, part.astype(B16), TN)


def tail_step(meta, start, gmiddle, slots, params, weights, grads):
    rows = start.shape[0]

    def block(width):
        return pl.BlockSpec((TILE, width), lambda i: (i, 0))

    vmem = pl.BlockSpec(memory_space=pltpu.VMEM)
    return pl.pallas_call(
        tail_kernel,
        name="tail_step",
        grid=(rows // TILE,),
        in_specs=[pl.BlockSpec(memory_space=pltpu.SMEM), block(768), block(768), block(128), vmem, vmem, vmem]
        + [block(768)] * 3,
        out_specs=[block(768), vmem, vmem],
        out_shape=(
            jax.ShapeDtypeStruct((rows, 768), F32),
            jax.ShapeDtypeStruct((128, 768), F32),
            jax.ShapeDtypeStruct((8, 768), F32),
        ),
        compiler_params=pltpu.CompilerParams(vmem_limit_bytes=VMEM_LIMIT),
    )(meta, start, gmiddle, slots, params, *weights, *grads)


def weight_grad_kernel(count, meta, left_ref, *refs):
    rights, own_ref, other_ref, acc = refs[:count], refs[count], refs[count + 1], refs[count + 2]
    for m in range(count):
        acc[...] = dotf(left_ref[...], rights[m][...], TN)
        put_parts(meta, acc, own_ref, other_ref, m)


def weight_grad(meta, left, rights, name):
    count, width = len(rights), rights[0].shape[1]
    shape = jax.ShapeDtypeStruct((4, 4, count, 24, width), B16)
    vmem = pl.BlockSpec(memory_space=pltpu.VMEM)
    return pl.pallas_call(
        partial(weight_grad_kernel, count),
        name=name,
        out_shape=(shape, shape),
        in_specs=[pl.BlockSpec(memory_space=pltpu.SMEM)] + [vmem] * (count + 1),
        out_specs=(vmem, vmem),
        scratch_shapes=[pltpu.VMEM((left.shape[1], width), F32)],
        compiler_params=pltpu.CompilerParams(vmem_limit_bytes=VMEM_LIMIT),
    )(meta, left, *rights)


def pack_small(small):
    low = small[:NPROMPT].astype(B16)
    rest = small[NPROMPT:]
    high = rest.astype(B16)
    return jnp.concatenate([low, high, (rest - high.astype(F32)).astype(B16), jnp.zeros((6, small.shape[1]), B16)])


def open_small(packed):
    wide = packed.astype(F32)
    at = NPROMPT + 12
    return jnp.concatenate([wide[:NPROMPT], wide[NPROMPT:at] + wide[at : at + 12]])


def add_parts(own, got):
    return own.astype(F32) + got.astype(F32)


def three_parts(x):
    high = x.astype(B16).astype(F32)
    mid = (x - high).astype(B16).astype(F32)
    return high, mid, (x - high) - mid


def attention_forward_kernel(qf_ref, kf_ref, q_ref, k_ref, v_ref, mixed_ref, lse_ref):
    half = lax.broadcasted_iota(jnp.int32, (1, 128), 1) < 64
    q = q_ref[...] * jnp.asarray(0.125, B16)
    k, v = k_ref[...], v_ref[...]
    qf, kf = qf_ref[...], kf_ref[...]
    one = jnp.ones((), B16)
    sides = []
    for e in range(2):
        own = half if e == 0 else ~half
        sides.append((jnp.where(own, q, qf), jnp.where(own, k, kf), jnp.where(own, v, one)))
    for first in range(0, ROW, TILE):
        low, high = key_window(first, TILE)
        outs, peaks = [], []
        for qe, ke, ve in sides:
            s = dotf(qe[first : first + TILE], ke[low:high], NT)
            peak = jnp.max(s, axis=-1, keepdims=True)
            p = jnp.exp(s - peak).astype(B16)
            outs.append(dotf(p, ve[low:high]))
            peaks.append(peak)
        data = jnp.where(half, outs[0], outs[1])
        total = pltpu.roll(jnp.where(half, outs[1], outs[0]), 64, 1)
        mixed_ref[first : first + TILE, :] = (data / total).astype(B16)
        lse_ref[first : first + TILE, :] = jnp.where(half, peaks[0], peaks[1]) + jnp.log(total)


def pair_specs(rows):
    full = pl.BlockSpec((ROW, 128), lambda r, s, p, meta: (r, 0))
    blocks = [pl.BlockSpec((ROW, 128), lambda r, s, p, meta, c=c: (r, 9 * s + 3 * c + p)) for c in range(3)]
    whole = pl.BlockSpec((ROW, 128), lambda r, s, p, meta: (r, 3 * jnp.bitwise_xor(meta[0] % 2, s) + p))
    return (rows // ROW, 2, 3), full, blocks, whole


def attention_forward(meta, qf, kf, qkv):
    rows = qkv.shape[0]
    grid, full, blocks, whole = pair_specs(rows)

    def kernel(meta, *refs):
        attention_forward_kernel(*refs)

    return pl.pallas_call(
        kernel,
        name="attention_forward",
        grid_spec=pltpu.PrefetchScalarGridSpec(
            num_scalar_prefetch=1, grid=grid, in_specs=[full, full] + blocks, out_specs=[whole, whole]
        ),
        out_shape=(
            jax.ShapeDtypeStruct((rows, 768), B16),
            jax.ShapeDtypeStruct((rows, 768), F32),
        ),
        compiler_params=pltpu.CompilerParams(vmem_limit_bytes=VMEM_LIMIT),
    )(meta, qf, kf, qkv, qkv, qkv)


def attention_backward_kernel(
    qf_ref, kf_ref, q_ref, k_ref, v_ref, g_ref, mixed_ref, lse_ref, dq_ref, dk_ref, dv_ref, dk_acc, dv_acc
):
    lane = lax.broadcasted_iota(jnp.int32, (1, 128), 1)
    half = lane < 64
    spot = lane % 64
    q = q_ref[...] * jnp.asarray(0.125, B16)
    k, v, g = k_ref[...], v_ref[...], g_ref[...]
    qf, kf = qf_ref[...].astype(F32), kf_ref[...]
    prod = g.astype(F32) * mixed_ref[...].astype(F32)
    d0 = jnp.sum(jnp.where(half, prod, 0.0), axis=-1, keepdims=True)
    d1 = jnp.sum(jnp.where(half, 0.0, prod), axis=-1, keepdims=True)
    delta = jnp.where(half, d1, d0)
    lse = pltpu.roll(lse_ref[...], 64, 1)

    def spread(base, x):
        a, b, c = three_parts(-x)
        return jnp.where(spot == 7, a, jnp.where(spot == 8, b, jnp.where(spot == 9, c, base))).astype(B16)

    q_extra = spread(qf, lse)
    g_extra = spread(jnp.zeros_like(qf), delta)
    v_extra = jnp.where((spot >= 7) & (spot <= 9), 1.0, 0.0).astype(B16)
    dk_acc[...] = jnp.zeros_like(dk_acc)
    dv_acc[...] = jnp.zeros_like(dv_acc)
    sides = []
    for e in range(2):
        own = half if e == 0 else ~half
        sides.append(
            (
                jnp.where(own, q, q_extra),
                jnp.where(own, k, kf),
                jnp.where(own, g, g_extra),
                jnp.where(own, v, v_extra),
            )
        )
    for first in range(0, ROW, TILE):
        low, high = key_window(first, TILE)
        dqs, dks, dvs = [], [], []
        for qe, ke, ge, ve in sides:
            s = dotf(qe[first : first + TILE], ke[low:high], NT)
            p = jnp.exp(s)
            d = dotf(ge[first : first + TILE], ve[low:high], NT)
            ds = (p * d).astype(B16)
            dqs.append(dotf(ds, k[low:high]))
            dks.append(dotf(ds, q[first : first + TILE], TN))
            dvs.append(dotf(p.astype(B16), g[first : first + TILE], TN))
        dq_ref[first : first + TILE, :] = (jnp.where(half, dqs[0], dqs[1]) * 0.125).astype(B16)
        dk_acc[low:high, :] += jnp.where(half, dks[0], dks[1])
        dv_acc[low:high, :] += jnp.where(half, dvs[0], dvs[1])
    dk_ref[...] = dk_acc[...].astype(B16)
    dv_ref[...] = dv_acc[...].astype(B16)


def attention_backward(meta, qf, kf, qkv, grad, mixed, lse):
    rows = qkv.shape[0]
    grid, full, blocks, whole = pair_specs(rows)
    shape = jax.ShapeDtypeStruct((rows, 768), B16)

    def kernel(meta, *refs):
        attention_backward_kernel(*refs)

    return pl.pallas_call(
        kernel,
        name="attention_backward",
        grid_spec=pltpu.PrefetchScalarGridSpec(
            num_scalar_prefetch=1,
            grid=grid,
            in_specs=[full, full] + blocks + [whole] * 3,
            out_specs=[whole] * 3,
            scratch_shapes=[pltpu.VMEM((ROW, 128), F32), pltpu.VMEM((ROW, 128), F32)],
        ),
        out_shape=(shape, shape, shape),
        compiler_params=pltpu.CompilerParams(vmem_limit_bytes=VMEM_LIMIT),
    )(meta, qf, kf, qkv, qkv, qkv, grad, mixed, lse)


SUB = 256
PER = 768 // SUB


def mlp_kernel(fast, base, *refs):
    meta, n_ref, c_ref, b_ref = refs[:4]
    count = 4 if fast else 1
    pieces, refs = refs[4 : 4 + count], refs[4 + count :]
    if base:
        held, refs = refs[:2], refs[2:]
    branch_ref, gn_ref, db_ref, own_ref, other_ref = refs[:5]
    w, nt, ct, dw, wsem, dsem = refs[5:]
    t = pl.program_id(0)
    jl, sub = t // PER, t % PER
    me_mp, me_dp = meta[0] % 4, meta[0] // 4

    def loads(j):
        if not fast:
            source = pieces[0].at[:, :, pl.ds(768 * (base + j), 768)]
            return [pltpu.make_async_copy(source, w.at[j], wsem.at[j, 0])]
        out = []
        for dr in range(8):
            rows = pl.multiple_of(96 * jnp.bitwise_xor(me_dp, dr), 32)
            source = pieces[2 * j + (dr & 1)].at[dr >> 1]
            out.append(pltpu.make_async_copy(source, w.at[j, :, pl.ds(rows, 96), :], wsem.at[j, dr]))
        return out

    def stores(j):
        out = []
        for dr in range(8):
            target = (other_ref if j else own_ref).at[dr & 1, dr >> 1]
            out.append(pltpu.make_async_copy(dw.at[j, dr], target, dsem.at[j, dr]))
        return out

    @pl.when(t == 0)
    def _():
        for j in range(2):
            for copy in loads(j):
                copy.start()
        nt[...] = n_ref[...].T
        ct[...] = c_ref[...].T
        if base:
            branch_ref[...] = held[0][...]
            gn_ref[...] = held[1][...]
        else:
            branch_ref[...] = jnp.zeros_like(branch_ref)
            gn_ref[...] = jnp.zeros_like(gn_ref)

    for j in range(2):

        @pl.when(t == PER * j)
        def _():
            for copy in loads(j):
                copy.wait()

    spot = jnp.bitwise_xor(me_mp, base + jl) if fast else base + jl
    cols = pl.ds(pl.multiple_of(sub * SUB, SUB), SUB)
    w1 = w[jl, 0, :, cols]
    w2 = w[jl, 1, :, cols]
    u = dotf(n_ref[...], w1) + b_ref[spot, :, cols]
    cdf = 0.5 * (1.0 + lax.erf(u * 0.7071067811865476))
    hidden = (u * cdf).astype(B16)
    slope = cdf + u * (0.3989422804014327 * jnp.exp(-0.5 * u * u))
    gb = (dotf(c_ref[...], w2) * slope).astype(B16)
    db_ref[jl, :, cols] = jnp.sum(gb.astype(F32), axis=0, keepdims=True)
    branch_ref[...] += dotf(hidden, w2, NT)
    gn_ref[...] += dotf(gb, w1, NT)
    dw1 = dotf(nt[...], gb).astype(B16)
    dw2 = dotf(ct[...], hidden).astype(B16)
    for a in range(8):
        dr = jnp.bitwise_xor(me_dp, a) if fast else a
        dw[jl, dr, 0, :, cols] = dw1[96 * a : 96 * a + 96]
        dw[jl, dr, 1, :, cols] = dw2[96 * a : 96 * a + 96]

    for j in range(2):

        @pl.when(t == PER * j + PER - 1)
        def _():
            for copy in stores(j):
                copy.start()

    @pl.when(t == 2 * PER - 1)
    def _():
        for j in range(2):
            for copy in stores(j):
                copy.wait()


def mlp(meta, normed, cot, bias, pieces, base, held):
    fast = len(pieces) == 4
    tokens = normed.shape[0]
    vmem = pl.BlockSpec(memory_space=pltpu.VMEM)
    anys = pl.BlockSpec(memory_space=pl.ANY)
    shape = jax.ShapeDtypeStruct((2, 4, 2, 96, 768), B16)
    at = 4 + len(pieces)
    return pl.pallas_call(
        partial(mlp_kernel, fast, base),
        name="mlp",
        grid=(2 * PER,),
        in_specs=[pl.BlockSpec(memory_space=pltpu.SMEM), vmem, vmem, vmem]
        + [anys] * len(pieces)
        + [vmem] * len(held),
        out_specs=[vmem, vmem, vmem, anys, anys],
        out_shape=(
            jax.ShapeDtypeStruct((tokens, 768), F32),
            jax.ShapeDtypeStruct((tokens, 768), F32),
            jax.ShapeDtypeStruct((2, 1, 768), F32),
            shape,
            shape,
        ),
        scratch_shapes=[
            pltpu.VMEM((2, 2, 768, 768), B16),
            pltpu.VMEM((768, tokens), B16),
            pltpu.VMEM((768, tokens), B16),
            pltpu.VMEM((2, 8, 2, 96, 768), B16),
            pltpu.SemaphoreType.DMA((2, 8)),
            pltpu.SemaphoreType.DMA((2, 8)),
        ],
        compiler_params=pltpu.CompilerParams(vmem_limit_bytes=VMEM_LIMIT),
    )(meta, normed, cot, bias.reshape(4, 1, 768), *pieces, *held)


def local(
    fast,
    tokens,
    cotangent,
    prompts,
    segments,
    prompt_slot_index,
    norm_gain,
    norm_shift,
    attn_qkv,
    attn_bias,
    attn_out,
    mlp_weight,
    mlp_bias_up,
    mlp_bias_down,
):
    width = tokens.shape[1]
    device = lax.axis_index("dp") * lax.axis_size("mp") + lax.axis_index("mp")
    meta = jnp.reshape(device, (1,)).astype(jnp.int32)
    core = device % 2
    if fast:
        piece = pair_rows(meta, attn_qkv, attn_out)
        piece, tokens, prompts, segments, prompt_slot_index = tie(
            piece, tokens, prompts, segments, prompt_slot_index
        )
        held = z_stage(piece)
    table = jnp.concatenate([prompts, jnp.zeros((128 - NPROMPT, width), F32)], 0)
    start, normed_one, onehot, qf, kf = embed(
        tokens, prompt_slot_index, segments, table, jnp.stack([norm_gain[0], norm_shift[0]])
    )
    bias = jnp.stack([attn_bias[0], jnp.zeros_like(attn_bias[0]), attn_bias[1]])[:, None]
    out_params = jnp.stack([attn_bias[2], norm_gain[1], norm_shift[1]])

    if fast:
        held, mlp_piece, x = tie(held, mlp_weight, (normed_one, start, qf, kf, onehot))
        mlp_z = [mlp_piece] + [px(mlp_piece, 8 * k) for k in range(1, 4)]
        quad, mlp_z, x = tie(xy_stage(held), mlp_z, x)
        own = assemble(meta, quad, "assemble")
        own, mlp_z = tie(own, mlp_z)
        other = px(own, 1)
        stack_mlp = stack(mlp_z, "stack_z")
        normed_one, start, qf, kf, onehot = x
        qkv = project(meta, normed_one, own, bias, 0, ())
        other, stack_mlp, qkv = tie(other, stack_mlp, qkv)
        mlp_x, mlp_y = px(stack_mlp, 2), px(stack_mlp, 4)
        stack_mlp_other = px(stack_mlp, 1)
    else:
        qkv_all = lax.all_gather(attn_qkv, AXES, axis=1, tiled=True)
        out_all = lax.all_gather(attn_out, AXES, axis=0, tiled=True)
        mlp_all = lax.all_gather(mlp_weight, "dp", axis=1, tiled=True)
        mlp_all = lax.all_gather(mlp_all, "mp", axis=2, tiled=True)
        four_all = jnp.concatenate([qkv_all, out_all[None]])
        own = lax.dynamic_slice_in_dim(four_all, 384 * core, 384, 2)
        other = lax.dynamic_slice_in_dim(four_all, 384 * (1 - core), 384, 2)
        qkv = project(meta, normed_one, own, bias, 0, ())
    qkv = project(meta, normed_one, other, bias, 1, (qkv,))
    mixed, lse = attention_forward(meta, qf, kf, qkv)
    if fast:
        mlp_y, mlp_x, stack_mlp, mixed = tie(mlp_y, mlp_x, (stack_mlp, stack_mlp_other), mixed)
        mlp_y_other, mlp_x_other, mlp_xy = px(mlp_y, 1), px(mlp_x, 1), px(stack_mlp[0], 6)
    middle, normed_two, out_weight = out_projection(meta, mixed, start, own, other, out_params)
    if fast:
        mlp_y_other, normed_two = tie(mlp_y_other, normed_two)
        pieces_a = [stack_mlp[0], mlp_y, stack_mlp[1], mlp_y_other]
        branch, grad_two, up_a, own_a, other_a = mlp(meta, normed_two, cotangent, mlp_bias_up, pieces_a, 0, ())
        mlp_x, mlp_xy, other_a, branch, grad_two = tie(
            (mlp_x, mlp_x_other), mlp_xy, other_a, branch, grad_two
        )
        pieces_b = [mlp_x[0], mlp_xy, mlp_x[1], px(mlp_xy, 1)]
        got_a = px(other_a, 1)
        branch, grad_two, up_b, own_b, other_b = mlp(
            meta, normed_two, cotangent, mlp_bias_up, pieces_b, 2, (branch, grad_two)
        )
        other_b, got_a, grad_two, branch = tie(other_b, got_a, grad_two, branch)
        got_b = px(other_b, 1)
        up_rows = jnp.concatenate([up_a[:, 0], up_b[:, 0]])
        spots = jnp.bitwise_xor(jnp.arange(4), device % 4)
        grad_up = (jnp.arange(4)[:, None] == spots[None, :]).astype(F32)
        grad_up = jnp.sum(grad_up[:, :, None] * up_rows[None], axis=1)
    else:
        branch, grad_two, up_a, own_a, other_a = mlp(meta, normed_two, cotangent, mlp_bias_up, [mlp_all], 0, ())
        branch, grad_two, up_b, own_b, other_b = mlp(
            meta, normed_two, cotangent, mlp_bias_up, [mlp_all], 2, (branch, grad_two)
        )
        grad_up = jnp.concatenate([up_a[:, 0], up_b[:, 0]])
    turn_params = jnp.stack([norm_gain[1], mlp_bias_down])
    output, grad_middle, grad_mixed, own_out, other_out, sums_two = turn(
        meta, middle, branch, grad_two, cotangent, mixed, out_weight, turn_params
    )
    if fast:
        got_b, grad_mixed, other_out = tie(got_b, grad_mixed, other_out)
        sum_a = add_parts(own_a, got_a)
        sum_b = add_parts(own_b, got_b)
        send_x = sum_b[:, :, 0].astype(B16)
        send_y = jnp.stack([sum_a[1, :, 1], sum_b[1, :, 1]]).astype(B16)
        send_x, send_y, grad_mixed, other_out = tie(send_x, send_y, grad_mixed, other_out)
        got_x, got_y, got_out = px(send_x, 2), px(send_y, 4), px(other_out, 1)
    grads = attention_backward(meta, qf, kf, qkv, grad_mixed, mixed, lse)
    if fast:
        got_x, got_y, got_out, grads, grad_middle = tie(got_x, got_y, got_out, grads, grad_middle)
        first = add_parts(sum_a[:, :, 0], got_x)
        second = [add_parts(sum_a[0, :, 1], got_y[0]), add_parts(sum_b[0, :, 1], got_y[1])]
        send_x, send_y, grads = tie(second[1].astype(B16), first[1].astype(B16), grads)
        got_x, got_y = px(send_x, 2), px(send_y, 4)
        own_w, other_w = weight_grad(meta, normed_one, grads, "weight_grad_qkv")
        other_w, got_x, got_y, grads, grad_middle = tie(other_w, got_x, got_y, grads, grad_middle)
        got_w = px(other_w, 1)
        col = [add_parts(first[0], got_y), add_parts(second[0], got_x)]
        col_send = [jnp.stack([c[i].astype(B16) for c in col]) for i in range(1, 4)]
        got_w, col_send, grads = tie(got_w, col_send, grads)
        keep, *sends = gather_sums(own_w, got_w, own_out, got_out)
        sends, col_send, grads, grad_middle = tie(sends, col_send, grads, grad_middle)
        moved = [px(x, 2 * i + 2) for i, x in enumerate(sends)]
        last_mlp = [px(x, 8 * i + 8) for i, x in enumerate(col_send)]
    input_grad, prompt_sums, sums_one = tail_step(
        meta, start, grad_middle, onehot, norm_gain[0:1], (own, other), grads
    )

    small = jnp.concatenate(
        [
            prompt_sums[:NPROMPT],
            sums_one[0:1],
            sums_two[0:1],
            sums_one[1:2],
            sums_two[1:2],
            sums_one[2:4],
            sums_two[2:4],
            grad_up,
        ]
    )
    if fast:
        packed = pack_small(small)
        packed = pack_small(open_small(packed) + open_small(px(packed, 1)))
        packed = pack_small(open_small(packed) + open_small(px(packed, 2)))
        packed = pack_small(open_small(packed) + open_small(px(packed, 4)))
        moved, packed = tie(moved, packed)
        col_attn, *last = plane_sums(keep, moved)
        last = [px(x, 8 * i + 8) for i, x in enumerate(last)]
        small = four([open_small(x) for x in [packed] + [px(packed, 8 * i) for i in range(1, 4)]])
        mine = jnp.stack([c[0] for c in col])
        mlp_grad = four([mine] + [x.astype(F32) for x in last_mlp])
        qkv_grad, out_grad = line_sums(col_attn, last)
    else:
        mlp_grad = jnp.stack([own_a, other_a, own_b, other_b]).transpose(3, 2, 1, 4, 0, 5)
        mlp_grad = mlp_grad.reshape(2, 768, 3072)
        mlp_grad = lax.psum_scatter(mlp_grad, "dp", scatter_dimension=1, tiled=True)
        mlp_grad = lax.psum_scatter(mlp_grad, "mp", scatter_dimension=2, tiled=True).astype(F32)
        grad_out_weight = dotf(mixed, grad_middle.astype(B16), TN)
        grad_qkv = jnp.stack([dotf(normed_one, g, TN) for g in grads])
        qkv_grad = lax.psum_scatter(grad_qkv, AXES, scatter_dimension=1, tiled=True)
        out_grad = lax.psum_scatter(grad_out_weight, AXES, scatter_dimension=0, tiled=True)
        small = lax.psum(small, AXES)
    at = NPROMPT
    return (
        output.astype(B16),
        input_grad,
        small[:at],
        small[at : at + 2],
        small[at + 2 : at + 4],
        qkv_grad,
        small[at + 4 : at + 7],
        out_grad,
        mlp_grad,
        small[at + 8 :].reshape(-1),
        small[at + 7],
    )


def solution(mesh):
    fast = dict(mesh.shape) == {"dp": 8, "mp": 4}
    return jax.shard_map(
        partial(local, fast),
        mesh=mesh,
        in_specs=(
            P(AXES, None),
            P(AXES, None),
            P(),
            P(AXES),
            P(AXES),
            P(),
            P(),
            P(None, AXES, None),
            P(),
            P(AXES, None),
            P(None, "dp", "mp"),
            P(),
            P(),
        ),
        out_specs=(
            P(AXES, None),
            P(AXES, None),
            P(),
            P(),
            P(),
            P(None, AXES, None),
            P(),
            P(AXES, None),
            P(None, "dp", "mp"),
            P(),
            P(),
        ),
        check_vma=False,
    )
```

time: 448 us -> 351 us (0.78); the launches traced: 440 us -> 348 us
  waiting for transfers between devices: 164 us -> 71.1 us
  Pallas kernels: 127 us -> 188 us
  matrix products: 32.3 us -> 0 us
  other arithmetic: 46.1 us -> 19.8 us
  starting transfers between devices: 53.5 us -> 39.7 us
  local copies, waits for them, and re-layouts: 15.9 us -> 27.7 us
    ppermute x60 -> x41, waiting for transfers between devices: 164 us -> 71.1 us  [px(): return lax.ppermute(x, AXES, [(i, i ^ k) for i in range(32)])]
    pallas_call x5 -> x18, Pallas kernels: 120 us -> 185 us  [the longest x2 54.2 us: mlp(): pl.pallas_call(partial(mlp_kernel, fast, base), name='mlp', grid=(2 * PER...]
    dot_general x14 -> x0, matrix products: 32.3 us -> none  [the longest x8 18.3 us: dotf(): return lax.dot_general(a, b, dims, preferred_element_type=F32)]
    ppermute x60 -> x41, starting transfers between devices: 53.5 us -> 39.7 us  [px(): return lax.ppermute(x, AXES, [(i, i ^ k) for i in range(32)])]
    convert_element_type x9 -> x16, other arithmetic: 14.6 us -> 2.71 us  [the longest x1 2.2 us: local(): second[1].astype(B16)]
    reduce_sum x7 -> x1, other arithmetic: 11.3 us -> 0.11 us  [local(): grad_up = jnp.sum(grad_up[:, :, None] * up_rows[None], axis=1)]
    another operation x7 -> x10, other arithmetic: 10.3 us -> 9.03 us
  transfers between devices with their start and end apart: 60 -> 41, of which waited for: 22 -> 14; matrix products, arithmetic and copies ran while one was open for 18% -> 7% of each run, Pallas kernels for 19% -> 46%
where the time goes in v2:
time: 351 us; the launch traced here: 348 us
  Pallas kernels  188 us (54%)
  waiting for transfers between devices  71.1 us (20%)
  starting transfers between devices  39.7 us (11%)
  local copies, waits for them, and re-layouts  27.7 us (8%)
  other arithmetic  19.8 us (6%)
    ppermute x41, waiting for transfers between devices, px(): return lax.ppermute(x, AXES, [(i, i ^ k) for i in range(32)])  71.1 us
    pallas_call x2, Pallas kernels, mlp(): pl.pallas_call(partial(mlp_kernel, fast, base), name='mlp', grid=(2 * PER...  54.2 us
    ppermute x41, starting transfers between devices, px(): return lax.ppermute(x, AXES, [(i, i ^ k) for i in range(32)])  39.7 us
    pallas_call x1, Pallas kernels, attention_backward(): pl.pallas_call(kernel, name='attention_backward', grid_spec=pltpu.Prefetc...  32 us
    pallas_call x1, Pallas kernels, attention_forward(): pl.pallas_call(kernel, name='attention_forward', grid_spec=pltpu.Prefetch...  23 us
    pallas_call x1, Pallas kernels, tail_step(): pl.pallas_call(tail_kernel, name='tail_step', grid=(rows // TILE,), in_sp...  13.9 us
    pallas_call x2, Pallas kernels, project(): pl.pallas_call(partial(project_kernel, side), name='project', grid=(rows...  12.1 us
    pallas_call x1, Pallas kernels, turn(): pl.pallas_call(turn_kernel, name='turn', grid=(rows // TILE,), in_specs=[...  11.3 us
  transfers between devices with their start and end apart: 41, of which 14 were waited for; matrix products, arithmetic and copies ran while one was open for 7% of the time, Pallas kernels for 46%

profile of v2, /device:TPU:16, one launch (start us, length us, event | category | flops | bytes accessed | tf_op | source)
XLA Modules:
  0.0 348.0 jit_solution(18182490520932435009)
XLA Ops:
  0.6 1.6 split.1
  4.3 1.6 join.1.refs_0_
  5.9 1.6 collective-permute-start.1
  7.8 1.6 collective-permute-start.3
  9.4 1.4 fusion.25
  12.1 1.7 copy.35.slots_ref
  13.8 1.7 copy.36.segs_ref
  15.5 1.7 concatenate.51.table_ref
  17.2 5.9 %embed.1 = (f32[1024,768]{1,0:T(8,128)}, bf16[1024,768]{1,0:T(8,128)(2,1)}, bf16[1024,128]{1,0:T(8,128)(2,1)}, bf16[1024,128]{1,0:T(8,128)(2,1)}, bf16[1024,128]{1,0:T(8,128)(2,1)}) custom-call(bf16[1024,768]{1,0:T(8,128)(2,1)} %tokens_ref, s32[1024,1]{1,0:T(8,128)} %copy.35.slots_ref, s32[1024,1]{1,0:T(8,128)} %copy.36.segs_ref, ...), custom_call_target="tpu_custom_call" | custom-call | tf_op jit(solution)/shard_map/embed/pallas_call | solution.py:196
  24.5 2.0 stack_z.2.refs_0_
  26.5 2.5 collective-permute-start.7
  28.9 1.5 collective-permute-start.4
  30.4 1.5 collective-permute-start.5
  32.4 4.4 %collective-permute-done.7.refs_1_ = bf16[2,96,768]{2,1,0:T(8,128)(2,1)S(1)} collective-permute-done((bf16[2,96,768]{2,1,0:T(8,128)(2,1)S(1)}, bf16[2,96,768]{2,1,0:T(8,128)(2,1)S(1)}, u32[]{:S(2)}, u32[]{:S(2)}) %collective-permute-start.7) | collective-permute-done | bytes 294944 | tf_op jit(solution)/shard_map/ppermute | solution.py:50
  37.4 14.8 %collective-permute-done.8.refs_2_ = bf16[2,96,768]{2,1,0:T(8,128)(2,1)S(1)} collective-permute-done((bf16[2,96,768]{2,1,0:T(8,128)(2,1)S(1)}, bf16[2,96,768]{2,1,0:T(8,128)(2,1)S(1)}, u32[]{:S(2)}, u32[]{:S(2)}) %collective-permute-start.8) | collective-permute-done | bytes 294944 | tf_op jit(solution)/shard_map/ppermute | solution.py:50
  52.2 6.0 %collective-permute-done.9.refs_3_ = bf16[2,96,768]{2,1,0:T(8,128)(2,1)S(1)} collective-permute-done((bf16[2,96,768]{2,1,0:T(8,128)(2,1)S(1)}, bf16[2,96,768]{2,1,0:T(8,128)(2,1)S(1)}, u32[]{:S(2)}, u32[]{:S(2)}) %collective-permute-start.9) | collective-permute-done | bytes 294944 | tf_op jit(solution)/shard_map/ppermute | solution.py:50
  60.2 3.3 assemble.1.w_ref.own_ref.refs_0_
  63.6 1.4 fusion.23
  65.7 6.1 %project.2.refs_0_ = bf16[1024,2304]{1,0:T(8,128)(2,1)} custom-call(s32[1]{0:T(128)} %bitcast.meta.refs_0_, bf16[1024,768]{1,0:T(8,128)(2,1)} %get-tuple-element.186.x_ref.left_ref, bf16[4,768,384]{2,1,0:T(8,128)(2,1)} %assemble.1.w_ref.own_ref.refs_0_, f32[3,1,768]{2,1,0:T(1,128)} %broadcast_in_dim.16.b_ref), custom_call_target="tpu_custom_call" | custom-call | tf_op jit(solution)/shard_map/project/pallas_call | solution.py:150
  71.7 2.3 stack_z.3.refs_4_
  74.1 1.5 collective-permute-start.11
  75.6 1.5 collective-permute-start.12
  77.1 6.1 %project.3.refs_2_.refs_3_.refs_4_ = bf16[1024,2304]{1,0:T(8,128)(2,1)} custom-call(s32[1]{0:T(128)} %bitcast.meta.refs_0_, bf16[1024,768]{1,0:T(8,128)(2,1)} %get-tuple-element.186.x_ref.left_ref, bf16[4,768,384]{2,1,0:T(8,128)(2,1)} %copy-done, f32[3,1,768]{2,1,0:T(1,128)} %broadcast_in_dim.16.b_ref, ...), custom_call_target="tpu_custom_call", output_to_operand_aliasing={{}: (4, {})} | custom-call | tf_op jit(solution)/shard_map/project/pallas_call | solution.py:150
  83.2 23.0 %attention_forward.1 = (bf16[1024,768]{1,0:T(8,128)(2,1)}, f32[1024,768]{1,0:T(8,128)}) custom-call(s32[1]{0:T(128)} %bitcast.meta.refs_0_, bf16[1024,128]{1,0:T(8,128)(2,1)} %get-tuple-element.188.refs_0_, bf16[1024,128]{1,0:T(8,128)(2,1)} %get-tuple-element.189.refs_1_, bf16[1024,2304]{1,0:T(8,128)(2,1)} %project.3.refs_2_.refs_3_.refs_4_, ...), custom_call_target="tpu_custom_call" | custom-call | tf_op jit(solution)/shard_map/attention_forward/pallas_call | solution.py:532
  108.4 7.8 %out_projection.1 = (f32[1024,768]{1,0:T(8,128)}, bf16[1024,768]{1,0:T(8,128)(2,1)}, bf16[768,768]{1,0:T(8,128)(2,1)}) custom-call(s32[1]{0:T(128)} %bitcast.meta.refs_0_, bf16[1024,768]{1,0:T(8,128)(2,1)} %get-tuple-element.193.x_ref.mixed_ref.refs_6_, f32[1024,768]{1,0:T(8,128)} %get-tuple-element.194.start_ref, ...), custom_call_target="tpu_custom_call" | custom-call | tf_op jit(solution)/shard_map/out_projection/pallas_call | solution.py:312
  116.1 26.1 %mlp.2 = (f32[1024,768]{1,0:T(8,128)}, f32[1024,768]{1,0:T(8,128)}, f32[2,1,768]{2,1,0:T(1,128)}, bf16[2,4,2,96,768]{4,3,2,1,0:T(8,128)(2,1)}, bf16[2,4,2,96,768]{4,3,2,1,0:T(8,128)(2,1)}) custom-call(s32[1]{0:T(128)} %bitcast.meta.refs_0_, bf16[1024,768]{1,0:T(8,128)(2,1)} %get-tuple-element.198.refs_1_, bf16[1024,768]{1,0:T(8,128)(2,1)} %cot_ref.1, ...), custom_call_target="tpu_custom_call" | custom-call | tf_op jit(solution)/shard_map/mlp/pallas_call | solution.py:717
  142.3 1.0 copy-done.6
  143.3 1.8 copy.37
  145.7 5.7 %collective-permute-done.17.refs_7_ = bf16[4,2,96,768]{3,2,1,0:T(8,128)(2,1)S(1)} collective-permute-done((bf16[4,2,96,768]{3,2,1,0:T(8,128)(2,1)}, bf16[4,2,96,768]{3,2,1,0:T(8,128)(2,1)S(1)}, u32[]{:S(2)}, u32[]{:S(2)}) %collective-permute-start.17) | collective-permute-done | bytes 1179680 | tf_op jit(solution)/shard_map/ppermute | solution.py:50
  151.4 1.0 copy-done.7
  152.5 28.1 %mlp.3 = (f32[1024,768]{1,0:T(8,128)}, f32[1024,768]{1,0:T(8,128)}, f32[2,1,768]{2,1,0:T(1,128)}, bf16[2,4,2,96,768]{4,3,2,1,0:T(8,128)(2,1)}, bf16[2,4,2,96,768]{4,3,2,1,0:T(8,128)(2,1)}) custom-call(s32[1]{0:T(128)} %bitcast.meta.refs_0_, bf16[1024,768]{1,0:T(8,128)(2,1)} %get-tuple-element.198.refs_1_, bf16[1024,768]{1,0:T(8,128)(2,1)} %cot_ref.1, ...), custom_call_target="tpu_custom_call" | custom-call | tf_op jit(solution)/shard_map/mlp/pallas_call | solution.py:717
  180.8 11.3 %turn.1 = (bf16[1024,768]{1,0:T(8,128)(2,1)}, f32[1024,768]{1,0:T(8,128)}, bf16[1024,768]{1,0:T(8,128)(2,1)}, bf16[4,4,1,24,768]{4,3,2,1,0:T(8,128)(2,1)}, bf16[...) custom-call(s32[1]{0:T(128)} %bitcast.meta.refs_0_, f32[1024,768]{1,0:T(8,128)} %get-tuple-element.195.middle_ref, ...), custom_call_target="tpu_custom_call" | custom-call | tf_op jit(solution)/shard_map/turn/pallas_call | solution.py:378
  192.1 2.4 convert_add_fusion
  194.5 2.2 copy-done.1
  196.8 4.7 %fusion.11 = (bf16[2,4,2,96,768]{4,3,2,1,0:T(8,128)(2,1)S(1)}, f32[2,4,2,96,768]{4,3,2,1,0:T(8,128)}) fusion(bf16[2,4,2,96,768]{4,3,2,1,0:T(8,128)(2,1)} %collective-permute-done.19, bf16[2,4,2,96,768]{4,3,2,1,0:T(8,128)(2,1)S(1)} %copy-done.4), kind=kLoop, calls=%fused_computation.71 | loop fusion | flops 4718592 | bytes 11796480 | tf_op jit(solution)/shard_map/convert.19
  201.7 1.1 collective-permute-start.20
  202.9 1.5 collective-permute-start.21
  204.4 32.0 %attention_backward.1 = (bf16[1024,768]{1,0:T(8,128)(2,1)}, bf16[1024,768]{1,0:T(8,128)(2,1)}, bf16[1024,768]{1,0:T(8,128)(2,1)}) custom-call(s32[1]{0:T(128)} %bitcast.meta.refs_0_, bf16[1024,128]{1,0:T(8,128)(2,1)} %get-tuple-element.188.refs_0_, bf16[1024,128]{1,0:T(8,128)(2,1)} %get-tuple-element.189.refs_1_, ...), custom_call_target="tpu_custom_call" | custom-call | tf_op jit(solution)/shard_map/attention_backward/pallas_call | solution.py:607
  236.4 2.3 fusion
  239.5 2.2 fusion.5
  243.9 8.8 %weight_grad_qkv.1 = (bf16[4,4,3,24,768]{4,3,2,1,0:T(8,128)(2,1)}, bf16[4,4,3,24,768]{4,3,2,1,0:T(8,128)(2,1)}) custom-call(s32[1]{0:T(128)} %bitcast.meta.refs_0_, bf16[1024,768]{1,0:T(8,128)(2,1)} %get-tuple-element.186.x_ref.left_ref, bf16[1024,768]{1,0:T(8,128)(2,1)} %get-tuple-element.271.refs_0_.refs_2_, ...), custom_call_target="tpu_custom_call" | custom-call | tf_op jit(solution)/shard_map/weight_grad_qkv/pallas_call | solution.py:459
  252.7 5.1 %collective-permute-done.23 = bf16[4,96,768]{2,1,0:T(8,128)(2,1)} collective-permute-done((bf16[4,96,768]{2,1,0:T(8,128)(2,1)}, bf16[4,96,768]{2,1,0:T(8,128)(2,1)}, u32[]{:S(2)}, u32[]{:S(2)}) %collective-permute-start.23) | collective-permute-done | bytes 589856 | tf_op jit(solution)/shard_map/ppermute | solution.py:50
  259.4 1.2 fusion.15
  260.6 1.6 fusion.17
  262.5 4.0 %gather_sums.1 = (f32[4,4,24,768]{3,2,1,0:T(8,128)}, bf16[4,4,24,768]{3,2,1,0:T(8,128)(2,1)}, bf16[4,4,24,768]{3,2,1,0:T(8,128)(2,1)}, bf16[4,4,24,768]{3,2,1,0:T(8,128)(2,1)}) custom-call(bf16[4,4,3,24,768]{4,3,2,1,0:T(8,128)(2,1)} %get-tuple-element.245.own_ref, bf16[4,4,3,24,768]{4,3,2,1,0:T(8,128)(2,1)} %collective-permute-done.25.got_ref, ...), custom_call_target="tpu_custom_call" | custom-call | tf_op jit(solution)/shard_map/gather_sums/pallas_call | solution.py:229
  266.5 13.9 %tail_step.1 = (f32[1024,768]{1,0:T(8,128)}, f32[128,768]{1,0:T(8,128)}, f32[8,768]{1,0:T(8,128)}) custom-call(s32[1]{0:T(128)} %bitcast.meta.refs_0_, f32[1024,768]{1,0:T(8,128)} %get-tuple-element.194.start_ref, f32[1024,768]{1,0:T(8,128)} %get-tuple-element.269.gmiddle_ref, bf16[1024,128]{1,0:T(8,128)(2,1)} %get-tuple-element.270.slots_ref, ...), custom_call_target="tpu_custom_call" | custom-call | tf_op jit(solution)/shard_map/tail_step/pallas_call | solution.py:432
  282.0 0.9 slice.416
  283.7 1.5 collective-permute-start.26
  285.7 2.1 collective-permute-start.39
  288.1 1.0 collective-permute-start.30
  289.1 12.7 %collective-permute-done.30 = bf16[80,768]{1,0:T(8,128)(2,1)S(1)} collective-permute-done((bf16[80,768]{1,0:T(8,128)(2,1)S(1)}, bf16[80,768]{1,0:T(8,128)(2,1)S(1)}, u32[]{:S(2)}, u32[]{:S(2)}) %collective-permute-start.30) | collective-permute-done | bytes 122912 | tf_op jit(solution)/shard_map/ppermute | solution.py:50
  302.7 1.5 collective-permute-start.28
  304.2 3.4 collective-permute-start.31
  307.7 8.0 %collective-permute-done.40 = bf16[2,96,768]{2,1,0:T(8,128)(2,1)S(1)} collective-permute-done((bf16[2,96,768]{2,1,0:T(8,128)(2,1)S(1)}, bf16[2,96,768]{2,1,0:T(8,128)(2,1)S(1)}, u32[]{:S(2)}, u32[]{:S(2)}) %collective-permute-start.40) | collective-permute-done | bytes 294944 | tf_op jit(solution)/shard_map/ppermute | solution.py:50
  315.6 1.0 fusion.8
  316.6 3.8 %collective-permute-done.31 = bf16[80,768]{1,0:T(8,128)(2,1)S(1)} collective-permute-done((bf16[80,768]{1,0:T(8,128)(2,1)S(1)}, bf16[80,768]{1,0:T(8,128)(2,1)S(1)}, u32[]{:S(2)}, u32[]{:S(2)}) %collective-permute-start.31) | collective-permute-done | bytes 122912 | tf_op jit(solution)/shard_map/ppermute | solution.py:50
  320.7 1.5 collective-permute-start.34
  322.2 2.0 collective-permute-start.32
  324.3 2.7 plane_sums.1
  327.1 2.9 collective-permute-start.36
  330.2 2.4 collective-permute-start.37
  336.7 5.7 %collective-permute-done.36.refs_1_ = bf16[4,24,768]{2,1,0:T(8,128)(2,1)S(1)} collective-permute-done((bf16[4,24,768]{2,1,0:T(8,128)(2,1)}, bf16[4,24,768]{2,1,0:T(8,128)(2,1)S(1)}, u32[]{:S(2)}, u32[]{:S(2)}) %collective-permute-start.36) | collective-permute-done | bytes 147488 | tf_op jit(solution)/shard_map/ppermute | solution.py:50
  342.4 3.1 collective-permute-done.37.refs_2_
  346.1 1.9 line_sums.1
  (201 shorter events, 26.0 us)
Async XLA Ops:
  2.2 1.5 collective-permute-start
  3.0 68.7 %copy-start.25 = (f32[1,768]{1,0:T(1,128)}, f32[1,768]{1,0:T(1,128)S(1)}, u32[]{:S(2)}) copy-start(f32[1,768]{1,0:T(1,128)S(1)} %get-tuple-element.333.p_ref) | copy-start | bytes 9220
  5.9 17.2 %collective-permute-start.1 = (bf16[4,48,384]{2,1,0:T(8,128)(2,1)}, bf16[4,48,384]{2,1,0:T(8,128)(2,1)S(1)}, u32[]{:S(2)}, u32[]{:S(2)}) collective-permute-start(bf16[4,48,384]{2,1,0:T(8,128)(2,1)} %join.1.refs_0_), channel_id=1, source_target_pairs={{0,8},{1,9},{2,10},{3,11},{4,12},{5,13},{6,14},{7,15},{8,0},{9,1},... | collective-permute-start | bytes 442376 | tf_op jit(solution)/shard_map/ppermute | solution.py:50
  7.5 15.6 %collective-permute-start.2 = (bf16[4,48,384]{2,1,0:T(8,128)(2,1)}, bf16[4,48,384]{2,1,0:T(8,128)(2,1)S(1)}, u32[]{:S(2)}, u32[]{:S(2)}) collective-permute-start(bf16[4,48,384]{2,1,0:T(8,128)(2,1)} %join.1.refs_0_), channel_id=1, source_target_pairs={{0,16},{1,17},{2,18},{3,19},{4,20},{5,21},{6,22},{7,23},{8,24},{9,... | collective-permute-start | bytes 442376 | tf_op jit(solution)/shard_map/ppermute | solution.py:50
  7.8 15.3 %collective-permute-start.3 = (bf16[4,48,384]{2,1,0:T(8,128)(2,1)}, bf16[4,48,384]{2,1,0:T(8,128)(2,1)S(1)}, u32[]{:S(2)}, u32[]{:S(2)}) collective-permute-start(bf16[4,48,384]{2,1,0:T(8,128)(2,1)} %join.1.refs_0_), channel_id=1, source_target_pairs={{0,24},{1,25},{2,26},{3,27},{4,28},{5,29},{6,30},{7,31},{8,16},{9,... | collective-permute-start | bytes 442376 | tf_op jit(solution)/shard_map/ppermute | solution.py:50
  15.5 11.0 %copy-start.14 = (bf16[2,96,768]{2,1,0:T(8,128)(2,1)S(1)}, bf16[2,96,768]{2,1,0:T(8,128)(2,1)}, u32[]{:S(2)}) copy-start(bf16[2,96,768]{2,1,0:T(8,128)(2,1)} %refs_0_) | copy-start | bytes 884740
  26.5 10.3 %collective-permute-start.7 = (bf16[2,96,768]{2,1,0:T(8,128)(2,1)S(1)}, bf16[2,96,768]{2,1,0:T(8,128)(2,1)S(1)}, u32[]{:S(2)}, u32[]{:S(2)}) collective-permute-start(bf16[2,96,768]{2,1,0:T(8,128)(2,1)S(1)} %copy-done.14), channel_id=1, source_target_pairs={{0,8},{1,9},{2,10},{3,11},{4,12},{5,13},{6,14},{7,15},{8,0},{9,1},... | collective-permute-start | bytes 884744 | tf_op jit(solution)/shard_map/ppermute | solution.py:50
  28.9 29.3 %collective-permute-start.4 = (bf16[4,4,48,384]{3,2,1,0:T(8,128)(2,1)}, bf16[4,4,48,384]{3,2,1,0:T(8,128)(2,1)S(1)}, u32[]{:S(2)}, u32[]{:S(2)}) collective-permute-start(bf16[4,4,48,384]{3,2,1,0:T(8,128)(2,1)} %stack_z.2.refs_0_), channel_id=1, source_target_pairs={{0,2},{1,3},{2,0},{3,1},{4,6},{5,7},{6,4},{7,5},{8,10},{9,11},{10,... | collective-permute-start | bytes 1769480 | tf_op jit(solution)/shard_map/ppermute | solution.py:50
  30.4 27.8 %collective-permute-start.5 = (bf16[4,4,48,384]{3,2,1,0:T(8,128)(2,1)}, bf16[4,4,48,384]{3,2,1,0:T(8,128)(2,1)S(1)}, u32[]{:S(2)}, u32[]{:S(2)}) collective-permute-start(bf16[4,4,48,384]{3,2,1,0:T(8,128)(2,1)} %stack_z.2.refs_0_), channel_id=1, source_target_pairs={{0,4},{1,5},{2,6},{3,7},{4,0},{5,1},{6,2},{7,3},{8,12},{9,13},{10,... | collective-permute-start | bytes 1769480 | tf_op jit(solution)/shard_map/ppermute | solution.py:50
  31.9 26.3 %collective-permute-start.6 = (bf16[4,4,48,384]{3,2,1,0:T(8,128)(2,1)}, bf16[4,4,48,384]{3,2,1,0:T(8,128)(2,1)S(1)}, u32[]{:S(2)}, u32[]{:S(2)}) collective-permute-start(bf16[4,4,48,384]{3,2,1,0:T(8,128)(2,1)} %stack_z.2.refs_0_), channel_id=1, source_target_pairs={{0,6},{1,7},{2,4},{3,5},{4,2},{5,3},{6,0},{7,1},{8,14},{9,15},{10,... | collective-permute-start | bytes 1769480 | tf_op jit(solution)/shard_map/ppermute | solution.py:50
  32.4 19.8 %collective-permute-start.8 = (bf16[2,96,768]{2,1,0:T(8,128)(2,1)S(1)}, bf16[2,96,768]{2,1,0:T(8,128)(2,1)S(1)}, u32[]{:S(2)}, u32[]{:S(2)}) collective-permute-start(bf16[2,96,768]{2,1,0:T(8,128)(2,1)S(1)} %copy-done.14), channel_id=1, source_target_pairs={{0,16},{1,17},{2,18},{3,19},{4,20},{5,21},{6,22},{7,23},{8,24},{9,... | collective-permute-start | bytes 884744 | tf_op jit(solution)/shard_map/ppermute | solution.py:50
  36.8 34.9 %copy-start.15 = (bf16[2,96,768]{2,1,0:T(8,128)(2,1)}, bf16[2,96,768]{2,1,0:T(8,128)(2,1)S(1)}, u32[]{:S(2)}) copy-start(bf16[2,96,768]{2,1,0:T(8,128)(2,1)S(1)} %collective-permute-done.7.refs_1_) | copy-start | bytes 884740
  36.8 21.5 %collective-permute-start.9 = (bf16[2,96,768]{2,1,0:T(8,128)(2,1)S(1)}, bf16[2,96,768]{2,1,0:T(8,128)(2,1)S(1)}, u32[]{:S(2)}, u32[]{:S(2)}) collective-permute-start(bf16[2,96,768]{2,1,0:T(8,128)(2,1)S(1)} %copy-done.14), channel_id=1, source_target_pairs={{0,24},{1,25},{2,26},{3,27},{4,28},{5,29},{6,30},{7,31},{8,16},{9,... | collective-permute-start | bytes 884744 | tf_op jit(solution)/shard_map/ppermute | solution.py:50
  52.2 19.5 %copy-start.16 = (bf16[2,96,768]{2,1,0:T(8,128)(2,1)}, bf16[2,96,768]{2,1,0:T(8,128)(2,1)S(1)}, u32[]{:S(2)}) copy-start(bf16[2,96,768]{2,1,0:T(8,128)(2,1)S(1)} %collective-permute-done.8.refs_2_) | copy-start | bytes 884740
  58.3 13.5 %copy-start.17 = (bf16[2,96,768]{2,1,0:T(8,128)(2,1)}, bf16[2,96,768]{2,1,0:T(8,128)(2,1)S(1)}, u32[]{:S(2)}) copy-start(bf16[2,96,768]{2,1,0:T(8,128)(2,1)S(1)} %collective-permute-done.9.refs_3_) | copy-start | bytes 884740
  63.4 10.6 %collective-permute-start.10 = (bf16[4,768,384]{2,1,0:T(8,128)(2,1)}, bf16[4,768,384]{2,1,0:T(8,128)(2,1)S(1)}, u32[]{:S(2)}, u32[]{:S(2)}) collective-permute-start(bf16[4,768,384]{2,1,0:T(8,128)(2,1)} %assemble.1.w_ref.own_ref.refs_0_), channel_id=1, source_target_pairs={{0,1},{1,0},{2,3},{3,2},{4,5},{5,4},{6,7},{7,6},{8,9},{9,8},{10,11... | collective-permute-start | bytes 7077896 | tf_op jit(solution)/shard_map/ppermute | solution.py:50
  74.1 32.1 %collective-permute-start.11 = (bf16[4,2,96,768]{3,2,1,0:T(8,128)(2,1)}, bf16[4,2,96,768]{3,2,1,0:T(8,128)(2,1)}, u32[]{:S(2)}, u32[]{:S(2)}) collective-permute-start(bf16[4,2,96,768]{3,2,1,0:T(8,128)(2,1)} %stack_z.3.refs_4_), channel_id=1, source_target_pairs={{0,4},{1,5},{2,6},{3,7},{4,0},{5,1},{6,2},{7,3},{8,12},{9,13},{10,... | collective-permute-start | bytes 3538952 | tf_op jit(solution)/shard_map/ppermute | solution.py:50
  75.6 30.6 %collective-permute-start.12 = (bf16[4,2,96,768]{3,2,1,0:T(8,128)(2,1)}, bf16[4,2,96,768]{3,2,1,0:T(8,128)(2,1)S(1)}, u32[]{:S(2)}, u32[]{:S(2)}) collective-permute-start(bf16[4,2,96,768]{3,2,1,0:T(8,128)(2,1)} %stack_z.3.refs_4_), channel_id=1, source_target_pairs={{0,2},{1,3},{2,0},{3,1},{4,6},{5,7},{6,4},{7,5},{8,10},{9,11},{10,... | collective-permute-start | bytes 3538952 | tf_op jit(solution)/shard_map/ppermute | solution.py:50
  77.1 29.1 %collective-permute-start.13 = (bf16[4,2,96,768]{3,2,1,0:T(8,128)(2,1)}, bf16[4,2,96,768]{3,2,1,0:T(8,128)(2,1)}, u32[]{:S(2)}, u32[]{:S(2)}) collective-permute-start(bf16[4,2,96,768]{3,2,1,0:T(8,128)(2,1)} %stack_z.3.refs_4_), channel_id=1, source_target_pairs={{0,1},{1,0},{2,3},{3,2},{4,5},{5,4},{6,7},{7,6},{8,9},{9,8},{10,11... | collective-permute-start | bytes 3538952 | tf_op jit(solution)/shard_map/ppermute | solution.py:50
  83.2 23.7 %copy-start.2 = (bf16[4,2,96,768]{3,2,1,0:T(8,128)(2,1)S(1)}, bf16[4,2,96,768]{3,2,1,0:T(8,128)(2,1)}, u32[]{:S(2)}) copy-start(bf16[4,2,96,768]{3,2,1,0:T(8,128)(2,1)} %stack_z.3.refs_4_) | copy-start | bytes 3538948
  83.2 24.6 %copy-start.28 = (f32[1,768]{1,0:T(1,128)S(1)}, f32[1,768]{1,0:T(1,128)}, u32[]{:S(2)}) copy-start(f32[1,768]{1,0:T(1,128)} %get-tuple-element.329) | copy-start | bytes 9220
  83.2 24.6 %copy-start.29 = (f32[1,768]{1,0:T(1,128)S(1)}, f32[1,768]{1,0:T(1,128)}, u32[]{:S(2)}) copy-start(f32[1,768]{1,0:T(1,128)} %get-tuple-element.334) | copy-start | bytes 9220
  106.2 9.9 %copy-start.5 = (bf16[4,2,96,768]{3,2,1,0:T(8,128)(2,1)}, bf16[4,2,96,768]{3,2,1,0:T(8,128)(2,1)S(1)}, u32[]{:S(2)}) copy-start(bf16[4,2,96,768]{3,2,1,0:T(8,128)(2,1)S(1)} %collective-permute-done.12.refs_4_) | copy-start | bytes 3538948
  106.2 9.9 %collective-permute-start.14 = (bf16[4,2,96,768]{3,2,1,0:T(8,128)(2,1)}, bf16[4,2,96,768]{3,2,1,0:T(8,128)(2,1)}, u32[]{:S(2)}, u32[]{:S(2)}) collective-permute-start(bf16[4,2,96,768]{3,2,1,0:T(8,128)(2,1)} %collective-permute-done.11.refs_5_), channel_id=1, source_target_pairs={{0,1},{1,0},{2,3},{3,2},{4,5},{5,4},{6,7},{7,6},{8,9},{9,8},{10,11... | collective-permute-start | bytes 3538952 | tf_op jit(solution)/shard_map/ppermute | solution.py:50
  106.8 35.5 %collective-permute-start.15 = (bf16[4,2,96,768]{3,2,1,0:T(8,128)(2,1)S(1)}, bf16[4,2,96,768]{3,2,1,0:T(8,128)(2,1)S(1)}, u32[]{:S(2)}, u32[]{:S(2)}) collective-permute-start(bf16[4,2,96,768]{3,2,1,0:T(8,128)(2,1)S(1)} %collective-permute-done.12.refs_4_), channel_id=1, source_target_pairs={{0,1},{1,0},{2,3},{3,2},{4,5},{5,4},{6,7},{7,6},{8,9},{9,8},{10,11... | collective-permute-start | bytes 3538952 | tf_op jit(solution)/shard_map/ppermute | solution.py:50
  106.9 35.4 %collective-permute-start.16 = (bf16[4,2,96,768]{3,2,1,0:T(8,128)(2,1)S(1)}, bf16[4,2,96,768]{3,2,1,0:T(8,128)(2,1)}, u32[]{:S(2)}, u32[]{:S(2)}) collective-permute-start(bf16[4,2,96,768]{3,2,1,0:T(8,128)(2,1)S(1)} %copy-done.2), channel_id=1, source_target_pairs={{0,6},{1,7},{2,4},{3,5},{4,2},{5,3},{6,0},{7,1},{8,14},{9,15},{10,... | collective-permute-start | bytes 3538952 | tf_op jit(solution)/shard_map/ppermute | solution.py:50
  145.1 35.4 %collective-permute-start.18 = (bf16[2,4,2,96,768]{4,3,1,0,2:T(8,128)(2,1)S(1)}, bf16[2,4,2,96,768]{4,3,1,0,2:T(8,128)(2,1)}, u32[]{:S(2)}, u32[]{:S(2)}) collective-permute-start(bf16[2,4,2,96,768]{4,3,1,0,2:T(8,128)(2,1)S(1)} %copy.37), channel_id=1, source_target_pairs={{0,1},{1,0},{2,3},{3,2},{4,5},{5,4},{6,7},{7,6},{8,9},{9,8},{10,11... | collective-permute-start | bytes 7077896 | tf_op jit(solution)/shard_map/ppermute | solution.py:50
  145.4 6.1 %collective-permute-start.17 = (bf16[4,2,96,768]{3,2,1,0:T(8,128)(2,1)}, bf16[4,2,96,768]{3,2,1,0:T(8,128)(2,1)S(1)}, u32[]{:S(2)}, u32[]{:S(2)}) collective-permute-start(bf16[4,2,96,768]{3,2,1,0:T(8,128)(2,1)} %collective-permute-done.16.refs_5_), channel_id=1, source_target_pairs={{0,1},{1,0},{2,3},{3,2},{4,5},{5,4},{6,7},{7,6},{8,9},{9,8},{10,11... | collective-permute-start | bytes 3538952 | tf_op jit(solution)/shard_map/ppermute | solution.py:50
  180.6 16.2 %collective-permute-start.19 = (bf16[2,4,2,96,768]{4,3,2,1,0:T(8,128)(2,1)}, bf16[2,4,2,96,768]{4,3,2,1,0:T(8,128)(2,1)}, u32[]{:S(2)}, u32[]{:S(2)}) collective-permute-start(bf16[2,4,2,96,768]{4,3,2,1,0:T(8,128)(2,1)} %get-tuple-element.220), channel_id=1, source_target_pairs={{0,1},{1,0},{2,3},{3,2},{4,5},{5,4},{6,7},{7,6},{8,9},{9,8},{10,11... | collective-permute-start | bytes 7077896 | tf_op jit(solution)/shard_map/ppermute | solution.py:50
  180.8 11.3 %copy-start.3 = (bf16[2,4,2,96,768]{4,3,2,1,0:T(8,128)(2,1)S(1)}, bf16[2,4,2,96,768]{4,3,2,1,0:T(8,128)(2,1)}, u32[]{:S(2)}) copy-start(bf16[2,4,2,96,768]{4,3,2,1,0:T(8,128)(2,1)} %get-tuple-element.224) | copy-start | bytes 7077892
  192.1 4.7 %copy-start.4 = (bf16[2,4,2,96,768]{4,3,2,1,0:T(8,128)(2,1)S(1)}, bf16[2,4,2,96,768]{4,3,2,1,0:T(8,128)(2,1)}, u32[]{:S(2)}) copy-start(bf16[2,4,2,96,768]{4,3,2,1,0:T(8,128)(2,1)} %get-tuple-element.219) | copy-start | bytes 7077892
  201.7 34.6 %collective-permute-start.20 = (bf16[2,4,96,768]{3,2,1,0:T(8,128)(2,1)S(1)}, bf16[2,4,96,768]{3,2,1,0:T(8,128)(2,1)}, u32[]{:S(2)}, u32[]{:S(2)}) collective-permute-start(bf16[2,4,96,768]{3,2,1,0:T(8,128)(2,1)S(1)} %slice_bitcast_fusion.3), channel_id=1, source_target_pairs={{0,2},{1,3},{2,0},{3,1},{4,6},{5,7},{6,4},{7,5},{8,10},{9,11},{10,... | collective-permute-start | bytes 3538952 | tf_op jit(solution)/shard_map/ppermute | solution.py:50
  202.9 33.5 %collective-permute-start.21 = (bf16[2,4,96,768]{3,2,1,0:T(8,128)(2,1)S(1)}, bf16[2,4,96,768]{3,2,1,0:T(8,128)(2,1)S(1)}, u32[]{:S(2)}, u32[]{:S(2)}) collective-permute-start(bf16[2,4,96,768]{3,2,1,0:T(8,128)(2,1)S(1)} %pad_maximum_fusion), channel_id=1, source_target_pairs={{0,4},{1,5},{2,6},{3,7},{4,0},{5,1},{6,2},{7,3},{8,12},{9,13},{10,... | collective-permute-start | bytes 3538952 | tf_op jit(solution)/shard_map/ppermute | solution.py:50
  204.4 32.0 %collective-permute-start.22 = (bf16[4,4,1,24,768]{4,3,2,1,0:T(8,128)(2,1)}, bf16[4,4,1,24,768]{4,3,2,1,0:T(8,128)(2,1)}, u32[]{:S(2)}, u32[]{:S(2)}) collective-permute-start(bf16[4,4,1,24,768]{4,3,2,1,0:T(8,128)(2,1)} %get-tuple-element.230), channel_id=1, source_target_pairs={{0,1},{1,0},{2,3},{3,2},{4,5},{5,4},{6,7},{7,6},{8,9},{9,8},{10,11... | collective-permute-start | bytes 1769480 | tf_op jit(solution)/shard_map/ppermute | solution.py:50
  238.6 5.2 %copy-start.32 = (f32[2,1,768]{2,1,0:T(1,128)S(1)}, f32[2,1,768]{2,1,0:T(1,128)}, u32[]{:S(2)}) copy-start(f32[2,1,768]{2,1,0:T(1,128)} %get-tuple-element.281) | copy-start | bytes 18436
  238.6 5.2 %copy-start.33 = (f32[2,1,768]{2,1,0:T(1,128)S(1)}, f32[2,1,768]{2,1,0:T(1,128)}, u32[]{:S(2)}) copy-start(f32[2,1,768]{2,1,0:T(1,128)} %get-tuple-element.282) | copy-start | bytes 18436
  241.7 16.1 %collective-permute-start.23 = (bf16[4,96,768]{2,1,0:T(8,128)(2,1)}, bf16[4,96,768]{2,1,0:T(8,128)(2,1)}, u32[]{:S(2)}, u32[]{:S(2)}) collective-permute-start(bf16[4,96,768]{2,1,0:T(8,128)(2,1)} %fusion.5), channel_id=1, source_target_pairs={{0,2},{1,3},{2,0},{3,1},{4,6},{5,7},{6,4},{7,5},{8,10},{9,11},{10,... | collective-permute-start | bytes 1769480 | tf_op jit(solution)/shard_map/ppermute | solution.py:50
  242.3 15.8 %collective-permute-start.24 = (bf16[4,96,768]{2,1,0:T(8,128)(2,1)}, bf16[4,96,768]{2,1,0:T(8,128)(2,1)}, u32[]{:S(2)}, u32[]{:S(2)}) collective-permute-start(bf16[4,96,768]{2,1,0:T(8,128)(2,1)} %fusion.7), channel_id=1, source_target_pairs={{0,4},{1,5},{2,6},{3,7},{4,0},{5,1},{6,2},{7,3},{8,12},{9,13},{10,... | collective-permute-start | bytes 1769480 | tf_op jit(solution)/shard_map/ppermute | solution.py:50
  243.9 14.3 %copy-start.31 = (f32[8,768]{1,0:T(8,128)S(1)}, f32[8,768]{1,0:T(8,128)}, u32[]{:S(2)}) copy-start(f32[8,768]{1,0:T(8,128)} %get-tuple-element.280) | copy-start | bytes 73732
  258.1 4.4 %collective-permute-start.25 = (bf16[4,4,3,24,768]{4,3,2,1,0:T(8,128)(2,1)}, bf16[4,4,3,24,768]{4,3,2,1,0:T(8,128)(2,1)}, u32[]{:S(2)}, u32[]{:S(2)}) collective-permute-start(bf16[4,4,3,24,768]{4,3,2,1,0:T(8,128)(2,1)} %get-tuple-element.250), channel_id=1, source_target_pairs={{0,1},{1,0},{2,3},{3,2},{4,5},{5,4},{6,7},{7,6},{8,9},{9,8},{10,11... | collective-permute-start | bytes 5308424 | tf_op jit(solution)/shard_map/ppermute | solution.py:50
  266.5 15.5 %copy-start.26 = (f32[2,768]{1,0:T(2,128)S(1)}, f32[2,768]{1,0:T(2,128)}, u32[]{:S(2)}) copy-start(f32[2,768]{1,0:T(2,128)} %slice.267) | copy-start | bytes 18436
  266.5 15.5 %copy-start.27 = (f32[1,768]{1,0:T(1,128)S(1)}, f32[1,768]{1,0:T(1,128)}, u32[]{:S(2)}) copy-start(f32[1,768]{1,0:T(1,128)} %get-tuple-element.326) | copy-start | bytes 9220
  266.5 16.5 %copy-start.30 = (bf16[80]{0:T(256)(128)(2,1)S(1)}, bf16[80]{0:T(256)(128)(2,1)}, u32[]{:S(2)}) copy-start(bf16[80]{0:T(256)(128)(2,1)} %pad.38.clone) | copy-start | bytes 484
  283.1 4.7 %collective-permute-start.29 = (bf16[80,768]{1,0:T(8,128)(2,1)S(1)}, bf16[80,768]{1,0:T(8,128)(2,1)S(1)}, u32[]{:S(2)}, u32[]{:S(2)}) collective-permute-start(bf16[80,768]{1,0:T(8,128)(2,1)S(1)} %get-tuple-element.308), channel_id=1, source_target_pairs={{0,1},{1,0},{2,3},{3,2},{4,5},{5,4},{6,7},{7,6},{8,9},{9,8},{10,11... | collective-permute-start | bytes 368648 | tf_op jit(solution)/shard_map/ppermute | solution.py:50
  283.7 37.0 %collective-permute-start.26 = (bf16[4,4,24,768]{3,2,1,0:T(8,128)(2,1)}, bf16[4,4,24,768]{3,2,1,0:T(8,128)(2,1)S(1)}, u32[]{:S(2)}, u32[]{:S(2)}) collective-permute-start(bf16[4,4,24,768]{3,2,1,0:T(8,128)(2,1)} %get-tuple-element.275), channel_id=1, source_target_pairs={{0,2},{1,3},{2,0},{3,1},{4,6},{5,7},{6,4},{7,5},{8,10},{9,11},{10,... | collective-permute-start | bytes 1769480 | tf_op jit(solution)/shard_map/ppermute | solution.py:50
  285.2 35.5 %collective-permute-start.27 = (bf16[4,4,24,768]{3,2,1,0:T(8,128)(2,1)}, bf16[4,4,24,768]{3,2,1,0:T(8,128)(2,1)S(1)}, u32[]{:S(2)}, u32[]{:S(2)}) collective-permute-start(bf16[4,4,24,768]{3,2,1,0:T(8,128)(2,1)} %get-tuple-element.276), channel_id=1, source_target_pairs={{0,4},{1,5},{2,6},{3,7},{4,0},{5,1},{6,2},{7,3},{8,12},{9,13},{10,... | collective-permute-start | bytes 1769480 | tf_op jit(solution)/shard_map/ppermute | solution.py:50
  285.7 17.0 %collective-permute-start.38 = (bf16[2,96,768]{2,1,0:T(8,128)(2,1)S(1)}, bf16[2,96,768]{2,1,0:T(8,128)(2,1)S(1)}, u32[]{:S(2)}, u32[]{:S(2)}) collective-permute-start(bf16[2,96,768]{2,1,0:T(8,128)(2,1)S(1)} %pad_maximum_fusion.1), channel_id=1, source_target_pairs={{0,8},{1,9},{2,10},{3,11},{4,12},{5,13},{6,14},{7,15},{8,0},{9,1},... | collective-permute-start | bytes 884744 | tf_op jit(solution)/shard_map/ppermute | solution.py:50
  285.7 18.5 %collective-permute-start.39 = (bf16[2,96,768]{2,1,0:T(8,128)(2,1)S(1)}, bf16[2,96,768]{2,1,0:T(8,128)(2,1)S(1)}, u32[]{:S(2)}, u32[]{:S(2)}) collective-permute-start(bf16[2,96,768]{2,1,0:T(8,128)(2,1)S(1)} %pad_maximum_fusion.2), channel_id=1, source_target_pairs={{0,16},{1,17},{2,18},{3,19},{4,20},{5,21},{6,22},{7,23},{8,24},{9,... | collective-permute-start | bytes 884744 | tf_op jit(solution)/shard_map/ppermute | solution.py:50
  287.9 14.8 %copy-start.34 = (bf16[4,4,24,768]{3,2,1,0:T(8,128)(2,1)S(1)}, bf16[4,4,24,768]{3,2,1,0:T(8,128)(2,1)}, u32[]{:S(2)}) copy-start(bf16[4,4,24,768]{3,2,1,0:T(8,128)(2,1)} %get-tuple-element.277) | copy-start | bytes 1769476
  288.1 13.8 %collective-permute-start.30 = (bf16[80,768]{1,0:T(8,128)(2,1)S(1)}, bf16[80,768]{1,0:T(8,128)(2,1)S(1)}, u32[]{:S(2)}, u32[]{:S(2)}) collective-permute-start(bf16[80,768]{1,0:T(8,128)(2,1)S(1)} %get-tuple-element.304), channel_id=1, source_target_pairs={{0,2},{1,3},{2,0},{3,1},{4,6},{5,7},{6,4},{7,5},{8,10},{9,11},{10,... | collective-permute-start | bytes 368648 | tf_op jit(solution)/shard_map/ppermute | solution.py:50
  301.8 13.8 %collective-permute-start.40 = (bf16[2,96,768]{2,1,0:T(8,128)(2,1)S(1)}, bf16[2,96,768]{2,1,0:T(8,128)(2,1)S(1)}, u32[]{:S(2)}, u32[]{:S(2)}) collective-permute-start(bf16[2,96,768]{2,1,0:T(8,128)(2,1)S(1)} %pad_maximum_fusion.3), channel_id=1, source_target_pairs={{0,24},{1,25},{2,26},{3,27},{4,28},{5,29},{6,30},{7,31},{8,16},{9,... | collective-permute-start | bytes 884744 | tf_op jit(solution)/shard_map/ppermute | solution.py:50
  302.7 18.0 %collective-permute-start.28 = (bf16[4,4,24,768]{3,2,1,0:T(8,128)(2,1)S(1)}, bf16[4,4,24,768]{3,2,1,0:T(8,128)(2,1)S(1)}, u32[]{:S(2)}, u32[]{:S(2)}) collective-permute-start(bf16[4,4,24,768]{3,2,1,0:T(8,128)(2,1)S(1)} %copy-done.34), channel_id=1, source_target_pairs={{0,6},{1,7},{2,4},{3,5},{4,2},{5,3},{6,0},{7,1},{8,14},{9,15},{10,... | collective-permute-start | bytes 1769480 | tf_op jit(solution)/shard_map/ppermute | solution.py:50
  304.2 16.2 %collective-permute-start.31 = (bf16[80,768]{1,0:T(8,128)(2,1)S(1)}, bf16[80,768]{1,0:T(8,128)(2,1)S(1)}, u32[]{:S(2)}, u32[]{:S(2)}) collective-permute-start(bf16[80,768]{1,0:T(8,128)(2,1)S(1)} %get-tuple-element.300), channel_id=1, source_target_pairs={{0,4},{1,5},{2,6},{3,7},{4,0},{5,1},{6,2},{7,3},{8,12},{9,13},{10,... | collective-permute-start | bytes 368648 | tf_op jit(solution)/shard_map/ppermute | solution.py:50
  320.7 3.7 %copy-start.11 = (bf16[4,4,24,768]{3,2,1,0:T(8,128)(2,1)}, bf16[4,4,24,768]{3,2,1,0:T(8,128)(2,1)S(1)}, u32[]{:S(2)}) copy-start(bf16[4,4,24,768]{3,2,1,0:T(8,128)(2,1)S(1)} %collective-permute-done.26.refs_0_) | copy-start | bytes 1769476
  320.7 3.6 %copy-start.12 = (bf16[4,4,24,768]{3,2,1,0:T(8,128)(2,1)}, bf16[4,4,24,768]{3,2,1,0:T(8,128)(2,1)S(1)}, u32[]{:S(2)}) copy-start(bf16[4,4,24,768]{3,2,1,0:T(8,128)(2,1)S(1)} %collective-permute-done.27.refs_1_) | copy-start | bytes 1769476
  320.7 3.6 %copy-start.13 = (bf16[4,4,24,768]{3,2,1,0:T(8,128)(2,1)}, bf16[4,4,24,768]{3,2,1,0:T(8,128)(2,1)S(1)}, u32[]{:S(2)}) copy-start(bf16[4,4,24,768]{3,2,1,0:T(8,128)(2,1)S(1)} %collective-permute-done.28.refs_2_) | copy-start | bytes 1769476
  320.7 9.5 %collective-permute-start.34 = (bf16[80,768]{1,0:T(8,128)(2,1)S(1)}, bf16[80,768]{1,0:T(8,128)(2,1)S(1)}, u32[]{:S(2)}, u32[]{:S(2)}) collective-permute-start(bf16[80,768]{1,0:T(8,128)(2,1)S(1)} %maximum_maximum_fusion.3), channel_id=1, source_target_pairs={{0,24},{1,25},{2,26},{3,27},{4,28},{5,29},{6,30},{7,31},{8,16},{9,... | collective-permute-start | bytes 368648 | tf_op jit(solution)/shard_map/ppermute | solution.py:50
  322.2 11.0 %collective-permute-start.33 = (bf16[80,768]{1,0:T(8,128)(2,1)S(1)}, bf16[80,768]{1,0:T(8,128)(2,1)S(1)}, u32[]{:S(2)}, u32[]{:S(2)}) collective-permute-start(bf16[80,768]{1,0:T(8,128)(2,1)S(1)} %maximum_maximum_fusion.3), channel_id=1, source_target_pairs={{0,16},{1,17},{2,18},{3,19},{4,20},{5,21},{6,22},{7,23},{8,24},{9,... | collective-permute-start | bytes 368648 | tf_op jit(solution)/shard_map/ppermute | solution.py:50
  322.2 11.1 %collective-permute-start.32 = (bf16[80,768]{1,0:T(8,128)(2,1)S(1)}, bf16[80,768]{1,0:T(8,128)(2,1)S(1)}, u32[]{:S(2)}, u32[]{:S(2)}) collective-permute-start(bf16[80,768]{1,0:T(8,128)(2,1)S(1)} %maximum_maximum_fusion.3), channel_id=1, source_target_pairs={{0,8},{1,9},{2,10},{3,11},{4,12},{5,13},{6,14},{7,15},{8,0},{9,1},... | collective-permute-start | bytes 368648 | tf_op jit(solution)/shard_map/ppermute | solution.py:50
  327.1 9.7 %collective-permute-start.35 = (bf16[4,24,768]{2,1,0:T(8,128)(2,1)}, bf16[4,24,768]{2,1,0:T(8,128)(2,1)S(1)}, u32[]{:S(2)}, u32[]{:S(2)}) collective-permute-start(bf16[4,24,768]{2,1,0:T(8,128)(2,1)} %get-tuple-element.289), channel_id=1, source_target_pairs={{0,8},{1,9},{2,10},{3,11},{4,12},{5,13},{6,14},{7,15},{8,0},{9,1},... | collective-permute-start | bytes 442376 | tf_op jit(solution)/shard_map/ppermute | solution.py:50
  327.1 15.3 %collective-permute-start.36 = (bf16[4,24,768]{2,1,0:T(8,128)(2,1)}, bf16[4,24,768]{2,1,0:T(8,128)(2,1)S(1)}, u32[]{:S(2)}, u32[]{:S(2)}) collective-permute-start(bf16[4,24,768]{2,1,0:T(8,128)(2,1)} %get-tuple-element.290), channel_id=1, source_target_pairs={{0,16},{1,17},{2,18},{3,19},{4,20},{5,21},{6,22},{7,23},{8,24},{9,... | collective-permute-start | bytes 442376 | tf_op jit(solution)/shard_map/ppermute | solution.py:50
  330.2 15.2 %collective-permute-start.37 = (bf16[4,24,768]{2,1,0:T(8,128)(2,1)}, bf16[4,24,768]{2,1,0:T(8,128)(2,1)S(1)}, u32[]{:S(2)}, u32[]{:S(2)}) collective-permute-start(bf16[4,24,768]{2,1,0:T(8,128)(2,1)} %get-tuple-element.291), channel_id=1, source_target_pairs={{0,24},{1,25},{2,26},{3,27},{4,28},{5,29},{6,30},{7,31},{8,16},{9,... | collective-permute-start | bytes 442376 | tf_op jit(solution)/shard_map/ppermute | solution.py:50
  336.7 8.8 %copy-start.21 = (bf16[4,24,768]{2,1,0:T(8,128)(2,1)}, bf16[4,24,768]{2,1,0:T(8,128)(2,1)S(1)}, u32[]{:S(2)}) copy-start(bf16[4,24,768]{2,1,0:T(8,128)(2,1)S(1)} %collective-permute-done.35.refs_0_) | copy-start | bytes 442372
  342.4 3.1 copy-start.22
  (12 other events, 13.3 us)

commit v3 on v2

--- a/solution.py
+++ b/solution.py
@@ -17,6 +17,8 @@
 F32 = jnp.float32
 AXES = ("dp", "mp")
 TILE = 256
+STEP = 512
+QROWS = 512
 NT = (((1,), (1,)), ((), ()))
 TN = (((0,), (0,)), ((), ()))
 VMEM_LIMIT = 60 * 1024 * 1024
@@ -72,6 +74,24 @@
 
 def z_stage(piece):
     return stack([piece] + [px(piece, 8 * k) for k in range(1, 4)], "stack_z")
+
+
+def stack_pair_kernel(*refs):
+    for i, ref in enumerate(refs[:-2]):
+        for c in range(2):
+            refs[c - 2][i] = ref[c]
+
+
+def stack_pair(parts):
+    vmem = pl.BlockSpec(memory_space=pltpu.VMEM)
+    shape = jax.ShapeDtypeStruct((len(parts),) + parts[0].shape[1:], parts[0].dtype)
+    return pl.pallas_call(
+        stack_pair_kernel,
+        name="stack_pair",
+        out_shape=(shape, shape),
+        in_specs=[vmem] * len(parts),
+        out_specs=(vmem, vmem),
+    )(*parts)
 
 
 def xy_stage(parts):
@@ -139,9 +159,8 @@
 def project_kernel(side, meta, x_ref, w_ref, b_ref, *refs):
     half = jnp.bitwise_xor(meta[0] % 2, side)
     cols = pl.ds(pl.multiple_of(384 * half, 128), 384)
-    for c in range(3):
-        y = dotf(x_ref[...], w_ref[c]) + b_ref[c, :, cols]
-        refs[-1][:, 384 * c : 384 * c + 384] = y.astype(B16)
+    y = dotf(x_ref[...], w_ref[0]) + b_ref[pl.program_id(0), :, cols]
+    refs[-1][...] = y.astype(B16)
 
 
 def project(meta, x, weight, bias, side, held):
@@ -150,16 +169,16 @@
     return pl.pallas_call(
         partial(project_kernel, side),
         name="project",
-        grid=(rows // TILE,),
+        grid=(3,),
         out_shape=jax.ShapeDtypeStruct((rows, 2304), B16),
         in_specs=[
             pl.BlockSpec(memory_space=pltpu.SMEM),
-            pl.BlockSpec((TILE, 768), lambda i: (i, 0)),
-            pl.BlockSpec((3, 768, 384), lambda i: (0, 0, 0), pipeline_mode=pl.Buffered(1)),
+            vmem,
+            pl.BlockSpec((1, 768, 384), lambda c: (c, 0, 0)),
             vmem,
         ]
         + [pl.BlockSpec(memory_space=pl.ANY)] * len(held),
-        out_specs=pl.BlockSpec((TILE, 1152), lambda i: (i, side)),
+        out_specs=pl.BlockSpec((rows, 384), lambda c: (0, 3 * side + c)),
         input_output_aliases={4 + i: i for i in range(len(held))},
         compiler_params=pltpu.CompilerParams(vmem_limit_bytes=VMEM_LIMIT),
     )(meta, x, weight, bias, *held)
@@ -307,12 +326,12 @@
 
 def out_projection(meta, mixed, start, own, other, params):
     rows = mixed.shape[0]
-    block = pl.BlockSpec((TILE, 768), lambda i: (i, 0))
+    block = pl.BlockSpec((STEP, 768), lambda i: (i, 0))
     vmem = pl.BlockSpec(memory_space=pltpu.VMEM)
     return pl.pallas_call(
         out_kernel,
         name="out_projection",
-        grid=(rows // TILE,),
+        grid=(rows // STEP,),
         in_specs=[pl.BlockSpec(memory_space=pltpu.SMEM), block, block, vmem, vmem, vmem],
         out_specs=[block, block, vmem],
         out_shape=(
@@ -372,13 +391,13 @@
 
 def turn(meta, middle, branch, grad, cot, mixed, weight, params):
     rows = middle.shape[0]
-    block = pl.BlockSpec((TILE, 768), lambda i: (i, 0))
+    block = pl.BlockSpec((STEP, 768), lambda i: (i, 0))
     vmem = pl.BlockSpec(memory_space=pltpu.VMEM)
     parts = jax.ShapeDtypeStruct((4, 4, 1, 24, 768), B16)
     return pl.pallas_call(
         turn_kernel,
         name="turn",
-        grid=(rows // TILE,),
+        grid=(rows // STEP,),
         in_specs=[pl.BlockSpec(memory_space=pltpu.SMEM)] + [block] * 5 + [vmem, vmem],
         out_specs=[block, block, block, vmem, vmem, vmem],
         out_shape=(
@@ -394,9 +413,9 @@
     )(meta, middle, branch, grad, cot, mixed, weight, params)
 
 
-def tail_kernel(meta, start_ref, gmiddle_ref, slots_ref, p_ref, *refs):
+def tail_kernel(meta, start_ref, gmiddle_ref, slots_ref, p_ref, turn_ref, up_ref, *refs):
     weights, grads = refs[:2], refs[2:5]
-    input_ref, prompt_ref, sums_ref = refs[5:]
+    input_ref, packed_ref, prompt_ref, sums_ref = refs[5:]
     core = meta[0] % 2
 
     @pl.when(pl.program_id(0) == 0)
@@ -412,7 +431,8 @@
             term = dotf(left, weights[side][c], NT)
             total = term if total is None else total + term
     normal, rate = centred(start_ref[...])
-    for row, x in enumerate((normal * total, total, grads[0][...].astype(F32), grads[2][...].astype(F32))):
+    rows = ((0, normal * total), (2, total), (4, grads[0][...].astype(F32)), (5, grads[2][...].astype(F32)))
+    for row, x in rows:
         sums_ref[row : row + 1, :] += row_sum(x)
     gstart = gmiddle_ref[...] + norm_backward(normal, rate, total, p_ref[0:1])
     slots = slots_ref[...]
@@ -421,28 +441,41 @@
     for part in three_parts(gstart):
         prompt_ref[...] += dotf(slots, part.astype(B16), TN)
 
-
-def tail_step(meta, start, gmiddle, slots, params, weights, grads):
+    @pl.when(pl.program_id(0) == pl.num_programs(0) - 1)
+    def _():
+        for row, source in ((1, 0), (3, 1), (6, 2), (7, 3)):
+            sums_ref[row : row + 1, :] = turn_ref[source : source + 1, :]
+        for row in range(4):
+            sums_ref[8 + row : 9 + row, :] = up_ref[row]
+        packed_ref[0:64, :] = prompt_ref[0:64, :].astype(B16)
+        high, low = split_rows(sums_ref[...])
+        packed_ref[64:80, :] = high
+        packed_ref[80:96, :] = low
+
+
+def tail_step(meta, start, gmiddle, slots, params, sums_two, up, weights, grads):
     rows = start.shape[0]
 
     def block(width):
-        return pl.BlockSpec((TILE, width), lambda i: (i, 0))
+        return pl.BlockSpec((STEP, width), lambda i: (i, 0))
 
     vmem = pl.BlockSpec(memory_space=pltpu.VMEM)
     return pl.pallas_call(
         tail_kernel,
         name="tail_step",
-        grid=(rows // TILE,),
-        in_specs=[pl.BlockSpec(memory_space=pltpu.SMEM), block(768), block(768), block(128), vmem, vmem, vmem]
+        grid=(rows // STEP,),
+        in_specs=[pl.BlockSpec(memory_space=pltpu.SMEM), block(768), block(768), block(128)]
+        + [vmem] * 3
+        + [pl.BlockSpec((3, 768, 384), lambda i: (0, 0, 0))] * 2
         + [block(768)] * 3,
-        out_specs=[block(768), vmem, vmem],
+        out_specs=[block(768), vmem],
         out_shape=(
             jax.ShapeDtypeStruct((rows, 768), F32),
-            jax.ShapeDtypeStruct((128, 768), F32),
-            jax.ShapeDtypeStruct((8, 768), F32),
+            jax.ShapeDtypeStruct((96, 768), B16),
         ),
+        scratch_shapes=[pltpu.VMEM((128, 768), F32), pltpu.VMEM((16, 768), F32)],
         compiler_params=pltpu.CompilerParams(vmem_limit_bytes=VMEM_LIMIT),
-    )(meta, start, gmiddle, slots, params, *weights, *grads)
+    )(meta, start, gmiddle, slots, params, sums_two, up, *weights, *grads)
 
 
 def weight_grad_kernel(count, meta, left_ref, *refs):
@@ -467,17 +500,22 @@
     )(meta, left, *rights)
 
 
-def pack_small(small):
-    low = small[:NPROMPT].astype(B16)
-    rest = small[NPROMPT:]
+def split_rows(rest):
     high = rest.astype(B16)
-    return jnp.concatenate([low, high, (rest - high.astype(F32)).astype(B16), jnp.zeros((6, small.shape[1]), B16)])
-
-
-def open_small(packed):
-    wide = packed.astype(F32)
-    at = NPROMPT + 12
-    return jnp.concatenate([wide[:NPROMPT], wide[NPROMPT:at] + wide[at : at + 12]])
+    return high, (rest - high.astype(F32)).astype(B16)
+
+
+def add_small(x, y):
+    x, y = x.astype(F32), y.astype(F32)
+    return jnp.concatenate([x[:64] + y[:64], (x[64:80] + x[80:]) + (y[64:80] + y[80:])])
+
+
+def pack_small(x):
+    return jnp.concatenate([x[:64].astype(B16), *split_rows(x[64:])])
+
+
+def exchange_small(x, k):
+    return add_small(x, px(x, k))
 
 
 def add_parts(own, got):
@@ -500,19 +538,19 @@
     for e in range(2):
         own = half if e == 0 else ~half
         sides.append((jnp.where(own, q, qf), jnp.where(own, k, kf), jnp.where(own, v, one)))
-    for first in range(0, ROW, TILE):
-        low, high = key_window(first, TILE)
+    for first in range(0, ROW, QROWS):
+        low, high = key_window(first, QROWS)
         outs, peaks = [], []
         for qe, ke, ve in sides:
-            s = dotf(qe[first : first + TILE], ke[low:high], NT)
+            s = dotf(qe[first : first + QROWS], ke[low:high], NT)
             peak = jnp.max(s, axis=-1, keepdims=True)
             p = jnp.exp(s - peak).astype(B16)
             outs.append(dotf(p, ve[low:high]))
             peaks.append(peak)
         data = jnp.where(half, outs[0], outs[1])
         total = pltpu.roll(jnp.where(half, outs[1], outs[0]), 64, 1)
-        mixed_ref[first : first + TILE, :] = (data / total).astype(B16)
-        lse_ref[first : first + TILE, :] = jnp.where(half, peaks[0], peaks[1]) + jnp.log(total)
+        mixed_ref[first : first + QROWS, :] = (data / total).astype(B16)
+        lse_ref[first : first + QROWS, :] = jnp.where(half, peaks[0], peaks[1]) + jnp.log(total)
 
 
 def pair_specs(rows):
@@ -623,122 +661,118 @@
 PER = 768 // SUB
 
 
-def mlp_kernel(fast, base, *refs):
+def mlp_kernel(fast, *refs):
     meta, n_ref, c_ref, b_ref = refs[:4]
-    count = 4 if fast else 1
+    count = 16 if fast else 1
     pieces, refs = refs[4 : 4 + count], refs[4 + count :]
-    if base:
-        held, refs = refs[:2], refs[2:]
     branch_ref, gn_ref, db_ref, own_ref, other_ref = refs[:5]
     w, nt, ct, dw, wsem, dsem = refs[5:]
     t = pl.program_id(0)
-    jl, sub = t // PER, t % PER
+    jr, sub = t // PER, t % PER
     me_mp, me_dp = meta[0] % 4, meta[0] // 4
 
     def loads(j):
         if not fast:
-            source = pieces[0].at[:, :, pl.ds(768 * (base + j), 768)]
-            return [pltpu.make_async_copy(source, w.at[j], wsem.at[j, 0])]
+            source = pieces[0].at[:, :, pl.ds(768 * j, 768)]
+            return [pltpu.make_async_copy(source, w.at[j], wsem.at[j, 0, 0])]
         out = []
         for dr in range(8):
             rows = pl.multiple_of(96 * jnp.bitwise_xor(me_dp, dr), 32)
-            source = pieces[2 * j + (dr & 1)].at[dr >> 1]
-            out.append(pltpu.make_async_copy(source, w.at[j, :, pl.ds(rows, 96), :], wsem.at[j, dr]))
+            for c in range(2):
+                source = pieces[8 * (j & 1) + 4 * c + (j >> 1) + 2 * (dr & 1)].at[dr >> 1]
+                out.append(pltpu.make_async_copy(source, w.at[j, c, pl.ds(rows, 96), :], wsem.at[j, dr, c]))
         return out
 
     def stores(j):
+        if not fast:
+            return [pltpu.make_async_copy(dw.at[j], own_ref.at[j], dsem.at[j, 0, 0])]
         out = []
         for dr in range(8):
-            target = (other_ref if j else own_ref).at[dr & 1, dr >> 1]
-            out.append(pltpu.make_async_copy(dw.at[j, dr], target, dsem.at[j, dr]))
+            x, y = j >> 1, dr & 1
+            for c, spot in enumerate((2 * x + y, 2 * y + x)):
+                target = (other_ref if j & 1 else own_ref).at[c, spot, dr >> 1]
+                out.append(pltpu.make_async_copy(dw.at[j, dr, c], target, dsem.at[j, dr, c]))
         return out
 
     @pl.when(t == 0)
     def _():
-        for j in range(2):
+        for j in range(4):
             for copy in loads(j):
                 copy.start()
         nt[...] = n_ref[...].T
         ct[...] = c_ref[...].T
-        if base:
-            branch_ref[...] = held[0][...]
-            gn_ref[...] = held[1][...]
-        else:
-            branch_ref[...] = jnp.zeros_like(branch_ref)
-            gn_ref[...] = jnp.zeros_like(gn_ref)
-
-    for j in range(2):
+        branch_ref[...] = jnp.zeros_like(branch_ref)
+        gn_ref[...] = jnp.zeros_like(gn_ref)
+
+    for j in range(4):
 
         @pl.when(t == PER * j)
         def _():
             for copy in loads(j):
                 copy.wait()
 
-    spot = jnp.bitwise_xor(me_mp, base + jl) if fast else base + jl
+    spot = jnp.bitwise_xor(me_mp, jr) if fast else jr
     cols = pl.ds(pl.multiple_of(sub * SUB, SUB), SUB)
-    w1 = w[jl, 0, :, cols]
-    w2 = w[jl, 1, :, cols]
+    w1 = w[jr, 0, :, cols]
+    w2 = w[jr, 1, :, cols]
     u = dotf(n_ref[...], w1) + b_ref[spot, :, cols]
     cdf = 0.5 * (1.0 + lax.erf(u * 0.7071067811865476))
     hidden = (u * cdf).astype(B16)
     slope = cdf + u * (0.3989422804014327 * jnp.exp(-0.5 * u * u))
     gb = (dotf(c_ref[...], w2) * slope).astype(B16)
-    db_ref[jl, :, cols] = jnp.sum(gb.astype(F32), axis=0, keepdims=True)
+    db_ref[spot, :, cols] = jnp.sum(gb.astype(F32), axis=0, keepdims=True)
     branch_ref[...] += dotf(hidden, w2, NT)
     gn_ref[...] += dotf(gb, w1, NT)
     dw1 = dotf(nt[...], gb).astype(B16)
     dw2 = dotf(ct[...], hidden).astype(B16)
     for a in range(8):
         dr = jnp.bitwise_xor(me_dp, a) if fast else a
-        dw[jl, dr, 0, :, cols] = dw1[96 * a : 96 * a + 96]
-        dw[jl, dr, 1, :, cols] = dw2[96 * a : 96 * a + 96]
-
-    for j in range(2):
+        dw[jr, dr, 0, :, cols] = dw1[96 * a : 96 * a + 96]
+        dw[jr, dr, 1, :, cols] = dw2[96 * a : 96 * a + 96]
+
+    for j in range(4):
 
         @pl.when(t == PER * j + PER - 1)
         def _():
             for copy in stores(j):
                 copy.start()
 
-    @pl.when(t == 2 * PER - 1)
+    @pl.when(t == 4 * PER - 1)
     def _():
-        for j in range(2):
+        for j in range(4):
             for copy in stores(j):
                 copy.wait()
 
 
-def mlp(meta, normed, cot, bias, pieces, base, held):
-    fast = len(pieces) == 4
+def mlp(meta, normed, cot, bias, pieces):
+    fast = len(pieces) == 16
     tokens = normed.shape[0]
     vmem = pl.BlockSpec(memory_space=pltpu.VMEM)
     anys = pl.BlockSpec(memory_space=pl.ANY)
-    shape = jax.ShapeDtypeStruct((2, 4, 2, 96, 768), B16)
-    at = 4 + len(pieces)
-    return pl.pallas_call(
-        partial(mlp_kernel, fast, base),
+    shape = jax.ShapeDtypeStruct((2, 4, 4, 96, 768) if fast else (4, 8, 2, 96, 768), B16)
+    return pl.pallas_call(
+        partial(mlp_kernel, fast),
         name="mlp",
-        grid=(2 * PER,),
-        in_specs=[pl.BlockSpec(memory_space=pltpu.SMEM), vmem, vmem, vmem]
-        + [anys] * len(pieces)
-        + [vmem] * len(held),
+        grid=(4 * PER,),
+        in_specs=[pl.BlockSpec(memory_space=pltpu.SMEM), vmem, vmem, vmem] + [anys] * len(pieces),
         out_specs=[vmem, vmem, vmem, anys, anys],
         out_shape=(
             jax.ShapeDtypeStruct((tokens, 768), F32),
             jax.ShapeDtypeStruct((tokens, 768), F32),
-            jax.ShapeDtypeStruct((2, 1, 768), F32),
+            jax.ShapeDtypeStruct((4, 1, 768), F32),
             shape,
             shape,
         ),
         scratch_shapes=[
-            pltpu.VMEM((2, 2, 768, 768), B16),
+            pltpu.VMEM((4, 2, 768, 768), B16),
             pltpu.VMEM((768, tokens), B16),
             pltpu.VMEM((768, tokens), B16),
-            pltpu.VMEM((2, 8, 2, 96, 768), B16),
-            pltpu.SemaphoreType.DMA((2, 8)),
-            pltpu.SemaphoreType.DMA((2, 8)),
+            pltpu.VMEM((4, 8, 2, 96, 768), B16),
+            pltpu.SemaphoreType.DMA((4, 8, 2)),
+            pltpu.SemaphoreType.DMA((4, 8, 2)),
         ],
         compiler_params=pltpu.CompilerParams(vmem_limit_bytes=VMEM_LIMIT),
-    )(meta, normed, cot, bias.reshape(4, 1, 768), *pieces, *held)
+    )(meta, normed, cot, bias.reshape(4, 1, 768), *pieces)
 
 
 def local(
@@ -763,10 +797,10 @@
     core = device % 2
     if fast:
         piece = pair_rows(meta, attn_qkv, attn_out)
-        piece, tokens, prompts, segments, prompt_slot_index = tie(
-            piece, tokens, prompts, segments, prompt_slot_index
+        held = z_stage(piece)
+        held, mlp_piece, tokens, prompts, segments, prompt_slot_index = tie(
+            held, mlp_weight, tokens, prompts, segments, prompt_slot_index
         )
-        held = z_stage(piece)
     table = jnp.concatenate([prompts, jnp.zeros((128 - NPROMPT, width), F32)], 0)
     start, normed_one, onehot, qf, kf = embed(
         tokens, prompt_slot_index, segments, table, jnp.stack([norm_gain[0], norm_shift[0]])
@@ -775,18 +809,17 @@
     out_params = jnp.stack([attn_bias[2], norm_gain[1], norm_shift[1]])
 
     if fast:
-        held, mlp_piece, x = tie(held, mlp_weight, (normed_one, start, qf, kf, onehot))
+        x = (normed_one, start, qf, kf, onehot)
         mlp_z = [mlp_piece] + [px(mlp_piece, 8 * k) for k in range(1, 4)]
         quad, mlp_z, x = tie(xy_stage(held), mlp_z, x)
+        normed_one, start, qf, kf, onehot = x
         own = assemble(meta, quad, "assemble")
-        own, mlp_z = tie(own, mlp_z)
-        other = px(own, 1)
-        stack_mlp = stack(mlp_z, "stack_z")
-        normed_one, start, qf, kf, onehot = x
+        s1, s2 = stack_pair(mlp_z)
+        own, s1, s2 = tie(own, s1, s2)
+        other, y1, x2 = px(own, 1), px(s1, 4), px(s2, 2)
+        s_other = [px(s1, 1), px(s2, 1)]
         qkv = project(meta, normed_one, own, bias, 0, ())
-        other, stack_mlp, qkv = tie(other, stack_mlp, qkv)
-        mlp_x, mlp_y = px(stack_mlp, 2), px(stack_mlp, 4)
-        stack_mlp_other = px(stack_mlp, 1)
+        other, qkv = tie(other, qkv)
     else:
         qkv_all = lax.all_gather(attn_qkv, AXES, axis=1, tiled=True)
         out_all = lax.all_gather(attn_out, AXES, axis=0, tiled=True)
@@ -797,94 +830,73 @@
         other = lax.dynamic_slice_in_dim(four_all, 384 * (1 - core), 384, 2)
         qkv = project(meta, normed_one, own, bias, 0, ())
     qkv = project(meta, normed_one, other, bias, 1, (qkv,))
+    if fast:
+        y1, x2, s_other, qkv = tie(y1, x2, s_other, qkv)
+        x1, xy1, y2, xy2 = px(s1, 2), px(y1, 2), px(s2, 4), px(x2, 4)
     mixed, lse = attention_forward(meta, qf, kf, qkv)
     if fast:
-        mlp_y, mlp_x, stack_mlp, mixed = tie(mlp_y, mlp_x, (stack_mlp, stack_mlp_other), mixed)
-        mlp_y_other, mlp_x_other, mlp_xy = px(mlp_y, 1), px(mlp_x, 1), px(stack_mlp[0], 6)
+        x1, xy1, y2, xy2, mixed = tie(x1, xy1, y2, xy2, mixed)
+        one = [px(v, 1) for v in (x1, y1, xy1)]
+        two = [px(v, 1) for v in (x2, y2, xy2)]
+        mlp_pieces = [s1, x1, y1, xy1, s2, x2, y2, xy2, s_other[0], *one, s_other[1], *two]
+    else:
+        mlp_pieces = [mlp_all]
     middle, normed_two, out_weight = out_projection(meta, mixed, start, own, other, out_params)
+    branch, grad_two, grad_up, own_mlp, other_mlp = mlp(meta, normed_two, cotangent, mlp_bias_up, mlp_pieces)
     if fast:
-        mlp_y_other, normed_two = tie(mlp_y_other, normed_two)
-        pieces_a = [stack_mlp[0], mlp_y, stack_mlp[1], mlp_y_other]
-        branch, grad_two, up_a, own_a, other_a = mlp(meta, normed_two, cotangent, mlp_bias_up, pieces_a, 0, ())
-        mlp_x, mlp_xy, other_a, branch, grad_two = tie(
-            (mlp_x, mlp_x_other), mlp_xy, other_a, branch, grad_two
-        )
-        pieces_b = [mlp_x[0], mlp_xy, mlp_x[1], px(mlp_xy, 1)]
-        got_a = px(other_a, 1)
-        branch, grad_two, up_b, own_b, other_b = mlp(
-            meta, normed_two, cotangent, mlp_bias_up, pieces_b, 2, (branch, grad_two)
-        )
-        other_b, got_a, grad_two, branch = tie(other_b, got_a, grad_two, branch)
-        got_b = px(other_b, 1)
-        up_rows = jnp.concatenate([up_a[:, 0], up_b[:, 0]])
-        spots = jnp.bitwise_xor(jnp.arange(4), device % 4)
-        grad_up = (jnp.arange(4)[:, None] == spots[None, :]).astype(F32)
-        grad_up = jnp.sum(grad_up[:, :, None] * up_rows[None], axis=1)
-    else:
-        branch, grad_two, up_a, own_a, other_a = mlp(meta, normed_two, cotangent, mlp_bias_up, [mlp_all], 0, ())
-        branch, grad_two, up_b, own_b, other_b = mlp(
-            meta, normed_two, cotangent, mlp_bias_up, [mlp_all], 2, (branch, grad_two)
-        )
-        grad_up = jnp.concatenate([up_a[:, 0], up_b[:, 0]])
+        other_mlp, grad_two, branch = tie(other_mlp, grad_two, branch)
+        got_mlp = px(other_mlp, 1)
     turn_params = jnp.stack([norm_gain[1], mlp_bias_down])
     output, grad_middle, grad_mixed, own_out, other_out, sums_two = turn(
         meta, middle, branch, grad_two, cotangent, mixed, out_weight, turn_params
     )
     if fast:
-        got_b, grad_mixed, other_out = tie(got_b, grad_mixed, other_out)
-        sum_a = add_parts(own_a, got_a)
-        sum_b = add_parts(own_b, got_b)
-        send_x = sum_b[:, :, 0].astype(B16)
-        send_y = jnp.stack([sum_a[1, :, 1], sum_b[1, :, 1]]).astype(B16)
-        send_x, send_y, grad_mixed, other_out = tie(send_x, send_y, grad_mixed, other_out)
-        got_x, got_y, got_out = px(send_x, 2), px(send_y, 4), px(other_out, 1)
+        got_mlp, grad_mixed, other_out = tie(got_mlp, grad_mixed, other_out)
+        send = [add_parts(own_mlp[c, 2:], got_mlp[c, 2:]).astype(B16) for c in range(2)]
+        send, grad_mixed, other_out = tie(send, grad_mixed, other_out)
+        got_1, got_2, got_out = px(send[0], 2), px(send[1], 4), px(other_out, 1)
     grads = attention_backward(meta, qf, kf, qkv, grad_mixed, mixed, lse)
     if fast:
-        got_x, got_y, got_out, grads, grad_middle = tie(got_x, got_y, got_out, grads, grad_middle)
-        first = add_parts(sum_a[:, :, 0], got_x)
-        second = [add_parts(sum_a[0, :, 1], got_y[0]), add_parts(sum_b[0, :, 1], got_y[1])]
-        send_x, send_y, grads = tie(second[1].astype(B16), first[1].astype(B16), grads)
-        got_x, got_y = px(send_x, 2), px(send_y, 4)
-        own_w, other_w = weight_grad(meta, normed_one, grads, "weight_grad_qkv")
-        other_w, got_x, got_y, grads, grad_middle = tie(other_w, got_x, got_y, grads, grad_middle)
-        got_w = px(other_w, 1)
-        col = [add_parts(first[0], got_y), add_parts(second[0], got_x)]
-        col_send = [jnp.stack([c[i].astype(B16) for c in col]) for i in range(1, 4)]
-        got_w, col_send, grads = tie(got_w, col_send, grads)
-        keep, *sends = gather_sums(own_w, got_w, own_out, got_out)
-        sends, col_send, grads, grad_middle = tie(sends, col_send, grads, grad_middle)
-        moved = [px(x, 2 * i + 2) for i, x in enumerate(sends)]
-        last_mlp = [px(x, 8 * i + 8) for i, x in enumerate(col_send)]
-    input_grad, prompt_sums, sums_one = tail_step(
-        meta, start, grad_middle, onehot, norm_gain[0:1], (own, other), grads
-    )
-
-    small = jnp.concatenate(
-        [
-            prompt_sums[:NPROMPT],
-            sums_one[0:1],
-            sums_two[0:1],
-            sums_one[1:2],
-            sums_two[1:2],
-            sums_one[2:4],
-            sums_two[2:4],
-            grad_up,
+        got_1, got_2, got_out, grads, grad_middle = tie(got_1, got_2, got_out, grads, grad_middle)
+        plane = [
+            add_parts(own_mlp[c, :2], got_mlp[c, :2]) + got.astype(F32) for c, got in enumerate((got_1, got_2))
         ]
+        send, grads = tie([p[1].astype(B16) for p in plane], grads)
+        got_1, got_2 = px(send[0], 4), px(send[1], 2)
+    input_grad, packed = tail_step(
+        meta, start, grad_middle, onehot, norm_gain[0:1], sums_two, grad_up, (own, other), grads
     )
     if fast:
-        packed = pack_small(small)
-        packed = pack_small(open_small(packed) + open_small(px(packed, 1)))
-        packed = pack_small(open_small(packed) + open_small(px(packed, 2)))
-        packed = pack_small(open_small(packed) + open_small(px(packed, 4)))
-        moved, packed = tie(moved, packed)
+        packed, grads, got_1, got_2 = tie(packed, grads, got_1, got_2)
+        got_small = px(packed, 1)
+        own_w, other_w = weight_grad(meta, normed_one, grads, "weight_grad_qkv")
+        got_small, other_w = tie(got_small, other_w)
+        got_w = px(other_w, 1)
+        packed = pack_small(add_small(packed, got_small))
+        got_small = px(packed, 2)
+        got_w, got_small, packed = tie(got_w, got_small, packed)
+        packed = pack_small(add_small(packed, got_small))
+        got_small = px(packed, 4)
+        col = [add_parts(plane[0][0], got_1), add_parts(plane[1][0], got_2)]
+        send = jnp.stack([c[2:].astype(B16) for c in col])
+        keep, *sends = gather_sums(own_w, got_w, own_out, got_out)
+        send, sends, got_small, packed = tie(send, sends, got_small, packed)
+        got_far = px(send, 16)
+        moved = [px(x, 2 * i + 2) for i, x in enumerate(sends)]
+        packed = pack_small(add_small(packed, got_small))
+        got_small = px(packed, 8)
+        moved, got_far, got_small, packed = tie(moved, got_far, got_small, packed)
         col_attn, *last = plane_sums(keep, moved)
+        near = [add_parts(col[c][:2], got_far[c]) for c in range(2)]
+        send = jnp.stack([x[1].astype(B16) for x in near])
+        last, send = tie(last, send)
         last = [px(x, 8 * i + 8) for i, x in enumerate(last)]
-        small = four([open_small(x) for x in [packed] + [px(packed, 8 * i) for i in range(1, 4)]])
-        mine = jnp.stack([c[0] for c in col])
-        mlp_grad = four([mine] + [x.astype(F32) for x in last_mlp])
+        got_near = px(send, 8)
+        small = exchange_small(pack_small(add_small(packed, got_small)), 16)
+        mlp_grad = jnp.stack([x[0] for x in near]) + got_near.astype(F32)
         qkv_grad, out_grad = line_sums(col_attn, last)
     else:
-        mlp_grad = jnp.stack([own_a, other_a, own_b, other_b]).transpose(3, 2, 1, 4, 0, 5)
+        mlp_grad = own_mlp.transpose(2, 1, 3, 0, 4)
         mlp_grad = mlp_grad.reshape(2, 768, 3072)
         mlp_grad = lax.psum_scatter(mlp_grad, "dp", scatter_dimension=1, tiled=True)
         mlp_grad = lax.psum_scatter(mlp_grad, "mp", scatter_dimension=2, tiled=True).astype(F32)
@@ -892,20 +904,20 @@
         grad_qkv = jnp.stack([dotf(normed_one, g, TN) for g in grads])
         qkv_grad = lax.psum_scatter(grad_qkv, AXES, scatter_dimension=1, tiled=True)
         out_grad = lax.psum_scatter(grad_out_weight, AXES, scatter_dimension=0, tiled=True)
-        small = lax.psum(small, AXES)
-    at = NPROMPT
+        x = packed.astype(F32)
+        small = lax.psum(jnp.concatenate([x[:64], x[64:80] + x[80:]]), AXES)
     return (
-        output.astype(B16),
+        output,
         input_grad,
-        small[:at],
-        small[at : at + 2],
-        small[at + 2 : at + 4],
+        small[:NPROMPT],
+        small[64:66],
+        small[66:68],
         qkv_grad,
-        small[at + 4 : at + 7],
+        small[68:71],
         out_grad,
         mlp_grad,
-        small[at + 8 :].reshape(-1),
-        small[at + 7],
+        small[72:76].reshape(-1),
+        small[71],
     )
 
 

time: 351 us -> 325 us (0.926)
  Pallas kernels: 188 us -> 178 us
  local copies, waits for them, and re-layouts: 27.7 us -> 20.1 us
  other arithmetic: 19.8 us -> 13.5 us
  waiting for transfers between devices: 71.1 us -> 66.1 us
    another operation x7 -> x2, other arithmetic: 7.73 us -> 0.09 us  [the longest x1 0.06 us: local(): send = jnp.stack([c[2:].astype(B16) for c in col])]
    pallas_call x7, Pallas kernels: 99.3 us -> 93.5 us  [the longest x1 46.4 us: mlp(): pl.pallas_call(partial(mlp_kernel, fast), name='mlp', grid=(4 * PER,), in...]
    ppermute x41 -> x45, waiting for transfers between devices: 71.1 us -> 66.1 us  [px(): return lax.ppermute(x, AXES, [(i, i ^ k) for i in range(32)])]
    add x15 -> x4, other arithmetic: 1.29 us -> 5.13 us  [the longest x1 3.57 us: local(): add_parts(own_mlp[c, :2], got_mlp[c, :2]) + got.astype(F32)]
    ppermute x41 -> x45, starting transfers between devices: 39.7 us -> 42.9 us  [px(): return lax.ppermute(x, AXES, [(i, i ^ k) for i in range(32)])]
    unnamed x72 -> x82, local copies, waits for them, and re-layouts: 8.84 us -> 9.81 us
  transfers between devices with their start and end apart: 41 -> 45, of which waited for: 14 -> 14; matrix products, arithmetic and copies ran while one was open for 7% -> 5% of each run, Pallas kernels for 46% -> 38%
where the time goes in v3:
time: 325 us; the launch traced here: 322 us
  Pallas kernels  178 us (55%)
  waiting for transfers between devices  66.1 us (20%)
  starting transfers between devices  42.9 us (13%)
  local copies, waits for them, and re-layouts  20.1 us (6%)
  other arithmetic  13.5 us (4%)
    ppermute x45, waiting for transfers between devices, px(): return lax.ppermute(x, AXES, [(i, i ^ k) for i in range(32)])  66.1 us
    pallas_call x1, Pallas kernels, mlp(): pl.pallas_call(partial(mlp_kernel, fast), name='mlp', grid=(4 * PER,), in...  46.4 us
    ppermute x45, starting transfers between devices, px(): return lax.ppermute(x, AXES, [(i, i ^ k) for i in range(32)])  42.9 us
    pallas_call x1, Pallas kernels, attention_backward(): pl.pallas_call(kernel, name='attention_backward', grid_spec=pltpu.Prefetc...  32 us
    pallas_call x1, Pallas kernels, attention_forward(): pl.pallas_call(kernel, name='attention_forward', grid_spec=pltpu.Prefetch...  21.1 us
    pallas_call x1, Pallas kernels, tail_step(): pl.pallas_call(tail_kernel, name='tail_step', grid=(rows // STEP,), in_sp...  14.7 us
    pallas_call x2, Pallas kernels, project(): pl.pallas_call(partial(project_kernel, side), name='project', grid=(3,),...  11.8 us
    pallas_call x1, Pallas kernels, turn(): pl.pallas_call(turn_kernel, name='turn', grid=(rows // STEP,), in_specs=[...  11.2 us
  transfers between devices with their start and end apart: 45, of which 14 were waited for; matrix products, arithmetic and copies ran while one was open for 5% of the time, Pallas kernels for 38%

profile of v3, /device:TPU:16, one launch (start us, length us, event | category | flops | bytes accessed | tf_op | source)
XLA Modules:
  0.0 322.2 jit_solution(14702748663493973477)
XLA Ops:
  0.7 1.6 split.1
  2.3 1.5 collective-permute-done.got_ref
  4.4 1.6 join.1.refs_0_
  6.4 3.5 %collective-permute-start.2 = (bf16[4,48,384]{2,1,0:T(8,128)(2,1)}, bf16[4,48,384]{2,1,0:T(8,128)(2,1)S(1)}, u32[]{:S(2)}, u32[]{:S(2)}) collective-permute-start(bf16[4,48,384]{2,1,0:T(8,128)(2,1)} %join.1.refs_0_), channel_id=1, source_target_pairs={{0,16},{1,17},{2,18},{3,19},{4,20},{5,21},{6,22},{7,23},{8,24},{9,... | collective-permute-start | bytes 442376 | tf_op jit(solution)/shard_map/ppermute | solution.py:52
  9.9 9.3 %collective-permute-done.3.refs_3_ = bf16[4,48,384]{2,1,0:T(8,128)(2,1)S(1)} collective-permute-done((bf16[4,48,384]{2,1,0:T(8,128)(2,1)}, bf16[4,48,384]{2,1,0:T(8,128)(2,1)S(1)}, u32[]{:S(2)}, u32[]{:S(2)}) %collective-permute-start.3) | collective-permute-done | bytes 147488 | tf_op jit(solution)/shard_map/ppermute | solution.py:52
  21.0 2.0 stack_z.1.refs_0_
  23.0 1.6 collective-permute-start.9
  24.5 2.4 collective-permute-start.6
  28.7 0.8 fusion.22
  29.5 4.2 %collective-permute-start.8 = (bf16[2,96,768]{2,1,0:T(8,128)(2,1)}, bf16[2,96,768]{2,1,0:T(8,128)(2,1)S(1)}, u32[]{:S(2)}, u32[]{:S(2)}) collective-permute-start(bf16[2,96,768]{2,1,0:T(8,128)(2,1)} %refs_0_), channel_id=1, source_target_pairs={{0,16},{1,17},{2,18},{3,19},{4,20},{5,21},{6,22},{7,23},{8,24},{9,... | collective-permute-start | bytes 884744 | tf_op jit(solution)/shard_map/ppermute | solution.py:52
  33.8 11.9 %collective-permute-done.9.refs_3_ = bf16[2,96,768]{2,1,0:T(8,128)(2,1)S(1)} collective-permute-done((bf16[2,96,768]{2,1,0:T(8,128)(2,1)}, bf16[2,96,768]{2,1,0:T(8,128)(2,1)S(1)}, u32[]{:S(2)}, u32[]{:S(2)}) %collective-permute-start.9) | collective-permute-done | bytes 294944 | tf_op jit(solution)/shard_map/ppermute | solution.py:52
  45.7 1.4 fusion.23
  47.7 1.7 copy.25.slots_ref
  49.4 1.0 copy.26.segs_ref
  50.4 0.8 concatenate.15.table_ref
  51.2 5.8 %embed.1 = (f32[1024,768]{1,0:T(8,128)}, bf16[1024,768]{1,0:T(8,128)(2,1)}, bf16[1024,128]{1,0:T(8,128)(2,1)}, bf16[1024,128]{1,0:T(8,128)(2,1)}, bf16[1024,128]{1,0:T(8,128)(2,1)}) custom-call(bf16[1024,768]{1,0:T(8,128)(2,1)} %tokens_ref, s32[1024,1]{1,0:T(8,128)} %copy.25.slots_ref, s32[1024,1]{1,0:T(8,128)} %copy.26.segs_ref, ...), custom_call_target="tpu_custom_call" | custom-call | tf_op jit(solution)/shard_map/embed/pallas_call | solution.py:215
  57.1 0.8 copy-done.7
  58.4 3.3 %assemble.1.w_ref.own_ref.refs_0_ = bf16[4,768,384]{2,1,0:T(8,128)(2,1)} custom-call(s32[1]{0:T(128)} %bitcast.meta.refs_0_, bf16[4,4,48,384]{3,2,1,0:T(8,128)(2,1)} %stack_z.1.refs_0_, bf16[4,4,48,384]{3,2,1,0:T(8,128)(2,1)} %copy-done.9, bf16[4,4,48,384]{3,2,1,0:T(8,128)(2,1)} %copy-done.8, bf16[4,4,48,384]{3,2,1,0:T(8,128)(2,1)} %copy-done.7), custom_call_target="tpu_custom_call" | custom-call | tf_op jit(solution)/shard_map/assemble/pallas_call | solution.py:149
  61.8 2.3 stack_pair.1
  64.6 1.5 collective-permute-start.11
  66.1 1.5 collective-permute-start.12
  68.9 5.9 %project.2.refs_0_ = bf16[1024,2304]{1,0:T(8,128)(2,1)} custom-call(s32[1]{0:T(128)} %bitcast.meta.refs_0_, bf16[1024,768]{1,0:T(8,128)(2,1)} %get-tuple-element.161.x_ref.left_ref, bf16[4,768,384]{2,1,0:T(8,128)(2,1)} %assemble.1.w_ref.own_ref.refs_0_, f32[3,1,768]{2,1,0:T(1,128)} %broadcast_in_dim.12.b_ref), custom_call_target="tpu_custom_call" | custom-call | tf_op jit(solution)/shard_map/project/pallas_call | solution.py:169
  75.5 0.8 copy-done
  76.2 5.9 %project.3.refs_2_.refs_3_.refs_4_ = bf16[1024,2304]{1,0:T(8,128)(2,1)} custom-call(s32[1]{0:T(128)} %bitcast.meta.refs_0_, bf16[1024,768]{1,0:T(8,128)(2,1)} %get-tuple-element.161.x_ref.left_ref, bf16[4,768,384]{2,1,0:T(8,128)(2,1)} %copy-done, f32[3,1,768]{2,1,0:T(1,128)} %broadcast_in_dim.12.b_ref, ...), custom_call_target="tpu_custom_call", output_to_operand_aliasing={{}: (4, {})} | custom-call | tf_op jit(solution)/shard_map/project/pallas_call | solution.py:169
  82.7 1.4 collective-permute-start.16
  84.1 0.9 collective-permute-start.18
  85.0 21.1 %attention_forward.1 = (bf16[1024,768]{1,0:T(8,128)(2,1)}, f32[1024,768]{1,0:T(8,128)}) custom-call(s32[1]{0:T(128)} %bitcast.meta.refs_0_, bf16[1024,128]{1,0:T(8,128)(2,1)} %get-tuple-element.167.refs_0_, bf16[1024,128]{1,0:T(8,128)(2,1)} %get-tuple-element.168.refs_1_, bf16[1024,2304]{1,0:T(8,128)(2,1)} %project.3.refs_2_.refs_3_.refs_4_, ...), custom_call_target="tpu_custom_call" | custom-call | tf_op jit(solution)/shard_map/attention_forward/pallas_call | solution.py:570
  107.3 3.0 collective-permute-done.18.refs_11_
  111.3 1.3 pad_maximum_fusion.7.p_ref
  112.7 7.1 %out_projection.1 = (f32[1024,768]{1,0:T(8,128)}, bf16[1024,768]{1,0:T(8,128)(2,1)}, bf16[768,768]{1,0:T(8,128)(2,1)}) custom-call(s32[1]{0:T(128)} %bitcast.meta.refs_0_, bf16[1024,768]{1,0:T(8,128)(2,1)} %get-tuple-element.171.x_ref.mixed_ref.refs_6_, f32[1024,768]{1,0:T(8,128)} %get-tuple-element.172.start_ref, ...), custom_call_target="tpu_custom_call" | custom-call | tf_op jit(solution)/shard_map/out_projection/pallas_call | solution.py:331
  119.9 0.8 copy-done.20
  121.0 46.4 %mlp.1 = (f32[1024,768]{1,0:T(8,128)}, f32[1024,768]{1,0:T(8,128)}, f32[4,1,768]{2,1,0:T(1,128)}, bf16[2,4,4,96,768]{4,3,2,1,0:T(8,128)(2,1)}, bf16[2,4,4,96,768]{4,3,2,1,0:T(8,128)(2,1)}) custom-call(s32[1]{0:T(128)} %bitcast.meta.refs_0_, bf16[1024,768]{1,0:T(8,128)(2,1)} %get-tuple-element.174.refs_1_, bf16[1024,768]{1,0:T(8,128)(2,1)} %cot_ref.1, ...), custom_call_target="tpu_custom_call" | custom-call | tf_op jit(solution)/shard_map/mlp/pallas_call | solution.py:753
  167.7 11.2 %turn.1 = (bf16[1024,768]{1,0:T(8,128)(2,1)}, f32[1024,768]{1,0:T(8,128)}, bf16[1024,768]{1,0:T(8,128)(2,1)}, bf16[4,4,1,24,768]{4,3,2,1,0:T(8,128)(2,1)}, bf16[...) custom-call(s32[1]{0:T(128)} %bitcast.meta.refs_0_, f32[1024,768]{1,0:T(8,128)} %get-tuple-element.173.middle_ref, ...), custom_call_target="tpu_custom_call" | custom-call | tf_op jit(solution)/shard_map/turn/pallas_call | solution.py:397
  178.8 4.1 %fusion.1 = (bf16[2,4,96,768]{3,2,1,0:T(8,128)(2,1)S(1)}, bf16[2,4,96,768]{3,2,1,0:T(8,128)(2,1)}) fusion(bf16[2,4,4,96,768]{4,3,2,1,0:T(8,128)(2,1)} %collective-permute-done.25, bf16[2,4,4,96,768]{4,3,2,1,0:T(8,128)(2,1)} %get-tuple-element.188), kind=kLoop, calls=%fused_computation.5 | loop fusion | flops 4718592 | bytes 7077888 | tf_op jit(solution)/shard_map/convert_element_type | solution.py:855
  183.9 32.0 %attention_backward.1 = (bf16[1024,768]{1,0:T(8,128)(2,1)}, bf16[1024,768]{1,0:T(8,128)(2,1)}, bf16[1024,768]{1,0:T(8,128)(2,1)}) custom-call(s32[1]{0:T(128)} %bitcast.meta.refs_0_, bf16[1024,128]{1,0:T(8,128)(2,1)} %get-tuple-element.167.refs_0_, bf16[1024,128]{1,0:T(8,128)(2,1)} %get-tuple-element.168.refs_1_, ...), custom_call_target="tpu_custom_call" | custom-call | tf_op jit(solution)/shard_map/attention_backward/pallas_call | solution.py:645
  216.0 1.1 copy-done.5
  217.0 3.6 %bitcast_add_fusion = (f32[2,4,96,768]{3,2,1,0:T(8,128)S(1)}, f32[2,4,96,768]{3,2,1,0:T(8,128)S(1)}) fusion(bf16[2,4,96,768]{3,2,1,0:T(8,128)(2,1)} %copy-done.5, bf16[2,4,4,96,768]{4,3,2,1,0:T(8,128)(2,1)} %collective-permute-done.25, bf16[2,4,4,96,768]{4,3,2,1,0:T(8,128)(2,1)} %get-tuple-element.188, bf16[2,4,96,768]{3,2,1,0:T(8,128)(2,1)S(1)} %collective-permute-done.26), kind=kLoop, calls=%fused_computation | loop fusion | flops 5898240 | bytes 11796480 | tf_op jit(solution)/shard_map/add | solution.py:862
  220.6 1.4 copy-done.1
  222.2 1.6 collective-permute-start.29
  223.8 1.5 collective-permute-start.30
  225.3 14.7 %tail_step.1 = (f32[1024,768]{1,0:T(8,128)}, bf16[96,768]{1,0:T(8,128)(2,1)}) custom-call(s32[1]{0:T(128)} %bitcast.meta.refs_0_, f32[1024,768]{1,0:T(8,128)} %get-tuple-element.172.start_ref, f32[1024,768]{1,0:T(8,128)} %get-tuple-element.204.gmiddle_ref, bf16[1024,128]{1,0:T(8,128)(2,1)} %get-tuple-element.205.slots_ref, f32[1,768]{1,0:T(1,128)} %copy-done.37, ...), custom_call_target="tpu_custom_call" | custom-call | tf_op jit(solution)/shard_map/tail_step/pallas_call | solution.py:463
  240.1 8.8 %weight_grad_qkv.1 = (bf16[4,4,3,24,768]{4,3,2,1,0:T(8,128)(2,1)}, bf16[4,4,3,24,768]{4,3,2,1,0:T(8,128)(2,1)}) custom-call(s32[1]{0:T(128)} %bitcast.meta.refs_0_, bf16[1024,768]{1,0:T(8,128)(2,1)} %get-tuple-element.161.x_ref.left_ref, bf16[1024,768]{1,0:T(8,128)(2,1)} %get-tuple-element.222.refs_2_.refs_0_, ...), custom_call_target="tpu_custom_call" | custom-call | tf_op jit(solution)/shard_map/weight_grad_qkv/pallas_call | solution.py:492
  249.6 1.5 fusion.2
  251.3 0.8 copy-done.32
  252.2 0.9 collective-permute-start.33
  253.1 5.4 %collective-permute-done.33 = bf16[96,768]{1,0:T(8,128)(2,1)S(1)} collective-permute-done((bf16[96,768]{1,0:T(8,128)(2,1)S(1)}, bf16[96,768]{1,0:T(8,128)(2,1)S(1)}, u32[]{:S(2)}, u32[]{:S(2)}) %collective-permute-start.33) | collective-permute-done | bytes 147488 | tf_op jit(solution)/shard_map/ppermute | solution.py:52
  259.7 4.1 %gather_sums.1 = (f32[4,4,24,768]{3,2,1,0:T(8,128)}, bf16[4,4,24,768]{3,2,1,0:T(8,128)(2,1)}, bf16[4,4,24,768]{3,2,1,0:T(8,128)(2,1)}, bf16[4,4,24,768]{3,2,1,0:T(8,128)(2,1)}) custom-call(bf16[4,4,3,24,768]{4,3,2,1,0:T(8,128)(2,1)} %get-tuple-element.225.own_ref, bf16[4,4,3,24,768]{4,3,2,1,0:T(8,128)(2,1)} %copy-done.4, ...), custom_call_target="tpu_custom_call" | custom-call | tf_op jit(solution)/shard_map/gather_sums/pallas_call | solution.py:248
  264.0 0.9 collective-permute-start.35
  264.9 0.8 collective-permute-start.36
  265.8 1.8 collective-permute-start.37
  267.6 3.0 collective-permute-start.38
  270.8 14.7 %collective-permute-done.39 = bf16[96,768]{1,0:T(8,128)(2,1)S(1)} collective-permute-done((bf16[96,768]{1,0:T(8,128)(2,1)S(1)}, bf16[96,768]{1,0:T(8,128)(2,1)S(1)}, u32[]{:S(2)}, u32[]{:S(2)}) %collective-permute-start.39) | collective-permute-done | bytes 147488 | tf_op jit(solution)/shard_map/ppermute | solution.py:52
  285.5 6.5 %collective-permute-done.36.refs_1_ = bf16[4,4,24,768]{3,2,1,0:T(8,128)(2,1)S(1)} collective-permute-done((bf16[4,4,24,768]{3,2,1,0:T(8,128)(2,1)}, bf16[4,4,24,768]{3,2,1,0:T(8,128)(2,1)S(1)}, u32[]{:S(2)}, u32[]{:S(2)}) %collective-permute-start.36) | collective-permute-done | bytes 589856 | tf_op jit(solution)/shard_map/ppermute | solution.py:52
  292.0 1.9 collective-permute-done.38
  294.1 3.4 %collective-permute-start.40 = (bf16[96,768]{1,0:T(8,128)(2,1)S(1)}, bf16[96,768]{1,0:T(8,128)(2,1)S(1)}, u32[]{:S(2)}, u32[]{:S(2)}) collective-permute-start(bf16[96,768]{1,0:T(8,128)(2,1)S(1)} %get-tuple-element.276), channel_id=1, source_target_pairs={{0,16},{1,17},{2,18},{3,19},{4,20},{5,21},{6,22},{7,23},{8,24},{9,... | collective-permute-start | bytes 442376 | tf_op jit(solution)/shard_map/ppermute | solution.py:52
  297.8 2.7 plane_sums.1
  300.6 2.3 collective-permute-start.42
  302.9 1.2 collective-permute-start.43
  304.1 1.0 collective-permute-start.44
  307.1 2.9 collective-permute-done.41.refs_0_
  309.9 3.6 %collective-permute-done.42.refs_1_ = bf16[4,24,768]{2,1,0:T(8,128)(2,1)S(1)} collective-permute-done((bf16[4,24,768]{2,1,0:T(8,128)(2,1)}, bf16[4,24,768]{2,1,0:T(8,128)(2,1)S(1)}, u32[]{:S(2)}, u32[]{:S(2)}) %collective-permute-start.42) | collective-permute-done | bytes 147488 | tf_op jit(solution)/shard_map/ppermute | solution.py:52
  313.6 3.9 %collective-permute-done.43.refs_2_ = bf16[4,24,768]{2,1,0:T(8,128)(2,1)S(1)} collective-permute-done((bf16[4,24,768]{2,1,0:T(8,128)(2,1)}, bf16[4,24,768]{2,1,0:T(8,128)(2,1)S(1)}, u32[]{:S(2)}, u32[]{:S(2)}) %collective-permute-start.43) | collective-permute-done | bytes 147488 | tf_op jit(solution)/shard_map/ppermute | solution.py:52
  318.1 1.9 line_sums.1
  321.3 0.9 maximum_add_fusion
  (185 shorter events, 19.8 us)
Async XLA Ops:
  0.6 48.7 %copy-start.40 = (s32[1024]{0:T(1024)S(1)}, s32[1024]{0:T(1024)}, u32[]{:S(2)}) copy-start(s32[1024]{0:T(1024)} %param.16) | copy-start | bytes 12292
  0.7 49.8 %copy-start.26 = (f32[50,768]{1,0:T(8,128)S(1)}, f32[50,768]{1,0:T(8,128)}, u32[]{:S(2)}) copy-start(f32[50,768]{1,0:T(8,128)} %param.15) | copy-start | bytes 460804
  2.3 1.5 collective-permute-start
  6.0 13.2 %collective-permute-start.3 = (bf16[4,48,384]{2,1,0:T(8,128)(2,1)}, bf16[4,48,384]{2,1,0:T(8,128)(2,1)S(1)}, u32[]{:S(2)}, u32[]{:S(2)}) collective-permute-start(bf16[4,48,384]{2,1,0:T(8,128)(2,1)} %join.1.refs_0_), channel_id=1, source_target_pairs={{0,24},{1,25},{2,26},{3,27},{4,28},{5,29},{6,30},{7,31},{8,16},{9,... | collective-permute-start | bytes 442376 | tf_op jit(solution)/shard_map/ppermute | solution.py:52
  6.4 13.2 %collective-permute-start.2 = (bf16[4,48,384]{2,1,0:T(8,128)(2,1)}, bf16[4,48,384]{2,1,0:T(8,128)(2,1)S(1)}, u32[]{:S(2)}, u32[]{:S(2)}) collective-permute-start(bf16[4,48,384]{2,1,0:T(8,128)(2,1)} %join.1.refs_0_), channel_id=1, source_target_pairs={{0,16},{1,17},{2,18},{3,19},{4,20},{5,21},{6,22},{7,23},{8,24},{9,... | collective-permute-start | bytes 442376 | tf_op jit(solution)/shard_map/ppermute | solution.py:52
  9.9 9.7 %collective-permute-start.1 = (bf16[4,48,384]{2,1,0:T(8,128)(2,1)}, bf16[4,48,384]{2,1,0:T(8,128)(2,1)S(1)}, u32[]{:S(2)}, u32[]{:S(2)}) collective-permute-start(bf16[4,48,384]{2,1,0:T(8,128)(2,1)} %join.1.refs_0_), channel_id=1, source_target_pairs={{0,8},{1,9},{2,10},{3,11},{4,12},{5,13},{6,14},{7,15},{8,0},{9,1},... | collective-permute-start | bytes 442376 | tf_op jit(solution)/shard_map/ppermute | solution.py:52
  23.0 22.7 %collective-permute-start.9 = (bf16[2,96,768]{2,1,0:T(8,128)(2,1)}, bf16[2,96,768]{2,1,0:T(8,128)(2,1)S(1)}, u32[]{:S(2)}, u32[]{:S(2)}) collective-permute-start(bf16[2,96,768]{2,1,0:T(8,128)(2,1)} %refs_0_), channel_id=1, source_target_pairs={{0,24},{1,25},{2,26},{3,27},{4,28},{5,29},{6,30},{7,31},{8,16},{9,... | collective-permute-start | bytes 884744 | tf_op jit(solution)/shard_map/ppermute | solution.py:52
  24.5 32.5 %collective-permute-start.6 = (bf16[4,4,48,384]{3,2,1,0:T(8,128)(2,1)}, bf16[4,4,48,384]{3,2,1,0:T(8,128)(2,1)S(1)}, u32[]{:S(2)}, u32[]{:S(2)}) collective-permute-start(bf16[4,4,48,384]{3,2,1,0:T(8,128)(2,1)} %stack_z.1.refs_0_), channel_id=1, source_target_pairs={{0,6},{1,7},{2,4},{3,5},{4,2},{5,3},{6,0},{7,1},{8,14},{9,15},{10,... | collective-permute-start | bytes 1769480 | tf_op jit(solution)/shard_map/ppermute | solution.py:52
  27.0 30.1 %collective-permute-start.5 = (bf16[4,4,48,384]{3,2,1,0:T(8,128)(2,1)}, bf16[4,4,48,384]{3,2,1,0:T(8,128)(2,1)S(1)}, u32[]{:S(2)}, u32[]{:S(2)}) collective-permute-start(bf16[4,4,48,384]{3,2,1,0:T(8,128)(2,1)} %stack_z.1.refs_0_), channel_id=1, source_target_pairs={{0,4},{1,5},{2,6},{3,7},{4,0},{5,1},{6,2},{7,3},{8,12},{9,13},{10,... | collective-permute-start | bytes 1769480 | tf_op jit(solution)/shard_map/ppermute | solution.py:52
  27.5 29.6 %collective-permute-start.4 = (bf16[4,4,48,384]{3,2,1,0:T(8,128)(2,1)}, bf16[4,4,48,384]{3,2,1,0:T(8,128)(2,1)S(1)}, u32[]{:S(2)}, u32[]{:S(2)}) collective-permute-start(bf16[4,4,48,384]{3,2,1,0:T(8,128)(2,1)} %stack_z.1.refs_0_), channel_id=1, source_target_pairs={{0,2},{1,3},{2,0},{3,1},{4,6},{5,7},{6,4},{7,5},{8,10},{9,11},{10,... | collective-permute-start | bytes 1769480 | tf_op jit(solution)/shard_map/ppermute | solution.py:52
  29.5 17.6 %copy-start.37 = (f32[1,768]{1,0:T(1,128)}, f32[1,768]{1,0:T(1,128)S(1)}, u32[]{:S(2)}) copy-start(f32[1,768]{1,0:T(1,128)S(1)} %get-tuple-element.283.p_ref) | copy-start | bytes 9220
  29.5 18.2 %copy-start.38 = (f32[1,768]{1,0:T(1,128)}, f32[1,768]{1,0:T(1,128)S(1)}, u32[]{:S(2)}) copy-start(f32[1,768]{1,0:T(1,128)S(1)} %get-tuple-element.282) | copy-start | bytes 9220
  29.5 27.5 %collective-permute-start.8 = (bf16[2,96,768]{2,1,0:T(8,128)(2,1)}, bf16[2,96,768]{2,1,0:T(8,128)(2,1)S(1)}, u32[]{:S(2)}, u32[]{:S(2)}) collective-permute-start(bf16[2,96,768]{2,1,0:T(8,128)(2,1)} %refs_0_), channel_id=1, source_target_pairs={{0,16},{1,17},{2,18},{3,19},{4,20},{5,21},{6,22},{7,23},{8,24},{9,... | collective-permute-start | bytes 884744 | tf_op jit(solution)/shard_map/ppermute | solution.py:52
  45.7 11.3 %copy-start.23 = (bf16[2,96,768]{2,1,0:T(8,128)(2,1)}, bf16[2,96,768]{2,1,0:T(8,128)(2,1)S(1)}, u32[]{:S(2)}) copy-start(bf16[2,96,768]{2,1,0:T(8,128)(2,1)S(1)} %collective-permute-done.9.refs_3_) | copy-start | bytes 884740
  45.7 11.4 %collective-permute-start.7 = (bf16[2,96,768]{2,1,0:T(8,128)(2,1)}, bf16[2,96,768]{2,1,0:T(8,128)(2,1)S(1)}, u32[]{:S(2)}, u32[]{:S(2)}) collective-permute-start(bf16[2,96,768]{2,1,0:T(8,128)(2,1)} %refs_0_), channel_id=1, source_target_pairs={{0,8},{1,9},{2,10},{3,11},{4,12},{5,13},{6,14},{7,15},{8,0},{9,1},... | collective-permute-start | bytes 884744 | tf_op jit(solution)/shard_map/ppermute | solution.py:52
  58.4 9.2 %copy-start.39 = (f32[3,768]{1,0:T(4,128)S(1)}, f32[3,768]{1,0:T(4,128)}, u32[]{:S(2)}) copy-start(f32[3,768]{1,0:T(4,128)} %param.21) | copy-start | bytes 27652
  64.1 10.8 %collective-permute-start.15 = (bf16[4,768,384]{2,1,0:T(8,128)(2,1)}, bf16[4,768,384]{2,1,0:T(8,128)(2,1)S(1)}, u32[]{:S(2)}, u32[]{:S(2)}) collective-permute-start(bf16[4,768,384]{2,1,0:T(8,128)(2,1)} %assemble.1.w_ref.own_ref.refs_0_), channel_id=1, source_target_pairs={{0,1},{1,0},{2,3},{3,2},{4,5},{5,4},{6,7},{7,6},{8,9},{9,8},{10,11... | collective-permute-start | bytes 7077896 | tf_op jit(solution)/shard_map/ppermute | solution.py:52
  64.1 18.1 %collective-permute-start.13 = (bf16[4,96,768]{2,1,0:T(8,128)(2,1)}, bf16[4,96,768]{2,1,0:T(8,128)(2,1)S(1)}, u32[]{:S(2)}, u32[]{:S(2)}) collective-permute-start(bf16[4,96,768]{2,1,0:T(8,128)(2,1)} %get-tuple-element.159.refs_4_), channel_id=1, source_target_pairs={{0,1},{1,0},{2,3},{3,2},{4,5},{5,4},{6,7},{7,6},{8,9},{9,8},{10,11... | collective-permute-start | bytes 1769480 | tf_op jit(solution)/shard_map/ppermute | solution.py:52
  64.6 18.1 %collective-permute-start.11 = (bf16[4,96,768]{2,1,0:T(8,128)(2,1)}, bf16[4,96,768]{2,1,0:T(8,128)(2,1)}, u32[]{:S(2)}, u32[]{:S(2)}) collective-permute-start(bf16[4,96,768]{2,1,0:T(8,128)(2,1)} %get-tuple-element.159.refs_4_), channel_id=1, source_target_pairs={{0,4},{1,5},{2,6},{3,7},{4,0},{5,1},{6,2},{7,3},{8,12},{9,13},{10,... | collective-permute-start | bytes 1769480 | tf_op jit(solution)/shard_map/ppermute | solution.py:52
  66.1 16.6 %collective-permute-start.14 = (bf16[4,96,768]{2,1,0:T(8,128)(2,1)}, bf16[4,96,768]{2,1,0:T(8,128)(2,1)}, u32[]{:S(2)}, u32[]{:S(2)}) collective-permute-start(bf16[4,96,768]{2,1,0:T(8,128)(2,1)} %get-tuple-element.160.refs_8_), channel_id=1, source_target_pairs={{0,1},{1,0},{2,3},{3,2},{4,5},{5,4},{6,7},{7,6},{8,9},{9,8},{10,11... | collective-permute-start | bytes 1769480 | tf_op jit(solution)/shard_map/ppermute | solution.py:52
  66.1 16.6 %collective-permute-start.12 = (bf16[4,96,768]{2,1,0:T(8,128)(2,1)}, bf16[4,96,768]{2,1,0:T(8,128)(2,1)}, u32[]{:S(2)}, u32[]{:S(2)}) collective-permute-start(bf16[4,96,768]{2,1,0:T(8,128)(2,1)} %get-tuple-element.160.refs_8_), channel_id=1, source_target_pairs={{0,2},{1,3},{2,0},{3,1},{4,6},{5,7},{6,4},{7,5},{8,10},{9,11},{10,... | collective-permute-start | bytes 1769480 | tf_op jit(solution)/shard_map/ppermute | solution.py:52
  68.9 5.9 %copy-start.13 = (bf16[4,96,768]{2,1,0:T(8,128)(2,1)S(1)}, bf16[4,96,768]{2,1,0:T(8,128)(2,1)}, u32[]{:S(2)}) copy-start(bf16[4,96,768]{2,1,0:T(8,128)(2,1)} %get-tuple-element.159.refs_4_) | copy-start | bytes 1769476
  74.8 7.3 %copy-start.14 = (bf16[4,96,768]{2,1,0:T(8,128)(2,1)S(1)}, bf16[4,96,768]{2,1,0:T(8,128)(2,1)}, u32[]{:S(2)}) copy-start(bf16[4,96,768]{2,1,0:T(8,128)(2,1)} %get-tuple-element.160.refs_8_) | copy-start | bytes 1769476
  74.9 31.2 %collective-permute-start.10 = (bf16[4,96,768]{2,1,0:T(8,128)(2,1)S(1)}, bf16[4,96,768]{2,1,0:T(8,128)(2,1)}, u32[]{:S(2)}, u32[]{:S(2)}) collective-permute-start(bf16[4,96,768]{2,1,0:T(8,128)(2,1)S(1)} %copy-done.13), channel_id=1, source_target_pairs={{0,2},{1,3},{2,0},{3,1},{4,6},{5,7},{6,4},{7,5},{8,10},{9,11},{10,... | collective-permute-start | bytes 1769480 | tf_op jit(solution)/shard_map/ppermute | solution.py:52
  82.1 24.0 %copy-start.15 = (bf16[4,96,768]{2,1,0:T(8,128)(2,1)}, bf16[4,96,768]{2,1,0:T(8,128)(2,1)S(1)}, u32[]{:S(2)}) copy-start(bf16[4,96,768]{2,1,0:T(8,128)(2,1)S(1)} %collective-permute-done.13.refs_12_) | copy-start | bytes 1769476
  82.1 24.5 %collective-permute-start.17 = (bf16[4,96,768]{2,1,0:T(8,128)(2,1)S(1)}, bf16[4,96,768]{2,1,0:T(8,128)(2,1)S(1)}, u32[]{:S(2)}, u32[]{:S(2)}) collective-permute-start(bf16[4,96,768]{2,1,0:T(8,128)(2,1)S(1)} %copy-done.14), channel_id=1, source_target_pairs={{0,4},{1,5},{2,6},{3,7},{4,0},{5,1},{6,2},{7,3},{8,12},{9,13},{10,... | collective-permute-start | bytes 1769480 | tf_op jit(solution)/shard_map/ppermute | solution.py:52
  82.7 24.6 %collective-permute-start.16 = (bf16[4,96,768]{2,1,0:T(8,128)(2,1)}, bf16[4,96,768]{2,1,0:T(8,128)(2,1)S(1)}, u32[]{:S(2)}, u32[]{:S(2)}) collective-permute-start(bf16[4,96,768]{2,1,0:T(8,128)(2,1)} %collective-permute-done.11.refs_6_), channel_id=1, source_target_pairs={{0,2},{1,3},{2,0},{3,1},{4,6},{5,7},{6,4},{7,5},{8,10},{9,11},{10,... | collective-permute-start | bytes 1769480 | tf_op jit(solution)/shard_map/ppermute | solution.py:52
  84.1 26.2 %collective-permute-start.18 = (bf16[4,96,768]{2,1,0:T(8,128)(2,1)}, bf16[4,96,768]{2,1,0:T(8,128)(2,1)S(1)}, u32[]{:S(2)}, u32[]{:S(2)}) collective-permute-start(bf16[4,96,768]{2,1,0:T(8,128)(2,1)} %collective-permute-done.12.refs_9_), channel_id=1, source_target_pairs={{0,4},{1,5},{2,6},{3,7},{4,0},{5,1},{6,2},{7,3},{8,12},{9,13},{10,... | collective-permute-start | bytes 1769480 | tf_op jit(solution)/shard_map/ppermute | solution.py:52
  85.0 25.8 %collective-permute-start.20 = (bf16[4,96,768]{2,1,0:T(8,128)(2,1)}, bf16[4,96,768]{2,1,0:T(8,128)(2,1)S(1)}, u32[]{:S(2)}, u32[]{:S(2)}) collective-permute-start(bf16[4,96,768]{2,1,0:T(8,128)(2,1)} %collective-permute-done.11.refs_6_), channel_id=1, source_target_pairs={{0,1},{1,0},{2,3},{3,2},{4,5},{5,4},{6,7},{7,6},{8,9},{9,8},{10,11... | collective-permute-start | bytes 1769480 | tf_op jit(solution)/shard_map/ppermute | solution.py:52
  106.1 13.7 %collective-permute-start.22 = (bf16[4,96,768]{2,1,0:T(8,128)(2,1)}, bf16[4,96,768]{2,1,0:T(8,128)(2,1)S(1)}, u32[]{:S(2)}, u32[]{:S(2)}) collective-permute-start(bf16[4,96,768]{2,1,0:T(8,128)(2,1)} %collective-permute-done.12.refs_9_), channel_id=1, source_target_pairs={{0,1},{1,0},{2,3},{3,2},{4,5},{5,4},{6,7},{7,6},{8,9},{9,8},{10,11... | collective-permute-start | bytes 1769480 | tf_op jit(solution)/shard_map/ppermute | solution.py:52
  106.6 13.1 %copy-start.16 = (bf16[4,96,768]{2,1,0:T(8,128)(2,1)}, bf16[4,96,768]{2,1,0:T(8,128)(2,1)S(1)}, u32[]{:S(2)}) copy-start(bf16[4,96,768]{2,1,0:T(8,128)(2,1)S(1)} %collective-permute-done.17.refs_10_) | copy-start | bytes 1769476
  107.3 12.4 %copy-start.17 = (bf16[4,96,768]{2,1,0:T(8,128)(2,1)}, bf16[4,96,768]{2,1,0:T(8,128)(2,1)S(1)}, u32[]{:S(2)}) copy-start(bf16[4,96,768]{2,1,0:T(8,128)(2,1)S(1)} %collective-permute-done.16.refs_7_) | copy-start | bytes 1769476
  110.3 9.5 %copy-start.18 = (bf16[4,96,768]{2,1,0:T(8,128)(2,1)}, bf16[4,96,768]{2,1,0:T(8,128)(2,1)S(1)}, u32[]{:S(2)}) copy-start(bf16[4,96,768]{2,1,0:T(8,128)(2,1)S(1)} %collective-permute-done.18.refs_11_) | copy-start | bytes 1769476
  110.3 9.5 %collective-permute-start.19 = (bf16[4,96,768]{2,1,0:T(8,128)(2,1)}, bf16[4,96,768]{2,1,0:T(8,128)(2,1)S(1)}, u32[]{:S(2)}, u32[]{:S(2)}) collective-permute-start(bf16[4,96,768]{2,1,0:T(8,128)(2,1)} %collective-permute-done.10.refs_5_), channel_id=1, source_target_pairs={{0,1},{1,0},{2,3},{3,2},{4,5},{5,4},{6,7},{7,6},{8,9},{9,8},{10,11... | collective-permute-start | bytes 1769480 | tf_op jit(solution)/shard_map/ppermute | solution.py:52
  110.3 9.5 %collective-permute-start.21 = (bf16[4,96,768]{2,1,0:T(8,128)(2,1)S(1)}, bf16[4,96,768]{2,1,0:T(8,128)(2,1)S(1)}, u32[]{:S(2)}, u32[]{:S(2)}) collective-permute-start(bf16[4,96,768]{2,1,0:T(8,128)(2,1)S(1)} %collective-permute-done.16.refs_7_), channel_id=1, source_target_pairs={{0,1},{1,0},{2,3},{3,2},{4,5},{5,4},{6,7},{7,6},{8,9},{9,8},{10,11... | collective-permute-start | bytes 1769480 | tf_op jit(solution)/shard_map/ppermute | solution.py:52
  110.8 9.0 %collective-permute-start.23 = (bf16[4,96,768]{2,1,0:T(8,128)(2,1)S(1)}, bf16[4,96,768]{2,1,0:T(8,128)(2,1)}, u32[]{:S(2)}, u32[]{:S(2)}) collective-permute-start(bf16[4,96,768]{2,1,0:T(8,128)(2,1)S(1)} %collective-permute-done.17.refs_10_), channel_id=1, source_target_pairs={{0,1},{1,0},{2,3},{3,2},{4,5},{5,4},{6,7},{7,6},{8,9},{9,8},{10,11... | collective-permute-start | bytes 1769480 | tf_op jit(solution)/shard_map/ppermute | solution.py:52
  110.8 9.0 %copy-start.19 = (bf16[4,96,768]{2,1,0:T(8,128)(2,1)}, bf16[4,96,768]{2,1,0:T(8,128)(2,1)S(1)}, u32[]{:S(2)}) copy-start(bf16[4,96,768]{2,1,0:T(8,128)(2,1)S(1)} %collective-permute-done.20.refs_14_) | copy-start | bytes 1769476
  110.8 9.0 %collective-permute-start.24 = (bf16[4,96,768]{2,1,0:T(8,128)(2,1)S(1)}, bf16[4,96,768]{2,1,0:T(8,128)(2,1)}, u32[]{:S(2)}, u32[]{:S(2)}) collective-permute-start(bf16[4,96,768]{2,1,0:T(8,128)(2,1)S(1)} %collective-permute-done.18.refs_11_), channel_id=1, source_target_pairs={{0,1},{1,0},{2,3},{3,2},{4,5},{5,4},{6,7},{7,6},{8,9},{9,8},{10,11... | collective-permute-start | bytes 1769480 | tf_op jit(solution)/shard_map/ppermute | solution.py:52
  167.4 11.4 %collective-permute-start.25 = (bf16[2,4,4,96,768]{4,3,2,1,0:T(8,128)(2,1)}, bf16[2,4,4,96,768]{4,3,2,1,0:T(8,128)(2,1)}, u32[]{:S(2)}, u32[]{:S(2)}) collective-permute-start(bf16[2,4,4,96,768]{4,3,2,1,0:T(8,128)(2,1)} %get-tuple-element.189), channel_id=1, source_target_pairs={{0,1},{1,0},{2,3},{3,2},{4,5},{5,4},{6,7},{7,6},{8,9},{9,8},{10,11... | collective-permute-start | bytes 14155784 | tf_op jit(solution)/shard_map/ppermute | solution.py:52
  182.9 33.0 %collective-permute-start.26 = (bf16[2,4,96,768]{3,2,1,0:T(8,128)(2,1)}, bf16[2,4,96,768]{3,2,1,0:T(8,128)(2,1)S(1)}, u32[]{:S(2)}, u32[]{:S(2)}) collective-permute-start(bf16[2,4,96,768]{3,2,1,0:T(8,128)(2,1)} %get-tuple-element.195), channel_id=1, source_target_pairs={{0,2},{1,3},{2,0},{3,1},{4,6},{5,7},{6,4},{7,5},{8,10},{9,11},{10,... | collective-permute-start | bytes 3538952 | tf_op jit(solution)/shard_map/ppermute | solution.py:52
  183.4 32.5 %collective-permute-start.27 = (bf16[2,4,96,768]{3,2,1,0:T(8,128)(2,1)S(1)}, bf16[2,4,96,768]{3,2,1,0:T(8,128)(2,1)S(1)}, u32[]{:S(2)}, u32[]{:S(2)}) collective-permute-start(bf16[2,4,96,768]{3,2,1,0:T(8,128)(2,1)S(1)} %get-tuple-element.196), channel_id=1, source_target_pairs={{0,4},{1,5},{2,6},{3,7},{4,0},{5,1},{6,2},{7,3},{8,12},{9,13},{10,... | collective-permute-start | bytes 3538952 | tf_op jit(solution)/shard_map/ppermute | solution.py:52
  183.9 32.0 %collective-permute-start.28 = (bf16[4,4,1,24,768]{4,3,2,1,0:T(8,128)(2,1)}, bf16[4,4,1,24,768]{4,3,2,1,0:T(8,128)(2,1)S(1)}, u32[]{:S(2)}, u32[]{:S(2)}) collective-permute-start(bf16[4,4,1,24,768]{4,3,2,1,0:T(8,128)(2,1)} %get-tuple-element.197), channel_id=1, source_target_pairs={{0,1},{1,0},{2,3},{3,2},{4,5},{5,4},{6,7},{7,6},{8,9},{9,8},{10,11... | collective-permute-start | bytes 1769480 | tf_op jit(solution)/shard_map/ppermute | solution.py:52
  222.2 17.8 %collective-permute-start.29 = (bf16[4,96,768]{2,1,0:T(8,128)(2,1)S(1)}, bf16[4,96,768]{2,1,0:T(8,128)(2,1)S(1)}, u32[]{:S(2)}, u32[]{:S(2)}) collective-permute-start(bf16[4,96,768]{2,1,0:T(8,128)(2,1)S(1)} %fusion.4), channel_id=1, source_target_pairs={{0,4},{1,5},{2,6},{3,7},{4,0},{5,1},{6,2},{7,3},{8,12},{9,13},{10,... | collective-permute-start | bytes 1769480 | tf_op jit(solution)/shard_map/ppermute | solution.py:52
  223.8 16.2 %collective-permute-start.30 = (bf16[4,96,768]{2,1,0:T(8,128)(2,1)S(1)}, bf16[4,96,768]{2,1,0:T(8,128)(2,1)}, u32[]{:S(2)}, u32[]{:S(2)}) collective-permute-start(bf16[4,96,768]{2,1,0:T(8,128)(2,1)S(1)} %fusion.5), channel_id=1, source_target_pairs={{0,2},{1,3},{2,0},{3,1},{4,6},{5,7},{6,4},{7,5},{8,10},{9,11},{10,... | collective-permute-start | bytes 1769480 | tf_op jit(solution)/shard_map/ppermute | solution.py:52
  240.0 9.6 %copy-start.30 = (bf16[96,768]{1,0:T(8,128)(2,1)S(1)}, bf16[96,768]{1,0:T(8,128)(2,1)}, u32[]{:S(2)}) copy-start(bf16[96,768]{1,0:T(8,128)(2,1)} %get-tuple-element.226) | copy-start | bytes 442372
  240.0 8.9 %collective-permute-start.31 = (bf16[96,768]{1,0:T(8,128)(2,1)}, bf16[96,768]{1,0:T(8,128)(2,1)S(1)}, u32[]{:S(2)}, u32[]{:S(2)}) collective-permute-start(bf16[96,768]{1,0:T(8,128)(2,1)} %get-tuple-element.226), channel_id=1, source_target_pairs={{0,1},{1,0},{2,3},{3,2},{4,5},{5,4},{6,7},{7,6},{8,9},{9,8},{10,11... | collective-permute-start | bytes 442376 | tf_op jit(solution)/shard_map/ppermute | solution.py:52
  248.9 9.5 %collective-permute-start.32 = (bf16[4,4,3,24,768]{4,3,2,1,0:T(8,128)(2,1)}, bf16[4,4,3,24,768]{4,3,2,1,0:T(8,128)(2,1)S(1)}, u32[]{:S(2)}, u32[]{:S(2)}) collective-permute-start(bf16[4,4,3,24,768]{4,3,2,1,0:T(8,128)(2,1)} %get-tuple-element.228), channel_id=1, source_target_pairs={{0,1},{1,0},{2,3},{3,2},{4,5},{5,4},{6,7},{7,6},{8,9},{9,8},{10,11... | collective-permute-start | bytes 5308424 | tf_op jit(solution)/shard_map/ppermute | solution.py:52
  252.1 6.5 %copy-start.2 = (f32[4,96,768]{2,1,0:T(8,128)}, f32[4,96,768]{2,1,0:T(8,128)S(1)}, u32[]{:S(2)}) copy-start(f32[4,96,768]{2,1,0:T(8,128)S(1)} %fusion.3) | copy-start | bytes 3538948
  252.2 6.3 %collective-permute-start.33 = (bf16[96,768]{1,0:T(8,128)(2,1)S(1)}, bf16[96,768]{1,0:T(8,128)(2,1)S(1)}, u32[]{:S(2)}, u32[]{:S(2)}) collective-permute-start(bf16[96,768]{1,0:T(8,128)(2,1)S(1)} %pad_maximum_fusion.2), channel_id=1, source_target_pairs={{0,2},{1,3},{2,0},{3,1},{4,6},{5,7},{6,4},{7,5},{8,10},{9,11},{10,... | collective-permute-start | bytes 442376 | tf_op jit(solution)/shard_map/ppermute | solution.py:52
  258.6 5.4 %collective-permute-start.34 = (bf16[96,768]{1,0:T(8,128)(2,1)S(1)}, bf16[96,768]{1,0:T(8,128)(2,1)S(1)}, u32[]{:S(2)}, u32[]{:S(2)}) collective-permute-start(bf16[96,768]{1,0:T(8,128)(2,1)S(1)} %pad_maximum_fusion.3), channel_id=1, source_target_pairs={{0,4},{1,5},{2,6},{3,7},{4,0},{5,1},{6,2},{7,3},{8,12},{9,13},{10,... | collective-permute-start | bytes 442376 | tf_op jit(solution)/shard_map/ppermute | solution.py:52
  264.0 33.5 %copy-start.3 = (f32[4,96,768]{2,1,0:T(8,128)S(1)}, f32[4,96,768]{2,1,0:T(8,128)}, u32[]{:S(2)}) copy-start(f32[4,96,768]{2,1,0:T(8,128)} %copy-done.2) | copy-start | bytes 3538948
  264.0 21.5 %collective-permute-start.35 = (bf16[4,4,24,768]{3,2,1,0:T(8,128)(2,1)}, bf16[4,4,24,768]{3,2,1,0:T(8,128)(2,1)S(1)}, u32[]{:S(2)}, u32[]{:S(2)}) collective-permute-start(bf16[4,4,24,768]{3,2,1,0:T(8,128)(2,1)} %get-tuple-element.238), channel_id=1, source_target_pairs={{0,2},{1,3},{2,0},{3,1},{4,6},{5,7},{6,4},{7,5},{8,10},{9,11},{10,... | collective-permute-start | bytes 1769480 | tf_op jit(solution)/shard_map/ppermute | solution.py:52
  264.9 27.1 %collective-permute-start.36 = (bf16[4,4,24,768]{3,2,1,0:T(8,128)(2,1)}, bf16[4,4,24,768]{3,2,1,0:T(8,128)(2,1)S(1)}, u32[]{:S(2)}, u32[]{:S(2)}) collective-permute-start(bf16[4,4,24,768]{3,2,1,0:T(8,128)(2,1)} %get-tuple-element.239), channel_id=1, source_target_pairs={{0,4},{1,5},{2,6},{3,7},{4,0},{5,1},{6,2},{7,3},{8,12},{9,13},{10,... | collective-permute-start | bytes 1769480 | tf_op jit(solution)/shard_map/ppermute | solution.py:52
  265.8 26.3 %collective-permute-start.37 = (bf16[4,4,24,768]{3,2,1,0:T(8,128)(2,1)}, bf16[4,4,24,768]{3,2,1,0:T(8,128)(2,1)S(1)}, u32[]{:S(2)}, u32[]{:S(2)}) collective-permute-start(bf16[4,4,24,768]{3,2,1,0:T(8,128)(2,1)} %get-tuple-element.240), channel_id=1, source_target_pairs={{0,6},{1,7},{2,4},{3,5},{4,2},{5,3},{6,0},{7,1},{8,14},{9,15},{10,... | collective-permute-start | bytes 1769480 | tf_op jit(solution)/shard_map/ppermute | solution.py:52
  267.6 26.3 %collective-permute-start.38 = (bf16[2,2,96,768]{3,2,1,0:T(8,128)(2,1)S(1)}, bf16[2,2,96,768]{3,2,1,0:T(8,128)(2,1)S(1)}, u32[]{:S(2)}, u32[]{:S(2)}) collective-permute-start(bf16[2,2,96,768]{3,2,1,0:T(8,128)(2,1)S(1)} %pad_maximum_fusion), channel_id=1, source_target_pairs={{0,16},{1,17},{2,18},{3,19},{4,20},{5,21},{6,22},{7,23},{8,24},{9,... | collective-permute-start | bytes 1769480 | tf_op jit(solution)/shard_map/ppermute | solution.py:52
  270.7 14.8 %collective-permute-start.39 = (bf16[96,768]{1,0:T(8,128)(2,1)S(1)}, bf16[96,768]{1,0:T(8,128)(2,1)S(1)}, u32[]{:S(2)}, u32[]{:S(2)}) collective-permute-start(bf16[96,768]{1,0:T(8,128)(2,1)S(1)} %pad_maximum_fusion.4), channel_id=1, source_target_pairs={{0,8},{1,9},{2,10},{3,11},{4,12},{5,13},{6,14},{7,15},{8,0},{9,1},... | collective-permute-start | bytes 442376 | tf_op jit(solution)/shard_map/ppermute | solution.py:52
  285.5 12.1 %copy-start.10 = (bf16[4,4,24,768]{3,2,1,0:T(8,128)(2,1)}, bf16[4,4,24,768]{3,2,1,0:T(8,128)(2,1)S(1)}, u32[]{:S(2)}) copy-start(bf16[4,4,24,768]{3,2,1,0:T(8,128)(2,1)S(1)} %collective-permute-done.35.refs_0_) | copy-start | bytes 1769476
  292.0 5.7 %copy-start.12 = (bf16[4,4,24,768]{3,2,1,0:T(8,128)(2,1)}, bf16[4,4,24,768]{3,2,1,0:T(8,128)(2,1)S(1)}, u32[]{:S(2)}) copy-start(bf16[4,4,24,768]{3,2,1,0:T(8,128)(2,1)S(1)} %collective-permute-done.37.refs_2_) | copy-start | bytes 1769476
  294.1 11.0 %collective-permute-start.40 = (bf16[96,768]{1,0:T(8,128)(2,1)S(1)}, bf16[96,768]{1,0:T(8,128)(2,1)S(1)}, u32[]{:S(2)}, u32[]{:S(2)}) collective-permute-start(bf16[96,768]{1,0:T(8,128)(2,1)S(1)} %get-tuple-element.276), channel_id=1, source_target_pairs={{0,16},{1,17},{2,18},{3,19},{4,20},{5,21},{6,22},{7,23},{8,24},{9,... | collective-permute-start | bytes 442376 | tf_op jit(solution)/shard_map/ppermute | solution.py:52
  300.5 9.4 %collective-permute-start.41 = (bf16[4,24,768]{2,1,0:T(8,128)(2,1)}, bf16[4,24,768]{2,1,0:T(8,128)(2,1)S(1)}, u32[]{:S(2)}, u32[]{:S(2)}) collective-permute-start(bf16[4,24,768]{2,1,0:T(8,128)(2,1)} %get-tuple-element.255), channel_id=1, source_target_pairs={{0,8},{1,9},{2,10},{3,11},{4,12},{5,13},{6,14},{7,15},{8,0},{9,1},... | collective-permute-start | bytes 442376 | tf_op jit(solution)/shard_map/ppermute | solution.py:52
  300.6 12.9 %collective-permute-start.42 = (bf16[4,24,768]{2,1,0:T(8,128)(2,1)}, bf16[4,24,768]{2,1,0:T(8,128)(2,1)S(1)}, u32[]{:S(2)}, u32[]{:S(2)}) collective-permute-start(bf16[4,24,768]{2,1,0:T(8,128)(2,1)} %get-tuple-element.256), channel_id=1, source_target_pairs={{0,16},{1,17},{2,18},{3,19},{4,20},{5,21},{6,22},{7,23},{8,24},{9,... | collective-permute-start | bytes 442376 | tf_op jit(solution)/shard_map/ppermute | solution.py:52
  302.9 14.6 %collective-permute-start.43 = (bf16[4,24,768]{2,1,0:T(8,128)(2,1)}, bf16[4,24,768]{2,1,0:T(8,128)(2,1)S(1)}, u32[]{:S(2)}, u32[]{:S(2)}) collective-permute-start(bf16[4,24,768]{2,1,0:T(8,128)(2,1)} %get-tuple-element.257), channel_id=1, source_target_pairs={{0,24},{1,25},{2,26},{3,27},{4,28},{5,29},{6,30},{7,31},{8,16},{9,... | collective-permute-start | bytes 442376 | tf_op jit(solution)/shard_map/ppermute | solution.py:52
  304.1 17.2 %collective-permute-start.44 = (bf16[2,96,768]{2,1,0:T(8,128)(2,1)S(1)}, bf16[2,96,768]{2,1,0:T(8,128)(2,1)S(1)}, u32[]{:S(2)}, u32[]{:S(2)}) collective-permute-start(bf16[2,96,768]{2,1,0:T(8,128)(2,1)S(1)} %pad_maximum_fusion.1), channel_id=1, source_target_pairs={{0,8},{1,9},{2,10},{3,11},{4,12},{5,13},{6,14},{7,15},{8,0},{9,1},... | collective-permute-start | bytes 884744 | tf_op jit(solution)/shard_map/ppermute | solution.py:52
  309.9 7.5 %copy-start.33 = (bf16[4,24,768]{2,1,0:T(8,128)(2,1)}, bf16[4,24,768]{2,1,0:T(8,128)(2,1)S(1)}, u32[]{:S(2)}) copy-start(bf16[4,24,768]{2,1,0:T(8,128)(2,1)S(1)} %collective-permute-done.41.refs_0_) | copy-start | bytes 442372
  (22 other events, 39.8 us)

commit v4 on v3

--- a/solution.py
+++ b/solution.py
@@ -317,7 +317,7 @@
     @pl.when(pl.program_id(0) == 0)
     def _():
         for ref, half in ((own_ref, core), (other_ref, 1 - core)):
-            w_ref[:, pl.ds(pl.multiple_of(384 * half, 128), 384)] = ref[3]
+            w_ref[:, pl.ds(pl.multiple_of(384 * half, 128), 384)] = ref[0]
 
     middle = start_ref[...] + dotf(x_ref[...], w_ref[...]) + p_ref[0:1]
     middle_ref[...] = middle
@@ -332,7 +332,9 @@
         out_kernel,
         name="out_projection",
         grid=(rows // STEP,),
-        in_specs=[pl.BlockSpec(memory_space=pltpu.SMEM), block, block, vmem, vmem, vmem],
+        in_specs=[pl.BlockSpec(memory_space=pltpu.SMEM), block, block]
+        + [pl.BlockSpec((1, 768, 384), lambda i: (3, 0, 0))] * 2
+        + [vmem],
         out_specs=[block, block, vmem],
         out_shape=(
             jax.ShapeDtypeStruct((rows, 768), F32),
@@ -662,11 +664,11 @@
 
 
 def mlp_kernel(fast, *refs):
-    meta, n_ref, c_ref, b_ref = refs[:4]
+    meta, n_ref, c_ref, ct, b_ref = refs[:5]
     count = 16 if fast else 1
-    pieces, refs = refs[4 : 4 + count], refs[4 + count :]
+    pieces, refs = refs[5 : 5 + count], refs[5 + count :]
     branch_ref, gn_ref, db_ref, own_ref, other_ref = refs[:5]
-    w, nt, ct, dw, wsem, dsem = refs[5:]
+    w, nt, dw, wsem, dsem = refs[5:]
     t = pl.program_id(0)
     jr, sub = t // PER, t % PER
     me_mp, me_dp = meta[0] % 4, meta[0] // 4
@@ -700,7 +702,6 @@
             for copy in loads(j):
                 copy.start()
         nt[...] = n_ref[...].T
-        ct[...] = c_ref[...].T
         branch_ref[...] = jnp.zeros_like(branch_ref)
         gn_ref[...] = jnp.zeros_like(gn_ref)
 
@@ -744,7 +745,7 @@
                 copy.wait()
 
 
-def mlp(meta, normed, cot, bias, pieces):
+def mlp(meta, normed, cot, cot_turned, bias, pieces):
     fast = len(pieces) == 16
     tokens = normed.shape[0]
     vmem = pl.BlockSpec(memory_space=pltpu.VMEM)
@@ -754,7 +755,7 @@
         partial(mlp_kernel, fast),
         name="mlp",
         grid=(4 * PER,),
-        in_specs=[pl.BlockSpec(memory_space=pltpu.SMEM), vmem, vmem, vmem] + [anys] * len(pieces),
+        in_specs=[pl.BlockSpec(memory_space=pltpu.SMEM)] + [vmem] * 4 + [anys] * len(pieces),
         out_specs=[vmem, vmem, vmem, anys, anys],
         out_shape=(
             jax.ShapeDtypeStruct((tokens, 768), F32),
@@ -766,13 +767,12 @@
         scratch_shapes=[
             pltpu.VMEM((4, 2, 768, 768), B16),
             pltpu.VMEM((768, tokens), B16),
-            pltpu.VMEM((768, tokens), B16),
             pltpu.VMEM((4, 8, 2, 96, 768), B16),
             pltpu.SemaphoreType.DMA((4, 8, 2)),
             pltpu.SemaphoreType.DMA((4, 8, 2)),
         ],
         compiler_params=pltpu.CompilerParams(vmem_limit_bytes=VMEM_LIMIT),
-    )(meta, normed, cot, bias.reshape(4, 1, 768), *pieces)
+    )(meta, normed, cot, cot_turned, bias.reshape(4, 1, 768), *pieces)
 
 
 def local(
@@ -798,8 +798,8 @@
     if fast:
         piece = pair_rows(meta, attn_qkv, attn_out)
         held = z_stage(piece)
-        held, mlp_piece, tokens, prompts, segments, prompt_slot_index = tie(
-            held, mlp_weight, tokens, prompts, segments, prompt_slot_index
+        held, mlp_near, mlp_piece, tokens, prompts, segments, prompt_slot_index = tie(
+            held, px(mlp_weight, 8), mlp_weight, tokens, prompts, segments, prompt_slot_index
         )
     table = jnp.concatenate([prompts, jnp.zeros((128 - NPROMPT, width), F32)], 0)
     start, normed_one, onehot, qf, kf = embed(
@@ -807,12 +807,14 @@
     )
     bias = jnp.stack([attn_bias[0], jnp.zeros_like(attn_bias[0]), attn_bias[1]])[:, None]
     out_params = jnp.stack([attn_bias[2], norm_gain[1], norm_shift[1]])
+    turn_params = jnp.stack([norm_gain[1], mlp_bias_down])
+    cot_turned = cotangent.T
 
     if fast:
-        x = (normed_one, start, qf, kf, onehot)
-        mlp_z = [mlp_piece] + [px(mlp_piece, 8 * k) for k in range(1, 4)]
+        x = (normed_one, start, qf, kf, onehot, bias, out_params, turn_params, cot_turned)
+        mlp_z = [mlp_piece, mlp_near] + [px(mlp_piece, 8 * k) for k in range(2, 4)]
         quad, mlp_z, x = tie(xy_stage(held), mlp_z, x)
-        normed_one, start, qf, kf, onehot = x
+        normed_one, start, qf, kf, onehot, bias, out_params, turn_params, cot_turned = x
         own = assemble(meta, quad, "assemble")
         s1, s2 = stack_pair(mlp_z)
         own, s1, s2 = tie(own, s1, s2)
@@ -842,11 +844,12 @@
     else:
         mlp_pieces = [mlp_all]
     middle, normed_two, out_weight = out_projection(meta, mixed, start, own, other, out_params)
-    branch, grad_two, grad_up, own_mlp, other_mlp = mlp(meta, normed_two, cotangent, mlp_bias_up, mlp_pieces)
+    branch, grad_two, grad_up, own_mlp, other_mlp = mlp(
+        meta, normed_two, cotangent, cot_turned, mlp_bias_up, mlp_pieces
+    )
     if fast:
         other_mlp, grad_two, branch = tie(other_mlp, grad_two, branch)
         got_mlp = px(other_mlp, 1)
-    turn_params = jnp.stack([norm_gain[1], mlp_bias_down])
     output, grad_middle, grad_mixed, own_out, other_out, sums_two = turn(
         meta, middle, branch, grad_two, cotangent, mixed, out_weight, turn_params
     )
@@ -858,10 +861,12 @@
     grads = attention_backward(meta, qf, kf, qkv, grad_mixed, mixed, lse)
     if fast:
         got_1, got_2, got_out, grads, grad_middle = tie(got_1, got_2, got_out, grads, grad_middle)
-        plane = [
-            add_parts(own_mlp[c, :2], got_mlp[c, :2]) + got.astype(F32) for c, got in enumerate((got_1, got_2))
-        ]
-        send, grads = tie([p[1].astype(B16) for p in plane], grads)
+        planes = (got_1, got_2)
+
+        def plane(c, i):
+            return add_parts(own_mlp[c, i], got_mlp[c, i]) + planes[c][i].astype(F32)
+
+        send, grads = tie([plane(c, 1).astype(B16) for c in range(2)], grads)
         got_1, got_2 = px(send[0], 4), px(send[1], 2)
     input_grad, packed = tail_step(
         meta, start, grad_middle, onehot, norm_gain[0:1], sums_two, grad_up, (own, other), grads
@@ -877,7 +882,7 @@
         got_w, got_small, packed = tie(got_w, got_small, packed)
         packed = pack_small(add_small(packed, got_small))
         got_small = px(packed, 4)
-        col = [add_parts(plane[0][0], got_1), add_parts(plane[1][0], got_2)]
+        col = [add_parts(plane(0, 0), got_1), add_parts(plane(1, 0), got_2)]
         send = jnp.stack([c[2:].astype(B16) for c in col])
         keep, *sends = gather_sums(own_w, got_w, own_out, got_out)
         send, sends, got_small, packed = tie(send, sends, got_small, packed)

time: 325 us -> 316 us (0.972)
  local copies, waits for them, and re-layouts: 20.1 us -> 14.7 us
    add x1 -> x0, other arithmetic: 3.57 us -> none  [local(): add_parts(own_mlp[c, :2], got_mlp[c, :2]) + got.astype(F32)]
    unnamed x82 -> x81, local copies, waits for them, and re-layouts: 9.81 us -> 7.75 us
  transfers between devices with their start and end apart: 45 -> 45, of which waited for: 14 -> 15; matrix products, arithmetic and copies ran while one was open for 5% -> 4% of each run, Pallas kernels for 38% -> 39%
where the time goes in v4:
time: 316 us; the launch traced here: 314 us
  Pallas kernels  178 us (56%)
  waiting for transfers between devices  63.4 us (20%)
  starting transfers between devices  43.2 us (14%)
  local copies, waits for them, and re-layouts  14.7 us (5%)
  other arithmetic  13.3 us (4%)
    ppermute x45, waiting for transfers between devices, px(): return lax.ppermute(x, AXES, [(i, i ^ k) for i in range(32)])  63.4 us
    pallas_call x1, Pallas kernels, mlp(): pl.pallas_call(partial(mlp_kernel, fast), name='mlp', grid=(4 * PER,), in...  46.8 us
    ppermute x45, starting transfers between devices, px(): return lax.ppermute(x, AXES, [(i, i ^ k) for i in range(32)])  43.2 us
    pallas_call x1, Pallas kernels, attention_backward(): pl.pallas_call(kernel, name='attention_backward', grid_spec=pltpu.Prefetc...  31.9 us
    pallas_call x1, Pallas kernels, attention_forward(): pl.pallas_call(kernel, name='attention_forward', grid_spec=pltpu.Prefetch...  21.1 us
    pallas_call x1, Pallas kernels, tail_step(): pl.pallas_call(tail_kernel, name='tail_step', grid=(rows // STEP,), in_sp...  14.7 us
    pallas_call x2, Pallas kernels, project(): pl.pallas_call(partial(project_kernel, side), name='project', grid=(3,),...  11.7 us
    pallas_call x1, Pallas kernels, turn(): pl.pallas_call(turn_kernel, name='turn', grid=(rows // STEP,), in_specs=[...  11 us
  transfers between devices with their start and end apart: 45, of which 15 were waited for; matrix products, arithmetic and copies ran while one was open for 4% of the time, Pallas kernels for 39%

profile of v4, /device:TPU:16, one launch (start us, length us, event | category | flops | bytes accessed | tf_op | source)
XLA Modules:
  0.0 313.7 jit_solution(14913031537453159756)
XLA Ops:
  0.7 1.7 split.1
  2.4 1.6 collective-permute-start.4
  4.7 1.6 join.1.refs_0_
  6.5 3.5 %collective-permute-start.2 = (bf16[4,48,384]{2,1,0:T(8,128)(2,1)}, bf16[4,48,384]{2,1,0:T(8,128)(2,1)S(1)}, u32[]{:S(2)}, u32[]{:S(2)}) collective-permute-start(bf16[4,48,384]{2,1,0:T(8,128)(2,1)} %join.1.refs_0_), channel_id=1, source_target_pairs={{0,16},{1,17},{2,18},{3,19},{4,20},{5,21},{6,22},{7,23},{8,24},{9,... | collective-permute-start | bytes 442376 | tf_op jit(solution)/shard_map/ppermute | solution.py:52
  10.0 0.8 fusion.21
  10.9 8.6 %collective-permute-done.3.refs_3_ = bf16[4,48,384]{2,1,0:T(8,128)(2,1)S(1)} collective-permute-done((bf16[4,48,384]{2,1,0:T(8,128)(2,1)}, bf16[4,48,384]{2,1,0:T(8,128)(2,1)S(1)}, u32[]{:S(2)}, u32[]{:S(2)}) %collective-permute-start.3) | collective-permute-done | bytes 147488 | tf_op jit(solution)/shard_map/ppermute | solution.py:52
  19.9 1.6 collective-permute-done.1.refs_1_
  22.1 2.0 stack_z.1.refs_0_
  24.1 2.4 collective-permute-start.7
  28.3 1.6 copy.28
  30.0 0.8 collective-permute-start.9
  30.8 4.2 %collective-permute-start.8 = (bf16[2,96,768]{2,1,0:T(8,128)(2,1)}, bf16[2,96,768]{2,1,0:T(8,128)(2,1)S(1)}, u32[]{:S(2)}, u32[]{:S(2)}) collective-permute-start(bf16[2,96,768]{2,1,0:T(8,128)(2,1)} %refs_0_), channel_id=1, source_target_pairs={{0,16},{1,17},{2,18},{3,19},{4,20},{5,21},{6,22},{7,23},{8,24},{9,... | collective-permute-start | bytes 884744 | tf_op jit(solution)/shard_map/ppermute | solution.py:52
  36.8 0.8 concatenate.15.table_ref
  37.6 1.0 copy.26.slots_ref
  38.6 1.0 copy.27.segs_ref
  39.6 5.9 %embed.1 = (f32[1024,768]{1,0:T(8,128)}, bf16[1024,768]{1,0:T(8,128)(2,1)}, bf16[1024,128]{1,0:T(8,128)(2,1)}, bf16[1024,128]{1,0:T(8,128)(2,1)}, bf16[1024,128]{1,0:T(8,128)(2,1)}) custom-call(bf16[1024,768]{1,0:T(8,128)(2,1)} %tokens_ref, s32[1024,1]{1,0:T(8,128)} %copy.26.slots_ref, s32[1024,1]{1,0:T(8,128)} %copy.27.segs_ref, ...), custom_call_target="tpu_custom_call" | custom-call | tf_op jit(solution)/shard_map/embed/pallas_call | solution.py:215
  45.5 7.3 %collective-permute-done.9.refs_3_ = bf16[2,96,768]{2,1,0:T(8,128)(2,1)S(1)} collective-permute-done((bf16[2,96,768]{2,1,0:T(8,128)(2,1)}, bf16[2,96,768]{2,1,0:T(8,128)(2,1)S(1)}, u32[]{:S(2)}, u32[]{:S(2)}) %collective-permute-start.9) | collective-permute-done | bytes 294944 | tf_op jit(solution)/shard_map/ppermute | solution.py:52
  52.8 2.3 collective-permute-done.8.refs_2_
  55.1 0.8 copy-done.12
  56.3 3.3 %assemble.1.w_ref.own_ref.refs_0_ = bf16[4,768,384]{2,1,0:T(8,128)(2,1)} custom-call(s32[1]{0:T(128)} %bitcast.meta.refs_0_, bf16[4,4,48,384]{3,2,1,0:T(8,128)(2,1)} %stack_z.1.refs_0_, bf16[4,4,48,384]{3,2,1,0:T(8,128)(2,1)} %copy-done.15, bf16[4,4,48,384]{3,2,1,0:T(8,128)(2,1)} %copy-done.13, bf16[4,4,48,384]{3,2,1,0:T(8,128)(2,1)} %copy-done.12), custom_call_target="tpu_custom_call" | custom-call | tf_op jit(solution)/shard_map/assemble/pallas_call | solution.py:149
  59.7 2.3 stack_pair.1
  62.5 1.5 collective-permute-start.11
  64.0 1.5 collective-permute-start.12
  65.5 5.8 %project.2.refs_0_ = bf16[1024,2304]{1,0:T(8,128)(2,1)} custom-call(s32[1]{0:T(128)} %bitcast.meta.refs_0_, bf16[1024,768]{1,0:T(8,128)(2,1)} %get-tuple-element.167.x_ref.left_ref, bf16[4,768,384]{2,1,0:T(8,128)(2,1)} %assemble.1.w_ref.own_ref.refs_0_, f32[3,1,768]{2,1,0:T(1,128)} %broadcast_in_dim.12.b_ref), custom_call_target="tpu_custom_call" | custom-call | tf_op jit(solution)/shard_map/project/pallas_call | solution.py:169
  72.0 0.8 copy-done
  72.8 5.9 %project.3.refs_2_.refs_3_.refs_4_ = bf16[1024,2304]{1,0:T(8,128)(2,1)} custom-call(s32[1]{0:T(128)} %bitcast.meta.refs_0_, bf16[1024,768]{1,0:T(8,128)(2,1)} %get-tuple-element.167.x_ref.left_ref, bf16[4,768,384]{2,1,0:T(8,128)(2,1)} %copy-done, f32[3,1,768]{2,1,0:T(1,128)} %broadcast_in_dim.12.b_ref, ...), custom_call_target="tpu_custom_call", output_to_operand_aliasing={{}: (4, {})} | custom-call | tf_op jit(solution)/shard_map/project/pallas_call | solution.py:169
  79.2 1.3 collective-permute-done.12.refs_10_
  80.5 1.5 collective-permute-start.16
  82.5 21.1 %attention_forward.1 = (bf16[1024,768]{1,0:T(8,128)(2,1)}, f32[1024,768]{1,0:T(8,128)}) custom-call(s32[1]{0:T(128)} %bitcast.meta.refs_0_, bf16[1024,128]{1,0:T(8,128)(2,1)} %get-tuple-element.174.refs_0_, bf16[1024,128]{1,0:T(8,128)(2,1)} %get-tuple-element.175.refs_1_, bf16[1024,2304]{1,0:T(8,128)(2,1)} %project.3.refs_2_.refs_3_.refs_4_, ...), custom_call_target="tpu_custom_call" | custom-call | tf_op jit(solution)/shard_map/attention_forward/pallas_call | solution.py:572
  104.2 1.1 collective-permute-done.16.refs_8_
  105.3 1.5 collective-permute-done.18.refs_12_
  107.8 5.9 %out_projection.1 = (f32[1024,768]{1,0:T(8,128)}, bf16[1024,768]{1,0:T(8,128)(2,1)}, bf16[768,768]{1,0:T(8,128)(2,1)}) custom-call(s32[1]{0:T(128)} %bitcast.meta.refs_0_, bf16[1024,768]{1,0:T(8,128)(2,1)} %get-tuple-element.178.x_ref.mixed_ref.refs_6_, f32[1024,768]{1,0:T(8,128)} %get-tuple-element.179.start_ref, ...), custom_call_target="tpu_custom_call" | custom-call | tf_op jit(solution)/shard_map/out_projection/pallas_call | solution.py:331
  113.9 0.7 copy-done.14
  115.1 46.8 %mlp.1 = (f32[1024,768]{1,0:T(8,128)}, f32[1024,768]{1,0:T(8,128)}, f32[4,1,768]{2,1,0:T(1,128)}, bf16[2,4,4,96,768]{4,3,2,1,0:T(8,128)(2,1)}, bf16[2,4,4,96,768]{4,3,2,1,0:T(8,128)(2,1)}) custom-call(s32[1]{0:T(128)} %bitcast.meta.refs_0_, bf16[1024,768]{1,0:T(8,128)(2,1)} %get-tuple-element.182.refs_1_, bf16[1024,768]{1,0:T(8,128)(2,1)} %cot_ref.1, ...), custom_call_target="tpu_custom_call" | custom-call | tf_op jit(solution)/shard_map/mlp/pallas_call | solution.py:754
  162.2 11.0 %turn.1 = (bf16[1024,768]{1,0:T(8,128)(2,1)}, f32[1024,768]{1,0:T(8,128)}, bf16[1024,768]{1,0:T(8,128)(2,1)}, bf16[4,4,1,24,768]{4,3,2,1,0:T(8,128)(2,1)}, bf16[...) custom-call(s32[1]{0:T(128)} %bitcast.meta.refs_0_, f32[1024,768]{1,0:T(8,128)} %get-tuple-element.181.middle_ref, ...), custom_call_target="tpu_custom_call" | custom-call | tf_op jit(solution)/shard_map/turn/pallas_call | solution.py:399
  173.2 4.1 %fusion.1 = (bf16[2,4,96,768]{3,2,1,0:T(8,128)(2,1)S(1)}, bf16[2,4,96,768]{3,2,1,0:T(8,128)(2,1)}) fusion(bf16[2,4,4,96,768]{4,3,2,1,0:T(8,128)(2,1)} %collective-permute-done.25, bf16[2,4,4,96,768]{4,3,2,1,0:T(8,128)(2,1)} %get-tuple-element.198), kind=kLoop, calls=%fused_computation.3 | loop fusion | flops 4718592 | bytes 7077888 | tf_op jit(solution)/shard_map/convert_element_type | solution.py:858
  178.3 31.9 %attention_backward.1 = (bf16[1024,768]{1,0:T(8,128)(2,1)}, bf16[1024,768]{1,0:T(8,128)(2,1)}, bf16[1024,768]{1,0:T(8,128)(2,1)}) custom-call(s32[1]{0:T(128)} %bitcast.meta.refs_0_, bf16[1024,128]{1,0:T(8,128)(2,1)} %get-tuple-element.174.refs_0_, bf16[1024,128]{1,0:T(8,128)(2,1)} %get-tuple-element.175.refs_1_, ...), custom_call_target="tpu_custom_call" | custom-call | tf_op jit(solution)/shard_map/attention_backward/pallas_call | solution.py:647
  210.3 2.7 fusion.4
  213.0 1.6 collective-permute-start.29
  214.6 1.5 collective-permute-start.30
  216.1 14.7 %tail_step.1 = (f32[1024,768]{1,0:T(8,128)}, bf16[96,768]{1,0:T(8,128)(2,1)}) custom-call(s32[1]{0:T(128)} %bitcast.meta.refs_0_, f32[1024,768]{1,0:T(8,128)} %get-tuple-element.179.start_ref, f32[1024,768]{1,0:T(8,128)} %get-tuple-element.214.gmiddle_ref, bf16[1024,128]{1,0:T(8,128)(2,1)} %get-tuple-element.215.slots_ref, f32[1,768]{1,0:T(1,128)} %copy-done.35, ...), custom_call_target="tpu_custom_call" | custom-call | tf_op jit(solution)/shard_map/tail_step/pallas_call | solution.py:465
  230.9 8.9 %weight_grad_qkv.1 = (bf16[4,4,3,24,768]{4,3,2,1,0:T(8,128)(2,1)}, bf16[4,4,3,24,768]{4,3,2,1,0:T(8,128)(2,1)}) custom-call(s32[1]{0:T(128)} %bitcast.meta.refs_0_, bf16[1024,768]{1,0:T(8,128)(2,1)} %get-tuple-element.167.x_ref.left_ref, bf16[1024,768]{1,0:T(8,128)(2,1)} %get-tuple-element.232.refs_2_.refs_0_, ...), custom_call_target="tpu_custom_call" | custom-call | tf_op jit(solution)/shard_map/weight_grad_qkv/pallas_call | solution.py:494
  240.6 2.5 fusion.3
  243.2 0.8 collective-permute-start.33
  244.1 5.3 %collective-permute-done.33 = bf16[96,768]{1,0:T(8,128)(2,1)S(1)} collective-permute-done((bf16[96,768]{1,0:T(8,128)(2,1)S(1)}, bf16[96,768]{1,0:T(8,128)(2,1)S(1)}, u32[]{:S(2)}, u32[]{:S(2)}) %collective-permute-start.33) | collective-permute-done | bytes 147488 | tf_op jit(solution)/shard_map/ppermute | solution.py:52
  250.6 4.1 %gather_sums.1 = (f32[4,4,24,768]{3,2,1,0:T(8,128)}, bf16[4,4,24,768]{3,2,1,0:T(8,128)(2,1)}, bf16[4,4,24,768]{3,2,1,0:T(8,128)(2,1)}, bf16[4,4,24,768]{3,2,1,0:T(8,128)(2,1)}) custom-call(bf16[4,4,3,24,768]{4,3,2,1,0:T(8,128)(2,1)} %get-tuple-element.235.own_ref, bf16[4,4,3,24,768]{4,3,2,1,0:T(8,128)(2,1)} %copy-done.2, ...), custom_call_target="tpu_custom_call" | custom-call | tf_op jit(solution)/shard_map/gather_sums/pallas_call | solution.py:248
  254.8 0.7 collective-permute-start.35
  255.6 1.0 collective-permute-start.36
  256.6 1.8 collective-permute-start.37
  258.4 3.3 %collective-permute-start.38 = (bf16[2,2,96,768]{3,2,1,0:T(8,128)(2,1)S(1)}, bf16[2,2,96,768]{3,2,1,0:T(8,128)(2,1)S(1)}, u32[]{:S(2)}, u32[]{:S(2)}) collective-permute-start(bf16[2,2,96,768]{3,2,1,0:T(8,128)(2,1)S(1)} %pad_maximum_fusion), channel_id=1, source_target_pairs={{0,16},{1,17},{2,18},{3,19},{4,20},{5,21},{6,22},{7,23},{8,24},{9,... | collective-permute-start | bytes 1769480 | tf_op jit(solution)/shard_map/ppermute | solution.py:52
  261.9 15.1 %collective-permute-done.39 = bf16[96,768]{1,0:T(8,128)(2,1)S(1)} collective-permute-done((bf16[96,768]{1,0:T(8,128)(2,1)S(1)}, bf16[96,768]{1,0:T(8,128)(2,1)S(1)}, u32[]{:S(2)}, u32[]{:S(2)}) %collective-permute-start.39) | collective-permute-done | bytes 147488 | tf_op jit(solution)/shard_map/ppermute | solution.py:52
  277.0 5.7 %collective-permute-done.36.refs_1_ = bf16[4,4,24,768]{3,2,1,0:T(8,128)(2,1)S(1)} collective-permute-done((bf16[4,4,24,768]{3,2,1,0:T(8,128)(2,1)}, bf16[4,4,24,768]{3,2,1,0:T(8,128)(2,1)S(1)}, u32[]{:S(2)}, u32[]{:S(2)}) %collective-permute-start.36) | collective-permute-done | bytes 589856 | tf_op jit(solution)/shard_map/ppermute | solution.py:52
  282.7 2.7 collective-permute-done.38
  285.6 3.4 %collective-permute-start.40 = (bf16[96,768]{1,0:T(8,128)(2,1)S(1)}, bf16[96,768]{1,0:T(8,128)(2,1)S(1)}, u32[]{:S(2)}, u32[]{:S(2)}) collective-permute-start(bf16[96,768]{1,0:T(8,128)(2,1)S(1)} %get-tuple-element.288), channel_id=1, source_target_pairs={{0,16},{1,17},{2,18},{3,19},{4,20},{5,21},{6,22},{7,23},{8,24},{9,... | collective-permute-start | bytes 442376 | tf_op jit(solution)/shard_map/ppermute | solution.py:52
  289.3 2.7 plane_sums.1
  292.1 1.9 collective-permute-start.42
  294.1 1.5 collective-permute-start.43
  295.6 1.0 collective-permute-start.44
  298.6 2.5 collective-permute-done.41.refs_0_
  301.1 3.7 %collective-permute-done.42.refs_1_ = bf16[4,24,768]{2,1,0:T(8,128)(2,1)S(1)} collective-permute-done((bf16[4,24,768]{2,1,0:T(8,128)(2,1)}, bf16[4,24,768]{2,1,0:T(8,128)(2,1)S(1)}, u32[]{:S(2)}, u32[]{:S(2)}) %collective-permute-start.42) | collective-permute-done | bytes 147488 | tf_op jit(solution)/shard_map/ppermute | solution.py:52
  304.8 4.2 %collective-permute-done.43.refs_2_ = bf16[4,24,768]{2,1,0:T(8,128)(2,1)S(1)} collective-permute-done((bf16[4,24,768]{2,1,0:T(8,128)(2,1)}, bf16[4,24,768]{2,1,0:T(8,128)(2,1)S(1)}, u32[]{:S(2)}, u32[]{:S(2)}) %collective-permute-start.43) | collective-permute-done | bytes 147488 | tf_op jit(solution)/shard_map/ppermute | solution.py:52
  309.6 1.9 line_sums.1
  312.1 0.7 slice_add_fusion.6
  312.8 0.9 maximum_add_fusion
  (181 shorter events, 17.6 us)
Async XLA Ops:
  0.6 27.1 %copy-start.39 = (f32[768]{0:T(1024)S(1)}, f32[768]{0:T(1024)}, u32[]{:S(2)}) copy-start(f32[768]{0:T(1024)} %param.25) | copy-start | bytes 9220
  0.7 27.7 %copy-start.1 = (bf16[1024,768]{1,0:T(8,128)(2,1)S(1)}, bf16[1024,768]{1,0:T(8,128)(2,1)}, u32[]{:S(2)}) copy-start(bf16[1024,768]{1,0:T(8,128)(2,1)} %cot_ref.1) | copy-start | bytes 4718596
  2.4 1.7 collective-permute-start
  2.4 21.8 %collective-permute-start.4 = (bf16[2,96,768]{2,1,0:T(8,128)(2,1)}, bf16[2,96,768]{2,1,0:T(8,128)(2,1)}, u32[]{:S(2)}, u32[]{:S(2)}) collective-permute-start(bf16[2,96,768]{2,1,0:T(8,128)(2,1)} %refs_0_), channel_id=1, source_target_pairs={{0,8},{1,9},{2,10},{3,11},{4,12},{5,13},{6,14},{7,15},{8,0},{9,1},... | collective-permute-start | bytes 884744 | tf_op jit(solution)/shard_map/ppermute | solution.py:52
  6.3 13.2 %collective-permute-start.3 = (bf16[4,48,384]{2,1,0:T(8,128)(2,1)}, bf16[4,48,384]{2,1,0:T(8,128)(2,1)S(1)}, u32[]{:S(2)}, u32[]{:S(2)}) collective-permute-start(bf16[4,48,384]{2,1,0:T(8,128)(2,1)} %join.1.refs_0_), channel_id=1, source_target_pairs={{0,24},{1,25},{2,26},{3,27},{4,28},{5,29},{6,30},{7,31},{8,16},{9,... | collective-permute-start | bytes 442376 | tf_op jit(solution)/shard_map/ppermute | solution.py:52
  6.5 13.3 %collective-permute-start.2 = (bf16[4,48,384]{2,1,0:T(8,128)(2,1)}, bf16[4,48,384]{2,1,0:T(8,128)(2,1)S(1)}, u32[]{:S(2)}, u32[]{:S(2)}) collective-permute-start(bf16[4,48,384]{2,1,0:T(8,128)(2,1)} %join.1.refs_0_), channel_id=1, source_target_pairs={{0,16},{1,17},{2,18},{3,19},{4,20},{5,21},{6,22},{7,23},{8,24},{9,... | collective-permute-start | bytes 442376 | tf_op jit(solution)/shard_map/ppermute | solution.py:52
  10.0 11.5 %collective-permute-start.1 = (bf16[4,48,384]{2,1,0:T(8,128)(2,1)}, bf16[4,48,384]{2,1,0:T(8,128)(2,1)S(1)}, u32[]{:S(2)}, u32[]{:S(2)}) collective-permute-start(bf16[4,48,384]{2,1,0:T(8,128)(2,1)} %join.1.refs_0_), channel_id=1, source_target_pairs={{0,8},{1,9},{2,10},{3,11},{4,12},{5,13},{6,14},{7,15},{8,0},{9,1},... | collective-permute-start | bytes 442376 | tf_op jit(solution)/shard_map/ppermute | solution.py:52
  24.1 30.9 %collective-permute-start.7 = (bf16[4,4,48,384]{3,2,1,0:T(8,128)(2,1)}, bf16[4,4,48,384]{3,2,1,0:T(8,128)(2,1)S(1)}, u32[]{:S(2)}, u32[]{:S(2)}) collective-permute-start(bf16[4,4,48,384]{3,2,1,0:T(8,128)(2,1)} %stack_z.1.refs_0_), channel_id=1, source_target_pairs={{0,6},{1,7},{2,4},{3,5},{4,2},{5,3},{6,0},{7,1},{8,14},{9,15},{10,... | collective-permute-start | bytes 1769480 | tf_op jit(solution)/shard_map/ppermute | solution.py:52
  26.6 28.5 %collective-permute-start.6 = (bf16[4,4,48,384]{3,2,1,0:T(8,128)(2,1)}, bf16[4,4,48,384]{3,2,1,0:T(8,128)(2,1)S(1)}, u32[]{:S(2)}, u32[]{:S(2)}) collective-permute-start(bf16[4,4,48,384]{3,2,1,0:T(8,128)(2,1)} %stack_z.1.refs_0_), channel_id=1, source_target_pairs={{0,4},{1,5},{2,6},{3,7},{4,0},{5,1},{6,2},{7,3},{8,12},{9,13},{10,... | collective-permute-start | bytes 1769480 | tf_op jit(solution)/shard_map/ppermute | solution.py:52
  27.1 28.0 %collective-permute-start.5 = (bf16[4,4,48,384]{3,2,1,0:T(8,128)(2,1)}, bf16[4,4,48,384]{3,2,1,0:T(8,128)(2,1)S(1)}, u32[]{:S(2)}, u32[]{:S(2)}) collective-permute-start(bf16[4,4,48,384]{3,2,1,0:T(8,128)(2,1)} %stack_z.1.refs_0_), channel_id=1, source_target_pairs={{0,2},{1,3},{2,0},{3,1},{4,6},{5,7},{6,4},{7,5},{8,10},{9,11},{10,... | collective-permute-start | bytes 1769480 | tf_op jit(solution)/shard_map/ppermute | solution.py:52
  28.3 8.5 %copy-start.24 = (f32[50,768]{1,0:T(8,128)S(1)}, f32[50,768]{1,0:T(8,128)}, u32[]{:S(2)}) copy-start(f32[50,768]{1,0:T(8,128)} %param.15) | copy-start | bytes 460804
  28.3 9.3 %copy-start.37 = (s32[1024]{0:T(1024)S(1)}, s32[1024]{0:T(1024)}, u32[]{:S(2)}) copy-start(s32[1024]{0:T(1024)} %param.17) | copy-start | bytes 12292
  28.3 10.3 %copy-start.38 = (s32[1024]{0:T(1024)S(1)}, s32[1024]{0:T(1024)}, u32[]{:S(2)}) copy-start(s32[1024]{0:T(1024)} %param.16) | copy-start | bytes 12292
  30.0 15.5 %copy-start.35 = (f32[1,768]{1,0:T(1,128)}, f32[1,768]{1,0:T(1,128)S(1)}, u32[]{:S(2)}) copy-start(f32[1,768]{1,0:T(1,128)S(1)} %get-tuple-element.295.p_ref) | copy-start | bytes 9220
  30.0 22.8 %collective-permute-start.9 = (bf16[2,96,768]{2,1,0:T(8,128)(2,1)}, bf16[2,96,768]{2,1,0:T(8,128)(2,1)S(1)}, u32[]{:S(2)}, u32[]{:S(2)}) collective-permute-start(bf16[2,96,768]{2,1,0:T(8,128)(2,1)} %refs_0_), channel_id=1, source_target_pairs={{0,24},{1,25},{2,26},{3,27},{4,28},{5,29},{6,30},{7,31},{8,16},{9,... | collective-permute-start | bytes 884744 | tf_op jit(solution)/shard_map/ppermute | solution.py:52
  30.8 24.3 %collective-permute-start.8 = (bf16[2,96,768]{2,1,0:T(8,128)(2,1)}, bf16[2,96,768]{2,1,0:T(8,128)(2,1)S(1)}, u32[]{:S(2)}, u32[]{:S(2)}) collective-permute-start(bf16[2,96,768]{2,1,0:T(8,128)(2,1)} %refs_0_), channel_id=1, source_target_pairs={{0,16},{1,17},{2,18},{3,19},{4,20},{5,21},{6,22},{7,23},{8,24},{9,... | collective-permute-start | bytes 884744 | tf_op jit(solution)/shard_map/ppermute | solution.py:52
  52.8 6.9 %copy-start.22 = (bf16[2,96,768]{2,1,0:T(8,128)(2,1)}, bf16[2,96,768]{2,1,0:T(8,128)(2,1)S(1)}, u32[]{:S(2)}) copy-start(bf16[2,96,768]{2,1,0:T(8,128)(2,1)S(1)} %collective-permute-done.9.refs_3_) | copy-start | bytes 884740
  55.1 4.6 %copy-start.23 = (bf16[2,96,768]{2,1,0:T(8,128)(2,1)}, bf16[2,96,768]{2,1,0:T(8,128)(2,1)S(1)}, u32[]{:S(2)}) copy-start(bf16[2,96,768]{2,1,0:T(8,128)(2,1)S(1)} %collective-permute-done.8.refs_2_) | copy-start | bytes 884740
  62.0 9.4 %copy-start.5 = (bf16[4,96,768]{2,1,0:T(8,128)(2,1)S(1)}, bf16[4,96,768]{2,1,0:T(8,128)(2,1)}, u32[]{:S(2)}) copy-start(bf16[4,96,768]{2,1,0:T(8,128)(2,1)} %get-tuple-element.165.refs_5_) | copy-start | bytes 1769476
  62.0 9.4 %collective-permute-start.15 = (bf16[4,768,384]{2,1,0:T(8,128)(2,1)}, bf16[4,768,384]{2,1,0:T(8,128)(2,1)S(1)}, u32[]{:S(2)}, u32[]{:S(2)}) collective-permute-start(bf16[4,768,384]{2,1,0:T(8,128)(2,1)} %assemble.1.w_ref.own_ref.refs_0_), channel_id=1, source_target_pairs={{0,1},{1,0},{2,3},{3,2},{4,5},{5,4},{6,7},{7,6},{8,9},{9,8},{10,11... | collective-permute-start | bytes 7077896 | tf_op jit(solution)/shard_map/ppermute | solution.py:52
  62.0 16.6 %collective-permute-start.13 = (bf16[4,96,768]{2,1,0:T(8,128)(2,1)}, bf16[4,96,768]{2,1,0:T(8,128)(2,1)S(1)}, u32[]{:S(2)}, u32[]{:S(2)}) collective-permute-start(bf16[4,96,768]{2,1,0:T(8,128)(2,1)} %get-tuple-element.165.refs_5_), channel_id=1, source_target_pairs={{0,1},{1,0},{2,3},{3,2},{4,5},{5,4},{6,7},{7,6},{8,9},{9,8},{10,11... | collective-permute-start | bytes 1769480 | tf_op jit(solution)/shard_map/ppermute | solution.py:52
  62.5 16.7 %collective-permute-start.11 = (bf16[4,96,768]{2,1,0:T(8,128)(2,1)}, bf16[4,96,768]{2,1,0:T(8,128)(2,1)}, u32[]{:S(2)}, u32[]{:S(2)}) collective-permute-start(bf16[4,96,768]{2,1,0:T(8,128)(2,1)} %get-tuple-element.165.refs_5_), channel_id=1, source_target_pairs={{0,4},{1,5},{2,6},{3,7},{4,0},{5,1},{6,2},{7,3},{8,12},{9,13},{10,... | collective-permute-start | bytes 1769480 | tf_op jit(solution)/shard_map/ppermute | solution.py:52
  64.0 15.2 %collective-permute-start.14 = (bf16[4,96,768]{2,1,0:T(8,128)(2,1)}, bf16[4,96,768]{2,1,0:T(8,128)(2,1)}, u32[]{:S(2)}, u32[]{:S(2)}) collective-permute-start(bf16[4,96,768]{2,1,0:T(8,128)(2,1)} %get-tuple-element.166.refs_9_), channel_id=1, source_target_pairs={{0,1},{1,0},{2,3},{3,2},{4,5},{5,4},{6,7},{7,6},{8,9},{9,8},{10,11... | collective-permute-start | bytes 1769480 | tf_op jit(solution)/shard_map/ppermute | solution.py:52
  64.0 16.5 %collective-permute-start.12 = (bf16[4,96,768]{2,1,0:T(8,128)(2,1)}, bf16[4,96,768]{2,1,0:T(8,128)(2,1)}, u32[]{:S(2)}, u32[]{:S(2)}) collective-permute-start(bf16[4,96,768]{2,1,0:T(8,128)(2,1)} %get-tuple-element.166.refs_9_), channel_id=1, source_target_pairs={{0,2},{1,3},{2,0},{3,1},{4,6},{5,7},{6,4},{7,5},{8,10},{9,11},{10,... | collective-permute-start | bytes 1769480 | tf_op jit(solution)/shard_map/ppermute | solution.py:52
  71.4 7.3 %copy-start.6 = (bf16[4,96,768]{2,1,0:T(8,128)(2,1)S(1)}, bf16[4,96,768]{2,1,0:T(8,128)(2,1)}, u32[]{:S(2)}) copy-start(bf16[4,96,768]{2,1,0:T(8,128)(2,1)} %get-tuple-element.166.refs_9_) | copy-start | bytes 1769476
  71.4 32.2 %collective-permute-start.10 = (bf16[4,96,768]{2,1,0:T(8,128)(2,1)S(1)}, bf16[4,96,768]{2,1,0:T(8,128)(2,1)}, u32[]{:S(2)}, u32[]{:S(2)}) collective-permute-start(bf16[4,96,768]{2,1,0:T(8,128)(2,1)S(1)} %copy-done.5), channel_id=1, source_target_pairs={{0,2},{1,3},{2,0},{3,1},{4,6},{5,7},{6,4},{7,5},{8,10},{9,11},{10,... | collective-permute-start | bytes 1769480 | tf_op jit(solution)/shard_map/ppermute | solution.py:52
  78.6 25.0 %copy-start.7 = (bf16[4,96,768]{2,1,0:T(8,128)(2,1)}, bf16[4,96,768]{2,1,0:T(8,128)(2,1)S(1)}, u32[]{:S(2)}) copy-start(bf16[4,96,768]{2,1,0:T(8,128)(2,1)S(1)} %collective-permute-done.13.refs_13_) | copy-start | bytes 1769476
  78.6 25.5 %collective-permute-start.17 = (bf16[4,96,768]{2,1,0:T(8,128)(2,1)S(1)}, bf16[4,96,768]{2,1,0:T(8,128)(2,1)S(1)}, u32[]{:S(2)}, u32[]{:S(2)}) collective-permute-start(bf16[4,96,768]{2,1,0:T(8,128)(2,1)S(1)} %copy-done.6), channel_id=1, source_target_pairs={{0,4},{1,5},{2,6},{3,7},{4,0},{5,1},{6,2},{7,3},{8,12},{9,13},{10,... | collective-permute-start | bytes 1769480 | tf_op jit(solution)/shard_map/ppermute | solution.py:52
  80.5 24.7 %collective-permute-start.16 = (bf16[4,96,768]{2,1,0:T(8,128)(2,1)}, bf16[4,96,768]{2,1,0:T(8,128)(2,1)S(1)}, u32[]{:S(2)}, u32[]{:S(2)}) collective-permute-start(bf16[4,96,768]{2,1,0:T(8,128)(2,1)} %collective-permute-done.11.refs_7_), channel_id=1, source_target_pairs={{0,2},{1,3},{2,0},{3,1},{4,6},{5,7},{6,4},{7,5},{8,10},{9,11},{10,... | collective-permute-start | bytes 1769480 | tf_op jit(solution)/shard_map/ppermute | solution.py:52
  82.0 24.8 %collective-permute-start.18 = (bf16[4,96,768]{2,1,0:T(8,128)(2,1)}, bf16[4,96,768]{2,1,0:T(8,128)(2,1)S(1)}, u32[]{:S(2)}, u32[]{:S(2)}) collective-permute-start(bf16[4,96,768]{2,1,0:T(8,128)(2,1)} %collective-permute-done.12.refs_10_), channel_id=1, source_target_pairs={{0,4},{1,5},{2,6},{3,7},{4,0},{5,1},{6,2},{7,3},{8,12},{9,13},{10,... | collective-permute-start | bytes 1769480 | tf_op jit(solution)/shard_map/ppermute | solution.py:52
  82.5 24.8 %collective-permute-start.20 = (bf16[4,96,768]{2,1,0:T(8,128)(2,1)}, bf16[4,96,768]{2,1,0:T(8,128)(2,1)S(1)}, u32[]{:S(2)}, u32[]{:S(2)}) collective-permute-start(bf16[4,96,768]{2,1,0:T(8,128)(2,1)} %collective-permute-done.11.refs_7_), channel_id=1, source_target_pairs={{0,1},{1,0},{2,3},{3,2},{4,5},{5,4},{6,7},{7,6},{8,9},{9,8},{10,11... | collective-permute-start | bytes 1769480 | tf_op jit(solution)/shard_map/ppermute | solution.py:52
  103.6 10.2 %collective-permute-start.22 = (bf16[4,96,768]{2,1,0:T(8,128)(2,1)}, bf16[4,96,768]{2,1,0:T(8,128)(2,1)S(1)}, u32[]{:S(2)}, u32[]{:S(2)}) collective-permute-start(bf16[4,96,768]{2,1,0:T(8,128)(2,1)} %collective-permute-done.12.refs_10_), channel_id=1, source_target_pairs={{0,1},{1,0},{2,3},{3,2},{4,5},{5,4},{6,7},{7,6},{8,9},{9,8},{10,11... | collective-permute-start | bytes 1769480 | tf_op jit(solution)/shard_map/ppermute | solution.py:52
  104.2 9.6 %copy-start.8 = (bf16[4,96,768]{2,1,0:T(8,128)(2,1)}, bf16[4,96,768]{2,1,0:T(8,128)(2,1)S(1)}, u32[]{:S(2)}) copy-start(bf16[4,96,768]{2,1,0:T(8,128)(2,1)S(1)} %collective-permute-done.17.refs_11_) | copy-start | bytes 1769476
  105.3 8.5 %copy-start.9 = (bf16[4,96,768]{2,1,0:T(8,128)(2,1)}, bf16[4,96,768]{2,1,0:T(8,128)(2,1)S(1)}, u32[]{:S(2)}) copy-start(bf16[4,96,768]{2,1,0:T(8,128)(2,1)S(1)} %collective-permute-done.16.refs_8_) | copy-start | bytes 1769476
  106.8 7.0 %copy-start.10 = (bf16[4,96,768]{2,1,0:T(8,128)(2,1)}, bf16[4,96,768]{2,1,0:T(8,128)(2,1)S(1)}, u32[]{:S(2)}) copy-start(bf16[4,96,768]{2,1,0:T(8,128)(2,1)S(1)} %collective-permute-done.18.refs_12_) | copy-start | bytes 1769476
  106.8 7.0 %collective-permute-start.19 = (bf16[4,96,768]{2,1,0:T(8,128)(2,1)}, bf16[4,96,768]{2,1,0:T(8,128)(2,1)S(1)}, u32[]{:S(2)}, u32[]{:S(2)}) collective-permute-start(bf16[4,96,768]{2,1,0:T(8,128)(2,1)} %collective-permute-done.10.refs_6_), channel_id=1, source_target_pairs={{0,1},{1,0},{2,3},{3,2},{4,5},{5,4},{6,7},{7,6},{8,9},{9,8},{10,11... | collective-permute-start | bytes 1769480 | tf_op jit(solution)/shard_map/ppermute | solution.py:52
  106.8 7.0 %collective-permute-start.21 = (bf16[4,96,768]{2,1,0:T(8,128)(2,1)S(1)}, bf16[4,96,768]{2,1,0:T(8,128)(2,1)S(1)}, u32[]{:S(2)}, u32[]{:S(2)}) collective-permute-start(bf16[4,96,768]{2,1,0:T(8,128)(2,1)S(1)} %collective-permute-done.16.refs_8_), channel_id=1, source_target_pairs={{0,1},{1,0},{2,3},{3,2},{4,5},{5,4},{6,7},{7,6},{8,9},{9,8},{10,11... | collective-permute-start | bytes 1769480 | tf_op jit(solution)/shard_map/ppermute | solution.py:52
  107.3 6.5 %collective-permute-start.23 = (bf16[4,96,768]{2,1,0:T(8,128)(2,1)S(1)}, bf16[4,96,768]{2,1,0:T(8,128)(2,1)}, u32[]{:S(2)}, u32[]{:S(2)}) collective-permute-start(bf16[4,96,768]{2,1,0:T(8,128)(2,1)S(1)} %collective-permute-done.17.refs_11_), channel_id=1, source_target_pairs={{0,1},{1,0},{2,3},{3,2},{4,5},{5,4},{6,7},{7,6},{8,9},{9,8},{10,11... | collective-permute-start | bytes 1769480 | tf_op jit(solution)/shard_map/ppermute | solution.py:52
  107.3 6.5 %copy-start.11 = (bf16[4,96,768]{2,1,0:T(8,128)(2,1)}, bf16[4,96,768]{2,1,0:T(8,128)(2,1)S(1)}, u32[]{:S(2)}) copy-start(bf16[4,96,768]{2,1,0:T(8,128)(2,1)S(1)} %collective-permute-done.20.refs_15_) | copy-start | bytes 1769476
  107.3 6.5 %collective-permute-start.24 = (bf16[4,96,768]{2,1,0:T(8,128)(2,1)S(1)}, bf16[4,96,768]{2,1,0:T(8,128)(2,1)}, u32[]{:S(2)}, u32[]{:S(2)}) collective-permute-start(bf16[4,96,768]{2,1,0:T(8,128)(2,1)S(1)} %collective-permute-done.18.refs_12_), channel_id=1, source_target_pairs={{0,1},{1,0},{2,3},{3,2},{4,5},{5,4},{6,7},{7,6},{8,9},{9,8},{10,11... | collective-permute-start | bytes 1769480 | tf_op jit(solution)/shard_map/ppermute | solution.py:52
  161.9 11.3 %collective-permute-start.25 = (bf16[2,4,4,96,768]{4,3,2,1,0:T(8,128)(2,1)}, bf16[2,4,4,96,768]{4,3,2,1,0:T(8,128)(2,1)}, u32[]{:S(2)}, u32[]{:S(2)}) collective-permute-start(bf16[2,4,4,96,768]{4,3,2,1,0:T(8,128)(2,1)} %get-tuple-element.199), channel_id=1, source_target_pairs={{0,1},{1,0},{2,3},{3,2},{4,5},{5,4},{6,7},{7,6},{8,9},{9,8},{10,11... | collective-permute-start | bytes 14155784 | tf_op jit(solution)/shard_map/ppermute | solution.py:52
  177.3 33.0 %collective-permute-start.26 = (bf16[2,4,96,768]{3,2,1,0:T(8,128)(2,1)}, bf16[2,4,96,768]{3,2,1,0:T(8,128)(2,1)S(1)}, u32[]{:S(2)}, u32[]{:S(2)}) collective-permute-start(bf16[2,4,96,768]{3,2,1,0:T(8,128)(2,1)} %get-tuple-element.205), channel_id=1, source_target_pairs={{0,2},{1,3},{2,0},{3,1},{4,6},{5,7},{6,4},{7,5},{8,10},{9,11},{10,... | collective-permute-start | bytes 3538952 | tf_op jit(solution)/shard_map/ppermute | solution.py:52
  177.8 32.5 %collective-permute-start.27 = (bf16[2,4,96,768]{3,2,1,0:T(8,128)(2,1)S(1)}, bf16[2,4,96,768]{3,2,1,0:T(8,128)(2,1)S(1)}, u32[]{:S(2)}, u32[]{:S(2)}) collective-permute-start(bf16[2,4,96,768]{3,2,1,0:T(8,128)(2,1)S(1)} %get-tuple-element.206), channel_id=1, source_target_pairs={{0,4},{1,5},{2,6},{3,7},{4,0},{5,1},{6,2},{7,3},{8,12},{9,13},{10,... | collective-permute-start | bytes 3538952 | tf_op jit(solution)/shard_map/ppermute | solution.py:52
  178.3 32.0 %collective-permute-start.28 = (bf16[4,4,1,24,768]{4,3,2,1,0:T(8,128)(2,1)}, bf16[4,4,1,24,768]{4,3,2,1,0:T(8,128)(2,1)S(1)}, u32[]{:S(2)}, u32[]{:S(2)}) collective-permute-start(bf16[4,4,1,24,768]{4,3,2,1,0:T(8,128)(2,1)} %get-tuple-element.207), channel_id=1, source_target_pairs={{0,1},{1,0},{2,3},{3,2},{4,5},{5,4},{6,7},{7,6},{8,9},{9,8},{10,11... | collective-permute-start | bytes 1769480 | tf_op jit(solution)/shard_map/ppermute | solution.py:52
  213.0 17.8 %collective-permute-start.29 = (bf16[4,96,768]{2,1,0:T(8,128)(2,1)S(1)}, bf16[4,96,768]{2,1,0:T(8,128)(2,1)S(1)}, u32[]{:S(2)}, u32[]{:S(2)}) collective-permute-start(bf16[4,96,768]{2,1,0:T(8,128)(2,1)S(1)} %get-tuple-element.228), channel_id=1, source_target_pairs={{0,4},{1,5},{2,6},{3,7},{4,0},{5,1},{6,2},{7,3},{8,12},{9,13},{10,... | collective-permute-start | bytes 1769480 | tf_op jit(solution)/shard_map/ppermute | solution.py:52
  214.6 16.2 %collective-permute-start.30 = (bf16[4,96,768]{2,1,0:T(8,128)(2,1)S(1)}, bf16[4,96,768]{2,1,0:T(8,128)(2,1)S(1)}, u32[]{:S(2)}, u32[]{:S(2)}) collective-permute-start(bf16[4,96,768]{2,1,0:T(8,128)(2,1)S(1)} %get-tuple-element.229), channel_id=1, source_target_pairs={{0,2},{1,3},{2,0},{3,1},{4,6},{5,7},{6,4},{7,5},{8,10},{9,11},{10,... | collective-permute-start | bytes 1769480 | tf_op jit(solution)/shard_map/ppermute | solution.py:52
  230.8 9.4 %copy-start.18 = (bf16[4,96,768]{2,1,0:T(8,128)(2,1)}, bf16[4,96,768]{2,1,0:T(8,128)(2,1)S(1)}, u32[]{:S(2)}) copy-start(bf16[4,96,768]{2,1,0:T(8,128)(2,1)S(1)} %collective-permute-done.30) | copy-start | bytes 1769476
  230.8 9.7 %copy-start.28 = (bf16[96,768]{1,0:T(8,128)(2,1)S(1)}, bf16[96,768]{1,0:T(8,128)(2,1)}, u32[]{:S(2)}) copy-start(bf16[96,768]{1,0:T(8,128)(2,1)} %get-tuple-element.236) | copy-start | bytes 442372
  230.9 9.0 %collective-permute-start.31 = (bf16[96,768]{1,0:T(8,128)(2,1)}, bf16[96,768]{1,0:T(8,128)(2,1)S(1)}, u32[]{:S(2)}, u32[]{:S(2)}) collective-permute-start(bf16[96,768]{1,0:T(8,128)(2,1)} %get-tuple-element.236), channel_id=1, source_target_pairs={{0,1},{1,0},{2,3},{3,2},{4,5},{5,4},{6,7},{7,6},{8,9},{9,8},{10,11... | collective-permute-start | bytes 442376 | tf_op jit(solution)/shard_map/ppermute | solution.py:52
  239.9 9.5 %collective-permute-start.32 = (bf16[4,4,3,24,768]{4,3,2,1,0:T(8,128)(2,1)}, bf16[4,4,3,24,768]{4,3,2,1,0:T(8,128)(2,1)S(1)}, u32[]{:S(2)}, u32[]{:S(2)}) collective-permute-start(bf16[4,4,3,24,768]{4,3,2,1,0:T(8,128)(2,1)} %get-tuple-element.238), channel_id=1, source_target_pairs={{0,1},{1,0},{2,3},{3,2},{4,5},{5,4},{6,7},{7,6},{8,9},{9,8},{10,11... | collective-permute-start | bytes 5308424 | tf_op jit(solution)/shard_map/ppermute | solution.py:52
  243.2 6.1 %collective-permute-start.33 = (bf16[96,768]{1,0:T(8,128)(2,1)S(1)}, bf16[96,768]{1,0:T(8,128)(2,1)S(1)}, u32[]{:S(2)}, u32[]{:S(2)}) collective-permute-start(bf16[96,768]{1,0:T(8,128)(2,1)S(1)} %pad_maximum_fusion.2), channel_id=1, source_target_pairs={{0,2},{1,3},{2,0},{3,1},{4,6},{5,7},{6,4},{7,5},{8,10},{9,11},{10,... | collective-permute-start | bytes 442376 | tf_op jit(solution)/shard_map/ppermute | solution.py:52
  249.5 5.3 %collective-permute-start.34 = (bf16[96,768]{1,0:T(8,128)(2,1)S(1)}, bf16[96,768]{1,0:T(8,128)(2,1)S(1)}, u32[]{:S(2)}, u32[]{:S(2)}) collective-permute-start(bf16[96,768]{1,0:T(8,128)(2,1)S(1)} %pad_maximum_fusion.3), channel_id=1, source_target_pairs={{0,4},{1,5},{2,6},{3,7},{4,0},{5,1},{6,2},{7,3},{8,12},{9,13},{10,... | collective-permute-start | bytes 442376 | tf_op jit(solution)/shard_map/ppermute | solution.py:52
  254.8 22.2 %collective-permute-start.35 = (bf16[4,4,24,768]{3,2,1,0:T(8,128)(2,1)}, bf16[4,4,24,768]{3,2,1,0:T(8,128)(2,1)S(1)}, u32[]{:S(2)}, u32[]{:S(2)}) collective-permute-start(bf16[4,4,24,768]{3,2,1,0:T(8,128)(2,1)} %get-tuple-element.248), channel_id=1, source_target_pairs={{0,2},{1,3},{2,0},{3,1},{4,6},{5,7},{6,4},{7,5},{8,10},{9,11},{10,... | collective-permute-start | bytes 1769480 | tf_op jit(solution)/shard_map/ppermute | solution.py:52
  255.6 27.2 %collective-permute-start.36 = (bf16[4,4,24,768]{3,2,1,0:T(8,128)(2,1)}, bf16[4,4,24,768]{3,2,1,0:T(8,128)(2,1)S(1)}, u32[]{:S(2)}, u32[]{:S(2)}) collective-permute-start(bf16[4,4,24,768]{3,2,1,0:T(8,128)(2,1)} %get-tuple-element.249), channel_id=1, source_target_pairs={{0,4},{1,5},{2,6},{3,7},{4,0},{5,1},{6,2},{7,3},{8,12},{9,13},{10,... | collective-permute-start | bytes 1769480 | tf_op jit(solution)/shard_map/ppermute | solution.py:52
  256.6 26.1 %collective-permute-start.37 = (bf16[4,4,24,768]{3,2,1,0:T(8,128)(2,1)}, bf16[4,4,24,768]{3,2,1,0:T(8,128)(2,1)S(1)}, u32[]{:S(2)}, u32[]{:S(2)}) collective-permute-start(bf16[4,4,24,768]{3,2,1,0:T(8,128)(2,1)} %get-tuple-element.250), channel_id=1, source_target_pairs={{0,6},{1,7},{2,4},{3,5},{4,2},{5,3},{6,0},{7,1},{8,14},{9,15},{10,... | collective-permute-start | bytes 1769480 | tf_op jit(solution)/shard_map/ppermute | solution.py:52
  258.4 27.0 %collective-permute-start.38 = (bf16[2,2,96,768]{3,2,1,0:T(8,128)(2,1)S(1)}, bf16[2,2,96,768]{3,2,1,0:T(8,128)(2,1)S(1)}, u32[]{:S(2)}, u32[]{:S(2)}) collective-permute-start(bf16[2,2,96,768]{3,2,1,0:T(8,128)(2,1)S(1)} %pad_maximum_fusion), channel_id=1, source_target_pairs={{0,16},{1,17},{2,18},{3,19},{4,20},{5,21},{6,22},{7,23},{8,24},{9,... | collective-permute-start | bytes 1769480 | tf_op jit(solution)/shard_map/ppermute | solution.py:52
  261.7 15.3 %collective-permute-start.39 = (bf16[96,768]{1,0:T(8,128)(2,1)S(1)}, bf16[96,768]{1,0:T(8,128)(2,1)S(1)}, u32[]{:S(2)}, u32[]{:S(2)}) collective-permute-start(bf16[96,768]{1,0:T(8,128)(2,1)S(1)} %pad_maximum_fusion.4), channel_id=1, source_target_pairs={{0,8},{1,9},{2,10},{3,11},{4,12},{5,13},{6,14},{7,15},{8,0},{9,1},... | collective-permute-start | bytes 442376 | tf_op jit(solution)/shard_map/ppermute | solution.py:52
  277.0 12.2 %copy-start.19 = (bf16[4,4,24,768]{3,2,1,0:T(8,128)(2,1)}, bf16[4,4,24,768]{3,2,1,0:T(8,128)(2,1)S(1)}, u32[]{:S(2)}) copy-start(bf16[4,4,24,768]{3,2,1,0:T(8,128)(2,1)S(1)} %collective-permute-done.35.refs_0_) | copy-start | bytes 1769476
  285.6 11.0 %collective-permute-start.40 = (bf16[96,768]{1,0:T(8,128)(2,1)S(1)}, bf16[96,768]{1,0:T(8,128)(2,1)S(1)}, u32[]{:S(2)}, u32[]{:S(2)}) collective-permute-start(bf16[96,768]{1,0:T(8,128)(2,1)S(1)} %get-tuple-element.288), channel_id=1, source_target_pairs={{0,16},{1,17},{2,18},{3,19},{4,20},{5,21},{6,22},{7,23},{8,24},{9,... | collective-permute-start | bytes 442376 | tf_op jit(solution)/shard_map/ppermute | solution.py:52
  292.0 9.0 %collective-permute-start.41 = (bf16[4,24,768]{2,1,0:T(8,128)(2,1)}, bf16[4,24,768]{2,1,0:T(8,128)(2,1)S(1)}, u32[]{:S(2)}, u32[]{:S(2)}) collective-permute-start(bf16[4,24,768]{2,1,0:T(8,128)(2,1)} %get-tuple-element.265), channel_id=1, source_target_pairs={{0,8},{1,9},{2,10},{3,11},{4,12},{5,13},{6,14},{7,15},{8,0},{9,1},... | collective-permute-start | bytes 442376 | tf_op jit(solution)/shard_map/ppermute | solution.py:52
  292.1 12.7 %collective-permute-start.42 = (bf16[4,24,768]{2,1,0:T(8,128)(2,1)}, bf16[4,24,768]{2,1,0:T(8,128)(2,1)S(1)}, u32[]{:S(2)}, u32[]{:S(2)}) collective-permute-start(bf16[4,24,768]{2,1,0:T(8,128)(2,1)} %get-tuple-element.266), channel_id=1, source_target_pairs={{0,16},{1,17},{2,18},{3,19},{4,20},{5,21},{6,22},{7,23},{8,24},{9,... | collective-permute-start | bytes 442376 | tf_op jit(solution)/shard_map/ppermute | solution.py:52
  294.1 14.9 %collective-permute-start.43 = (bf16[4,24,768]{2,1,0:T(8,128)(2,1)}, bf16[4,24,768]{2,1,0:T(8,128)(2,1)S(1)}, u32[]{:S(2)}, u32[]{:S(2)}) collective-permute-start(bf16[4,24,768]{2,1,0:T(8,128)(2,1)} %get-tuple-element.267), channel_id=1, source_target_pairs={{0,24},{1,25},{2,26},{3,27},{4,28},{5,29},{6,30},{7,31},{8,16},{9,... | collective-permute-start | bytes 442376 | tf_op jit(solution)/shard_map/ppermute | solution.py:52
  295.6 17.2 %collective-permute-start.44 = (bf16[2,96,768]{2,1,0:T(8,128)(2,1)S(1)}, bf16[2,96,768]{2,1,0:T(8,128)(2,1)S(1)}, u32[]{:S(2)}, u32[]{:S(2)}) collective-permute-start(bf16[2,96,768]{2,1,0:T(8,128)(2,1)S(1)} %pad_maximum_fusion.1), channel_id=1, source_target_pairs={{0,8},{1,9},{2,10},{3,11},{4,12},{5,13},{6,14},{7,15},{8,0},{9,1},... | collective-permute-start | bytes 884744 | tf_op jit(solution)/shard_map/ppermute | solution.py:52
  301.1 7.9 %copy-start.31 = (bf16[4,24,768]{2,1,0:T(8,128)(2,1)}, bf16[4,24,768]{2,1,0:T(8,128)(2,1)S(1)}, u32[]{:S(2)}) copy-start(bf16[4,24,768]{2,1,0:T(8,128)(2,1)S(1)} %collective-permute-done.41.refs_0_) | copy-start | bytes 442372
  (21 other events, 34.5 us)

commit v5 on v4

--- a/solution.py
+++ b/solution.py
@@ -440,7 +440,7 @@
     slots = slots_ref[...]
     is_prompt = jnp.sum(slots.astype(F32), axis=-1, keepdims=True) > 0.5
     input_ref[...] = jnp.where(is_prompt, 0.0, gstart)
-    for part in three_parts(gstart):
+    for part in three_parts(gstart)[:2]:
         prompt_ref[...] += dotf(slots, part.astype(B16), TN)
 
     @pl.when(pl.program_id(0) == pl.num_programs(0) - 1)
@@ -878,6 +878,7 @@
         got_small, other_w = tie(got_small, other_w)
         got_w = px(other_w, 1)
         packed = pack_small(add_small(packed, got_small))
+        packed, got_1, got_2 = tie(packed, got_1, got_2)
         got_small = px(packed, 2)
         got_w, got_small, packed = tie(got_w, got_small, packed)
         packed = pack_small(add_small(packed, got_small))

time: 316 us -> 313 us (level)
  transfers between devices with their start and end apart: 45 -> 45, of which waited for: 15 -> 15; matrix products, arithmetic and copies ran while one was open for 4% -> 4% of each run, Pallas kernels for 39% -> 40%
where the time goes in v5:
time: 313 us; the launch traced here: 310 us
  Pallas kernels  177 us (57%)
  waiting for transfers between devices  60.7 us (19%)
  starting transfers between devices  43.8 us (14%)
  local copies, waits for them, and re-layouts  14.3 us (5%)
  other arithmetic  13 us (4%)
    ppermute x45, waiting for transfers between devices, px(): return lax.ppermute(x, AXES, [(i, i ^ k) for i in range(32)])  60.7 us
    pallas_call x1, Pallas kernels, mlp(): pl.pallas_call(partial(mlp_kernel, fast), name='mlp', grid=(4 * PER,), in...  46.8 us
    ppermute x45, starting transfers between devices, px(): return lax.ppermute(x, AXES, [(i, i ^ k) for i in range(32)])  43.8 us
    pallas_call x1, Pallas kernels, attention_backward(): pl.pallas_call(kernel, name='attention_backward', grid_spec=pltpu.Prefetc...  31.9 us
    pallas_call x1, Pallas kernels, attention_forward(): pl.pallas_call(kernel, name='attention_forward', grid_spec=pltpu.Prefetch...  21.1 us
    pallas_call x1, Pallas kernels, tail_step(): pl.pallas_call(tail_kernel, name='tail_step', grid=(rows // STEP,), in_sp...  14.2 us
    pallas_call x2, Pallas kernels, project(): pl.pallas_call(partial(project_kernel, side), name='project', grid=(3,),...  11.7 us
    pallas_call x1, Pallas kernels, turn(): pl.pallas_call(turn_kernel, name='turn', grid=(rows // STEP,), in_specs=[...  11 us
  transfers between devices with their start and end apart: 45, of which 15 were waited for; matrix products, arithmetic and copies ran while one was open for 4% of the time, Pallas kernels for 40%

profile of v5, /device:TPU:16, one launch (start us, length us, event | category | flops | bytes accessed | tf_op | source)
XLA Modules:
  0.0 310.1 jit_solution(10666710352622152834)
XLA Ops:
  0.7 1.7 split.1
  2.4 1.6 collective-permute-start.4
  4.7 1.6 join.1.refs_0_
  6.5 3.5 %collective-permute-start.2 = (bf16[4,48,384]{2,1,0:T(8,128)(2,1)}, bf16[4,48,384]{2,1,0:T(8,128)(2,1)S(1)}, u32[]{:S(2)}, u32[]{:S(2)}) collective-permute-start(bf16[4,48,384]{2,1,0:T(8,128)(2,1)} %join.1.refs_0_), channel_id=1, source_target_pairs={{0,16},{1,17},{2,18},{3,19},{4,20},{5,21},{6,22},{7,23},{8,24},{9,... | collective-permute-start | bytes 442376 | tf_op jit(solution)/shard_map/ppermute | solution.py:52
  10.0 0.8 fusion.21
  10.9 8.6 %collective-permute-done.3.refs_3_ = bf16[4,48,384]{2,1,0:T(8,128)(2,1)S(1)} collective-permute-done((bf16[4,48,384]{2,1,0:T(8,128)(2,1)}, bf16[4,48,384]{2,1,0:T(8,128)(2,1)S(1)}, u32[]{:S(2)}, u32[]{:S(2)}) %collective-permute-start.3) | collective-permute-done | bytes 147488 | tf_op jit(solution)/shard_map/ppermute | solution.py:52
  19.9 1.6 collective-permute-done.1.refs_1_
  22.1 2.0 stack_z.1.refs_0_
  24.1 2.4 collective-permute-start.7
  28.3 1.6 copy.28
  30.0 0.8 collective-permute-start.9
  30.8 4.2 %collective-permute-start.8 = (bf16[2,96,768]{2,1,0:T(8,128)(2,1)}, bf16[2,96,768]{2,1,0:T(8,128)(2,1)S(1)}, u32[]{:S(2)}, u32[]{:S(2)}) collective-permute-start(bf16[2,96,768]{2,1,0:T(8,128)(2,1)} %refs_0_), channel_id=1, source_target_pairs={{0,16},{1,17},{2,18},{3,19},{4,20},{5,21},{6,22},{7,23},{8,24},{9,... | collective-permute-start | bytes 884744 | tf_op jit(solution)/shard_map/ppermute | solution.py:52
  36.8 0.8 concatenate.15.table_ref
  37.6 1.0 copy.26.slots_ref
  38.6 1.0 copy.27.segs_ref
  39.6 5.9 %embed.1 = (f32[1024,768]{1,0:T(8,128)}, bf16[1024,768]{1,0:T(8,128)(2,1)}, bf16[1024,128]{1,0:T(8,128)(2,1)}, bf16[1024,128]{1,0:T(8,128)(2,1)}, bf16[1024,128]{1,0:T(8,128)(2,1)}) custom-call(bf16[1024,768]{1,0:T(8,128)(2,1)} %tokens_ref, s32[1024,1]{1,0:T(8,128)} %copy.26.slots_ref, s32[1024,1]{1,0:T(8,128)} %copy.27.segs_ref, ...), custom_call_target="tpu_custom_call" | custom-call | tf_op jit(solution)/shard_map/embed/pallas_call | solution.py:215
  45.5 7.3 %collective-permute-done.9.refs_3_ = bf16[2,96,768]{2,1,0:T(8,128)(2,1)S(1)} collective-permute-done((bf16[2,96,768]{2,1,0:T(8,128)(2,1)}, bf16[2,96,768]{2,1,0:T(8,128)(2,1)S(1)}, u32[]{:S(2)}, u32[]{:S(2)}) %collective-permute-start.9) | collective-permute-done | bytes 294944 | tf_op jit(solution)/shard_map/ppermute | solution.py:52
  52.8 2.3 collective-permute-done.8.refs_2_
  55.1 0.8 copy-done.13
  56.3 3.3 %assemble.1.w_ref.own_ref.refs_0_ = bf16[4,768,384]{2,1,0:T(8,128)(2,1)} custom-call(s32[1]{0:T(128)} %bitcast.meta.refs_0_, bf16[4,4,48,384]{3,2,1,0:T(8,128)(2,1)} %stack_z.1.refs_0_, bf16[4,4,48,384]{3,2,1,0:T(8,128)(2,1)} %copy-done.18, bf16[4,4,48,384]{3,2,1,0:T(8,128)(2,1)} %copy-done.14, bf16[4,4,48,384]{3,2,1,0:T(8,128)(2,1)} %copy-done.13), custom_call_target="tpu_custom_call" | custom-call | tf_op jit(solution)/shard_map/assemble/pallas_call | solution.py:149
  59.7 2.3 stack_pair.1
  62.5 1.5 collective-permute-start.11
  64.0 1.5 collective-permute-start.12
  65.5 5.8 %project.2.refs_0_ = bf16[1024,2304]{1,0:T(8,128)(2,1)} custom-call(s32[1]{0:T(128)} %bitcast.meta.refs_0_, bf16[1024,768]{1,0:T(8,128)(2,1)} %get-tuple-element.170.x_ref.left_ref, bf16[4,768,384]{2,1,0:T(8,128)(2,1)} %assemble.1.w_ref.own_ref.refs_0_, f32[3,1,768]{2,1,0:T(1,128)} %broadcast_in_dim.12.b_ref), custom_call_target="tpu_custom_call" | custom-call | tf_op jit(solution)/shard_map/project/pallas_call | solution.py:169
  72.0 0.8 copy-done
  72.8 5.8 %project.3.refs_2_.refs_3_.refs_4_ = bf16[1024,2304]{1,0:T(8,128)(2,1)} custom-call(s32[1]{0:T(128)} %bitcast.meta.refs_0_, bf16[1024,768]{1,0:T(8,128)(2,1)} %get-tuple-element.170.x_ref.left_ref, bf16[4,768,384]{2,1,0:T(8,128)(2,1)} %copy-done, f32[3,1,768]{2,1,0:T(1,128)} %broadcast_in_dim.12.b_ref, ...), custom_call_target="tpu_custom_call", output_to_operand_aliasing={{}: (4, {})} | custom-call | tf_op jit(solution)/shard_map/project/pallas_call | solution.py:169
  79.2 1.3 collective-permute-done.12.refs_10_
  80.5 1.5 collective-permute-start.16
  82.5 21.1 %attention_forward.1 = (bf16[1024,768]{1,0:T(8,128)(2,1)}, f32[1024,768]{1,0:T(8,128)}) custom-call(s32[1]{0:T(128)} %bitcast.meta.refs_0_, bf16[1024,128]{1,0:T(8,128)(2,1)} %get-tuple-element.177.refs_0_, bf16[1024,128]{1,0:T(8,128)(2,1)} %get-tuple-element.178.refs_1_, bf16[1024,2304]{1,0:T(8,128)(2,1)} %project.3.refs_2_.refs_3_.refs_4_, ...), custom_call_target="tpu_custom_call" | custom-call | tf_op jit(solution)/shard_map/attention_forward/pallas_call | solution.py:572
  104.2 1.1 collective-permute-done.16.refs_8_
  105.3 1.5 collective-permute-done.18.refs_12_
  107.8 5.9 %out_projection.1 = (f32[1024,768]{1,0:T(8,128)}, bf16[1024,768]{1,0:T(8,128)(2,1)}, bf16[768,768]{1,0:T(8,128)(2,1)}) custom-call(s32[1]{0:T(128)} %bitcast.meta.refs_0_, bf16[1024,768]{1,0:T(8,128)(2,1)} %get-tuple-element.181.x_ref.mixed_ref.refs_6_, f32[1024,768]{1,0:T(8,128)} %get-tuple-element.182.start_ref, ...), custom_call_target="tpu_custom_call" | custom-call | tf_op jit(solution)/shard_map/out_projection/pallas_call | solution.py:331
  113.9 0.7 copy-done.15
  115.0 46.8 %mlp.1 = (f32[1024,768]{1,0:T(8,128)}, f32[1024,768]{1,0:T(8,128)}, f32[4,1,768]{2,1,0:T(1,128)}, bf16[2,4,4,96,768]{4,3,2,1,0:T(8,128)(2,1)}, bf16[2,4,4,96,768]{4,3,2,1,0:T(8,128)(2,1)}) custom-call(s32[1]{0:T(128)} %bitcast.meta.refs_0_, bf16[1024,768]{1,0:T(8,128)(2,1)} %get-tuple-element.185.refs_1_, bf16[1024,768]{1,0:T(8,128)(2,1)} %cot_ref.1, ...), custom_call_target="tpu_custom_call" | custom-call | tf_op jit(solution)/shard_map/mlp/pallas_call | solution.py:754
  162.2 11.0 %turn.1 = (bf16[1024,768]{1,0:T(8,128)(2,1)}, f32[1024,768]{1,0:T(8,128)}, bf16[1024,768]{1,0:T(8,128)(2,1)}, bf16[4,4,1,24,768]{4,3,2,1,0:T(8,128)(2,1)}, bf16[...) custom-call(s32[1]{0:T(128)} %bitcast.meta.refs_0_, f32[1024,768]{1,0:T(8,128)} %get-tuple-element.184.middle_ref, ...), custom_call_target="tpu_custom_call" | custom-call | tf_op jit(solution)/shard_map/turn/pallas_call | solution.py:399
  173.2 4.1 %fusion.1 = (bf16[2,4,96,768]{3,2,1,0:T(8,128)(2,1)S(1)}, bf16[2,4,96,768]{3,2,1,0:T(8,128)(2,1)}) fusion(bf16[2,4,4,96,768]{4,3,2,1,0:T(8,128)(2,1)} %collective-permute-done.25, bf16[2,4,4,96,768]{4,3,2,1,0:T(8,128)(2,1)} %get-tuple-element.201), kind=kLoop, calls=%fused_computation.3 | loop fusion | flops 4718592 | bytes 7077888 | tf_op jit(solution)/shard_map/convert_element_type | solution.py:858
  178.3 31.9 %attention_backward.1 = (bf16[1024,768]{1,0:T(8,128)(2,1)}, bf16[1024,768]{1,0:T(8,128)(2,1)}, bf16[1024,768]{1,0:T(8,128)(2,1)}) custom-call(s32[1]{0:T(128)} %bitcast.meta.refs_0_, bf16[1024,128]{1,0:T(8,128)(2,1)} %get-tuple-element.177.refs_0_, bf16[1024,128]{1,0:T(8,128)(2,1)} %get-tuple-element.178.refs_1_, ...), custom_call_target="tpu_custom_call" | custom-call | tf_op jit(solution)/shard_map/attention_backward/pallas_call | solution.py:647
  210.3 2.7 fusion.4
  213.0 1.6 collective-permute-start.29
  214.6 1.5 collective-permute-start.30
  216.1 14.2 %tail_step.1 = (f32[1024,768]{1,0:T(8,128)}, bf16[96,768]{1,0:T(8,128)(2,1)}) custom-call(s32[1]{0:T(128)} %bitcast.meta.refs_0_, f32[1024,768]{1,0:T(8,128)} %get-tuple-element.182.start_ref, f32[1024,768]{1,0:T(8,128)} %get-tuple-element.217.gmiddle_ref, bf16[1024,128]{1,0:T(8,128)(2,1)} %get-tuple-element.218.slots_ref, f32[1,768]{1,0:T(1,128)} %copy-done.35, ...), custom_call_target="tpu_custom_call" | custom-call | tf_op jit(solution)/shard_map/tail_step/pallas_call | solution.py:465
  230.4 9.0 %weight_grad_qkv.1 = (bf16[4,4,3,24,768]{4,3,2,1,0:T(8,128)(2,1)}, bf16[4,4,3,24,768]{4,3,2,1,0:T(8,128)(2,1)}) custom-call(s32[1]{0:T(128)} %bitcast.meta.refs_0_, bf16[1024,768]{1,0:T(8,128)(2,1)} %get-tuple-element.170.x_ref.left_ref, bf16[1024,768]{1,0:T(8,128)(2,1)} %get-tuple-element.234.refs_2_.refs_0_, ...), custom_call_target="tpu_custom_call" | custom-call | tf_op jit(solution)/shard_map/weight_grad_qkv/pallas_call | solution.py:494
  239.9 1.3 collective-permute-start.33
  241.2 2.2 fusion.3
  243.4 2.5 collective-permute-done.33
  247.2 4.0 %gather_sums.1 = (f32[4,4,24,768]{3,2,1,0:T(8,128)}, bf16[4,4,24,768]{3,2,1,0:T(8,128)(2,1)}, bf16[4,4,24,768]{3,2,1,0:T(8,128)(2,1)}, bf16[4,4,24,768]{3,2,1,0:T(8,128)(2,1)}) custom-call(bf16[4,4,3,24,768]{4,3,2,1,0:T(8,128)(2,1)} %get-tuple-element.243.own_ref, bf16[4,4,3,24,768]{4,3,2,1,0:T(8,128)(2,1)} %copy-done.2, ...), custom_call_target="tpu_custom_call" | custom-call | tf_op jit(solution)/shard_map/gather_sums/pallas_call | solution.py:248
  251.3 1.3 collective-permute-start.35
  252.6 1.0 collective-permute-start.36
  253.7 1.2 collective-permute-start.37
  254.9 3.3 %collective-permute-start.38 = (bf16[2,2,96,768]{3,2,1,0:T(8,128)(2,1)S(1)}, bf16[2,2,96,768]{3,2,1,0:T(8,128)(2,1)S(1)}, u32[]{:S(2)}, u32[]{:S(2)}) collective-permute-start(bf16[2,2,96,768]{3,2,1,0:T(8,128)(2,1)S(1)} %pad_maximum_fusion), channel_id=1, source_target_pairs={{0,16},{1,17},{2,18},{3,19},{4,20},{5,21},{6,22},{7,23},{8,24},{9,... | collective-permute-start | bytes 1769480 | tf_op jit(solution)/shard_map/ppermute | solution.py:52
  258.4 15.1 %collective-permute-done.39 = bf16[96,768]{1,0:T(8,128)(2,1)S(1)} collective-permute-done((bf16[96,768]{1,0:T(8,128)(2,1)S(1)}, bf16[96,768]{1,0:T(8,128)(2,1)S(1)}, u32[]{:S(2)}, u32[]{:S(2)}) %collective-permute-start.39) | collective-permute-done | bytes 147488 | tf_op jit(solution)/shard_map/ppermute | solution.py:52
  273.4 6.4 %collective-permute-done.36.refs_1_ = bf16[4,4,24,768]{3,2,1,0:T(8,128)(2,1)S(1)} collective-permute-done((bf16[4,4,24,768]{3,2,1,0:T(8,128)(2,1)}, bf16[4,4,24,768]{3,2,1,0:T(8,128)(2,1)S(1)}, u32[]{:S(2)}, u32[]{:S(2)}) %collective-permute-start.36) | collective-permute-done | bytes 589856 | tf_op jit(solution)/shard_map/ppermute | solution.py:52
  279.8 2.0 collective-permute-done.38
  282.0 3.4 %collective-permute-start.40 = (bf16[96,768]{1,0:T(8,128)(2,1)S(1)}, bf16[96,768]{1,0:T(8,128)(2,1)S(1)}, u32[]{:S(2)}, u32[]{:S(2)}) collective-permute-start(bf16[96,768]{1,0:T(8,128)(2,1)S(1)} %get-tuple-element.294), channel_id=1, source_target_pairs={{0,16},{1,17},{2,18},{3,19},{4,20},{5,21},{6,22},{7,23},{8,24},{9,... | collective-permute-start | bytes 442376 | tf_op jit(solution)/shard_map/ppermute | solution.py:52
  285.7 2.7 plane_sums.1
  288.5 1.9 collective-permute-start.42
  290.5 1.5 collective-permute-start.43
  292.0 1.0 collective-permute-start.44
  295.0 2.5 collective-permute-done.41.refs_0_
  297.5 3.7 %collective-permute-done.42.refs_1_ = bf16[4,24,768]{2,1,0:T(8,128)(2,1)S(1)} collective-permute-done((bf16[4,24,768]{2,1,0:T(8,128)(2,1)}, bf16[4,24,768]{2,1,0:T(8,128)(2,1)S(1)}, u32[]{:S(2)}, u32[]{:S(2)}) %collective-permute-start.42) | collective-permute-done | bytes 147488 | tf_op jit(solution)/shard_map/ppermute | solution.py:52
  301.2 4.2 %collective-permute-done.43.refs_2_ = bf16[4,24,768]{2,1,0:T(8,128)(2,1)S(1)} collective-permute-done((bf16[4,24,768]{2,1,0:T(8,128)(2,1)}, bf16[4,24,768]{2,1,0:T(8,128)(2,1)S(1)}, u32[]{:S(2)}, u32[]{:S(2)}) %collective-permute-start.43) | collective-permute-done | bytes 147488 | tf_op jit(solution)/shard_map/ppermute | solution.py:52
  306.1 1.9 line_sums.1
  308.6 0.7 slice_add_fusion.6
  309.3 0.9 maximum_add_fusion
  (181 shorter events, 17.3 us)
Async XLA Ops:
  0.6 27.1 %copy-start.39 = (f32[768]{0:T(1024)S(1)}, f32[768]{0:T(1024)}, u32[]{:S(2)}) copy-start(f32[768]{0:T(1024)} %param.25) | copy-start | bytes 9220
  0.7 27.7 %copy-start.1 = (bf16[1024,768]{1,0:T(8,128)(2,1)S(1)}, bf16[1024,768]{1,0:T(8,128)(2,1)}, u32[]{:S(2)}) copy-start(bf16[1024,768]{1,0:T(8,128)(2,1)} %cot_ref.1) | copy-start | bytes 4718596
  2.4 1.7 collective-permute-start
  2.4 21.8 %collective-permute-start.4 = (bf16[2,96,768]{2,1,0:T(8,128)(2,1)}, bf16[2,96,768]{2,1,0:T(8,128)(2,1)}, u32[]{:S(2)}, u32[]{:S(2)}) collective-permute-start(bf16[2,96,768]{2,1,0:T(8,128)(2,1)} %refs_0_), channel_id=1, source_target_pairs={{0,8},{1,9},{2,10},{3,11},{4,12},{5,13},{6,14},{7,15},{8,0},{9,1},... | collective-permute-start | bytes 884744 | tf_op jit(solution)/shard_map/ppermute | solution.py:52
  6.3 13.2 %collective-permute-start.3 = (bf16[4,48,384]{2,1,0:T(8,128)(2,1)}, bf16[4,48,384]{2,1,0:T(8,128)(2,1)S(1)}, u32[]{:S(2)}, u32[]{:S(2)}) collective-permute-start(bf16[4,48,384]{2,1,0:T(8,128)(2,1)} %join.1.refs_0_), channel_id=1, source_target_pairs={{0,24},{1,25},{2,26},{3,27},{4,28},{5,29},{6,30},{7,31},{8,16},{9,... | collective-permute-start | bytes 442376 | tf_op jit(solution)/shard_map/ppermute | solution.py:52
  6.5 13.3 %collective-permute-start.2 = (bf16[4,48,384]{2,1,0:T(8,128)(2,1)}, bf16[4,48,384]{2,1,0:T(8,128)(2,1)S(1)}, u32[]{:S(2)}, u32[]{:S(2)}) collective-permute-start(bf16[4,48,384]{2,1,0:T(8,128)(2,1)} %join.1.refs_0_), channel_id=1, source_target_pairs={{0,16},{1,17},{2,18},{3,19},{4,20},{5,21},{6,22},{7,23},{8,24},{9,... | collective-permute-start | bytes 442376 | tf_op jit(solution)/shard_map/ppermute | solution.py:52
  10.0 11.5 %collective-permute-start.1 = (bf16[4,48,384]{2,1,0:T(8,128)(2,1)}, bf16[4,48,384]{2,1,0:T(8,128)(2,1)S(1)}, u32[]{:S(2)}, u32[]{:S(2)}) collective-permute-start(bf16[4,48,384]{2,1,0:T(8,128)(2,1)} %join.1.refs_0_), channel_id=1, source_target_pairs={{0,8},{1,9},{2,10},{3,11},{4,12},{5,13},{6,14},{7,15},{8,0},{9,1},... | collective-permute-start | bytes 442376 | tf_op jit(solution)/shard_map/ppermute | solution.py:52
  24.1 30.9 %collective-permute-start.7 = (bf16[4,4,48,384]{3,2,1,0:T(8,128)(2,1)}, bf16[4,4,48,384]{3,2,1,0:T(8,128)(2,1)S(1)}, u32[]{:S(2)}, u32[]{:S(2)}) collective-permute-start(bf16[4,4,48,384]{3,2,1,0:T(8,128)(2,1)} %stack_z.1.refs_0_), channel_id=1, source_target_pairs={{0,6},{1,7},{2,4},{3,5},{4,2},{5,3},{6,0},{7,1},{8,14},{9,15},{10,... | collective-permute-start | bytes 1769480 | tf_op jit(solution)/shard_map/ppermute | solution.py:52
  26.6 28.5 %collective-permute-start.6 = (bf16[4,4,48,384]{3,2,1,0:T(8,128)(2,1)}, bf16[4,4,48,384]{3,2,1,0:T(8,128)(2,1)S(1)}, u32[]{:S(2)}, u32[]{:S(2)}) collective-permute-start(bf16[4,4,48,384]{3,2,1,0:T(8,128)(2,1)} %stack_z.1.refs_0_), channel_id=1, source_target_pairs={{0,4},{1,5},{2,6},{3,7},{4,0},{5,1},{6,2},{7,3},{8,12},{9,13},{10,... | collective-permute-start | bytes 1769480 | tf_op jit(solution)/shard_map/ppermute | solution.py:52
  27.1 28.0 %collective-permute-start.5 = (bf16[4,4,48,384]{3,2,1,0:T(8,128)(2,1)}, bf16[4,4,48,384]{3,2,1,0:T(8,128)(2,1)S(1)}, u32[]{:S(2)}, u32[]{:S(2)}) collective-permute-start(bf16[4,4,48,384]{3,2,1,0:T(8,128)(2,1)} %stack_z.1.refs_0_), channel_id=1, source_target_pairs={{0,2},{1,3},{2,0},{3,1},{4,6},{5,7},{6,4},{7,5},{8,10},{9,11},{10,... | collective-permute-start | bytes 1769480 | tf_op jit(solution)/shard_map/ppermute | solution.py:52
  28.3 8.5 %copy-start.26 = (f32[50,768]{1,0:T(8,128)S(1)}, f32[50,768]{1,0:T(8,128)}, u32[]{:S(2)}) copy-start(f32[50,768]{1,0:T(8,128)} %param.15) | copy-start | bytes 460804
  28.3 9.3 %copy-start.37 = (s32[1024]{0:T(1024)S(1)}, s32[1024]{0:T(1024)}, u32[]{:S(2)}) copy-start(s32[1024]{0:T(1024)} %param.17) | copy-start | bytes 12292
  28.3 10.3 %copy-start.38 = (s32[1024]{0:T(1024)S(1)}, s32[1024]{0:T(1024)}, u32[]{:S(2)}) copy-start(s32[1024]{0:T(1024)} %param.16) | copy-start | bytes 12292
  30.0 15.5 %copy-start.35 = (f32[1,768]{1,0:T(1,128)}, f32[1,768]{1,0:T(1,128)S(1)}, u32[]{:S(2)}) copy-start(f32[1,768]{1,0:T(1,128)S(1)} %get-tuple-element.301.p_ref) | copy-start | bytes 9220
  30.0 22.8 %collective-permute-start.9 = (bf16[2,96,768]{2,1,0:T(8,128)(2,1)}, bf16[2,96,768]{2,1,0:T(8,128)(2,1)S(1)}, u32[]{:S(2)}, u32[]{:S(2)}) collective-permute-start(bf16[2,96,768]{2,1,0:T(8,128)(2,1)} %refs_0_), channel_id=1, source_target_pairs={{0,24},{1,25},{2,26},{3,27},{4,28},{5,29},{6,30},{7,31},{8,16},{9,... | collective-permute-start | bytes 884744 | tf_op jit(solution)/shard_map/ppermute | solution.py:52
  30.8 24.3 %collective-permute-start.8 = (bf16[2,96,768]{2,1,0:T(8,128)(2,1)}, bf16[2,96,768]{2,1,0:T(8,128)(2,1)S(1)}, u32[]{:S(2)}, u32[]{:S(2)}) collective-permute-start(bf16[2,96,768]{2,1,0:T(8,128)(2,1)} %refs_0_), channel_id=1, source_target_pairs={{0,16},{1,17},{2,18},{3,19},{4,20},{5,21},{6,22},{7,23},{8,24},{9,... | collective-permute-start | bytes 884744 | tf_op jit(solution)/shard_map/ppermute | solution.py:52
  52.8 6.9 %copy-start.24 = (bf16[2,96,768]{2,1,0:T(8,128)(2,1)}, bf16[2,96,768]{2,1,0:T(8,128)(2,1)S(1)}, u32[]{:S(2)}) copy-start(bf16[2,96,768]{2,1,0:T(8,128)(2,1)S(1)} %collective-permute-done.9.refs_3_) | copy-start | bytes 884740
  55.1 4.6 %copy-start.25 = (bf16[2,96,768]{2,1,0:T(8,128)(2,1)}, bf16[2,96,768]{2,1,0:T(8,128)(2,1)S(1)}, u32[]{:S(2)}) copy-start(bf16[2,96,768]{2,1,0:T(8,128)(2,1)S(1)} %collective-permute-done.8.refs_2_) | copy-start | bytes 884740
  62.0 9.4 %copy-start.6 = (bf16[4,96,768]{2,1,0:T(8,128)(2,1)S(1)}, bf16[4,96,768]{2,1,0:T(8,128)(2,1)}, u32[]{:S(2)}) copy-start(bf16[4,96,768]{2,1,0:T(8,128)(2,1)} %get-tuple-element.168.refs_5_) | copy-start | bytes 1769476
  62.0 9.4 %collective-permute-start.15 = (bf16[4,768,384]{2,1,0:T(8,128)(2,1)}, bf16[4,768,384]{2,1,0:T(8,128)(2,1)S(1)}, u32[]{:S(2)}, u32[]{:S(2)}) collective-permute-start(bf16[4,768,384]{2,1,0:T(8,128)(2,1)} %assemble.1.w_ref.own_ref.refs_0_), channel_id=1, source_target_pairs={{0,1},{1,0},{2,3},{3,2},{4,5},{5,4},{6,7},{7,6},{8,9},{9,8},{10,11... | collective-permute-start | bytes 7077896 | tf_op jit(solution)/shard_map/ppermute | solution.py:52
  62.0 16.6 %collective-permute-start.13 = (bf16[4,96,768]{2,1,0:T(8,128)(2,1)}, bf16[4,96,768]{2,1,0:T(8,128)(2,1)S(1)}, u32[]{:S(2)}, u32[]{:S(2)}) collective-permute-start(bf16[4,96,768]{2,1,0:T(8,128)(2,1)} %get-tuple-element.168.refs_5_), channel_id=1, source_target_pairs={{0,1},{1,0},{2,3},{3,2},{4,5},{5,4},{6,7},{7,6},{8,9},{9,8},{10,11... | collective-permute-start | bytes 1769480 | tf_op jit(solution)/shard_map/ppermute | solution.py:52
  62.5 16.7 %collective-permute-start.11 = (bf16[4,96,768]{2,1,0:T(8,128)(2,1)}, bf16[4,96,768]{2,1,0:T(8,128)(2,1)}, u32[]{:S(2)}, u32[]{:S(2)}) collective-permute-start(bf16[4,96,768]{2,1,0:T(8,128)(2,1)} %get-tuple-element.168.refs_5_), channel_id=1, source_target_pairs={{0,4},{1,5},{2,6},{3,7},{4,0},{5,1},{6,2},{7,3},{8,12},{9,13},{10,... | collective-permute-start | bytes 1769480 | tf_op jit(solution)/shard_map/ppermute | solution.py:52
  64.0 15.2 %collective-permute-start.14 = (bf16[4,96,768]{2,1,0:T(8,128)(2,1)}, bf16[4,96,768]{2,1,0:T(8,128)(2,1)}, u32[]{:S(2)}, u32[]{:S(2)}) collective-permute-start(bf16[4,96,768]{2,1,0:T(8,128)(2,1)} %get-tuple-element.169.refs_9_), channel_id=1, source_target_pairs={{0,1},{1,0},{2,3},{3,2},{4,5},{5,4},{6,7},{7,6},{8,9},{9,8},{10,11... | collective-permute-start | bytes 1769480 | tf_op jit(solution)/shard_map/ppermute | solution.py:52
  64.0 16.5 %collective-permute-start.12 = (bf16[4,96,768]{2,1,0:T(8,128)(2,1)}, bf16[4,96,768]{2,1,0:T(8,128)(2,1)}, u32[]{:S(2)}, u32[]{:S(2)}) collective-permute-start(bf16[4,96,768]{2,1,0:T(8,128)(2,1)} %get-tuple-element.169.refs_9_), channel_id=1, source_target_pairs={{0,2},{1,3},{2,0},{3,1},{4,6},{5,7},{6,4},{7,5},{8,10},{9,11},{10,... | collective-permute-start | bytes 1769480 | tf_op jit(solution)/shard_map/ppermute | solution.py:52
  71.4 7.2 %copy-start.7 = (bf16[4,96,768]{2,1,0:T(8,128)(2,1)S(1)}, bf16[4,96,768]{2,1,0:T(8,128)(2,1)}, u32[]{:S(2)}) copy-start(bf16[4,96,768]{2,1,0:T(8,128)(2,1)} %get-tuple-element.169.refs_9_) | copy-start | bytes 1769476
  71.4 32.2 %collective-permute-start.10 = (bf16[4,96,768]{2,1,0:T(8,128)(2,1)S(1)}, bf16[4,96,768]{2,1,0:T(8,128)(2,1)}, u32[]{:S(2)}, u32[]{:S(2)}) collective-permute-start(bf16[4,96,768]{2,1,0:T(8,128)(2,1)S(1)} %copy-done.6), channel_id=1, source_target_pairs={{0,2},{1,3},{2,0},{3,1},{4,6},{5,7},{6,4},{7,5},{8,10},{9,11},{10,... | collective-permute-start | bytes 1769480 | tf_op jit(solution)/shard_map/ppermute | solution.py:52
  78.6 25.0 %copy-start.8 = (bf16[4,96,768]{2,1,0:T(8,128)(2,1)}, bf16[4,96,768]{2,1,0:T(8,128)(2,1)S(1)}, u32[]{:S(2)}) copy-start(bf16[4,96,768]{2,1,0:T(8,128)(2,1)S(1)} %collective-permute-done.13.refs_13_) | copy-start | bytes 1769476
  78.6 25.5 %collective-permute-start.17 = (bf16[4,96,768]{2,1,0:T(8,128)(2,1)S(1)}, bf16[4,96,768]{2,1,0:T(8,128)(2,1)S(1)}, u32[]{:S(2)}, u32[]{:S(2)}) collective-permute-start(bf16[4,96,768]{2,1,0:T(8,128)(2,1)S(1)} %copy-done.7), channel_id=1, source_target_pairs={{0,4},{1,5},{2,6},{3,7},{4,0},{5,1},{6,2},{7,3},{8,12},{9,13},{10,... | collective-permute-start | bytes 1769480 | tf_op jit(solution)/shard_map/ppermute | solution.py:52
  80.5 24.7 %collective-permute-start.16 = (bf16[4,96,768]{2,1,0:T(8,128)(2,1)}, bf16[4,96,768]{2,1,0:T(8,128)(2,1)S(1)}, u32[]{:S(2)}, u32[]{:S(2)}) collective-permute-start(bf16[4,96,768]{2,1,0:T(8,128)(2,1)} %collective-permute-done.11.refs_7_), channel_id=1, source_target_pairs={{0,2},{1,3},{2,0},{3,1},{4,6},{5,7},{6,4},{7,5},{8,10},{9,11},{10,... | collective-permute-start | bytes 1769480 | tf_op jit(solution)/shard_map/ppermute | solution.py:52
  82.0 24.8 %collective-permute-start.18 = (bf16[4,96,768]{2,1,0:T(8,128)(2,1)}, bf16[4,96,768]{2,1,0:T(8,128)(2,1)S(1)}, u32[]{:S(2)}, u32[]{:S(2)}) collective-permute-start(bf16[4,96,768]{2,1,0:T(8,128)(2,1)} %collective-permute-done.12.refs_10_), channel_id=1, source_target_pairs={{0,4},{1,5},{2,6},{3,7},{4,0},{5,1},{6,2},{7,3},{8,12},{9,13},{10,... | collective-permute-start | bytes 1769480 | tf_op jit(solution)/shard_map/ppermute | solution.py:52
  82.5 24.8 %collective-permute-start.20 = (bf16[4,96,768]{2,1,0:T(8,128)(2,1)}, bf16[4,96,768]{2,1,0:T(8,128)(2,1)S(1)}, u32[]{:S(2)}, u32[]{:S(2)}) collective-permute-start(bf16[4,96,768]{2,1,0:T(8,128)(2,1)} %collective-permute-done.11.refs_7_), channel_id=1, source_target_pairs={{0,1},{1,0},{2,3},{3,2},{4,5},{5,4},{6,7},{7,6},{8,9},{9,8},{10,11... | collective-permute-start | bytes 1769480 | tf_op jit(solution)/shard_map/ppermute | solution.py:52
  103.6 10.2 %collective-permute-start.22 = (bf16[4,96,768]{2,1,0:T(8,128)(2,1)}, bf16[4,96,768]{2,1,0:T(8,128)(2,1)S(1)}, u32[]{:S(2)}, u32[]{:S(2)}) collective-permute-start(bf16[4,96,768]{2,1,0:T(8,128)(2,1)} %collective-permute-done.12.refs_10_), channel_id=1, source_target_pairs={{0,1},{1,0},{2,3},{3,2},{4,5},{5,4},{6,7},{7,6},{8,9},{9,8},{10,11... | collective-permute-start | bytes 1769480 | tf_op jit(solution)/shard_map/ppermute | solution.py:52
  104.2 9.6 %copy-start.9 = (bf16[4,96,768]{2,1,0:T(8,128)(2,1)}, bf16[4,96,768]{2,1,0:T(8,128)(2,1)S(1)}, u32[]{:S(2)}) copy-start(bf16[4,96,768]{2,1,0:T(8,128)(2,1)S(1)} %collective-permute-done.17.refs_11_) | copy-start | bytes 1769476
  105.3 8.5 %copy-start.10 = (bf16[4,96,768]{2,1,0:T(8,128)(2,1)}, bf16[4,96,768]{2,1,0:T(8,128)(2,1)S(1)}, u32[]{:S(2)}) copy-start(bf16[4,96,768]{2,1,0:T(8,128)(2,1)S(1)} %collective-permute-done.16.refs_8_) | copy-start | bytes 1769476
  106.8 7.0 %copy-start.11 = (bf16[4,96,768]{2,1,0:T(8,128)(2,1)}, bf16[4,96,768]{2,1,0:T(8,128)(2,1)S(1)}, u32[]{:S(2)}) copy-start(bf16[4,96,768]{2,1,0:T(8,128)(2,1)S(1)} %collective-permute-done.18.refs_12_) | copy-start | bytes 1769476
  106.8 7.0 %collective-permute-start.19 = (bf16[4,96,768]{2,1,0:T(8,128)(2,1)}, bf16[4,96,768]{2,1,0:T(8,128)(2,1)S(1)}, u32[]{:S(2)}, u32[]{:S(2)}) collective-permute-start(bf16[4,96,768]{2,1,0:T(8,128)(2,1)} %collective-permute-done.10.refs_6_), channel_id=1, source_target_pairs={{0,1},{1,0},{2,3},{3,2},{4,5},{5,4},{6,7},{7,6},{8,9},{9,8},{10,11... | collective-permute-start | bytes 1769480 | tf_op jit(solution)/shard_map/ppermute | solution.py:52
  106.8 7.0 %collective-permute-start.21 = (bf16[4,96,768]{2,1,0:T(8,128)(2,1)S(1)}, bf16[4,96,768]{2,1,0:T(8,128)(2,1)S(1)}, u32[]{:S(2)}, u32[]{:S(2)}) collective-permute-start(bf16[4,96,768]{2,1,0:T(8,128)(2,1)S(1)} %collective-permute-done.16.refs_8_), channel_id=1, source_target_pairs={{0,1},{1,0},{2,3},{3,2},{4,5},{5,4},{6,7},{7,6},{8,9},{9,8},{10,11... | collective-permute-start | bytes 1769480 | tf_op jit(solution)/shard_map/ppermute | solution.py:52
  107.3 6.5 %collective-permute-start.23 = (bf16[4,96,768]{2,1,0:T(8,128)(2,1)S(1)}, bf16[4,96,768]{2,1,0:T(8,128)(2,1)}, u32[]{:S(2)}, u32[]{:S(2)}) collective-permute-start(bf16[4,96,768]{2,1,0:T(8,128)(2,1)S(1)} %collective-permute-done.17.refs_11_), channel_id=1, source_target_pairs={{0,1},{1,0},{2,3},{3,2},{4,5},{5,4},{6,7},{7,6},{8,9},{9,8},{10,11... | collective-permute-start | bytes 1769480 | tf_op jit(solution)/shard_map/ppermute | solution.py:52
  107.3 6.5 %copy-start.12 = (bf16[4,96,768]{2,1,0:T(8,128)(2,1)}, bf16[4,96,768]{2,1,0:T(8,128)(2,1)S(1)}, u32[]{:S(2)}) copy-start(bf16[4,96,768]{2,1,0:T(8,128)(2,1)S(1)} %collective-permute-done.20.refs_15_) | copy-start | bytes 1769476
  107.3 6.5 %collective-permute-start.24 = (bf16[4,96,768]{2,1,0:T(8,128)(2,1)S(1)}, bf16[4,96,768]{2,1,0:T(8,128)(2,1)}, u32[]{:S(2)}, u32[]{:S(2)}) collective-permute-start(bf16[4,96,768]{2,1,0:T(8,128)(2,1)S(1)} %collective-permute-done.18.refs_12_), channel_id=1, source_target_pairs={{0,1},{1,0},{2,3},{3,2},{4,5},{5,4},{6,7},{7,6},{8,9},{9,8},{10,11... | collective-permute-start | bytes 1769480 | tf_op jit(solution)/shard_map/ppermute | solution.py:52
  161.9 11.3 %collective-permute-start.25 = (bf16[2,4,4,96,768]{4,3,2,1,0:T(8,128)(2,1)}, bf16[2,4,4,96,768]{4,3,2,1,0:T(8,128)(2,1)}, u32[]{:S(2)}, u32[]{:S(2)}) collective-permute-start(bf16[2,4,4,96,768]{4,3,2,1,0:T(8,128)(2,1)} %get-tuple-element.202), channel_id=1, source_target_pairs={{0,1},{1,0},{2,3},{3,2},{4,5},{5,4},{6,7},{7,6},{8,9},{9,8},{10,11... | collective-permute-start | bytes 14155784 | tf_op jit(solution)/shard_map/ppermute | solution.py:52
  177.3 33.0 %collective-permute-start.26 = (bf16[2,4,96,768]{3,2,1,0:T(8,128)(2,1)}, bf16[2,4,96,768]{3,2,1,0:T(8,128)(2,1)S(1)}, u32[]{:S(2)}, u32[]{:S(2)}) collective-permute-start(bf16[2,4,96,768]{3,2,1,0:T(8,128)(2,1)} %get-tuple-element.208), channel_id=1, source_target_pairs={{0,2},{1,3},{2,0},{3,1},{4,6},{5,7},{6,4},{7,5},{8,10},{9,11},{10,... | collective-permute-start | bytes 3538952 | tf_op jit(solution)/shard_map/ppermute | solution.py:52
  177.8 32.5 %collective-permute-start.27 = (bf16[2,4,96,768]{3,2,1,0:T(8,128)(2,1)S(1)}, bf16[2,4,96,768]{3,2,1,0:T(8,128)(2,1)S(1)}, u32[]{:S(2)}, u32[]{:S(2)}) collective-permute-start(bf16[2,4,96,768]{3,2,1,0:T(8,128)(2,1)S(1)} %get-tuple-element.209), channel_id=1, source_target_pairs={{0,4},{1,5},{2,6},{3,7},{4,0},{5,1},{6,2},{7,3},{8,12},{9,13},{10,... | collective-permute-start | bytes 3538952 | tf_op jit(solution)/shard_map/ppermute | solution.py:52
  178.3 32.0 %collective-permute-start.28 = (bf16[4,4,1,24,768]{4,3,2,1,0:T(8,128)(2,1)}, bf16[4,4,1,24,768]{4,3,2,1,0:T(8,128)(2,1)S(1)}, u32[]{:S(2)}, u32[]{:S(2)}) collective-permute-start(bf16[4,4,1,24,768]{4,3,2,1,0:T(8,128)(2,1)} %get-tuple-element.210), channel_id=1, source_target_pairs={{0,1},{1,0},{2,3},{3,2},{4,5},{5,4},{6,7},{7,6},{8,9},{9,8},{10,11... | collective-permute-start | bytes 1769480 | tf_op jit(solution)/shard_map/ppermute | solution.py:52
  213.0 17.2 %collective-permute-start.29 = (bf16[4,96,768]{2,1,0:T(8,128)(2,1)S(1)}, bf16[4,96,768]{2,1,0:T(8,128)(2,1)S(1)}, u32[]{:S(2)}, u32[]{:S(2)}) collective-permute-start(bf16[4,96,768]{2,1,0:T(8,128)(2,1)S(1)} %get-tuple-element.231), channel_id=1, source_target_pairs={{0,4},{1,5},{2,6},{3,7},{4,0},{5,1},{6,2},{7,3},{8,12},{9,13},{10,... | collective-permute-start | bytes 1769480 | tf_op jit(solution)/shard_map/ppermute | solution.py:52
  214.6 15.7 %collective-permute-start.30 = (bf16[4,96,768]{2,1,0:T(8,128)(2,1)S(1)}, bf16[4,96,768]{2,1,0:T(8,128)(2,1)S(1)}, u32[]{:S(2)}, u32[]{:S(2)}) collective-permute-start(bf16[4,96,768]{2,1,0:T(8,128)(2,1)S(1)} %get-tuple-element.232), channel_id=1, source_target_pairs={{0,2},{1,3},{2,0},{3,1},{4,6},{5,7},{6,4},{7,5},{8,10},{9,11},{10,... | collective-permute-start | bytes 1769480 | tf_op jit(solution)/shard_map/ppermute | solution.py:52
  230.3 9.1 %copy-start.16 = (bf16[4,96,768]{2,1,0:T(8,128)(2,1)}, bf16[4,96,768]{2,1,0:T(8,128)(2,1)S(1)}, u32[]{:S(2)}) copy-start(bf16[4,96,768]{2,1,0:T(8,128)(2,1)S(1)} %collective-permute-done.30) | copy-start | bytes 1769476
  230.3 9.5 %copy-start.30 = (bf16[96,768]{1,0:T(8,128)(2,1)S(1)}, bf16[96,768]{1,0:T(8,128)(2,1)}, u32[]{:S(2)}) copy-start(bf16[96,768]{1,0:T(8,128)(2,1)} %get-tuple-element.233) | copy-start | bytes 442372
  230.3 9.1 %collective-permute-start.31 = (bf16[96,768]{1,0:T(8,128)(2,1)}, bf16[96,768]{1,0:T(8,128)(2,1)S(1)}, u32[]{:S(2)}, u32[]{:S(2)}) collective-permute-start(bf16[96,768]{1,0:T(8,128)(2,1)} %get-tuple-element.233), channel_id=1, source_target_pairs={{0,1},{1,0},{2,3},{3,2},{4,5},{5,4},{6,7},{7,6},{8,9},{9,8},{10,11... | collective-permute-start | bytes 442376 | tf_op jit(solution)/shard_map/ppermute | solution.py:52
  239.4 6.5 %collective-permute-start.32 = (bf16[4,4,3,24,768]{4,3,2,1,0:T(8,128)(2,1)}, bf16[4,4,3,24,768]{4,3,2,1,0:T(8,128)(2,1)S(1)}, u32[]{:S(2)}, u32[]{:S(2)}) collective-permute-start(bf16[4,4,3,24,768]{4,3,2,1,0:T(8,128)(2,1)} %get-tuple-element.244), channel_id=1, source_target_pairs={{0,1},{1,0},{2,3},{3,2},{4,5},{5,4},{6,7},{7,6},{8,9},{9,8},{10,11... | collective-permute-start | bytes 5308424 | tf_op jit(solution)/shard_map/ppermute | solution.py:52
  239.9 6.0 %collective-permute-start.33 = (bf16[96,768]{1,0:T(8,128)(2,1)S(1)}, bf16[96,768]{1,0:T(8,128)(2,1)S(1)}, u32[]{:S(2)}, u32[]{:S(2)}) collective-permute-start(bf16[96,768]{1,0:T(8,128)(2,1)S(1)} %pad_maximum_fusion.2), channel_id=1, source_target_pairs={{0,2},{1,3},{2,0},{3,1},{4,6},{5,7},{6,4},{7,5},{8,10},{9,11},{10,... | collective-permute-start | bytes 442376 | tf_op jit(solution)/shard_map/ppermute | solution.py:52
  246.1 5.2 %collective-permute-start.34 = (bf16[96,768]{1,0:T(8,128)(2,1)S(1)}, bf16[96,768]{1,0:T(8,128)(2,1)S(1)}, u32[]{:S(2)}, u32[]{:S(2)}) collective-permute-start(bf16[96,768]{1,0:T(8,128)(2,1)S(1)} %pad_maximum_fusion.3), channel_id=1, source_target_pairs={{0,4},{1,5},{2,6},{3,7},{4,0},{5,1},{6,2},{7,3},{8,12},{9,13},{10,... | collective-permute-start | bytes 442376 | tf_op jit(solution)/shard_map/ppermute | solution.py:52
  251.3 22.1 %collective-permute-start.35 = (bf16[4,4,24,768]{3,2,1,0:T(8,128)(2,1)}, bf16[4,4,24,768]{3,2,1,0:T(8,128)(2,1)S(1)}, u32[]{:S(2)}, u32[]{:S(2)}) collective-permute-start(bf16[4,4,24,768]{3,2,1,0:T(8,128)(2,1)} %get-tuple-element.254), channel_id=1, source_target_pairs={{0,2},{1,3},{2,0},{3,1},{4,6},{5,7},{6,4},{7,5},{8,10},{9,11},{10,... | collective-permute-start | bytes 1769480 | tf_op jit(solution)/shard_map/ppermute | solution.py:52
  252.6 27.2 %collective-permute-start.36 = (bf16[4,4,24,768]{3,2,1,0:T(8,128)(2,1)}, bf16[4,4,24,768]{3,2,1,0:T(8,128)(2,1)S(1)}, u32[]{:S(2)}, u32[]{:S(2)}) collective-permute-start(bf16[4,4,24,768]{3,2,1,0:T(8,128)(2,1)} %get-tuple-element.255), channel_id=1, source_target_pairs={{0,4},{1,5},{2,6},{3,7},{4,0},{5,1},{6,2},{7,3},{8,12},{9,13},{10,... | collective-permute-start | bytes 1769480 | tf_op jit(solution)/shard_map/ppermute | solution.py:52
  253.7 26.2 %collective-permute-start.37 = (bf16[4,4,24,768]{3,2,1,0:T(8,128)(2,1)}, bf16[4,4,24,768]{3,2,1,0:T(8,128)(2,1)S(1)}, u32[]{:S(2)}, u32[]{:S(2)}) collective-permute-start(bf16[4,4,24,768]{3,2,1,0:T(8,128)(2,1)} %get-tuple-element.256), channel_id=1, source_target_pairs={{0,6},{1,7},{2,4},{3,5},{4,2},{5,3},{6,0},{7,1},{8,14},{9,15},{10,... | collective-permute-start | bytes 1769480 | tf_op jit(solution)/shard_map/ppermute | solution.py:52
  254.9 27.0 %collective-permute-start.38 = (bf16[2,2,96,768]{3,2,1,0:T(8,128)(2,1)S(1)}, bf16[2,2,96,768]{3,2,1,0:T(8,128)(2,1)S(1)}, u32[]{:S(2)}, u32[]{:S(2)}) collective-permute-start(bf16[2,2,96,768]{3,2,1,0:T(8,128)(2,1)S(1)} %pad_maximum_fusion), channel_id=1, source_target_pairs={{0,16},{1,17},{2,18},{3,19},{4,20},{5,21},{6,22},{7,23},{8,24},{9,... | collective-permute-start | bytes 1769480 | tf_op jit(solution)/shard_map/ppermute | solution.py:52
  258.2 15.2 %collective-permute-start.39 = (bf16[96,768]{1,0:T(8,128)(2,1)S(1)}, bf16[96,768]{1,0:T(8,128)(2,1)S(1)}, u32[]{:S(2)}, u32[]{:S(2)}) collective-permute-start(bf16[96,768]{1,0:T(8,128)(2,1)S(1)} %pad_maximum_fusion.4), channel_id=1, source_target_pairs={{0,8},{1,9},{2,10},{3,11},{4,12},{5,13},{6,14},{7,15},{8,0},{9,1},... | collective-permute-start | bytes 442376 | tf_op jit(solution)/shard_map/ppermute | solution.py:52
  273.4 12.2 %copy-start.21 = (bf16[4,4,24,768]{3,2,1,0:T(8,128)(2,1)}, bf16[4,4,24,768]{3,2,1,0:T(8,128)(2,1)S(1)}, u32[]{:S(2)}) copy-start(bf16[4,4,24,768]{3,2,1,0:T(8,128)(2,1)S(1)} %collective-permute-done.35.refs_0_) | copy-start | bytes 1769476
  282.0 11.0 %collective-permute-start.40 = (bf16[96,768]{1,0:T(8,128)(2,1)S(1)}, bf16[96,768]{1,0:T(8,128)(2,1)S(1)}, u32[]{:S(2)}, u32[]{:S(2)}) collective-permute-start(bf16[96,768]{1,0:T(8,128)(2,1)S(1)} %get-tuple-element.294), channel_id=1, source_target_pairs={{0,16},{1,17},{2,18},{3,19},{4,20},{5,21},{6,22},{7,23},{8,24},{9,... | collective-permute-start | bytes 442376 | tf_op jit(solution)/shard_map/ppermute | solution.py:52
  288.4 9.1 %collective-permute-start.41 = (bf16[4,24,768]{2,1,0:T(8,128)(2,1)}, bf16[4,24,768]{2,1,0:T(8,128)(2,1)S(1)}, u32[]{:S(2)}, u32[]{:S(2)}) collective-permute-start(bf16[4,24,768]{2,1,0:T(8,128)(2,1)} %get-tuple-element.271), channel_id=1, source_target_pairs={{0,8},{1,9},{2,10},{3,11},{4,12},{5,13},{6,14},{7,15},{8,0},{9,1},... | collective-permute-start | bytes 442376 | tf_op jit(solution)/shard_map/ppermute | solution.py:52
  288.5 12.7 %collective-permute-start.42 = (bf16[4,24,768]{2,1,0:T(8,128)(2,1)}, bf16[4,24,768]{2,1,0:T(8,128)(2,1)S(1)}, u32[]{:S(2)}, u32[]{:S(2)}) collective-permute-start(bf16[4,24,768]{2,1,0:T(8,128)(2,1)} %get-tuple-element.272), channel_id=1, source_target_pairs={{0,16},{1,17},{2,18},{3,19},{4,20},{5,21},{6,22},{7,23},{8,24},{9,... | collective-permute-start | bytes 442376 | tf_op jit(solution)/shard_map/ppermute | solution.py:52
  290.5 14.9 %collective-permute-start.43 = (bf16[4,24,768]{2,1,0:T(8,128)(2,1)}, bf16[4,24,768]{2,1,0:T(8,128)(2,1)S(1)}, u32[]{:S(2)}, u32[]{:S(2)}) collective-permute-start(bf16[4,24,768]{2,1,0:T(8,128)(2,1)} %get-tuple-element.273), channel_id=1, source_target_pairs={{0,24},{1,25},{2,26},{3,27},{4,28},{5,29},{6,30},{7,31},{8,16},{9,... | collective-permute-start | bytes 442376 | tf_op jit(solution)/shard_map/ppermute | solution.py:52
  292.0 17.2 %collective-permute-start.44 = (bf16[2,96,768]{2,1,0:T(8,128)(2,1)S(1)}, bf16[2,96,768]{2,1,0:T(8,128)(2,1)S(1)}, u32[]{:S(2)}, u32[]{:S(2)}) collective-permute-start(bf16[2,96,768]{2,1,0:T(8,128)(2,1)S(1)} %pad_maximum_fusion.1), channel_id=1, source_target_pairs={{0,8},{1,9},{2,10},{3,11},{4,12},{5,13},{6,14},{7,15},{8,0},{9,1},... | collective-permute-start | bytes 884744 | tf_op jit(solution)/shard_map/ppermute | solution.py:52
  297.5 7.9 %copy-start.31 = (bf16[4,24,768]{2,1,0:T(8,128)(2,1)}, bf16[4,24,768]{2,1,0:T(8,128)(2,1)S(1)}, u32[]{:S(2)}) copy-start(bf16[4,24,768]{2,1,0:T(8,128)(2,1)S(1)} %collective-permute-done.41.refs_0_) | copy-start | bytes 442372
  (21 other events, 33.5 us)

commit v6 on v5

--- a/solution.py
+++ b/solution.py
@@ -892,10 +892,9 @@
         packed = pack_small(add_small(packed, got_small))
         got_small = px(packed, 8)
         moved, got_far, got_small, packed = tie(moved, got_far, got_small, packed)
+        near = [add_parts(col[c][:2], got_far[c]) for c in range(2)]
+        moved, send = tie(moved, jnp.stack([x[1].astype(B16) for x in near]))
         col_attn, *last = plane_sums(keep, moved)
-        near = [add_parts(col[c][:2], got_far[c]) for c in range(2)]
-        send = jnp.stack([x[1].astype(B16) for x in near])
-        last, send = tie(last, send)
         last = [px(x, 8 * i + 8) for i, x in enumerate(last)]
         got_near = px(send, 8)
         small = exchange_small(pack_small(add_small(packed, got_small)), 16)

time: 313 us -> 313 us (level)
  no operation moved by 1% of the time
where the time goes in v6:
time: 313 us; the launch traced here: 310 us
  Pallas kernels  177 us (57%)
  waiting for transfers between devices  60.8 us (19%)
  starting transfers between devices  43.7 us (14%)
  local copies, waits for them, and re-layouts  14.3 us (5%)
  other arithmetic  13 us (4%)
    ppermute x45, waiting for transfers between devices, px(): return lax.ppermute(x, AXES, [(i, i ^ k) for i in range(32)])  60.8 us
    pallas_call x1, Pallas kernels, mlp(): pl.pallas_call(partial(mlp_kernel, fast), name='mlp', grid=(4 * PER,), in...  46.8 us
    ppermute x45, starting transfers between devices, px(): return lax.ppermute(x, AXES, [(i, i ^ k) for i in range(32)])  43.7 us
    pallas_call x1, Pallas kernels, attention_backward(): pl.pallas_call(kernel, name='attention_backward', grid_spec=pltpu.Prefetc...  31.9 us
    pallas_call x1, Pallas kernels, attention_forward(): pl.pallas_call(kernel, name='attention_forward', grid_spec=pltpu.Prefetch...  21.1 us
    pallas_call x1, Pallas kernels, tail_step(): pl.pallas_call(tail_kernel, name='tail_step', grid=(rows // STEP,), in_sp...  14.2 us
    pallas_call x2, Pallas kernels, project(): pl.pallas_call(partial(project_kernel, side), name='project', grid=(3,),...  11.7 us
    pallas_call x1, Pallas kernels, turn(): pl.pallas_call(turn_kernel, name='turn', grid=(rows // STEP,), in_specs=[...  11 us
  transfers between devices with their start and end apart: 45, of which 15 were waited for; matrix products, arithmetic and copies ran while one was open for 4% of the time, Pallas kernels for 40%

profile of v6, /device:TPU:16, one launch (start us, length us, event | category | flops | bytes accessed | tf_op | source)
XLA Modules:
  0.0 310.1 jit_solution(11668216974830328547)
XLA Ops:
  0.7 1.7 split.1
  2.4 1.6 collective-permute-start.4
  4.7 1.6 join.1.refs_0_
  6.5 3.5 %collective-permute-start.2 = (bf16[4,48,384]{2,1,0:T(8,128)(2,1)}, bf16[4,48,384]{2,1,0:T(8,128)(2,1)S(1)}, u32[]{:S(2)}, u32[]{:S(2)}) collective-permute-start(bf16[4,48,384]{2,1,0:T(8,128)(2,1)} %join.1.refs_0_), channel_id=1, source_target_pairs={{0,16},{1,17},{2,18},{3,19},{4,20},{5,21},{6,22},{7,23},{8,24},{9,... | collective-permute-start | bytes 442376 | tf_op jit(solution)/shard_map/ppermute | solution.py:52
  10.0 0.8 fusion.21
  10.9 8.6 %collective-permute-done.3.refs_3_ = bf16[4,48,384]{2,1,0:T(8,128)(2,1)S(1)} collective-permute-done((bf16[4,48,384]{2,1,0:T(8,128)(2,1)}, bf16[4,48,384]{2,1,0:T(8,128)(2,1)S(1)}, u32[]{:S(2)}, u32[]{:S(2)}) %collective-permute-start.3) | collective-permute-done | bytes 147488 | tf_op jit(solution)/shard_map/ppermute | solution.py:52
  19.9 1.6 collective-permute-done.1.refs_1_
  22.1 2.0 stack_z.1.refs_0_
  24.1 2.4 collective-permute-start.7
  28.3 1.6 copy.28
  30.0 0.8 collective-permute-start.9
  30.8 4.2 %collective-permute-start.8 = (bf16[2,96,768]{2,1,0:T(8,128)(2,1)}, bf16[2,96,768]{2,1,0:T(8,128)(2,1)S(1)}, u32[]{:S(2)}, u32[]{:S(2)}) collective-permute-start(bf16[2,96,768]{2,1,0:T(8,128)(2,1)} %refs_0_), channel_id=1, source_target_pairs={{0,16},{1,17},{2,18},{3,19},{4,20},{5,21},{6,22},{7,23},{8,24},{9,... | collective-permute-start | bytes 884744 | tf_op jit(solution)/shard_map/ppermute | solution.py:52
  36.8 0.8 concatenate.15.table_ref
  37.6 1.0 copy.26.slots_ref
  38.6 1.0 copy.27.segs_ref
  39.6 5.9 %embed.1 = (f32[1024,768]{1,0:T(8,128)}, bf16[1024,768]{1,0:T(8,128)(2,1)}, bf16[1024,128]{1,0:T(8,128)(2,1)}, bf16[1024,128]{1,0:T(8,128)(2,1)}, bf16[1024,128]{1,0:T(8,128)(2,1)}) custom-call(bf16[1024,768]{1,0:T(8,128)(2,1)} %tokens_ref, s32[1024,1]{1,0:T(8,128)} %copy.26.slots_ref, s32[1024,1]{1,0:T(8,128)} %copy.27.segs_ref, ...), custom_call_target="tpu_custom_call" | custom-call | tf_op jit(solution)/shard_map/embed/pallas_call | solution.py:215
  45.5 7.3 %collective-permute-done.9.refs_3_ = bf16[2,96,768]{2,1,0:T(8,128)(2,1)S(1)} collective-permute-done((bf16[2,96,768]{2,1,0:T(8,128)(2,1)}, bf16[2,96,768]{2,1,0:T(8,128)(2,1)S(1)}, u32[]{:S(2)}, u32[]{:S(2)}) %collective-permute-start.9) | collective-permute-done | bytes 294944 | tf_op jit(solution)/shard_map/ppermute | solution.py:52
  52.8 2.3 collective-permute-done.8.refs_2_
  55.1 0.8 copy-done.13
  56.3 3.3 %assemble.1.w_ref.own_ref.refs_0_ = bf16[4,768,384]{2,1,0:T(8,128)(2,1)} custom-call(s32[1]{0:T(128)} %bitcast.meta.refs_0_, bf16[4,4,48,384]{3,2,1,0:T(8,128)(2,1)} %stack_z.1.refs_0_, bf16[4,4,48,384]{3,2,1,0:T(8,128)(2,1)} %copy-done.18, bf16[4,4,48,384]{3,2,1,0:T(8,128)(2,1)} %copy-done.14, bf16[4,4,48,384]{3,2,1,0:T(8,128)(2,1)} %copy-done.13), custom_call_target="tpu_custom_call" | custom-call | tf_op jit(solution)/shard_map/assemble/pallas_call | solution.py:149
  59.7 2.3 stack_pair.1
  62.5 1.5 collective-permute-start.11
  64.0 1.5 collective-permute-start.12
  65.5 5.8 %project.2.refs_0_ = bf16[1024,2304]{1,0:T(8,128)(2,1)} custom-call(s32[1]{0:T(128)} %bitcast.meta.refs_0_, bf16[1024,768]{1,0:T(8,128)(2,1)} %get-tuple-element.170.x_ref.left_ref, bf16[4,768,384]{2,1,0:T(8,128)(2,1)} %assemble.1.w_ref.own_ref.refs_0_, f32[3,1,768]{2,1,0:T(1,128)} %broadcast_in_dim.12.b_ref), custom_call_target="tpu_custom_call" | custom-call | tf_op jit(solution)/shard_map/project/pallas_call | solution.py:169
  72.0 0.8 copy-done
  72.8 5.8 %project.3.refs_2_.refs_3_.refs_4_ = bf16[1024,2304]{1,0:T(8,128)(2,1)} custom-call(s32[1]{0:T(128)} %bitcast.meta.refs_0_, bf16[1024,768]{1,0:T(8,128)(2,1)} %get-tuple-element.170.x_ref.left_ref, bf16[4,768,384]{2,1,0:T(8,128)(2,1)} %copy-done, f32[3,1,768]{2,1,0:T(1,128)} %broadcast_in_dim.12.b_ref, ...), custom_call_target="tpu_custom_call", output_to_operand_aliasing={{}: (4, {})} | custom-call | tf_op jit(solution)/shard_map/project/pallas_call | solution.py:169
  79.2 1.3 collective-permute-done.12.refs_10_
  80.5 1.5 collective-permute-start.16
  82.5 21.1 %attention_forward.1 = (bf16[1024,768]{1,0:T(8,128)(2,1)}, f32[1024,768]{1,0:T(8,128)}) custom-call(s32[1]{0:T(128)} %bitcast.meta.refs_0_, bf16[1024,128]{1,0:T(8,128)(2,1)} %get-tuple-element.177.refs_0_, bf16[1024,128]{1,0:T(8,128)(2,1)} %get-tuple-element.178.refs_1_, bf16[1024,2304]{1,0:T(8,128)(2,1)} %project.3.refs_2_.refs_3_.refs_4_, ...), custom_call_target="tpu_custom_call" | custom-call | tf_op jit(solution)/shard_map/attention_forward/pallas_call | solution.py:572
  104.2 1.1 collective-permute-done.16.refs_8_
  105.3 1.5 collective-permute-done.18.refs_12_
  107.8 5.9 %out_projection.1 = (f32[1024,768]{1,0:T(8,128)}, bf16[1024,768]{1,0:T(8,128)(2,1)}, bf16[768,768]{1,0:T(8,128)(2,1)}) custom-call(s32[1]{0:T(128)} %bitcast.meta.refs_0_, bf16[1024,768]{1,0:T(8,128)(2,1)} %get-tuple-element.181.x_ref.mixed_ref.refs_6_, f32[1024,768]{1,0:T(8,128)} %get-tuple-element.182.start_ref, ...), custom_call_target="tpu_custom_call" | custom-call | tf_op jit(solution)/shard_map/out_projection/pallas_call | solution.py:331
  113.9 0.7 copy-done.15
  115.0 46.8 %mlp.1 = (f32[1024,768]{1,0:T(8,128)}, f32[1024,768]{1,0:T(8,128)}, f32[4,1,768]{2,1,0:T(1,128)}, bf16[2,4,4,96,768]{4,3,2,1,0:T(8,128)(2,1)}, bf16[2,4,4,96,768]{4,3,2,1,0:T(8,128)(2,1)}) custom-call(s32[1]{0:T(128)} %bitcast.meta.refs_0_, bf16[1024,768]{1,0:T(8,128)(2,1)} %get-tuple-element.185.refs_1_, bf16[1024,768]{1,0:T(8,128)(2,1)} %cot_ref.1, ...), custom_call_target="tpu_custom_call" | custom-call | tf_op jit(solution)/shard_map/mlp/pallas_call | solution.py:754
  162.2 11.0 %turn.1 = (bf16[1024,768]{1,0:T(8,128)(2,1)}, f32[1024,768]{1,0:T(8,128)}, bf16[1024,768]{1,0:T(8,128)(2,1)}, bf16[4,4,1,24,768]{4,3,2,1,0:T(8,128)(2,1)}, bf16[...) custom-call(s32[1]{0:T(128)} %bitcast.meta.refs_0_, f32[1024,768]{1,0:T(8,128)} %get-tuple-element.184.middle_ref, ...), custom_call_target="tpu_custom_call" | custom-call | tf_op jit(solution)/shard_map/turn/pallas_call | solution.py:399
  173.2 4.1 %fusion.1 = (bf16[2,4,96,768]{3,2,1,0:T(8,128)(2,1)S(1)}, bf16[2,4,96,768]{3,2,1,0:T(8,128)(2,1)}) fusion(bf16[2,4,4,96,768]{4,3,2,1,0:T(8,128)(2,1)} %collective-permute-done.25, bf16[2,4,4,96,768]{4,3,2,1,0:T(8,128)(2,1)} %get-tuple-element.201), kind=kLoop, calls=%fused_computation.3 | loop fusion | flops 4718592 | bytes 7077888 | tf_op jit(solution)/shard_map/convert_element_type | solution.py:858
  178.3 31.9 %attention_backward.1 = (bf16[1024,768]{1,0:T(8,128)(2,1)}, bf16[1024,768]{1,0:T(8,128)(2,1)}, bf16[1024,768]{1,0:T(8,128)(2,1)}) custom-call(s32[1]{0:T(128)} %bitcast.meta.refs_0_, bf16[1024,128]{1,0:T(8,128)(2,1)} %get-tuple-element.177.refs_0_, bf16[1024,128]{1,0:T(8,128)(2,1)} %get-tuple-element.178.refs_1_, ...), custom_call_target="tpu_custom_call" | custom-call | tf_op jit(solution)/shard_map/attention_backward/pallas_call | solution.py:647
  210.3 2.7 fusion.4
  213.0 1.6 collective-permute-start.29
  214.6 1.5 collective-permute-start.30
  216.1 14.2 %tail_step.1 = (f32[1024,768]{1,0:T(8,128)}, bf16[96,768]{1,0:T(8,128)(2,1)}) custom-call(s32[1]{0:T(128)} %bitcast.meta.refs_0_, f32[1024,768]{1,0:T(8,128)} %get-tuple-element.182.start_ref, f32[1024,768]{1,0:T(8,128)} %get-tuple-element.217.gmiddle_ref, bf16[1024,128]{1,0:T(8,128)(2,1)} %get-tuple-element.218.slots_ref, f32[1,768]{1,0:T(1,128)} %copy-done.35, ...), custom_call_target="tpu_custom_call" | custom-call | tf_op jit(solution)/shard_map/tail_step/pallas_call | solution.py:465
  230.4 9.0 %weight_grad_qkv.1 = (bf16[4,4,3,24,768]{4,3,2,1,0:T(8,128)(2,1)}, bf16[4,4,3,24,768]{4,3,2,1,0:T(8,128)(2,1)}) custom-call(s32[1]{0:T(128)} %bitcast.meta.refs_0_, bf16[1024,768]{1,0:T(8,128)(2,1)} %get-tuple-element.170.x_ref.left_ref, bf16[1024,768]{1,0:T(8,128)(2,1)} %get-tuple-element.234.refs_2_.refs_0_, ...), custom_call_target="tpu_custom_call" | custom-call | tf_op jit(solution)/shard_map/weight_grad_qkv/pallas_call | solution.py:494
  239.9 1.3 collective-permute-start.33
  241.2 2.2 fusion.3
  243.4 2.5 collective-permute-done.33
  247.2 4.0 %gather_sums.1 = (f32[4,4,24,768]{3,2,1,0:T(8,128)}, bf16[4,4,24,768]{3,2,1,0:T(8,128)(2,1)}, bf16[4,4,24,768]{3,2,1,0:T(8,128)(2,1)}, bf16[4,4,24,768]{3,2,1,0:T(8,128)(2,1)}) custom-call(bf16[4,4,3,24,768]{4,3,2,1,0:T(8,128)(2,1)} %get-tuple-element.243.own_ref, bf16[4,4,3,24,768]{4,3,2,1,0:T(8,128)(2,1)} %copy-done.2, ...), custom_call_target="tpu_custom_call" | custom-call | tf_op jit(solution)/shard_map/gather_sums/pallas_call | solution.py:248
  251.3 1.3 collective-permute-start.35
  252.6 1.0 collective-permute-start.36
  253.7 1.2 collective-permute-start.37
  254.9 3.3 %collective-permute-start.38 = (bf16[2,2,96,768]{3,2,1,0:T(8,128)(2,1)S(1)}, bf16[2,2,96,768]{3,2,1,0:T(8,128)(2,1)S(1)}, u32[]{:S(2)}, u32[]{:S(2)}) collective-permute-start(bf16[2,2,96,768]{3,2,1,0:T(8,128)(2,1)S(1)} %pad_maximum_fusion), channel_id=1, source_target_pairs={{0,16},{1,17},{2,18},{3,19},{4,20},{5,21},{6,22},{7,23},{8,24},{9,... | collective-permute-start | bytes 1769480 | tf_op jit(solution)/shard_map/ppermute | solution.py:52
  258.4 15.1 %collective-permute-done.39 = bf16[96,768]{1,0:T(8,128)(2,1)S(1)} collective-permute-done((bf16[96,768]{1,0:T(8,128)(2,1)S(1)}, bf16[96,768]{1,0:T(8,128)(2,1)S(1)}, u32[]{:S(2)}, u32[]{:S(2)}) %collective-permute-start.39) | collective-permute-done | bytes 147488 | tf_op jit(solution)/shard_map/ppermute | solution.py:52
  273.4 6.4 %collective-permute-done.36.refs_1_ = bf16[4,4,24,768]{3,2,1,0:T(8,128)(2,1)S(1)} collective-permute-done((bf16[4,4,24,768]{3,2,1,0:T(8,128)(2,1)}, bf16[4,4,24,768]{3,2,1,0:T(8,128)(2,1)S(1)}, u32[]{:S(2)}, u32[]{:S(2)}) %collective-permute-start.36) | collective-permute-done | bytes 589856 | tf_op jit(solution)/shard_map/ppermute | solution.py:52
  279.8 2.0 collective-permute-done.38
  282.0 3.4 %collective-permute-start.40 = (bf16[96,768]{1,0:T(8,128)(2,1)S(1)}, bf16[96,768]{1,0:T(8,128)(2,1)S(1)}, u32[]{:S(2)}, u32[]{:S(2)}) collective-permute-start(bf16[96,768]{1,0:T(8,128)(2,1)S(1)} %get-tuple-element.294), channel_id=1, source_target_pairs={{0,16},{1,17},{2,18},{3,19},{4,20},{5,21},{6,22},{7,23},{8,24},{9,... | collective-permute-start | bytes 442376 | tf_op jit(solution)/shard_map/ppermute | solution.py:52
  285.8 2.7 plane_sums.1
  288.5 2.0 collective-permute-start.42
  290.4 1.5 collective-permute-start.43
  292.0 1.0 collective-permute-start.44
  294.8 2.6 collective-permute-done.41.refs_0_
  297.4 3.7 %collective-permute-done.42.refs_1_ = bf16[4,24,768]{2,1,0:T(8,128)(2,1)S(1)} collective-permute-done((bf16[4,24,768]{2,1,0:T(8,128)(2,1)}, bf16[4,24,768]{2,1,0:T(8,128)(2,1)S(1)}, u32[]{:S(2)}, u32[]{:S(2)}) %collective-permute-start.42) | collective-permute-done | bytes 147488 | tf_op jit(solution)/shard_map/ppermute | solution.py:52
  301.1 4.2 %collective-permute-done.43.refs_2_ = bf16[4,24,768]{2,1,0:T(8,128)(2,1)S(1)} collective-permute-done((bf16[4,24,768]{2,1,0:T(8,128)(2,1)}, bf16[4,24,768]{2,1,0:T(8,128)(2,1)S(1)}, u32[]{:S(2)}, u32[]{:S(2)}) %collective-permute-start.43) | collective-permute-done | bytes 147488 | tf_op jit(solution)/shard_map/ppermute | solution.py:52
  306.1 1.9 line_sums.1
  308.6 0.7 slice_add_fusion.6
  309.3 0.9 maximum_add_fusion
  (181 shorter events, 17.2 us)
Async XLA Ops:
  0.6 27.1 %copy-start.39 = (f32[768]{0:T(1024)S(1)}, f32[768]{0:T(1024)}, u32[]{:S(2)}) copy-start(f32[768]{0:T(1024)} %param.25) | copy-start | bytes 9220
  0.7 27.7 %copy-start.1 = (bf16[1024,768]{1,0:T(8,128)(2,1)S(1)}, bf16[1024,768]{1,0:T(8,128)(2,1)}, u32[]{:S(2)}) copy-start(bf16[1024,768]{1,0:T(8,128)(2,1)} %cot_ref.1) | copy-start | bytes 4718596
  2.4 1.7 collective-permute-start
  2.4 21.8 %collective-permute-start.4 = (bf16[2,96,768]{2,1,0:T(8,128)(2,1)}, bf16[2,96,768]{2,1,0:T(8,128)(2,1)}, u32[]{:S(2)}, u32[]{:S(2)}) collective-permute-start(bf16[2,96,768]{2,1,0:T(8,128)(2,1)} %refs_0_), channel_id=1, source_target_pairs={{0,8},{1,9},{2,10},{3,11},{4,12},{5,13},{6,14},{7,15},{8,0},{9,1},... | collective-permute-start | bytes 884744 | tf_op jit(solution)/shard_map/ppermute | solution.py:52
  6.3 13.2 %collective-permute-start.3 = (bf16[4,48,384]{2,1,0:T(8,128)(2,1)}, bf16[4,48,384]{2,1,0:T(8,128)(2,1)S(1)}, u32[]{:S(2)}, u32[]{:S(2)}) collective-permute-start(bf16[4,48,384]{2,1,0:T(8,128)(2,1)} %join.1.refs_0_), channel_id=1, source_target_pairs={{0,24},{1,25},{2,26},{3,27},{4,28},{5,29},{6,30},{7,31},{8,16},{9,... | collective-permute-start | bytes 442376 | tf_op jit(solution)/shard_map/ppermute | solution.py:52
  6.5 13.3 %collective-permute-start.2 = (bf16[4,48,384]{2,1,0:T(8,128)(2,1)}, bf16[4,48,384]{2,1,0:T(8,128)(2,1)S(1)}, u32[]{:S(2)}, u32[]{:S(2)}) collective-permute-start(bf16[4,48,384]{2,1,0:T(8,128)(2,1)} %join.1.refs_0_), channel_id=1, source_target_pairs={{0,16},{1,17},{2,18},{3,19},{4,20},{5,21},{6,22},{7,23},{8,24},{9,... | collective-permute-start | bytes 442376 | tf_op jit(solution)/shard_map/ppermute | solution.py:52
  10.0 11.5 %collective-permute-start.1 = (bf16[4,48,384]{2,1,0:T(8,128)(2,1)}, bf16[4,48,384]{2,1,0:T(8,128)(2,1)S(1)}, u32[]{:S(2)}, u32[]{:S(2)}) collective-permute-start(bf16[4,48,384]{2,1,0:T(8,128)(2,1)} %join.1.refs_0_), channel_id=1, source_target_pairs={{0,8},{1,9},{2,10},{3,11},{4,12},{5,13},{6,14},{7,15},{8,0},{9,1},... | collective-permute-start | bytes 442376 | tf_op jit(solution)/shard_map/ppermute | solution.py:52
  24.1 30.9 %collective-permute-start.7 = (bf16[4,4,48,384]{3,2,1,0:T(8,128)(2,1)}, bf16[4,4,48,384]{3,2,1,0:T(8,128)(2,1)S(1)}, u32[]{:S(2)}, u32[]{:S(2)}) collective-permute-start(bf16[4,4,48,384]{3,2,1,0:T(8,128)(2,1)} %stack_z.1.refs_0_), channel_id=1, source_target_pairs={{0,6},{1,7},{2,4},{3,5},{4,2},{5,3},{6,0},{7,1},{8,14},{9,15},{10,... | collective-permute-start | bytes 1769480 | tf_op jit(solution)/shard_map/ppermute | solution.py:52
  26.6 28.5 %collective-permute-start.6 = (bf16[4,4,48,384]{3,2,1,0:T(8,128)(2,1)}, bf16[4,4,48,384]{3,2,1,0:T(8,128)(2,1)S(1)}, u32[]{:S(2)}, u32[]{:S(2)}) collective-permute-start(bf16[4,4,48,384]{3,2,1,0:T(8,128)(2,1)} %stack_z.1.refs_0_), channel_id=1, source_target_pairs={{0,4},{1,5},{2,6},{3,7},{4,0},{5,1},{6,2},{7,3},{8,12},{9,13},{10,... | collective-permute-start | bytes 1769480 | tf_op jit(solution)/shard_map/ppermute | solution.py:52
  27.1 28.0 %collective-permute-start.5 = (bf16[4,4,48,384]{3,2,1,0:T(8,128)(2,1)}, bf16[4,4,48,384]{3,2,1,0:T(8,128)(2,1)S(1)}, u32[]{:S(2)}, u32[]{:S(2)}) collective-permute-start(bf16[4,4,48,384]{3,2,1,0:T(8,128)(2,1)} %stack_z.1.refs_0_), channel_id=1, source_target_pairs={{0,2},{1,3},{2,0},{3,1},{4,6},{5,7},{6,4},{7,5},{8,10},{9,11},{10,... | collective-permute-start | bytes 1769480 | tf_op jit(solution)/shard_map/ppermute | solution.py:52
  28.3 8.5 %copy-start.26 = (f32[50,768]{1,0:T(8,128)S(1)}, f32[50,768]{1,0:T(8,128)}, u32[]{:S(2)}) copy-start(f32[50,768]{1,0:T(8,128)} %param.15) | copy-start | bytes 460804
  28.3 9.3 %copy-start.37 = (s32[1024]{0:T(1024)S(1)}, s32[1024]{0:T(1024)}, u32[]{:S(2)}) copy-start(s32[1024]{0:T(1024)} %param.17) | copy-start | bytes 12292
  28.3 10.3 %copy-start.38 = (s32[1024]{0:T(1024)S(1)}, s32[1024]{0:T(1024)}, u32[]{:S(2)}) copy-start(s32[1024]{0:T(1024)} %param.16) | copy-start | bytes 12292
  30.0 15.5 %copy-start.35 = (f32[1,768]{1,0:T(1,128)}, f32[1,768]{1,0:T(1,128)S(1)}, u32[]{:S(2)}) copy-start(f32[1,768]{1,0:T(1,128)S(1)} %get-tuple-element.301.p_ref) | copy-start | bytes 9220
  30.0 22.8 %collective-permute-start.9 = (bf16[2,96,768]{2,1,0:T(8,128)(2,1)}, bf16[2,96,768]{2,1,0:T(8,128)(2,1)S(1)}, u32[]{:S(2)}, u32[]{:S(2)}) collective-permute-start(bf16[2,96,768]{2,1,0:T(8,128)(2,1)} %refs_0_), channel_id=1, source_target_pairs={{0,24},{1,25},{2,26},{3,27},{4,28},{5,29},{6,30},{7,31},{8,16},{9,... | collective-permute-start | bytes 884744 | tf_op jit(solution)/shard_map/ppermute | solution.py:52
  30.8 24.3 %collective-permute-start.8 = (bf16[2,96,768]{2,1,0:T(8,128)(2,1)}, bf16[2,96,768]{2,1,0:T(8,128)(2,1)S(1)}, u32[]{:S(2)}, u32[]{:S(2)}) collective-permute-start(bf16[2,96,768]{2,1,0:T(8,128)(2,1)} %refs_0_), channel_id=1, source_target_pairs={{0,16},{1,17},{2,18},{3,19},{4,20},{5,21},{6,22},{7,23},{8,24},{9,... | collective-permute-start | bytes 884744 | tf_op jit(solution)/shard_map/ppermute | solution.py:52
  52.8 6.9 %copy-start.24 = (bf16[2,96,768]{2,1,0:T(8,128)(2,1)}, bf16[2,96,768]{2,1,0:T(8,128)(2,1)S(1)}, u32[]{:S(2)}) copy-start(bf16[2,96,768]{2,1,0:T(8,128)(2,1)S(1)} %collective-permute-done.9.refs_3_) | copy-start | bytes 884740
  55.1 4.6 %copy-start.25 = (bf16[2,96,768]{2,1,0:T(8,128)(2,1)}, bf16[2,96,768]{2,1,0:T(8,128)(2,1)S(1)}, u32[]{:S(2)}) copy-start(bf16[2,96,768]{2,1,0:T(8,128)(2,1)S(1)} %collective-permute-done.8.refs_2_) | copy-start | bytes 884740
  62.0 9.4 %copy-start.6 = (bf16[4,96,768]{2,1,0:T(8,128)(2,1)S(1)}, bf16[4,96,768]{2,1,0:T(8,128)(2,1)}, u32[]{:S(2)}) copy-start(bf16[4,96,768]{2,1,0:T(8,128)(2,1)} %get-tuple-element.168.refs_5_) | copy-start | bytes 1769476
  62.0 9.4 %collective-permute-start.15 = (bf16[4,768,384]{2,1,0:T(8,128)(2,1)}, bf16[4,768,384]{2,1,0:T(8,128)(2,1)S(1)}, u32[]{:S(2)}, u32[]{:S(2)}) collective-permute-start(bf16[4,768,384]{2,1,0:T(8,128)(2,1)} %assemble.1.w_ref.own_ref.refs_0_), channel_id=1, source_target_pairs={{0,1},{1,0},{2,3},{3,2},{4,5},{5,4},{6,7},{7,6},{8,9},{9,8},{10,11... | collective-permute-start | bytes 7077896 | tf_op jit(solution)/shard_map/ppermute | solution.py:52
  62.0 16.6 %collective-permute-start.13 = (bf16[4,96,768]{2,1,0:T(8,128)(2,1)}, bf16[4,96,768]{2,1,0:T(8,128)(2,1)S(1)}, u32[]{:S(2)}, u32[]{:S(2)}) collective-permute-start(bf16[4,96,768]{2,1,0:T(8,128)(2,1)} %get-tuple-element.168.refs_5_), channel_id=1, source_target_pairs={{0,1},{1,0},{2,3},{3,2},{4,5},{5,4},{6,7},{7,6},{8,9},{9,8},{10,11... | collective-permute-start | bytes 1769480 | tf_op jit(solution)/shard_map/ppermute | solution.py:52
  62.5 16.7 %collective-permute-start.11 = (bf16[4,96,768]{2,1,0:T(8,128)(2,1)}, bf16[4,96,768]{2,1,0:T(8,128)(2,1)}, u32[]{:S(2)}, u32[]{:S(2)}) collective-permute-start(bf16[4,96,768]{2,1,0:T(8,128)(2,1)} %get-tuple-element.168.refs_5_), channel_id=1, source_target_pairs={{0,4},{1,5},{2,6},{3,7},{4,0},{5,1},{6,2},{7,3},{8,12},{9,13},{10,... | collective-permute-start | bytes 1769480 | tf_op jit(solution)/shard_map/ppermute | solution.py:52
  64.0 15.2 %collective-permute-start.14 = (bf16[4,96,768]{2,1,0:T(8,128)(2,1)}, bf16[4,96,768]{2,1,0:T(8,128)(2,1)}, u32[]{:S(2)}, u32[]{:S(2)}) collective-permute-start(bf16[4,96,768]{2,1,0:T(8,128)(2,1)} %get-tuple-element.169.refs_9_), channel_id=1, source_target_pairs={{0,1},{1,0},{2,3},{3,2},{4,5},{5,4},{6,7},{7,6},{8,9},{9,8},{10,11... | collective-permute-start | bytes 1769480 | tf_op jit(solution)/shard_map/ppermute | solution.py:52
  64.0 16.5 %collective-permute-start.12 = (bf16[4,96,768]{2,1,0:T(8,128)(2,1)}, bf16[4,96,768]{2,1,0:T(8,128)(2,1)}, u32[]{:S(2)}, u32[]{:S(2)}) collective-permute-start(bf16[4,96,768]{2,1,0:T(8,128)(2,1)} %get-tuple-element.169.refs_9_), channel_id=1, source_target_pairs={{0,2},{1,3},{2,0},{3,1},{4,6},{5,7},{6,4},{7,5},{8,10},{9,11},{10,... | collective-permute-start | bytes 1769480 | tf_op jit(solution)/shard_map/ppermute | solution.py:52
  71.4 7.2 %copy-start.7 = (bf16[4,96,768]{2,1,0:T(8,128)(2,1)S(1)}, bf16[4,96,768]{2,1,0:T(8,128)(2,1)}, u32[]{:S(2)}) copy-start(bf16[4,96,768]{2,1,0:T(8,128)(2,1)} %get-tuple-element.169.refs_9_) | copy-start | bytes 1769476
  71.4 32.2 %collective-permute-start.10 = (bf16[4,96,768]{2,1,0:T(8,128)(2,1)S(1)}, bf16[4,96,768]{2,1,0:T(8,128)(2,1)}, u32[]{:S(2)}, u32[]{:S(2)}) collective-permute-start(bf16[4,96,768]{2,1,0:T(8,128)(2,1)S(1)} %copy-done.6), channel_id=1, source_target_pairs={{0,2},{1,3},{2,0},{3,1},{4,6},{5,7},{6,4},{7,5},{8,10},{9,11},{10,... | collective-permute-start | bytes 1769480 | tf_op jit(solution)/shard_map/ppermute | solution.py:52
  78.6 25.0 %copy-start.8 = (bf16[4,96,768]{2,1,0:T(8,128)(2,1)}, bf16[4,96,768]{2,1,0:T(8,128)(2,1)S(1)}, u32[]{:S(2)}) copy-start(bf16[4,96,768]{2,1,0:T(8,128)(2,1)S(1)} %collective-permute-done.13.refs_13_) | copy-start | bytes 1769476
  78.6 25.5 %collective-permute-start.17 = (bf16[4,96,768]{2,1,0:T(8,128)(2,1)S(1)}, bf16[4,96,768]{2,1,0:T(8,128)(2,1)S(1)}, u32[]{:S(2)}, u32[]{:S(2)}) collective-permute-start(bf16[4,96,768]{2,1,0:T(8,128)(2,1)S(1)} %copy-done.7), channel_id=1, source_target_pairs={{0,4},{1,5},{2,6},{3,7},{4,0},{5,1},{6,2},{7,3},{8,12},{9,13},{10,... | collective-permute-start | bytes 1769480 | tf_op jit(solution)/shard_map/ppermute | solution.py:52
  80.5 24.7 %collective-permute-start.16 = (bf16[4,96,768]{2,1,0:T(8,128)(2,1)}, bf16[4,96,768]{2,1,0:T(8,128)(2,1)S(1)}, u32[]{:S(2)}, u32[]{:S(2)}) collective-permute-start(bf16[4,96,768]{2,1,0:T(8,128)(2,1)} %collective-permute-done.11.refs_7_), channel_id=1, source_target_pairs={{0,2},{1,3},{2,0},{3,1},{4,6},{5,7},{6,4},{7,5},{8,10},{9,11},{10,... | collective-permute-start | bytes 1769480 | tf_op jit(solution)/shard_map/ppermute | solution.py:52
  82.0 24.8 %collective-permute-start.18 = (bf16[4,96,768]{2,1,0:T(8,128)(2,1)}, bf16[4,96,768]{2,1,0:T(8,128)(2,1)S(1)}, u32[]{:S(2)}, u32[]{:S(2)}) collective-permute-start(bf16[4,96,768]{2,1,0:T(8,128)(2,1)} %collective-permute-done.12.refs_10_), channel_id=1, source_target_pairs={{0,4},{1,5},{2,6},{3,7},{4,0},{5,1},{6,2},{7,3},{8,12},{9,13},{10,... | collective-permute-start | bytes 1769480 | tf_op jit(solution)/shard_map/ppermute | solution.py:52
  82.5 24.8 %collective-permute-start.20 = (bf16[4,96,768]{2,1,0:T(8,128)(2,1)}, bf16[4,96,768]{2,1,0:T(8,128)(2,1)S(1)}, u32[]{:S(2)}, u32[]{:S(2)}) collective-permute-start(bf16[4,96,768]{2,1,0:T(8,128)(2,1)} %collective-permute-done.11.refs_7_), channel_id=1, source_target_pairs={{0,1},{1,0},{2,3},{3,2},{4,5},{5,4},{6,7},{7,6},{8,9},{9,8},{10,11... | collective-permute-start | bytes 1769480 | tf_op jit(solution)/shard_map/ppermute | solution.py:52
  103.6 10.2 %collective-permute-start.22 = (bf16[4,96,768]{2,1,0:T(8,128)(2,1)}, bf16[4,96,768]{2,1,0:T(8,128)(2,1)S(1)}, u32[]{:S(2)}, u32[]{:S(2)}) collective-permute-start(bf16[4,96,768]{2,1,0:T(8,128)(2,1)} %collective-permute-done.12.refs_10_), channel_id=1, source_target_pairs={{0,1},{1,0},{2,3},{3,2},{4,5},{5,4},{6,7},{7,6},{8,9},{9,8},{10,11... | collective-permute-start | bytes 1769480 | tf_op jit(solution)/shard_map/ppermute | solution.py:52
  104.2 9.6 %copy-start.9 = (bf16[4,96,768]{2,1,0:T(8,128)(2,1)}, bf16[4,96,768]{2,1,0:T(8,128)(2,1)S(1)}, u32[]{:S(2)}) copy-start(bf16[4,96,768]{2,1,0:T(8,128)(2,1)S(1)} %collective-permute-done.17.refs_11_) | copy-start | bytes 1769476
  105.3 8.5 %copy-start.10 = (bf16[4,96,768]{2,1,0:T(8,128)(2,1)}, bf16[4,96,768]{2,1,0:T(8,128)(2,1)S(1)}, u32[]{:S(2)}) copy-start(bf16[4,96,768]{2,1,0:T(8,128)(2,1)S(1)} %collective-permute-done.16.refs_8_) | copy-start | bytes 1769476
  106.8 7.0 %copy-start.11 = (bf16[4,96,768]{2,1,0:T(8,128)(2,1)}, bf16[4,96,768]{2,1,0:T(8,128)(2,1)S(1)}, u32[]{:S(2)}) copy-start(bf16[4,96,768]{2,1,0:T(8,128)(2,1)S(1)} %collective-permute-done.18.refs_12_) | copy-start | bytes 1769476
  106.8 7.0 %collective-permute-start.19 = (bf16[4,96,768]{2,1,0:T(8,128)(2,1)}, bf16[4,96,768]{2,1,0:T(8,128)(2,1)S(1)}, u32[]{:S(2)}, u32[]{:S(2)}) collective-permute-start(bf16[4,96,768]{2,1,0:T(8,128)(2,1)} %collective-permute-done.10.refs_6_), channel_id=1, source_target_pairs={{0,1},{1,0},{2,3},{3,2},{4,5},{5,4},{6,7},{7,6},{8,9},{9,8},{10,11... | collective-permute-start | bytes 1769480 | tf_op jit(solution)/shard_map/ppermute | solution.py:52
  106.8 7.0 %collective-permute-start.21 = (bf16[4,96,768]{2,1,0:T(8,128)(2,1)S(1)}, bf16[4,96,768]{2,1,0:T(8,128)(2,1)S(1)}, u32[]{:S(2)}, u32[]{:S(2)}) collective-permute-start(bf16[4,96,768]{2,1,0:T(8,128)(2,1)S(1)} %collective-permute-done.16.refs_8_), channel_id=1, source_target_pairs={{0,1},{1,0},{2,3},{3,2},{4,5},{5,4},{6,7},{7,6},{8,9},{9,8},{10,11... | collective-permute-start | bytes 1769480 | tf_op jit(solution)/shard_map/ppermute | solution.py:52
  107.3 6.5 %collective-permute-start.23 = (bf16[4,96,768]{2,1,0:T(8,128)(2,1)S(1)}, bf16[4,96,768]{2,1,0:T(8,128)(2,1)}, u32[]{:S(2)}, u32[]{:S(2)}) collective-permute-start(bf16[4,96,768]{2,1,0:T(8,128)(2,1)S(1)} %collective-permute-done.17.refs_11_), channel_id=1, source_target_pairs={{0,1},{1,0},{2,3},{3,2},{4,5},{5,4},{6,7},{7,6},{8,9},{9,8},{10,11... | collective-permute-start | bytes 1769480 | tf_op jit(solution)/shard_map/ppermute | solution.py:52
  107.3 6.5 %copy-start.12 = (bf16[4,96,768]{2,1,0:T(8,128)(2,1)}, bf16[4,96,768]{2,1,0:T(8,128)(2,1)S(1)}, u32[]{:S(2)}) copy-start(bf16[4,96,768]{2,1,0:T(8,128)(2,1)S(1)} %collective-permute-done.20.refs_15_) | copy-start | bytes 1769476
  107.3 6.5 %collective-permute-start.24 = (bf16[4,96,768]{2,1,0:T(8,128)(2,1)S(1)}, bf16[4,96,768]{2,1,0:T(8,128)(2,1)}, u32[]{:S(2)}, u32[]{:S(2)}) collective-permute-start(bf16[4,96,768]{2,1,0:T(8,128)(2,1)S(1)} %collective-permute-done.18.refs_12_), channel_id=1, source_target_pairs={{0,1},{1,0},{2,3},{3,2},{4,5},{5,4},{6,7},{7,6},{8,9},{9,8},{10,11... | collective-permute-start | bytes 1769480 | tf_op jit(solution)/shard_map/ppermute | solution.py:52
  161.9 11.3 %collective-permute-start.25 = (bf16[2,4,4,96,768]{4,3,2,1,0:T(8,128)(2,1)}, bf16[2,4,4,96,768]{4,3,2,1,0:T(8,128)(2,1)}, u32[]{:S(2)}, u32[]{:S(2)}) collective-permute-start(bf16[2,4,4,96,768]{4,3,2,1,0:T(8,128)(2,1)} %get-tuple-element.202), channel_id=1, source_target_pairs={{0,1},{1,0},{2,3},{3,2},{4,5},{5,4},{6,7},{7,6},{8,9},{9,8},{10,11... | collective-permute-start | bytes 14155784 | tf_op jit(solution)/shard_map/ppermute | solution.py:52
  177.3 33.0 %collective-permute-start.26 = (bf16[2,4,96,768]{3,2,1,0:T(8,128)(2,1)}, bf16[2,4,96,768]{3,2,1,0:T(8,128)(2,1)S(1)}, u32[]{:S(2)}, u32[]{:S(2)}) collective-permute-start(bf16[2,4,96,768]{3,2,1,0:T(8,128)(2,1)} %get-tuple-element.208), channel_id=1, source_target_pairs={{0,2},{1,3},{2,0},{3,1},{4,6},{5,7},{6,4},{7,5},{8,10},{9,11},{10,... | collective-permute-start | bytes 3538952 | tf_op jit(solution)/shard_map/ppermute | solution.py:52
  177.8 32.5 %collective-permute-start.27 = (bf16[2,4,96,768]{3,2,1,0:T(8,128)(2,1)S(1)}, bf16[2,4,96,768]{3,2,1,0:T(8,128)(2,1)S(1)}, u32[]{:S(2)}, u32[]{:S(2)}) collective-permute-start(bf16[2,4,96,768]{3,2,1,0:T(8,128)(2,1)S(1)} %get-tuple-element.209), channel_id=1, source_target_pairs={{0,4},{1,5},{2,6},{3,7},{4,0},{5,1},{6,2},{7,3},{8,12},{9,13},{10,... | collective-permute-start | bytes 3538952 | tf_op jit(solution)/shard_map/ppermute | solution.py:52
  178.3 32.0 %collective-permute-start.28 = (bf16[4,4,1,24,768]{4,3,2,1,0:T(8,128)(2,1)}, bf16[4,4,1,24,768]{4,3,2,1,0:T(8,128)(2,1)S(1)}, u32[]{:S(2)}, u32[]{:S(2)}) collective-permute-start(bf16[4,4,1,24,768]{4,3,2,1,0:T(8,128)(2,1)} %get-tuple-element.210), channel_id=1, source_target_pairs={{0,1},{1,0},{2,3},{3,2},{4,5},{5,4},{6,7},{7,6},{8,9},{9,8},{10,11... | collective-permute-start | bytes 1769480 | tf_op jit(solution)/shard_map/ppermute | solution.py:52
  213.0 17.2 %collective-permute-start.29 = (bf16[4,96,768]{2,1,0:T(8,128)(2,1)S(1)}, bf16[4,96,768]{2,1,0:T(8,128)(2,1)S(1)}, u32[]{:S(2)}, u32[]{:S(2)}) collective-permute-start(bf16[4,96,768]{2,1,0:T(8,128)(2,1)S(1)} %get-tuple-element.231), channel_id=1, source_target_pairs={{0,4},{1,5},{2,6},{3,7},{4,0},{5,1},{6,2},{7,3},{8,12},{9,13},{10,... | collective-permute-start | bytes 1769480 | tf_op jit(solution)/shard_map/ppermute | solution.py:52
  214.6 15.7 %collective-permute-start.30 = (bf16[4,96,768]{2,1,0:T(8,128)(2,1)S(1)}, bf16[4,96,768]{2,1,0:T(8,128)(2,1)S(1)}, u32[]{:S(2)}, u32[]{:S(2)}) collective-permute-start(bf16[4,96,768]{2,1,0:T(8,128)(2,1)S(1)} %get-tuple-element.232), channel_id=1, source_target_pairs={{0,2},{1,3},{2,0},{3,1},{4,6},{5,7},{6,4},{7,5},{8,10},{9,11},{10,... | collective-permute-start | bytes 1769480 | tf_op jit(solution)/shard_map/ppermute | solution.py:52
  230.3 9.1 %copy-start.16 = (bf16[4,96,768]{2,1,0:T(8,128)(2,1)}, bf16[4,96,768]{2,1,0:T(8,128)(2,1)S(1)}, u32[]{:S(2)}) copy-start(bf16[4,96,768]{2,1,0:T(8,128)(2,1)S(1)} %collective-permute-done.30) | copy-start | bytes 1769476
  230.3 9.5 %copy-start.30 = (bf16[96,768]{1,0:T(8,128)(2,1)S(1)}, bf16[96,768]{1,0:T(8,128)(2,1)}, u32[]{:S(2)}) copy-start(bf16[96,768]{1,0:T(8,128)(2,1)} %get-tuple-element.233) | copy-start | bytes 442372
  230.3 9.1 %collective-permute-start.31 = (bf16[96,768]{1,0:T(8,128)(2,1)}, bf16[96,768]{1,0:T(8,128)(2,1)S(1)}, u32[]{:S(2)}, u32[]{:S(2)}) collective-permute-start(bf16[96,768]{1,0:T(8,128)(2,1)} %get-tuple-element.233), channel_id=1, source_target_pairs={{0,1},{1,0},{2,3},{3,2},{4,5},{5,4},{6,7},{7,6},{8,9},{9,8},{10,11... | collective-permute-start | bytes 442376 | tf_op jit(solution)/shard_map/ppermute | solution.py:52
  239.4 6.5 %collective-permute-start.32 = (bf16[4,4,3,24,768]{4,3,2,1,0:T(8,128)(2,1)}, bf16[4,4,3,24,768]{4,3,2,1,0:T(8,128)(2,1)S(1)}, u32[]{:S(2)}, u32[]{:S(2)}) collective-permute-start(bf16[4,4,3,24,768]{4,3,2,1,0:T(8,128)(2,1)} %get-tuple-element.244), channel_id=1, source_target_pairs={{0,1},{1,0},{2,3},{3,2},{4,5},{5,4},{6,7},{7,6},{8,9},{9,8},{10,11... | collective-permute-start | bytes 5308424 | tf_op jit(solution)/shard_map/ppermute | solution.py:52
  239.9 6.0 %collective-permute-start.33 = (bf16[96,768]{1,0:T(8,128)(2,1)S(1)}, bf16[96,768]{1,0:T(8,128)(2,1)S(1)}, u32[]{:S(2)}, u32[]{:S(2)}) collective-permute-start(bf16[96,768]{1,0:T(8,128)(2,1)S(1)} %pad_maximum_fusion.2), channel_id=1, source_target_pairs={{0,2},{1,3},{2,0},{3,1},{4,6},{5,7},{6,4},{7,5},{8,10},{9,11},{10,... | collective-permute-start | bytes 442376 | tf_op jit(solution)/shard_map/ppermute | solution.py:52
  246.1 5.2 %collective-permute-start.34 = (bf16[96,768]{1,0:T(8,128)(2,1)S(1)}, bf16[96,768]{1,0:T(8,128)(2,1)S(1)}, u32[]{:S(2)}, u32[]{:S(2)}) collective-permute-start(bf16[96,768]{1,0:T(8,128)(2,1)S(1)} %pad_maximum_fusion.3), channel_id=1, source_target_pairs={{0,4},{1,5},{2,6},{3,7},{4,0},{5,1},{6,2},{7,3},{8,12},{9,13},{10,... | collective-permute-start | bytes 442376 | tf_op jit(solution)/shard_map/ppermute | solution.py:52
  251.3 22.1 %collective-permute-start.35 = (bf16[4,4,24,768]{3,2,1,0:T(8,128)(2,1)}, bf16[4,4,24,768]{3,2,1,0:T(8,128)(2,1)S(1)}, u32[]{:S(2)}, u32[]{:S(2)}) collective-permute-start(bf16[4,4,24,768]{3,2,1,0:T(8,128)(2,1)} %get-tuple-element.254), channel_id=1, source_target_pairs={{0,2},{1,3},{2,0},{3,1},{4,6},{5,7},{6,4},{7,5},{8,10},{9,11},{10,... | collective-permute-start | bytes 1769480 | tf_op jit(solution)/shard_map/ppermute | solution.py:52
  252.6 27.2 %collective-permute-start.36 = (bf16[4,4,24,768]{3,2,1,0:T(8,128)(2,1)}, bf16[4,4,24,768]{3,2,1,0:T(8,128)(2,1)S(1)}, u32[]{:S(2)}, u32[]{:S(2)}) collective-permute-start(bf16[4,4,24,768]{3,2,1,0:T(8,128)(2,1)} %get-tuple-element.255), channel_id=1, source_target_pairs={{0,4},{1,5},{2,6},{3,7},{4,0},{5,1},{6,2},{7,3},{8,12},{9,13},{10,... | collective-permute-start | bytes 1769480 | tf_op jit(solution)/shard_map/ppermute | solution.py:52
  253.7 26.2 %collective-permute-start.37 = (bf16[4,4,24,768]{3,2,1,0:T(8,128)(2,1)}, bf16[4,4,24,768]{3,2,1,0:T(8,128)(2,1)S(1)}, u32[]{:S(2)}, u32[]{:S(2)}) collective-permute-start(bf16[4,4,24,768]{3,2,1,0:T(8,128)(2,1)} %get-tuple-element.256), channel_id=1, source_target_pairs={{0,6},{1,7},{2,4},{3,5},{4,2},{5,3},{6,0},{7,1},{8,14},{9,15},{10,... | collective-permute-start | bytes 1769480 | tf_op jit(solution)/shard_map/ppermute | solution.py:52
  254.9 27.0 %collective-permute-start.38 = (bf16[2,2,96,768]{3,2,1,0:T(8,128)(2,1)S(1)}, bf16[2,2,96,768]{3,2,1,0:T(8,128)(2,1)S(1)}, u32[]{:S(2)}, u32[]{:S(2)}) collective-permute-start(bf16[2,2,96,768]{3,2,1,0:T(8,128)(2,1)S(1)} %pad_maximum_fusion), channel_id=1, source_target_pairs={{0,16},{1,17},{2,18},{3,19},{4,20},{5,21},{6,22},{7,23},{8,24},{9,... | collective-permute-start | bytes 1769480 | tf_op jit(solution)/shard_map/ppermute | solution.py:52
  258.2 15.2 %collective-permute-start.39 = (bf16[96,768]{1,0:T(8,128)(2,1)S(1)}, bf16[96,768]{1,0:T(8,128)(2,1)S(1)}, u32[]{:S(2)}, u32[]{:S(2)}) collective-permute-start(bf16[96,768]{1,0:T(8,128)(2,1)S(1)} %pad_maximum_fusion.4), channel_id=1, source_target_pairs={{0,8},{1,9},{2,10},{3,11},{4,12},{5,13},{6,14},{7,15},{8,0},{9,1},... | collective-permute-start | bytes 442376 | tf_op jit(solution)/shard_map/ppermute | solution.py:52
  273.4 12.2 %copy-start.21 = (bf16[4,4,24,768]{3,2,1,0:T(8,128)(2,1)}, bf16[4,4,24,768]{3,2,1,0:T(8,128)(2,1)S(1)}, u32[]{:S(2)}) copy-start(bf16[4,4,24,768]{3,2,1,0:T(8,128)(2,1)S(1)} %collective-permute-done.35.refs_0_) | copy-start | bytes 1769476
  282.0 10.9 %collective-permute-start.40 = (bf16[96,768]{1,0:T(8,128)(2,1)S(1)}, bf16[96,768]{1,0:T(8,128)(2,1)S(1)}, u32[]{:S(2)}, u32[]{:S(2)}) collective-permute-start(bf16[96,768]{1,0:T(8,128)(2,1)S(1)} %get-tuple-element.294), channel_id=1, source_target_pairs={{0,16},{1,17},{2,18},{3,19},{4,20},{5,21},{6,22},{7,23},{8,24},{9,... | collective-permute-start | bytes 442376 | tf_op jit(solution)/shard_map/ppermute | solution.py:52
  288.5 9.0 %collective-permute-start.41 = (bf16[4,24,768]{2,1,0:T(8,128)(2,1)}, bf16[4,24,768]{2,1,0:T(8,128)(2,1)S(1)}, u32[]{:S(2)}, u32[]{:S(2)}) collective-permute-start(bf16[4,24,768]{2,1,0:T(8,128)(2,1)} %get-tuple-element.271), channel_id=1, source_target_pairs={{0,8},{1,9},{2,10},{3,11},{4,12},{5,13},{6,14},{7,15},{8,0},{9,1},... | collective-permute-start | bytes 442376 | tf_op jit(solution)/shard_map/ppermute | solution.py:52
  288.5 12.7 %collective-permute-start.42 = (bf16[4,24,768]{2,1,0:T(8,128)(2,1)}, bf16[4,24,768]{2,1,0:T(8,128)(2,1)S(1)}, u32[]{:S(2)}, u32[]{:S(2)}) collective-permute-start(bf16[4,24,768]{2,1,0:T(8,128)(2,1)} %get-tuple-element.272), channel_id=1, source_target_pairs={{0,16},{1,17},{2,18},{3,19},{4,20},{5,21},{6,22},{7,23},{8,24},{9,... | collective-permute-start | bytes 442376 | tf_op jit(solution)/shard_map/ppermute | solution.py:52
  290.4 15.0 %collective-permute-start.43 = (bf16[4,24,768]{2,1,0:T(8,128)(2,1)}, bf16[4,24,768]{2,1,0:T(8,128)(2,1)S(1)}, u32[]{:S(2)}, u32[]{:S(2)}) collective-permute-start(bf16[4,24,768]{2,1,0:T(8,128)(2,1)} %get-tuple-element.273), channel_id=1, source_target_pairs={{0,24},{1,25},{2,26},{3,27},{4,28},{5,29},{6,30},{7,31},{8,16},{9,... | collective-permute-start | bytes 442376 | tf_op jit(solution)/shard_map/ppermute | solution.py:52
  292.0 17.3 %collective-permute-start.44 = (bf16[2,96,768]{2,1,0:T(8,128)(2,1)S(1)}, bf16[2,96,768]{2,1,0:T(8,128)(2,1)S(1)}, u32[]{:S(2)}, u32[]{:S(2)}) collective-permute-start(bf16[2,96,768]{2,1,0:T(8,128)(2,1)S(1)} %pad_maximum_fusion.1), channel_id=1, source_target_pairs={{0,8},{1,9},{2,10},{3,11},{4,12},{5,13},{6,14},{7,15},{8,0},{9,1},... | collective-permute-start | bytes 884744 | tf_op jit(solution)/shard_map/ppermute | solution.py:52
  297.4 8.0 %copy-start.31 = (bf16[4,24,768]{2,1,0:T(8,128)(2,1)}, bf16[4,24,768]{2,1,0:T(8,128)(2,1)S(1)}, u32[]{:S(2)}) copy-start(bf16[4,24,768]{2,1,0:T(8,128)(2,1)S(1)} %collective-permute-done.41.refs_0_) | copy-start | bytes 442372
  (21 other events, 33.6 us)
